TPU v7x, 32 devices: a whole 2x2x4 slice. The times are simulated.
32 devices in a mesh: seq: 8 (over z, x), head: 4 (over y, core).
Axes of the slice: x: 2, y: 2, z: 4, core: 2. Of those that a mesh axis runs over, the one named last changes fastest.
Arguments:
- queries: bfloat16 [2048, 4096], P('seq', 'head'), may hold values from -48 to 48
- key_rows: bfloat16 [2048, 4096], P('seq', 'head'), may hold values from -4 to 4
- value_rows: bfloat16 [2048, 4096], P('seq', 'head'), may hold values from -6 to 6
- out_grad: bfloat16 [2048, 2048], P('seq', 'head'), may hold values from -6 to 6
- out_proj: bfloat16 [4096, 2048], P('head'), may hold values from -0.125 to 0.125
- section_table: int32 [32, 3], P('head'), may hold values 0 or 1
- block_active: int32 [8, 3], P('seq'), may hold values 0 or 1
Outputs:
- query_grad: bfloat16 [2048, 4096], P('seq', 'head')
- key_grad: bfloat16 [2048, 4096], P('seq', 'head')
- value_grad: bfloat16 [2048, 4096], P('seq', 'head')
All inputs are finite; a program needn't handle non-finite values.
Results may differ from a plain program's by a relative error of at most 0.008.
Values may be sent and summed in bfloat16 or wider, within the bound.
No kernel may reach another device: no remote copies, remote signals or barrier semaphores. Data moves between devices by JAX's collectives and lax.ppermute only.
A program may use at most 64 MiB of HBM per device.

v0:
```python
import math

import jax
import jax.numpy as jnp
from jax import lax
from jax.experimental import pallas as pl
from jax.experimental.pallas import tpu as pltpu
from jax.sharding import PartitionSpec as P


HDIM = 128
SECTIONS = 3
CHUNK_HEADS = 2
NEG = -1e30
SCALE = 1.0 / math.sqrt(HDIM)
EXP_SCALE = SCALE * math.log2(math.e)


def shift(value, steps):
    count = lax.axis_size("seq")
    low, high = max(0, -steps), min(count, count - steps)
    return lax.ppermute(value, "seq", [(src, src + steps) for src in range(low, high)])


def swap(value, axis, bit):
    return lax.ppermute(value, axis, [(src, src ^ bit) for src in range(lax.axis_size(axis))])


def dot(lhs, rhs, lhs_dim, rhs_dim):
    return lax.dot_general(
        lhs, rhs, (((lhs_dim,), (rhs_dim,)), ((), ())), preferred_element_type=jnp.float32
    )


def gathered_pieces(out_grad):
    pieces = {0: out_grad}
    bit = lax.axis_size("head") // 2
    while bit:
        for offset in list(pieces):
            pieces[offset | bit] = swap(pieces[offset], "head", bit)
        bit //= 2
    return [pieces[offset] for offset in range(len(pieces))]


def grad_kernel(head_ref, *refs):
    *piece_refs, proj_ref, out_ref = refs
    width = piece_refs[0].shape[1]
    total = None
    for offset, piece in enumerate(piece_refs):
        start = pl.multiple_of((head_ref[0] ^ offset) * width, width)
        part = dot(piece[...], proj_ref[:, pl.ds(start, width)], 1, 1)
        total = part if total is None else total + part
    out_ref[...] = total.astype(out_ref.dtype)


def attn_grad_of(out_grad, out_proj):
    pieces = gathered_pieces(out_grad)
    rows, width = out_grad.shape
    cols, features = out_proj.shape
    block = 2 * HDIM
    return pl.pallas_call(
        grad_kernel,
        grid=(cols // block,),
        in_specs=[pl.BlockSpec(memory_space=pltpu.SMEM)]
        + [pl.BlockSpec((rows, width), lambda i: (0, 0)) for _ in pieces]
        + [pl.BlockSpec((block, features), lambda i: (i, 0))],
        out_specs=pl.BlockSpec((rows, block), lambda i: (0, i)),
        out_shape=jax.ShapeDtypeStruct((rows, cols), jnp.bfloat16),
        cost_estimate=pl.CostEstimate(
            flops=2 * rows * cols * features,
            bytes_accessed=2 * (rows * features + cols * features + rows * cols),
            transcendentals=0,
        ),
        name="grad_matmul",
    )(lax.axis_index("head").astype(jnp.int32).reshape(1), *pieces, out_proj)


def attn_kernel(first_head, usable_ref, q_ref, g_ref, *refs):
    sets = refs[:4]
    dq_ref, own_ref, near_ref, mid_ref, far_ref, score, pgrad = refs[-7:]
    outs = (own_ref, near_ref, mid_ref, far_ref)
    head = first_head + pl.program_id(0)
    rows = q_ref.shape[0]
    query = q_ref[...]
    grad = g_ref[...]
    key_at = lax.broadcasted_iota(jnp.int32, (rows, rows), 0)
    query_at = lax.broadcasted_iota(jnp.int32, (rows, rows), 1)
    bias = [0.0] + [jnp.where(usable_ref[head, k] > 0, 0.0, NEG) for k in range(3)]
    top = None
    for k, kv in enumerate(sets):
        raw = dot(kv[:rows, :], query, 1, 1)
        if k == 0:
            raw = jnp.where(key_at <= query_at, raw, NEG)
        score[k] = raw
        peak = jnp.max(raw, axis=0, keepdims=True) + bias[k]
        top = peak if top is None else jnp.maximum(top, peak)
    norm = jnp.zeros((1, rows), jnp.float32)
    delta = jnp.zeros((1, rows), jnp.float32)
    for k, kv in enumerate(sets):
        prob = jnp.exp2((score[k] - (top - bias[k])) * EXP_SCALE)
        pg = dot(kv[rows:, :], grad, 1, 1)
        norm = norm + jnp.sum(prob, axis=0, keepdims=True)
        delta = delta + jnp.sum(prob * pg, axis=0, keepdims=True)
        score[k] = prob
        pgrad[k] = pg
    inv = 1.0 / norm
    delta = delta * inv
    dq = None
    for k, kv in enumerate(sets):
        prob = score[k] * inv
        weight = prob.astype(jnp.bfloat16)
        dlogit = (prob * (pgrad[k] - delta)).astype(jnp.bfloat16)
        out = outs[k]
        out[:rows, :] = (dot(dlogit, query, 1, 0) * SCALE).astype(out.dtype)
        out[rows:, :] = dot(weight, grad, 1, 0).astype(out.dtype)
        part = dot(kv[:rows, :], dlogit, 0, 0)
        dq = part if dq is None else dq + part
    dq_ref[...] = (dq * SCALE).T.astype(dq_ref.dtype)


def attention_chunk(chunk, heads, usable, queries, grads, key_sets, previous):
    rows = queries.shape[0]
    width = heads * HDIM
    first = chunk * heads

    def wide(i):
        return (0, first + i)

    def local(i):
        return (0, i)

    term = pl.BlockSpec((2 * rows, HDIM), local)
    in_specs = [
        pl.BlockSpec(memory_space=pltpu.SMEM),
        pl.BlockSpec((rows, HDIM), wide),
        pl.BlockSpec((rows, HDIM), wide),
    ] + [term] * 4
    args = [usable, queries, grads, *key_sets]
    aliases = {}
    if previous is not None:
        in_specs.append(pl.BlockSpec(memory_space=pl.ANY))
        args.append(previous)
        aliases = {len(args) - 1: 0}
    sent = jax.ShapeDtypeStruct((2 * rows, width), jnp.bfloat16)

    def body(*refs):
        attn_kernel(first, *refs)

    return pl.pallas_call(
        body,
        grid=(heads,),
        in_specs=in_specs,
        out_specs=[pl.BlockSpec((rows, HDIM), wide)] + [term] * 4,
        out_shape=[
            jax.ShapeDtypeStruct(queries.shape, jnp.bfloat16),
            jax.ShapeDtypeStruct((2 * rows, width), jnp.float32),
            sent,
            sent,
            sent,
        ],
        scratch_shapes=[
            pltpu.VMEM((4, rows, rows), jnp.float32),
            pltpu.VMEM((4, rows, rows), jnp.float32),
        ],
        input_output_aliases=aliases,
        cost_estimate=pl.CostEstimate(
            flops=heads * 4 * 5 * 2 * rows * rows * HDIM * 2,
            bytes_accessed=heads * rows * HDIM * 2 * 20,
            transcendentals=heads * 4 * rows * rows,
        ),
        name="attn_chunk",
    )(*args)


def body(queries, key_rows, value_rows, out_grad, out_proj, section_table, block_active):
    seq_count = lax.axis_size("seq")
    position = lax.axis_index("seq")
    spans = [seq_count // 2 ** (index + 1) for index in range(SECTIONS)]
    far_span, mid_span, near_span = spans
    assert far_span == 2 * mid_span and mid_span == 2 * near_span
    rows, cols = queries.shape
    heads = CHUNK_HEADS
    width = heads * HDIM
    chunks = cols // width
    is_odd = (position // near_span) % 2 == 1
    reach = jnp.stack([position >= span for span in reversed(spans)]).astype(jnp.int32)
    usable = section_table[:, ::-1] * block_active[:, ::-1] * reach[None, :]

    packed = [
        jnp.concatenate(
            [array[:, chunk * width : (chunk + 1) * width] for array in (key_rows, value_rows)],
            axis=0,
        )
        for chunk in range(chunks)
    ]
    received = []
    for own in packed:
        mid = shift(own, mid_span)
        far = shift(mid, mid_span)
        near = swap(jnp.where(is_odd, mid, own), "seq", near_span)
        received.append((own, near, mid, far))
    grads = attn_grad_of(out_grad, out_proj)
    query_grad = None
    key_grad = jnp.zeros(queries.shape, jnp.bfloat16)
    value_grad = jnp.zeros(queries.shape, jnp.bfloat16)
    for chunk in range(chunks):
        query_grad, own, near, mid, far = attention_chunk(
            chunk, heads, usable, queries, grads, received[chunk], query_grad
        )
        far_back = shift(far, -mid_span)
        near_back = swap(near, "seq", near_span)
        relay = mid.astype(jnp.float32) + far_back.astype(jnp.float32)
        relay = relay + jnp.where(is_odd, near_back.astype(jnp.float32), 0.0)
        mid_back = shift(relay.astype(jnp.bfloat16), -mid_span)
        total = own + mid_back.astype(jnp.float32)
        total = total + jnp.where(is_odd, 0.0, near_back.astype(jnp.float32))
        total = total.astype(jnp.bfloat16)
        key_grad = lax.dynamic_update_slice(key_grad, total[:rows], (0, chunk * width))
        value_grad = lax.dynamic_update_slice(value_grad, total[rows:], (0, chunk * width))
    return query_grad, key_grad, value_grad


def solution(mesh):
    return jax.shard_map(
        body,
        mesh=mesh,
        in_specs=(
            P("seq", "head"),
            P("seq", "head"),
            P("seq", "head"),
            P("seq", "head"),
            P("head", None),
            P("head", None),
            P("seq", None),
        ),
        out_specs=(P("seq", "head"), P("seq", "head"), P("seq", "head")),
        check_vma=False,
    )
```

profile of v0, /device:TPU:0, one launch (start us, length us, event | category | flops | bytes accessed | tf_op | source)
XLA Modules:
  0.0 121.3 jit_solution(2751067538483166088)
XLA Ops:
  0.6 0.6 collective-permute-start
  1.2 2.6 %collective-permute-start.1 = (bf16[256,512]{1,0:T(8,128)(2,1)}, bf16[256,512]{1,0:T(8,128)(2,1)S(1)}, u32[]{:S(2)}, u32[]{:S(2)}) collective-permute-start(bf16[256,512]{1,0:T(8,128)(2,1)} %refs_0_.1), channel_id=1, source_target_pairs={{0,2},{1,3},{2,0},{3,1},{4,6},{5,7},{6,4},{7,5},{8,10},{9,11},{10,... | collective-permute-start | bytes 786440 | tf_op jit(solution)/shard_map/ppermute | solution.py:26
  3.8 1.4 %fusion.16 = (bf16[256,256]{1,0:T(8,128)(2,1)S(1)}, bf16[256,256]{1,0:T(8,128)(2,1)S(1)}, bf16[256,256]{1,0:T(8,128)(2,1)S(1)}, bf16[256,256]{1,0:T(8,128)(2,1)S...) fusion(bf16[256,1024]{1,0:T(8,128)(2,1)} %param.8, ...), kind=kLoop, calls=%fused_computation.40 | loop fusion | bytes 2097152 | tf_op jit(solution)/shard_map/slice | solution.py:191
  5.2 3.5 %collective-permute-start.9 = (bf16[512,256]{1,0:T(8,128)(2,1)S(1)}, bf16[512,256]{1,0:T(8,128)(2,1)S(1)}, u32[]{:S(2)}, u32[]{:S(2)}) collective-permute-start(bf16[512,256]{1,0:T(8,128)(2,1)S(1)} %pad_maximum_fusion.2.refs_3_), channel_id=1, source_target_pairs={{0,8},{4,12},{8,16},{12,20},{16,24},{20,28},{1,9},{5,13},{9,17},{1... | collective-permute-start | bytes 786440 | tf_op jit(solution)/shard_map/ppermute | solution.py:22
  8.7 3.5 %collective-permute-start.3 = (bf16[512,256]{1,0:T(8,128)(2,1)S(1)}, bf16[512,256]{1,0:T(8,128)(2,1)S(1)}, u32[]{:S(2)}, u32[]{:S(2)}) collective-permute-start(bf16[512,256]{1,0:T(8,128)(2,1)S(1)} %pad_maximum_fusion.refs_3_), channel_id=1, source_target_pairs={{0,8},{4,12},{8,16},{12,20},{16,24},{20,28},{1,9},{5,13},{9,17},{1... | collective-permute-start | bytes 786440 | tf_op jit(solution)/shard_map/ppermute | solution.py:22
  12.2 3.5 %collective-permute-start.12 = (bf16[512,256]{1,0:T(8,128)(2,1)S(1)}, bf16[512,256]{1,0:T(8,128)(2,1)S(1)}, u32[]{:S(2)}, u32[]{:S(2)}) collective-permute-start(bf16[512,256]{1,0:T(8,128)(2,1)S(1)} %pad_maximum_fusion.3.refs_3_), channel_id=1, source_target_pairs={{0,8},{4,12},{8,16},{12,20},{16,24},{20,28},{1,9},{5,13},{9,17},{1... | collective-permute-start | bytes 786440 | tf_op jit(solution)/shard_map/ppermute | solution.py:22
  15.8 0.7 rev.7
  16.5 0.8 copy.13
  17.4 0.6 multiply_multiply_fusion.refs_0_
  18.1 2.6 %collective-permute-start.6 = (bf16[512,256]{1,0:T(8,128)(2,1)S(1)}, bf16[512,256]{1,0:T(8,128)(2,1)}, u32[]{:S(2)}, u32[]{:S(2)}) collective-permute-start(bf16[512,256]{1,0:T(8,128)(2,1)S(1)} %pad_maximum_fusion.1.refs_3_), channel_id=1, source_target_pairs={{0,8},{4,12},{8,16},{12,20},{16,24},{20,28},{1,9},{5,13},{9,17},{1... | collective-permute-start | bytes 786440 | tf_op jit(solution)/shard_map/ppermute | solution.py:22
  20.8 5.8 %collective-permute-done.12.refs_5_ = bf16[512,256]{1,0:T(8,128)(2,1)S(1)} collective-permute-done((bf16[512,256]{1,0:T(8,128)(2,1)S(1)}, bf16[512,256]{1,0:T(8,128)(2,1)S(1)}, u32[]{:S(2)}, u32[]{:S(2)}) %collective-permute-start.12) | collective-permute-done | bytes 262176 | tf_op jit(solution)/shard_map/ppermute | solution.py:22
  26.6 1.5 %collective-permute-start.10 = (bf16[512,256]{1,0:T(8,128)(2,1)S(1)}, bf16[512,256]{1,0:T(8,128)(2,1)S(1)}, u32[]{:S(2)}, u32[]{:S(2)}) collective-permute-start(bf16[512,256]{1,0:T(8,128)(2,1)S(1)} %broadcast_select_fusion.1), channel_id=1, source_target_pairs={{0,4},{4,0},{8,12},{12,8},{16,20},{20,16},{24,28},{28,24},{1,5},{5... | collective-permute-start | bytes 786440 | tf_op jit(solution)/shard_map/ppermute | solution.py:26
  28.2 0.6 collective-permute-start.13
  28.8 0.8 broadcast_select_fusion.3
  29.6 5.1 %collective-permute-start.11 = (bf16[512,256]{1,0:T(8,128)(2,1)S(1)}, bf16[512,256]{1,0:T(8,128)(2,1)}, u32[]{:S(2)}, u32[]{:S(2)}) collective-permute-start(bf16[512,256]{1,0:T(8,128)(2,1)S(1)} %collective-permute-done.9.refs_5_), channel_id=1, source_target_pairs={{0,8},{4,12},{8,16},{12,20},{16,24},{20,28},{1,9},{5,13},{9,17},{1... | collective-permute-start | bytes 786440 | tf_op jit(solution)/shard_map/ppermute | solution.py:22
  34.7 3.5 %collective-permute-start.14 = (bf16[512,256]{1,0:T(8,128)(2,1)S(1)}, bf16[512,256]{1,0:T(8,128)(2,1)}, u32[]{:S(2)}, u32[]{:S(2)}) collective-permute-start(bf16[512,256]{1,0:T(8,128)(2,1)S(1)} %collective-permute-done.12.refs_5_), channel_id=1, source_target_pairs={{0,8},{4,12},{8,16},{12,20},{16,24},{20,28},{1,9},{5,13},{9,17},{1... | collective-permute-start | bytes 786440 | tf_op jit(solution)/shard_map/ppermute | solution.py:22
  38.3 2.5 %collective-permute-start.7 = (bf16[512,256]{1,0:T(8,128)(2,1)S(1)}, bf16[512,256]{1,0:T(8,128)(2,1)S(1)}, u32[]{:S(2)}, u32[]{:S(2)}) collective-permute-start(bf16[512,256]{1,0:T(8,128)(2,1)S(1)} %broadcast_select_fusion.2), channel_id=1, source_target_pairs={{0,4},{4,0},{8,12},{12,8},{16,20},{20,16},{24,28},{28,24},{1,5},{5... | collective-permute-start | bytes 786440 | tf_op jit(solution)/shard_map/ppermute | solution.py:26
  40.8 0.7 copy-done.24
  41.5 3.5 %collective-permute-start.8 = (bf16[512,256]{1,0:T(8,128)(2,1)}, bf16[512,256]{1,0:T(8,128)(2,1)}, u32[]{:S(2)}, u32[]{:S(2)}) collective-permute-start(bf16[512,256]{1,0:T(8,128)(2,1)} %collective-permute-done.6.refs_5_), channel_id=1, source_target_pairs={{0,8},{4,12},{8,16},{12,20},{16,24},{20,28},{1,9},{5,13},{9,17},{1... | collective-permute-start | bytes 786440 | tf_op jit(solution)/shard_map/ppermute | solution.py:22
  45.0 5.1 %grad_matmul.1.refs_2_ = bf16[256,1024]{1,0:T(8,128)(2,1)} custom-call(s32[1]{0:T(128)} %bitcast.4.head_ref, bf16[256,512]{1,0:T(8,128)(2,1)} %refs_0_.1, bf16[256,512]{1,0:T(8,128)(2,1)} %copy-done.6, bf16[256,512]{1,0:T(8,128)(2,1)} %copy-done.7, bf16[256,512]{1,0:T(8,128)(2,1)} %copy-done.8, bf16[1024,2048]{1,0:T(8,128)(2,1)} %refs_4_.1), custom_call_target="tpu_custom_call" | custom-call | flops 1073741824 | bytes 5767168 | tf_op jit(solution)/shard_map/grad_matmul/pallas_call | solution.py:61
  50.2 2.0 %collective-permute-start.5 = (bf16[512,256]{1,0:T(8,128)(2,1)S(1)}, bf16[512,256]{1,0:T(8,128)(2,1)}, u32[]{:S(2)}, u32[]{:S(2)}) collective-permute-start(bf16[512,256]{1,0:T(8,128)(2,1)S(1)} %collective-permute-done.3.refs_5_), channel_id=1, source_target_pairs={{0,8},{4,12},{8,16},{12,20},{16,24},{20,28},{1,9},{5,13},{9,17},{1... | collective-permute-start | bytes 786440 | tf_op jit(solution)/shard_map/ppermute | solution.py:22
  52.2 4.4 %attn_chunk.4 = (bf16[256,1024]{1,0:T(8,128)(2,1)}, f32[512,256]{1,0:T(8,128)}, bf16[512,256]{1,0:T(8,128)(2,1)}, bf16[512,256]{1,0:T(8,128)(2,1)}, bf16[512,256]{1,0:T(8,128)(2,1)}) custom-call(s32[8,3]{1,0:T(8,128)} %multiply_multiply_fusion.refs_0_, bf16[256,1024]{1,0:T(8,128)(2,1)} %refs_1_.7, bf16[256,1024]{1,0:T(8,128)(2,1)} %grad_matmul.1.refs_2_, ...), custom_call_target="tpu_custom_call" | custom-call | flops 1342177280 | bytes 2621440 | tf_op jit(solution)/shard_map/attn_chunk/pallas_call | solution.py:149
  56.6 4.4 %attn_chunk.5 = (bf16[256,1024]{1,0:T(8,128)(2,1)}, f32[512,256]{1,0:T(8,128)}, bf16[512,256]{1,0:T(8,128)(2,1)}, bf16[512,256]{1,0:T(8,128)(2,1)}, bf16[512,256]{1,0:T(8,128)(2,1)}) custom-call(s32[8,3]{1,0:T(8,128)} %multiply_multiply_fusion.refs_0_, bf16[256,1024]{1,0:T(8,128)(2,1)} %refs_1_.7, ...), custom_call_target="tpu_custom_call", output_to_operand_aliasing={{0}: (7, {})} | custom-call | flops 1342177280 | bytes 2621440 | tf_op jit(solution)/shard_map/attn_chunk/pallas_call | solution.py:149
  61.1 0.7 copy-done.26
  61.8 4.5 %attn_chunk.6 = (bf16[256,1024]{1,0:T(8,128)(2,1)}, f32[512,256]{1,0:T(8,128)}, bf16[512,256]{1,0:T(8,128)(2,1)}, bf16[512,256]{1,0:T(8,128)(2,1)}, bf16[512,256]{1,0:T(8,128)(2,1)}) custom-call(s32[8,3]{1,0:T(8,128)} %multiply_multiply_fusion.refs_0_, bf16[256,1024]{1,0:T(8,128)(2,1)} %refs_1_.7, ...), custom_call_target="tpu_custom_call", output_to_operand_aliasing={{0}: (7, {})} | custom-call | flops 1342177280 | bytes 2621440 | tf_op jit(solution)/shard_map/attn_chunk/pallas_call | solution.py:149
  66.3 4.6 %attn_chunk.7 = (bf16[256,1024]{1,0:T(8,128)(2,1)}, f32[512,256]{1,0:T(8,128)}, bf16[512,256]{1,0:T(8,128)(2,1)}, bf16[512,256]{1,0:T(8,128)(2,1)}, bf16[512,256]{1,0:T(8,128)(2,1)}) custom-call(s32[8,3]{1,0:T(8,128)} %multiply_multiply_fusion.refs_0_, bf16[256,1024]{1,0:T(8,128)(2,1)} %refs_1_.7, ...), custom_call_target="tpu_custom_call", output_to_operand_aliasing={{0}: (7, {})} | custom-call | flops 1342177280 | bytes 2621440 | tf_op jit(solution)/shard_map/attn_chunk/pallas_call | solution.py:149
  70.9 1.4 %collective-permute-start.24 = (bf16[512,256]{1,0:T(8,128)(2,1)}, bf16[512,256]{1,0:T(8,128)(2,1)S(1)}, u32[]{:S(2)}, u32[]{:S(2)}) collective-permute-start(bf16[512,256]{1,0:T(8,128)(2,1)} %get-tuple-element.41), channel_id=1, source_target_pairs={{8,0},{12,4},{16,8},{20,12},{24,16},{28,20},{9,1},{13,5},{17,9},{2... | collective-permute-start | bytes 786440 | tf_op jit(solution)/shard_map/ppermute | solution.py:22
  72.3 2.1 %collective-permute-start.25 = (bf16[512,256]{1,0:T(8,128)(2,1)}, bf16[512,256]{1,0:T(8,128)(2,1)S(1)}, u32[]{:S(2)}, u32[]{:S(2)}) collective-permute-start(bf16[512,256]{1,0:T(8,128)(2,1)} %get-tuple-element.42), channel_id=1, source_target_pairs={{0,4},{4,0},{8,12},{12,8},{16,20},{20,16},{24,28},{28,24},{1,5},{5... | collective-permute-start | bytes 786440 | tf_op jit(solution)/shard_map/ppermute | solution.py:26
  74.4 1.3 %collective-permute-start.15 = (bf16[512,256]{1,0:T(8,128)(2,1)S(1)}, bf16[512,256]{1,0:T(8,128)(2,1)S(1)}, u32[]{:S(2)}, u32[]{:S(2)}) collective-permute-start(bf16[512,256]{1,0:T(8,128)(2,1)S(1)} %copy-done.22), channel_id=1, source_target_pairs={{8,0},{12,4},{16,8},{20,12},{24,16},{28,20},{9,1},{13,5},{17,9},{2... | collective-permute-start | bytes 786440 | tf_op jit(solution)/shard_map/ppermute | solution.py:22
  75.8 1.3 %collective-permute-start.21 = (bf16[512,256]{1,0:T(8,128)(2,1)S(1)}, bf16[512,256]{1,0:T(8,128)(2,1)S(1)}, u32[]{:S(2)}, u32[]{:S(2)}) collective-permute-start(bf16[512,256]{1,0:T(8,128)(2,1)S(1)} %copy-done.25), channel_id=1, source_target_pairs={{8,0},{12,4},{16,8},{20,12},{24,16},{28,20},{9,1},{13,5},{17,9},{2... | collective-permute-start | bytes 786440 | tf_op jit(solution)/shard_map/ppermute | solution.py:22
  77.1 5.2 %collective-permute-done.24 = bf16[512,256]{1,0:T(8,128)(2,1)S(1)} collective-permute-done((bf16[512,256]{1,0:T(8,128)(2,1)}, bf16[512,256]{1,0:T(8,128)(2,1)S(1)}, u32[]{:S(2)}, u32[]{:S(2)}) %collective-permute-start.24) | collective-permute-done | bytes 262176 | tf_op jit(solution)/shard_map/ppermute | solution.py:22
  82.3 2.0 %collective-permute-start.22 = (bf16[512,256]{1,0:T(8,128)(2,1)S(1)}, bf16[512,256]{1,0:T(8,128)(2,1)S(1)}, u32[]{:S(2)}, u32[]{:S(2)}) collective-permute-start(bf16[512,256]{1,0:T(8,128)(2,1)S(1)} %copy-done.23), channel_id=1, source_target_pairs={{0,4},{4,0},{8,12},{12,8},{16,20},{20,16},{24,28},{28,24},{1,5},{5... | collective-permute-start | bytes 786440 | tf_op jit(solution)/shard_map/ppermute | solution.py:26
  84.3 1.3 %collective-permute-start.18 = (bf16[512,256]{1,0:T(8,128)(2,1)S(1)}, bf16[512,256]{1,0:T(8,128)(2,1)S(1)}, u32[]{:S(2)}, u32[]{:S(2)}) collective-permute-start(bf16[512,256]{1,0:T(8,128)(2,1)S(1)} %copy-done.20), channel_id=1, source_target_pairs={{8,0},{12,4},{16,8},{20,12},{24,16},{28,20},{9,1},{13,5},{17,9},{2... | collective-permute-start | bytes 786440 | tf_op jit(solution)/shard_map/ppermute | solution.py:22
  85.6 1.1 fusion.13
  86.8 1.2 collective-permute-done.15
  87.9 2.0 %collective-permute-start.19 = (bf16[512,256]{1,0:T(8,128)(2,1)S(1)}, bf16[512,256]{1,0:T(8,128)(2,1)S(1)}, u32[]{:S(2)}, u32[]{:S(2)}) collective-permute-start(bf16[512,256]{1,0:T(8,128)(2,1)S(1)} %copy-done.19), channel_id=1, source_target_pairs={{0,4},{4,0},{8,12},{12,8},{16,20},{20,16},{24,28},{28,24},{1,5},{5... | collective-permute-start | bytes 786440 | tf_op jit(solution)/shard_map/ppermute | solution.py:26
  89.9 1.3 %collective-permute-start.26 = (bf16[512,256]{1,0:T(8,128)(2,1)S(1)}, bf16[512,256]{1,0:T(8,128)(2,1)S(1)}, u32[]{:S(2)}, u32[]{:S(2)}) collective-permute-start(bf16[512,256]{1,0:T(8,128)(2,1)S(1)} %fusion.13), channel_id=1, source_target_pairs={{8,0},{12,4},{16,8},{20,12},{24,16},{28,20},{9,1},{13,5},{17,9},{2... | collective-permute-start | bytes 786440 | tf_op jit(solution)/shard_map/ppermute | solution.py:22
  91.2 0.1 fusion.1
  91.4 2.2 %collective-permute-done.21 = bf16[512,256]{1,0:T(8,128)(2,1)S(1)} collective-permute-done((bf16[512,256]{1,0:T(8,128)(2,1)S(1)}, bf16[512,256]{1,0:T(8,128)(2,1)S(1)}, u32[]{:S(2)}, u32[]{:S(2)}) %collective-permute-start.21) | collective-permute-done | bytes 262176 | tf_op jit(solution)/shard_map/ppermute | solution.py:22
  93.5 1.3 %collective-permute-start.17 = (bf16[512,256]{1,0:T(8,128)(2,1)S(1)}, bf16[512,256]{1,0:T(8,128)(2,1)S(1)}, u32[]{:S(2)}, u32[]{:S(2)}) collective-permute-start(bf16[512,256]{1,0:T(8,128)(2,1)S(1)} %fusion.1), channel_id=1, source_target_pairs={{8,0},{12,4},{16,8},{20,12},{24,16},{28,20},{9,1},{13,5},{17,9},{2... | collective-permute-start | bytes 786440 | tf_op jit(solution)/shard_map/ppermute | solution.py:22
  95.0 1.4 %collective-permute-start.23 = (bf16[512,256]{1,0:T(8,128)(2,1)S(1)}, bf16[512,256]{1,0:T(8,128)(2,1)S(1)}, u32[]{:S(2)}, u32[]{:S(2)}) collective-permute-start(bf16[512,256]{1,0:T(8,128)(2,1)S(1)} %fusion.9), channel_id=1, source_target_pairs={{8,0},{12,4},{16,8},{20,12},{24,16},{28,20},{9,1},{13,5},{17,9},{2... | collective-permute-start | bytes 786440 | tf_op jit(solution)/shard_map/ppermute | solution.py:22
  96.4 2.7 %collective-permute-done.18 = bf16[512,256]{1,0:T(8,128)(2,1)S(1)} collective-permute-done((bf16[512,256]{1,0:T(8,128)(2,1)S(1)}, bf16[512,256]{1,0:T(8,128)(2,1)S(1)}, u32[]{:S(2)}, u32[]{:S(2)}) %collective-permute-start.18) | collective-permute-done | bytes 262176 | tf_op jit(solution)/shard_map/ppermute | solution.py:22
  99.3 1.3 %collective-permute-start.20 = (bf16[512,256]{1,0:T(8,128)(2,1)S(1)}, bf16[512,256]{1,0:T(8,128)(2,1)S(1)}, u32[]{:S(2)}, u32[]{:S(2)}) collective-permute-start(bf16[512,256]{1,0:T(8,128)(2,1)S(1)} %fusion.5), channel_id=1, source_target_pairs={{8,0},{12,4},{16,8},{20,12},{24,16},{28,20},{9,1},{13,5},{17,9},{2... | collective-permute-start | bytes 786440 | tf_op jit(solution)/shard_map/ppermute | solution.py:22
  100.6 9.8 %collective-permute-done.17 = bf16[512,256]{1,0:T(8,128)(2,1)S(1)} collective-permute-done((bf16[512,256]{1,0:T(8,128)(2,1)S(1)}, bf16[512,256]{1,0:T(8,128)(2,1)S(1)}, u32[]{:S(2)}, u32[]{:S(2)}) %collective-permute-start.17) | collective-permute-done | bytes 262176 | tf_op jit(solution)/shard_map/ppermute | solution.py:22
  110.7 5.4 %collective-permute-done.23 = bf16[512,256]{1,0:T(8,128)(2,1)S(1)} collective-permute-done((bf16[512,256]{1,0:T(8,128)(2,1)S(1)}, bf16[512,256]{1,0:T(8,128)(2,1)S(1)}, u32[]{:S(2)}, u32[]{:S(2)}) %collective-permute-start.23) | collective-permute-done | bytes 262176 | tf_op jit(solution)/shard_map/ppermute | solution.py:22
  116.1 3.9 %collective-permute-done.20 = bf16[512,256]{1,0:T(8,128)(2,1)S(1)} collective-permute-done((bf16[512,256]{1,0:T(8,128)(2,1)S(1)}, bf16[512,256]{1,0:T(8,128)(2,1)S(1)}, u32[]{:S(2)}, u32[]{:S(2)}) %collective-permute-start.20) | collective-permute-done | bytes 262176 | tf_op jit(solution)/shard_map/ppermute | solution.py:22
  120.4 0.8 copy-done.4
  121.2 0.2 copy-done.5
  (93 shorter events, 1.6 us)
Async XLA Ops:
  0.6 28.9 %collective-permute-start = (bf16[256,512]{1,0:T(8,128)(2,1)}, bf16[256,512]{1,0:T(8,128)(2,1)S(1)}, u32[]{:S(2)}, u32[]{:S(2)}) collective-permute-start(bf16[256,512]{1,0:T(8,128)(2,1)} %refs_0_.1), channel_id=1, source_target_pairs={{0,1},{1,0},{2,3},{3,2},{4,5},{5,4},{6,7},{7,6},{8,9},{9,8},{10,11... | collective-permute-start | bytes 786440 | tf_op jit(solution)/shard_map/ppermute | solution.py:26
  1.2 27.0 %collective-permute-start.1 = (bf16[256,512]{1,0:T(8,128)(2,1)}, bf16[256,512]{1,0:T(8,128)(2,1)S(1)}, u32[]{:S(2)}, u32[]{:S(2)}) collective-permute-start(bf16[256,512]{1,0:T(8,128)(2,1)} %refs_0_.1), channel_id=1, source_target_pairs={{0,2},{1,3},{2,0},{3,1},{4,6},{5,7},{6,4},{7,5},{8,10},{9,11},{10,... | collective-permute-start | bytes 786440 | tf_op jit(solution)/shard_map/ppermute | solution.py:26
  5.2 44.9 %copy-start.10 = (bf16[512,256]{1,0:T(8,128)(2,1)}, bf16[512,256]{1,0:T(8,128)(2,1)S(1)}, u32[]{:S(2)}) copy-start(bf16[512,256]{1,0:T(8,128)(2,1)S(1)} %pad_maximum_fusion.2.refs_3_) | copy-start | bytes 786436
  5.2 12.9 %collective-permute-start.9 = (bf16[512,256]{1,0:T(8,128)(2,1)S(1)}, bf16[512,256]{1,0:T(8,128)(2,1)S(1)}, u32[]{:S(2)}, u32[]{:S(2)}) collective-permute-start(bf16[512,256]{1,0:T(8,128)(2,1)S(1)} %pad_maximum_fusion.2.refs_3_), channel_id=1, source_target_pairs={{0,8},{4,12},{8,16},{12,20},{16,24},{20,28},{1,9},{5,13},{9,17},{1... | collective-permute-start | bytes 786440 | tf_op jit(solution)/shard_map/ppermute | solution.py:22
  8.7 41.4 %copy-start.9 = (bf16[512,256]{1,0:T(8,128)(2,1)}, bf16[512,256]{1,0:T(8,128)(2,1)S(1)}, u32[]{:S(2)}) copy-start(bf16[512,256]{1,0:T(8,128)(2,1)S(1)} %pad_maximum_fusion.refs_3_) | copy-start | bytes 786436
  8.7 20.0 %collective-permute-start.3 = (bf16[512,256]{1,0:T(8,128)(2,1)S(1)}, bf16[512,256]{1,0:T(8,128)(2,1)S(1)}, u32[]{:S(2)}, u32[]{:S(2)}) collective-permute-start(bf16[512,256]{1,0:T(8,128)(2,1)S(1)} %pad_maximum_fusion.refs_3_), channel_id=1, source_target_pairs={{0,8},{4,12},{8,16},{12,20},{16,24},{20,28},{1,9},{5,13},{9,17},{1... | collective-permute-start | bytes 786440 | tf_op jit(solution)/shard_map/ppermute | solution.py:22
  12.2 37.9 %copy-start.12 = (bf16[512,256]{1,0:T(8,128)(2,1)}, bf16[512,256]{1,0:T(8,128)(2,1)S(1)}, u32[]{:S(2)}) copy-start(bf16[512,256]{1,0:T(8,128)(2,1)S(1)} %pad_maximum_fusion.3.refs_3_) | copy-start | bytes 786436
  12.2 14.3 %collective-permute-start.12 = (bf16[512,256]{1,0:T(8,128)(2,1)S(1)}, bf16[512,256]{1,0:T(8,128)(2,1)S(1)}, u32[]{:S(2)}, u32[]{:S(2)}) collective-permute-start(bf16[512,256]{1,0:T(8,128)(2,1)S(1)} %pad_maximum_fusion.3.refs_3_), channel_id=1, source_target_pairs={{0,8},{4,12},{8,16},{12,20},{16,24},{20,28},{1,9},{5,13},{9,17},{1... | collective-permute-start | bytes 786440 | tf_op jit(solution)/shard_map/ppermute | solution.py:22
  18.0 32.1 %copy-start.11 = (bf16[512,256]{1,0:T(8,128)(2,1)}, bf16[512,256]{1,0:T(8,128)(2,1)S(1)}, u32[]{:S(2)}) copy-start(bf16[512,256]{1,0:T(8,128)(2,1)S(1)} %pad_maximum_fusion.1.refs_3_) | copy-start | bytes 786436
  18.1 32.1 %copy-start.14 = (bf16[512,256]{1,0:T(8,128)(2,1)}, bf16[512,256]{1,0:T(8,128)(2,1)S(1)}, u32[]{:S(2)}) copy-start(bf16[512,256]{1,0:T(8,128)(2,1)S(1)} %collective-permute-done.9.refs_5_) | copy-start | bytes 786436
  18.1 16.6 %collective-permute-start.6 = (bf16[512,256]{1,0:T(8,128)(2,1)S(1)}, bf16[512,256]{1,0:T(8,128)(2,1)}, u32[]{:S(2)}, u32[]{:S(2)}) collective-permute-start(bf16[512,256]{1,0:T(8,128)(2,1)S(1)} %pad_maximum_fusion.1.refs_3_), channel_id=1, source_target_pairs={{0,8},{4,12},{8,16},{12,20},{16,24},{20,28},{1,9},{5,13},{9,17},{1... | collective-permute-start | bytes 786440 | tf_op jit(solution)/shard_map/ppermute | solution.py:22
  26.6 25.6 %copy-start.15 = (bf16[512,256]{1,0:T(8,128)(2,1)}, bf16[512,256]{1,0:T(8,128)(2,1)S(1)}, u32[]{:S(2)}) copy-start(bf16[512,256]{1,0:T(8,128)(2,1)S(1)} %collective-permute-done.12.refs_5_) | copy-start | bytes 786436
  26.6 14.2 %collective-permute-start.10 = (bf16[512,256]{1,0:T(8,128)(2,1)S(1)}, bf16[512,256]{1,0:T(8,128)(2,1)S(1)}, u32[]{:S(2)}, u32[]{:S(2)}) collective-permute-start(bf16[512,256]{1,0:T(8,128)(2,1)S(1)} %broadcast_select_fusion.1), channel_id=1, source_target_pairs={{0,4},{4,0},{8,12},{12,8},{16,20},{20,16},{24,28},{28,24},{1,5},{5... | collective-permute-start | bytes 786440 | tf_op jit(solution)/shard_map/ppermute | solution.py:26
  28.1 16.8 %copy-start.7 = (bf16[256,512]{1,0:T(8,128)(2,1)}, bf16[256,512]{1,0:T(8,128)(2,1)S(1)}, u32[]{:S(2)}) copy-start(bf16[256,512]{1,0:T(8,128)(2,1)S(1)} %collective-permute-done.1.refs_2_) | copy-start | bytes 786436
  28.2 22.0 %collective-permute-start.13 = (bf16[512,256]{1,0:T(8,128)(2,1)S(1)}, bf16[512,256]{1,0:T(8,128)(2,1)}, u32[]{:S(2)}, u32[]{:S(2)}) collective-permute-start(bf16[512,256]{1,0:T(8,128)(2,1)S(1)} %broadcast_select_fusion), channel_id=1, source_target_pairs={{0,4},{4,0},{8,12},{12,8},{16,20},{20,16},{24,28},{28,24},{1,5},{5... | collective-permute-start | bytes 786440 | tf_op jit(solution)/shard_map/ppermute | solution.py:26
  28.8 27.9 %copy-start.13 = (bf16[512,256]{1,0:T(8,128)(2,1)}, bf16[512,256]{1,0:T(8,128)(2,1)S(1)}, u32[]{:S(2)}) copy-start(bf16[512,256]{1,0:T(8,128)(2,1)S(1)} %collective-permute-done.3.refs_5_) | copy-start | bytes 786436
  28.8 9.5 %collective-permute-start.2 = (bf16[256,512]{1,0:T(8,128)(2,1)S(1)}, bf16[256,512]{1,0:T(8,128)(2,1)S(1)}, u32[]{:S(2)}, u32[]{:S(2)}) collective-permute-start(bf16[256,512]{1,0:T(8,128)(2,1)S(1)} %collective-permute-done.1.refs_2_), channel_id=1, source_target_pairs={{0,1},{1,0},{2,3},{3,2},{4,5},{5,4},{6,7},{7,6},{8,9},{9,8},{10,11... | collective-permute-start | bytes 786440 | tf_op jit(solution)/shard_map/ppermute | solution.py:26
  29.6 15.4 %copy-start.6 = (bf16[256,512]{1,0:T(8,128)(2,1)}, bf16[256,512]{1,0:T(8,128)(2,1)S(1)}, u32[]{:S(2)}) copy-start(bf16[256,512]{1,0:T(8,128)(2,1)S(1)} %collective-permute-done.refs_1_) | copy-start | bytes 786436
  29.6 27.1 %collective-permute-start.11 = (bf16[512,256]{1,0:T(8,128)(2,1)S(1)}, bf16[512,256]{1,0:T(8,128)(2,1)}, u32[]{:S(2)}, u32[]{:S(2)}) collective-permute-start(bf16[512,256]{1,0:T(8,128)(2,1)S(1)} %collective-permute-done.9.refs_5_), channel_id=1, source_target_pairs={{0,8},{4,12},{8,16},{12,20},{16,24},{20,28},{1,9},{5,13},{9,17},{1... | collective-permute-start | bytes 786440 | tf_op jit(solution)/shard_map/ppermute | solution.py:22
  34.7 15.6 %collective-permute-start.14 = (bf16[512,256]{1,0:T(8,128)(2,1)S(1)}, bf16[512,256]{1,0:T(8,128)(2,1)}, u32[]{:S(2)}, u32[]{:S(2)}) collective-permute-start(bf16[512,256]{1,0:T(8,128)(2,1)S(1)} %collective-permute-done.12.refs_5_), channel_id=1, source_target_pairs={{0,8},{4,12},{8,16},{12,20},{16,24},{20,28},{1,9},{5,13},{9,17},{1... | collective-permute-start | bytes 786440 | tf_op jit(solution)/shard_map/ppermute | solution.py:22
  38.3 22.8 %collective-permute-start.7 = (bf16[512,256]{1,0:T(8,128)(2,1)S(1)}, bf16[512,256]{1,0:T(8,128)(2,1)S(1)}, u32[]{:S(2)}, u32[]{:S(2)}) collective-permute-start(bf16[512,256]{1,0:T(8,128)(2,1)S(1)} %broadcast_select_fusion.2), channel_id=1, source_target_pairs={{0,4},{4,0},{8,12},{12,8},{16,20},{20,16},{24,28},{28,24},{1,5},{5... | collective-permute-start | bytes 786440 | tf_op jit(solution)/shard_map/ppermute | solution.py:26
  41.5 19.6 %collective-permute-start.8 = (bf16[512,256]{1,0:T(8,128)(2,1)}, bf16[512,256]{1,0:T(8,128)(2,1)}, u32[]{:S(2)}, u32[]{:S(2)}) collective-permute-start(bf16[512,256]{1,0:T(8,128)(2,1)} %collective-permute-done.6.refs_5_), channel_id=1, source_target_pairs={{0,8},{4,12},{8,16},{12,20},{16,24},{20,28},{1,9},{5,13},{9,17},{1... | collective-permute-start | bytes 786440 | tf_op jit(solution)/shard_map/ppermute | solution.py:22
  50.1 16.2 %collective-permute-start.4 = (bf16[512,256]{1,0:T(8,128)(2,1)}, bf16[512,256]{1,0:T(8,128)(2,1)}, u32[]{:S(2)}, u32[]{:S(2)}) collective-permute-start(bf16[512,256]{1,0:T(8,128)(2,1)} %broadcast_select_fusion.3), channel_id=1, source_target_pairs={{0,4},{4,0},{8,12},{12,8},{16,20},{20,16},{24,28},{28,24},{1,5},{5... | collective-permute-start | bytes 786440 | tf_op jit(solution)/shard_map/ppermute | solution.py:26
  50.2 16.1 %collective-permute-start.5 = (bf16[512,256]{1,0:T(8,128)(2,1)S(1)}, bf16[512,256]{1,0:T(8,128)(2,1)}, u32[]{:S(2)}, u32[]{:S(2)}) collective-permute-start(bf16[512,256]{1,0:T(8,128)(2,1)S(1)} %collective-permute-done.3.refs_5_), channel_id=1, source_target_pairs={{0,8},{4,12},{8,16},{12,20},{16,24},{20,28},{1,9},{5,13},{9,17},{1... | collective-permute-start | bytes 786440 | tf_op jit(solution)/shard_map/ppermute | solution.py:22
  61.8 12.6 %copy-start.22 = (bf16[512,256]{1,0:T(8,128)(2,1)S(1)}, bf16[512,256]{1,0:T(8,128)(2,1)}, u32[]{:S(2)}) copy-start(bf16[512,256]{1,0:T(8,128)(2,1)} %get-tuple-element.29) | copy-start | bytes 786436
  61.8 13.9 %copy-start.21 = (bf16[512,256]{1,0:T(8,128)(2,1)S(1)}, bf16[512,256]{1,0:T(8,128)(2,1)}, u32[]{:S(2)}) copy-start(bf16[512,256]{1,0:T(8,128)(2,1)} %get-tuple-element.30) | copy-start | bytes 786436
  61.8 22.6 %copy-start.20 = (bf16[512,256]{1,0:T(8,128)(2,1)S(1)}, bf16[512,256]{1,0:T(8,128)(2,1)}, u32[]{:S(2)}) copy-start(bf16[512,256]{1,0:T(8,128)(2,1)} %get-tuple-element.33) | copy-start | bytes 786436
  66.2 16.1 %copy-start.23 = (bf16[512,256]{1,0:T(8,128)(2,1)S(1)}, bf16[512,256]{1,0:T(8,128)(2,1)}, u32[]{:S(2)}) copy-start(bf16[512,256]{1,0:T(8,128)(2,1)} %get-tuple-element.38) | copy-start | bytes 786436
  66.3 21.7 %copy-start.19 = (bf16[512,256]{1,0:T(8,128)(2,1)S(1)}, bf16[512,256]{1,0:T(8,128)(2,1)}, u32[]{:S(2)}) copy-start(bf16[512,256]{1,0:T(8,128)(2,1)} %get-tuple-element.34) | copy-start | bytes 786436
  66.3 25.0 %copy-start.17 = (bf16[512,256]{1,0:T(8,128)(2,1)S(1)}, bf16[512,256]{1,0:T(8,128)(2,1)}, u32[]{:S(2)}) copy-start(bf16[512,256]{1,0:T(8,128)(2,1)} %get-tuple-element.28) | copy-start | bytes 786436
  66.3 28.6 %copy-start.18 = (bf16[512,256]{1,0:T(8,128)(2,1)S(1)}, bf16[512,256]{1,0:T(8,128)(2,1)}, u32[]{:S(2)}) copy-start(bf16[512,256]{1,0:T(8,128)(2,1)} %get-tuple-element.36) | copy-start | bytes 786436
  66.3 32.9 %copy-start.16 = (bf16[512,256]{1,0:T(8,128)(2,1)S(1)}, bf16[512,256]{1,0:T(8,128)(2,1)}, u32[]{:S(2)}) copy-start(bf16[512,256]{1,0:T(8,128)(2,1)} %get-tuple-element.32) | copy-start | bytes 786436
  66.3 44.1 %copy-start.2 = (f32[512,256]{1,0:T(8,128)S(1)}, f32[512,256]{1,0:T(8,128)}, u32[]{:S(2)}) copy-start(f32[512,256]{1,0:T(8,128)} %get-tuple-element.27) | copy-start | bytes 1572868
  70.9 45.1 %copy-start.3 = (f32[512,256]{1,0:T(8,128)S(1)}, f32[512,256]{1,0:T(8,128)}, u32[]{:S(2)}) copy-start(f32[512,256]{1,0:T(8,128)} %get-tuple-element.35) | copy-start | bytes 1572868
  70.9 11.4 %collective-permute-start.24 = (bf16[512,256]{1,0:T(8,128)(2,1)}, bf16[512,256]{1,0:T(8,128)(2,1)S(1)}, u32[]{:S(2)}, u32[]{:S(2)}) collective-permute-start(bf16[512,256]{1,0:T(8,128)(2,1)} %get-tuple-element.41), channel_id=1, source_target_pairs={{8,0},{12,4},{16,8},{20,12},{24,16},{28,20},{9,1},{13,5},{17,9},{2... | collective-permute-start | bytes 786440 | tf_op jit(solution)/shard_map/ppermute | solution.py:22
  72.3 12.0 %collective-permute-start.25 = (bf16[512,256]{1,0:T(8,128)(2,1)}, bf16[512,256]{1,0:T(8,128)(2,1)S(1)}, u32[]{:S(2)}, u32[]{:S(2)}) collective-permute-start(bf16[512,256]{1,0:T(8,128)(2,1)} %get-tuple-element.42), channel_id=1, source_target_pairs={{0,4},{4,0},{8,12},{12,8},{16,20},{20,16},{24,28},{28,24},{1,5},{5... | collective-permute-start | bytes 786440 | tf_op jit(solution)/shard_map/ppermute | solution.py:26
  74.4 13.5 %collective-permute-start.15 = (bf16[512,256]{1,0:T(8,128)(2,1)S(1)}, bf16[512,256]{1,0:T(8,128)(2,1)S(1)}, u32[]{:S(2)}, u32[]{:S(2)}) collective-permute-start(bf16[512,256]{1,0:T(8,128)(2,1)S(1)} %copy-done.22), channel_id=1, source_target_pairs={{8,0},{12,4},{16,8},{20,12},{24,16},{28,20},{9,1},{13,5},{17,9},{2... | collective-permute-start | bytes 786440 | tf_op jit(solution)/shard_map/ppermute | solution.py:22
  75.7 14.2 %collective-permute-start.16 = (bf16[512,256]{1,0:T(8,128)(2,1)S(1)}, bf16[512,256]{1,0:T(8,128)(2,1)S(1)}, u32[]{:S(2)}, u32[]{:S(2)}) collective-permute-start(bf16[512,256]{1,0:T(8,128)(2,1)S(1)} %copy-done.21), channel_id=1, source_target_pairs={{0,4},{4,0},{8,12},{12,8},{16,20},{20,16},{24,28},{28,24},{1,5},{5... | collective-permute-start | bytes 786440 | tf_op jit(solution)/shard_map/ppermute | solution.py:26
  75.8 17.7 %collective-permute-start.21 = (bf16[512,256]{1,0:T(8,128)(2,1)S(1)}, bf16[512,256]{1,0:T(8,128)(2,1)S(1)}, u32[]{:S(2)}, u32[]{:S(2)}) collective-permute-start(bf16[512,256]{1,0:T(8,128)(2,1)S(1)} %copy-done.25), channel_id=1, source_target_pairs={{8,0},{12,4},{16,8},{20,12},{24,16},{28,20},{9,1},{13,5},{17,9},{2... | collective-permute-start | bytes 786440 | tf_op jit(solution)/shard_map/ppermute | solution.py:22
  82.3 12.5 %collective-permute-start.22 = (bf16[512,256]{1,0:T(8,128)(2,1)S(1)}, bf16[512,256]{1,0:T(8,128)(2,1)S(1)}, u32[]{:S(2)}, u32[]{:S(2)}) collective-permute-start(bf16[512,256]{1,0:T(8,128)(2,1)S(1)} %copy-done.23), channel_id=1, source_target_pairs={{0,4},{4,0},{8,12},{12,8},{16,20},{20,16},{24,28},{28,24},{1,5},{5... | collective-permute-start | bytes 786440 | tf_op jit(solution)/shard_map/ppermute | solution.py:26
  84.3 14.8 %collective-permute-start.18 = (bf16[512,256]{1,0:T(8,128)(2,1)S(1)}, bf16[512,256]{1,0:T(8,128)(2,1)S(1)}, u32[]{:S(2)}, u32[]{:S(2)}) collective-permute-start(bf16[512,256]{1,0:T(8,128)(2,1)S(1)} %copy-done.20), channel_id=1, source_target_pairs={{8,0},{12,4},{16,8},{20,12},{24,16},{28,20},{9,1},{13,5},{17,9},{2... | collective-permute-start | bytes 786440 | tf_op jit(solution)/shard_map/ppermute | solution.py:22
  85.6 34.4 %copy-start = (f32[512,256]{1,0:T(8,128)S(1)}, f32[512,256]{1,0:T(8,128)}, u32[]{:S(2)}) copy-start(f32[512,256]{1,0:T(8,128)} %get-tuple-element.31) | copy-start | bytes 1572868
  87.9 11.2 %collective-permute-start.19 = (bf16[512,256]{1,0:T(8,128)(2,1)S(1)}, bf16[512,256]{1,0:T(8,128)(2,1)S(1)}, u32[]{:S(2)}, u32[]{:S(2)}) collective-permute-start(bf16[512,256]{1,0:T(8,128)(2,1)S(1)} %copy-done.19), channel_id=1, source_target_pairs={{0,4},{4,0},{8,12},{12,8},{16,20},{20,16},{24,28},{28,24},{1,5},{5... | collective-permute-start | bytes 786440 | tf_op jit(solution)/shard_map/ppermute | solution.py:26
  89.9 30.2 %collective-permute-start.26 = (bf16[512,256]{1,0:T(8,128)(2,1)S(1)}, bf16[512,256]{1,0:T(8,128)(2,1)S(1)}, u32[]{:S(2)}, u32[]{:S(2)}) collective-permute-start(bf16[512,256]{1,0:T(8,128)(2,1)S(1)} %fusion.13), channel_id=1, source_target_pairs={{8,0},{12,4},{16,8},{20,12},{24,16},{28,20},{9,1},{13,5},{17,9},{2... | collective-permute-start | bytes 786440 | tf_op jit(solution)/shard_map/ppermute | solution.py:22
  93.5 16.9 %collective-permute-start.17 = (bf16[512,256]{1,0:T(8,128)(2,1)S(1)}, bf16[512,256]{1,0:T(8,128)(2,1)S(1)}, u32[]{:S(2)}, u32[]{:S(2)}) collective-permute-start(bf16[512,256]{1,0:T(8,128)(2,1)S(1)} %fusion.1), channel_id=1, source_target_pairs={{8,0},{12,4},{16,8},{20,12},{24,16},{28,20},{9,1},{13,5},{17,9},{2... | collective-permute-start | bytes 786440 | tf_op jit(solution)/shard_map/ppermute | solution.py:22
  95.0 25.2 %copy-start.1 = (f32[512,256]{1,0:T(8,128)S(1)}, f32[512,256]{1,0:T(8,128)}, u32[]{:S(2)}) copy-start(f32[512,256]{1,0:T(8,128)} %get-tuple-element.39) | copy-start | bytes 1572868
  95.0 21.0 %collective-permute-start.23 = (bf16[512,256]{1,0:T(8,128)(2,1)S(1)}, bf16[512,256]{1,0:T(8,128)(2,1)S(1)}, u32[]{:S(2)}, u32[]{:S(2)}) collective-permute-start(bf16[512,256]{1,0:T(8,128)(2,1)S(1)} %fusion.9), channel_id=1, source_target_pairs={{8,0},{12,4},{16,8},{20,12},{24,16},{28,20},{9,1},{13,5},{17,9},{2... | collective-permute-start | bytes 786440 | tf_op jit(solution)/shard_map/ppermute | solution.py:22
  99.3 20.7 %collective-permute-start.20 = (bf16[512,256]{1,0:T(8,128)(2,1)S(1)}, bf16[512,256]{1,0:T(8,128)(2,1)S(1)}, u32[]{:S(2)}, u32[]{:S(2)}) collective-permute-start(bf16[512,256]{1,0:T(8,128)(2,1)S(1)} %fusion.5), channel_id=1, source_target_pairs={{8,0},{12,4},{16,8},{20,12},{24,16},{28,20},{9,1},{13,5},{17,9},{2... | collective-permute-start | bytes 786440 | tf_op jit(solution)/shard_map/ppermute | solution.py:22
  (6 other events, 19.5 us)
where the time goes:
time: 122 us; the launch traced here: 121 us
  starting transfers between devices  51.8 us (42%)
  waiting for transfers between devices  36.2 us (30%)
  Pallas kernels  22.9 us (19%)
  local copies, waits for them, and re-layouts  5.58 us (5%)
  other arithmetic  3.63 us (3%)
  between operations  1.23 us (1%)
    ppermute x16, starting transfers between devices, shift(): lax.ppermute(value, 'seq', [(src, src + steps) for src in range(low, high)])  37.7 us
    ppermute x16, waiting for transfers between devices, shift(): lax.ppermute(value, 'seq', [(src, src + steps) for src in range(low, high)])  36.2 us
    pallas_call x4, Pallas kernels, attention_chunk(): pl.pallas_call(body, grid=(heads,), in_specs=in_specs, out_specs=[pl.Bloc...  17.8 us
    ppermute x11, starting transfers between devices, swap(): lax.ppermute(value, axis, [(src, src ^ bit) for src in range(lax.axis_siz...  14 us
    pallas_call x1, Pallas kernels, attn_grad_of(): pl.pallas_call(grad_kernel, grid=(cols // block,), in_specs=[pl.BlockSpec...  5.08 us
    unnamed x55, local copies, waits for them, and re-layouts  3.2 us
  transfers between devices with their start and end apart: 27, of which 8 were waited for; matrix products, arithmetic and copies ran while one was open for 5% of the time, Pallas kernels for 15%

commit v1 on v0

v1 whole, which is shorter than its diff:
```python
import math

import jax
import jax.numpy as jnp
from jax import lax
from jax.experimental import pallas as pl
from jax.experimental.pallas import tpu as pltpu
from jax.sharding import PartitionSpec as P


HDIM = 128
FAR, MID, NEAR = range(3)
SECTIONS = 3
GROUPS = 2
STAT_ROWS = 8
BIG = 1e30
SCALE = 1.0 / math.sqrt(HDIM)
LOG2E = math.log2(math.e)
EXP_SCALE = SCALE * LOG2E


def shift(value, steps):
    count = lax.axis_size("seq")
    low, high = max(0, -steps), min(count, count - steps)
    return lax.ppermute(value, "seq", [(src, src + steps) for src in range(low, high)])


def swap(value, axis, bit):
    pairs = [(src, src ^ bit) for src in range(lax.axis_size(axis))]
    return lax.ppermute(value, axis, pairs)


def dot(lhs, rhs, lhs_dim, rhs_dim):
    return lax.dot_general(
        lhs, rhs, (((lhs_dim,), (rhs_dim,)), ((), ())), preferred_element_type=jnp.float32
    )


def call(kernel, grid, ins, outs, work, aliases=None, scratch=()):
    arrays, in_specs = zip(*ins)
    shapes, out_specs = zip(*outs)
    moved = sum(math.prod(a.shape) * a.dtype.itemsize for a in (*arrays, *shapes))
    return pl.pallas_call(
        kernel,
        grid=grid,
        in_specs=in_specs,
        out_specs=out_specs,
        out_shape=shapes,
        scratch_shapes=scratch,
        input_output_aliases=aliases or {},
        cost_estimate=pl.CostEstimate(
            flops=2 * work, bytes_accessed=moved, transcendentals=work // HDIM
        ),
    )(*arrays)


def gathered_pieces(out_grad):
    pieces = {0: out_grad}
    bit = lax.axis_size("head") // 2
    while bit:
        for offset in list(pieces):
            pieces[offset | bit] = swap(pieces[offset], "head", bit)
        bit //= 2
    return [pieces[offset] for offset in range(len(pieces))]


def grad_kernel(head_ref, *refs):
    *piece_refs, proj_ref, out_ref = refs
    width = piece_refs[0].shape[1]
    total = None
    for offset, piece in enumerate(piece_refs):
        start = pl.multiple_of((head_ref[0] ^ offset) * width, width)
        part = dot(piece[...], proj_ref[:, pl.ds(start, width)], 1, 1)
        total = part if total is None else total + part
    out_ref[...] = total.astype(out_ref.dtype)


def attn_grad_of(out_grad, out_proj):
    pieces = gathered_pieces(out_grad)
    rows, width = out_grad.shape
    cols, features = out_proj.shape
    block = 2 * HDIM
    head = lax.axis_index("head").astype(jnp.int32).reshape(1)
    (result,) = call(
        grad_kernel,
        (cols // block,),
        [(head, pl.BlockSpec(memory_space=pltpu.SMEM))]
        + [(piece, pl.BlockSpec((rows, width), lambda i: (0, 0))) for piece in pieces]
        + [(out_proj, pl.BlockSpec((block, features), lambda i: (i, 0)))],
        [
            (
                jax.ShapeDtypeStruct((rows, cols), jnp.bfloat16),
                pl.BlockSpec((rows, block), lambda i: (0, i)),
            )
        ],
        rows * cols * features,
    )
    return result


def causal(raw, fill):
    key_at = lax.broadcasted_iota(jnp.int32, raw.shape, 0)
    query_at = lax.broadcasted_iota(jnp.int32, raw.shape, 1)
    return jnp.where(key_at <= query_at, raw, fill)


class Flags:
    def __init__(self, spans, table_ref, active_ref, place_ref):
        self.spans, self.table = spans, table_ref
        self.active, self.place = active_ref, place_ref

    def usable(self, head, section):
        used = self.table[head, section] * self.active[0, section] > 0
        return used & (self.place[0] >= self.spans[section])

    def is_odd(self):
        return (self.place[0] // self.spans[NEAR]) % 2 == 1


def row_stats(raws, pgrads):
    top = None
    for raw in raws:
        peak = jnp.max(raw, axis=0, keepdims=True)
        top = peak if top is None else jnp.maximum(top, peak)
    norm, delta = 0.0, 0.0
    for raw, pgrad in zip(raws, pgrads):
        prob = jnp.exp2((raw - top) * EXP_SCALE)
        norm = norm + jnp.sum(prob, axis=0, keepdims=True)
        delta = delta + jnp.sum(prob * pgrad, axis=0, keepdims=True)
    return top, norm, delta


def put_rows(ref, *rows):
    for index, row in enumerate(rows):
        ref[0, index : index + 1, :] = row


def stats_own_kernel(spans, t, a, p, q, g, k, v, k_up, v_up, out):
    flags = Flags(spans, t, a, p)
    bias = jnp.where(flags.usable(pl.program_id(0), MID), 0.0, -BIG)
    query, grad = q[...], g[...]
    raws = [causal(dot(k[...], query, 1, 1), -BIG), dot(k_up[...], query, 1, 1) + bias]
    pgrads = [dot(v[...], grad, 1, 1), dot(v_up[...], grad, 1, 1)]
    put_rows(out, *row_stats(raws, pgrads))


def near_keys(odd, own, up):
    return jnp.where(odd, up[...], own[...])


def stats_guest_kernel(spans, t, a, p, qf, gf, qn, gn, k, v, k_up, v_up, far, near):
    odd = Flags(spans, t, a, p).is_odd()
    for query, grad, keys, values, out in (
        (qf, gf, k_up[...], v_up[...], far),
        (qn, gn, near_keys(odd, k, k_up), near_keys(odd, v, v_up), near),
    ):
        raw = dot(keys, query[...], 1, 1)
        pgrad = dot(values, grad[...], 1, 1)
        put_rows(out, *row_stats([raw], [pgrad]))


def combine_kernel(spans, t, a, p, own, far, near, own_out, far_out, near_out):
    flags = Flags(spans, t, a, p)
    for head in range(own.shape[0]):
        uses = [(own, True, own_out)]
        uses += [(far, flags.usable(head, FAR), far_out)]
        uses += [(near, flags.usable(head, NEAR), near_out)]
        peaks = []
        for ref, usable, _ in uses:
            peak = ref[head, 0:1, :]
            peaks.append(peak if usable is True else jnp.where(usable, peak, -BIG))
        top = jnp.maximum(jnp.maximum(peaks[0], peaks[1]), peaks[2])
        norm, delta = 0.0, 0.0
        for (ref, _, _), peak in zip(uses, peaks):
            factor = jnp.exp2((peak - top) * EXP_SCALE)
            norm = norm + factor * ref[head, 1:2, :]
            delta = delta + factor * ref[head, 2:3, :]
        offset = top * EXP_SCALE + jnp.log(norm) * LOG2E
        delta = delta / norm
        for _, usable, out in uses:
            out[head, 0:1, :] = offset if usable is True else jnp.where(usable, offset, BIG)
            out[head, 1:2, :] = delta


def pair_terms(query, grad, keys, values, offset, delta, diagonal=False):
    raw = dot(keys, query, 1, 1)
    prob = jnp.exp2(raw * EXP_SCALE - offset)
    if diagonal:
        prob = causal(prob, 0.0)
    pgrad = dot(values, grad, 1, 1)
    weight = prob.astype(jnp.bfloat16)
    dlogit = (prob * (pgrad - delta)).astype(jnp.bfloat16)
    key_term = dot(dlogit, query, 1, 0)
    value_term = dot(weight, grad, 1, 0)
    query_term = dot(keys, dlogit, 0, 0)
    return query_term, key_term, value_term


def own_kernel(q, g, k, v, stats, dq, dk, dv):
    query_term, key_term, value_term = pair_terms(
        q[...], g[...], k[...], v[...], stats[0, 0:1, :], stats[0, 1:2, :], True
    )
    dq[...] = query_term.T
    dk[...] = key_term
    dv[...] = value_term


def pairs_kernel(
    spans, first, t, a, p, q, g, qf, gf, qn, gn, k, v, k_up, v_up, own_st, far_st, near_st,
    dq_own, dk_own, dv_own, *refs,
):
    dq, dqf, dqn, back, dk, dv = refs[-6:]
    flags = Flags(spans, t, a, p)
    odd = flags.is_odd()
    rows = q.shape[0]
    bias = jnp.where(flags.usable(first + pl.program_id(0), MID), 0.0, BIG)
    keys, values = k_up[...], v_up[...]
    query_term, key_up, value_up = pair_terms(
        q[...], g[...], keys, values, own_st[0, 0:1, :] + bias, own_st[0, 1:2, :]
    )
    dq[...] = (dq_own[...] + query_term.T) * SCALE
    query_term, key_term, value_term = pair_terms(
        qf[...], gf[...], keys, values, far_st[0, 0:1, :], far_st[0, 1:2, :]
    )
    dqf[...] = (query_term * SCALE).T.astype(dqf.dtype)
    key_up = key_up + key_term
    value_up = value_up + value_term
    query_term, key_term, value_term = pair_terms(
        qn[...], gn[...], near_keys(odd, k, k_up), near_keys(odd, v, v_up),
        near_st[0, 0:1, :], near_st[0, 1:2, :],
    )
    dqn[...] = (query_term * SCALE).T.astype(dqn.dtype)
    zero = jnp.zeros_like(key_term)
    back[:rows, :] = ((key_up + jnp.where(odd, key_term, zero)) * SCALE).astype(back.dtype)
    back[rows:, :] = (value_up + jnp.where(odd, value_term, zero)).astype(back.dtype)
    dk[...] = (dk_own[...] + jnp.where(odd, zero, key_term)) * SCALE
    dv[...] = dv_own[...] + jnp.where(odd, zero, value_term)


def body(queries, key_rows, value_rows, out_grad, out_proj, section_table, block_active):
    seq_count = lax.axis_size("seq")
    place = lax.axis_index("seq")
    spans = [seq_count // 2 ** (index + 1) for index in range(SECTIONS)]
    mid_span, near_span = spans[MID], spans[NEAR]
    assert spans[FAR] == 2 * mid_span and mid_span == 2 * near_span
    assert block_active.shape[0] == 1
    rows, cols = queries.shape
    heads = cols // HDIM
    group = heads // GROUPS
    pair_work = rows * rows * HDIM

    smem = pl.BlockSpec(memory_space=pltpu.SMEM)
    flags = [
        (section_table, smem),
        (block_active, smem),
        (place.astype(jnp.int32).reshape(1), smem),
    ]

    def tile(first=0):
        return pl.BlockSpec((rows, HDIM), lambda i: (0, first + i))

    def stat(first=0):
        return pl.BlockSpec((1, STAT_ROWS, rows), lambda i: (first + i, 0, 0))

    def tiles(*arrays, first=0):
        return [(array, tile(first)) for array in arrays]

    stat_shape = jax.ShapeDtypeStruct((heads, STAT_ROWS, rows), jnp.float32)
    wide_f32 = jax.ShapeDtypeStruct((rows, cols), jnp.float32)
    wide_bf16 = jax.ShapeDtypeStruct((rows, cols), jnp.bfloat16)

    key_up = shift(key_rows, mid_span)
    value_up = shift(value_rows, mid_span)
    query_far = shift(queries, -mid_span)
    query_near = swap(queries, "seq", near_span)
    grads = attn_grad_of(out_grad, out_proj)
    grad_far = shift(grads, -mid_span)
    grad_near = swap(grads, "seq", near_span)

    local = (key_rows, value_rows, key_up, value_up)
    guests = (query_far, grad_far, query_near, grad_near)

    def stats_own(*refs):
        stats_own_kernel(spans, *refs)

    def stats_guest(*refs):
        stats_guest_kernel(spans, *refs)

    def combine(*refs):
        combine_kernel(spans, *refs)

    (own_stats,) = call(
        stats_own,
        (heads,),
        flags + tiles(queries, grads, *local),
        [(stat_shape, stat())],
        heads * 4 * pair_work,
    )
    far_stats, near_stats = call(
        stats_guest,
        (heads,),
        flags + tiles(*guests, *local),
        [(stat_shape, stat())] * 2,
        heads * 4 * pair_work,
    )
    far_stats = shift(far_stats, mid_span)
    near_stats = swap(near_stats, "seq", near_span)
    whole = pl.BlockSpec((heads, STAT_ROWS, rows), lambda i: (0, 0, 0))
    own_norm, far_norm, near_norm = call(
        combine,
        (1,),
        flags + [(array, whole) for array in (own_stats, far_stats, near_stats)],
        [(stat_shape, whole)] * 3,
        heads * rows * HDIM,
    )
    far_norm = shift(far_norm, -mid_span)
    near_norm = swap(near_norm, "seq", near_span)
    own_parts = call(
        own_kernel,
        (heads,),
        tiles(queries, grads, key_rows, value_rows) + [(own_norm, stat())],
        [(wide_f32, tile())] * 3,
        heads * 5 * pair_work,
    )

    query_part = query_far_part = query_near_part = None
    key_grad = jnp.zeros((rows, cols), jnp.bfloat16)
    value_grad = jnp.zeros((rows, cols), jnp.bfloat16)
    for index in range(GROUPS):
        first = index * group

        def pairs(*refs, first=first):
            pairs_kernel(spans, first, *refs)

        ins = flags + tiles(queries, grads, *guests, *local, first=first)
        ins += [(array, stat(first)) for array in (own_norm, far_norm, near_norm)]
        ins += tiles(*own_parts, first=first)
        aliases = {}
        if index:
            for number, array in enumerate((query_part, query_far_part, query_near_part)):
                aliases[len(ins)] = number
                ins.append((array, pl.BlockSpec(memory_space=pl.ANY)))
        half_f32 = jax.ShapeDtypeStruct((rows, group * HDIM), jnp.float32)
        half_back = jax.ShapeDtypeStruct((2 * rows, group * HDIM), jnp.bfloat16)
        query_part, query_far_part, query_near_part, back, key_part, value_part = call(
            pairs,
            (group,),
            ins,
            [
                (wide_f32, tile(first)),
                (wide_bf16, tile(first)),
                (wide_bf16, tile(first)),
                (half_back, pl.BlockSpec((2 * rows, HDIM), lambda i: (0, i))),
                (half_f32, tile()),
                (half_f32, tile()),
            ],
            group * 15 * pair_work,
            aliases,
        )
        back = shift(back, -mid_span).astype(jnp.float32)
        key_part = (key_part + back[:rows]).astype(jnp.bfloat16)
        value_part = (value_part + back[rows:]).astype(jnp.bfloat16)
        at = (0, first * HDIM)
        key_grad = lax.dynamic_update_slice(key_grad, key_part, at)
        value_grad = lax.dynamic_update_slice(value_grad, value_part, at)
    query_far_part = shift(query_far_part, mid_span)
    query_near_part = swap(query_near_part, "seq", near_span)
    query_grad = query_part + query_far_part.astype(jnp.float32)
    query_grad = query_grad + query_near_part.astype(jnp.float32)
    return query_grad.astype(jnp.bfloat16), key_grad, value_grad


def solution(mesh):
    return jax.shard_map(
        body,
        mesh=mesh,
        in_specs=(
            P("seq", "head"),
            P("seq", "head"),
            P("seq", "head"),
            P("seq", "head"),
            P("head", None),
            P("head", None),
            P("seq", None),
        ),
        out_specs=(P("seq", "head"), P("seq", "head"), P("seq", "head")),
        check_vma=False,
    )
```

time: 122 us -> 109 us (0.89); the launches traced: 121 us -> 107 us
  starting transfers between devices: 51.8 us -> 31.9 us
  Pallas kernels: 22.9 us -> 41.3 us
  waiting for transfers between devices: 36.2 us -> 25.5 us
  local copies, waits for them, and re-layouts: 5.58 us -> 4.19 us
    pallas_call x5 -> x7, Pallas kernels: 22.9 us -> 41.3 us  [call(): pl.pallas_call(kernel, grid=grid, in_specs=in_specs, out_specs=out_specs,...]
    ppermute x16 -> x9, starting transfers between devices: 37.7 us -> 24.1 us  [shift(): lax.ppermute(value, 'seq', [(src, src + steps) for src in range(low, high)])]
    ppermute x16 -> x9, waiting for transfers between devices: 36.2 us -> 22.5 us  [shift(): lax.ppermute(value, 'seq', [(src, src + steps) for src in range(low, high)])]
    ppermute x11 -> x8, starting transfers between devices: 14 us -> 7.88 us  [swap(): return lax.ppermute(value, axis, pairs)]
    ppermute x11 -> x8, waiting for transfers between devices: 0.03 us -> 2.94 us  [swap(): return lax.ppermute(value, axis, pairs)]
    slice x2 -> x0, local copies, waits for them, and re-layouts: 1.38 us -> none  [the longest x1 1.36 us: body(): array[:, chunk * width:(chunk + 1) * width]]
    unnamed x55 -> x39, local copies, waits for them, and re-layouts: 3.2 us -> 4.19 us
  transfers between devices with their start and end apart: 27 -> 17, of which waited for: 8 -> 5; matrix products, arithmetic and copies ran while one was open for 5% -> 2% of each run, Pallas kernels for 15% -> 24%
where the time goes in v1:
time: 109 us; the launch traced here: 107 us
  Pallas kernels  41.3 us (38%)
  starting transfers between devices  31.9 us (29%)
  waiting for transfers between devices  25.5 us (23%)
  local copies, waits for them, and re-layouts  4.19 us (4%)
  other arithmetic  2.91 us (3%)
    pallas_call x7, Pallas kernels, call(): pl.pallas_call(kernel, grid=grid, in_specs=in_specs, out_specs=out_specs,...  41.3 us
    ppermute x9, starting transfers between devices, shift(): lax.ppermute(value, 'seq', [(src, src + steps) for src in range(low, high)])  24.1 us
    ppermute x9, waiting for transfers between devices, shift(): lax.ppermute(value, 'seq', [(src, src + steps) for src in range(low, high)])  22.5 us
    ppermute x8, starting transfers between devices, swap(): return lax.ppermute(value, axis, pairs)  7.88 us
    unnamed x39, local copies, waits for them, and re-layouts  4.19 us
    ppermute x8, waiting for transfers between devices, swap(): return lax.ppermute(value, axis, pairs)  2.94 us
  transfers between devices with their start and end apart: 17, of which 5 were waited for; matrix products, arithmetic and copies ran while one was open for 2% of the time, Pallas kernels for 24%

profile of v1, /device:TPU:0, one launch (start us, length us, event | category | flops | bytes accessed | tf_op | source)
XLA Modules:
  0.0 106.8 jit_solution(7604552018092024697)
XLA Ops:
  0.6 3.1 %collective-permute-start.1 = (bf16[256,512]{1,0:T(8,128)(2,1)}, bf16[256,512]{1,0:T(8,128)(2,1)S(1)}, u32[]{:S(2)}, u32[]{:S(2)}) collective-permute-start(bf16[256,512]{1,0:T(8,128)(2,1)} %refs_0_.6), channel_id=1, source_target_pairs={{0,2},{1,3},{2,0},{3,1},{4,6},{5,7},{6,4},{7,5},{8,10},{9,11},{10,... | collective-permute-start | bytes 786440 | tf_op jit(solution)/shard_map/ppermute | solution.py:30
  3.7 3.5 %collective-permute-start.7 = (bf16[256,1024]{1,0:T(8,128)(2,1)}, bf16[256,1024]{1,0:T(8,128)(2,1)S(1)}, u32[]{:S(2)}, u32[]{:S(2)}) collective-permute-start(bf16[256,1024]{1,0:T(8,128)(2,1)} %refs_9_.3), channel_id=1, source_target_pairs={{0,8},{4,12},{8,16},{12,20},{16,24},{20,28},{1,9},{5,13},{9,17},{1... | collective-permute-start | bytes 1572872 | tf_op jit(solution)/shard_map/ppermute | solution.py:25
  7.2 0.1 collective-permute-start
  7.3 2.9 %collective-permute-done.1.refs_2_ = bf16[256,512]{1,0:T(8,128)(2,1)S(1)} collective-permute-done((bf16[256,512]{1,0:T(8,128)(2,1)}, bf16[256,512]{1,0:T(8,128)(2,1)S(1)}, u32[]{:S(2)}, u32[]{:S(2)}) %collective-permute-start.1) | collective-permute-done | bytes 262176 | tf_op jit(solution)/shard_map/ppermute | solution.py:30
  10.2 1.3 %collective-permute-start.3 = (bf16[256,1024]{1,0:T(8,128)(2,1)}, bf16[256,1024]{1,0:T(8,128)(2,1)S(1)}, u32[]{:S(2)}, u32[]{:S(2)}) collective-permute-start(bf16[256,1024]{1,0:T(8,128)(2,1)} %refs_3_.5), channel_id=1, source_target_pairs={{8,0},{12,4},{16,8},{20,12},{24,16},{28,20},{9,1},{13,5},{17,9},{2... | collective-permute-start | bytes 1572872 | tf_op jit(solution)/shard_map/ppermute | solution.py:25
  11.5 1.8 %collective-permute-start.5 = (bf16[256,1024]{1,0:T(8,128)(2,1)}, bf16[256,1024]{1,0:T(8,128)(2,1)S(1)}, u32[]{:S(2)}, u32[]{:S(2)}) collective-permute-start(bf16[256,1024]{1,0:T(8,128)(2,1)} %refs_3_.5), channel_id=1, source_target_pairs={{0,4},{4,0},{8,12},{12,8},{16,20},{20,16},{24,28},{28,24},{1,5},{5... | collective-permute-start | bytes 1572872 | tf_op jit(solution)/shard_map/ppermute | solution.py:30
  13.3 4.6 %collective-permute-start.8 = (bf16[256,1024]{1,0:T(8,128)(2,1)}, bf16[256,1024]{1,0:T(8,128)(2,1)S(1)}, u32[]{:S(2)}, u32[]{:S(2)}) collective-permute-start(bf16[256,1024]{1,0:T(8,128)(2,1)} %refs_10_.3), channel_id=1, source_target_pairs={{0,8},{4,12},{8,16},{12,20},{16,24},{20,28},{1,9},{5,13},{9,17},{1... | collective-permute-start | bytes 1572872 | tf_op jit(solution)/shard_map/ppermute | solution.py:25
  17.9 0.0 collective-permute-done.2.refs_3_
  17.9 0.7 copy-done.18
  18.6 5.1 %shard_map.94.refs_4_.g = bf16[256,1024]{1,0:T(8,128)(2,1)} custom-call(s32[1]{0:T(128)} %bitcast.1.head_ref, bf16[256,512]{1,0:T(8,128)(2,1)} %refs_0_.6, bf16[256,512]{1,0:T(8,128)(2,1)} %copy-done.17, bf16[256,512]{1,0:T(8,128)(2,1)} %copy-done.16, bf16[256,512]{1,0:T(8,128)(2,1)} %copy-done.18, bf16[1024,2048]{1,0:T(8,128)(2,1)} %refs_4_.1), custom_call_target="tpu_custom_call" | custom-call | flops 1073741824 | bytes 5767172 | tf_op jit(solution)/shard_map/pallas_call | solution.py:43
  23.7 1.3 %collective-permute-start.4 = (bf16[256,1024]{1,0:T(8,128)(2,1)}, bf16[256,1024]{1,0:T(8,128)(2,1)S(1)}, u32[]{:S(2)}, u32[]{:S(2)}) collective-permute-start(bf16[256,1024]{1,0:T(8,128)(2,1)} %shard_map.94.refs_4_.g), channel_id=1, source_target_pairs={{8,0},{12,4},{16,8},{20,12},{24,16},{28,20},{9,1},{13,5},{17,9},{2... | collective-permute-start | bytes 1572872 | tf_op jit(solution)/shard_map/ppermute | solution.py:25
  25.0 0.4 collective-permute-start.6
  25.3 0.7 copy.17.refs_0_
  26.0 3.6 %collective-permute-done.8.refs_8_.refs_10_.refs_12_ = bf16[256,1024]{1,0:T(8,128)(2,1)S(1)} collective-permute-done((bf16[256,1024]{1,0:T(8,128)(2,1)}, bf16[256,1024]{1,0:T(8,128)(2,1)S(1)}, u32[]{:S(2)}, u32[]{:S(2)}) %collective-permute-start.8) | collective-permute-done | bytes 524320 | tf_op jit(solution)/shard_map/ppermute | solution.py:25
  29.6 0.0 collective-permute-done.5.refs_5_.refs_7_
  29.6 9.6 %collective-permute-done.4.refs_4_.refs_6_ = bf16[256,1024]{1,0:T(8,128)(2,1)S(1)} collective-permute-done((bf16[256,1024]{1,0:T(8,128)(2,1)}, bf16[256,1024]{1,0:T(8,128)(2,1)S(1)}, u32[]{:S(2)}, u32[]{:S(2)}) %collective-permute-start.4) | collective-permute-done | bytes 524320 | tf_op jit(solution)/shard_map/ppermute | solution.py:25
  39.3 0.8 copy-done.4
  40.0 0.2 copy-done.5
  40.2 7.0 %shard_map.96 = (f32[8,8,256]{2,1,0:T(8,128)}, f32[8,8,256]{2,1,0:T(8,128)}) custom-call(s32[8,3]{1,0:T(8,128)} %copy.17.refs_0_, s32[1,3]{1,0:T(1,128)} %refs_1_.9, s32[1]{0:T(128)} %bitcast.refs_2_, bf16[256,1024]{1,0:T(8,128)(2,1)} %copy-done.1, bf16[256,1024]{1,0:T(8,128)(2,1)} %copy-done.4, bf16[256,1024]{1,0:T(8,128)(2,1)} %copy-done.2, ...), custom_call_target="tpu_custom_call" | custom-call | flops 536870912 | bytes 4325488 | tf_op jit(solution)/shard_map/pallas_call | solution.py:43
  47.3 0.4 collective-permute-start.10
  47.7 3.6 %collective-permute-start.9 = (f32[8,8,256]{2,1,0:T(8,128)}, f32[8,8,256]{2,1,0:T(8,128)S(1)}, u32[]{:S(2)}, u32[]{:S(2)}) collective-permute-start(f32[8,8,256]{2,1,0:T(8,128)} %get-tuple-element.23), channel_id=1, source_target_pairs={{0,8},{4,12},{8,16},{12,20},{16,24},{20,28},{1,9},{5,13},{9,17},{1... | collective-permute-start | bytes 196616 | tf_op jit(solution)/shard_map/ppermute | solution.py:25
  51.3 6.8 %shard_map.95.refs_3_ = f32[8,8,256]{2,1,0:T(8,128)} custom-call(s32[8,3]{1,0:T(8,128)} %copy.17.refs_0_, s32[1,3]{1,0:T(1,128)} %refs_1_.9, s32[1]{0:T(128)} %bitcast.refs_2_, bf16[256,1024]{1,0:T(8,128)(2,1)} %refs_3_.5, bf16[256,1024]{1,0:T(8,128)(2,1)} %shard_map.94.refs_4_.g, bf16[256,1024]{1,0:T(8,128)(2,1)} %refs_9_.3, bf16[256,1024]{1,0:T(8,128)(2,1)} %refs_10_.3, ...), custom_call_target="tpu_custom_call" | custom-call | flops 536870912 | bytes 3211376 | tf_op jit(solution)/shard_map/pallas_call | solution.py:43
  58.1 0.0 collective-permute-done.9.refs_4_
  58.1 0.6 copy-done.13
  58.7 0.6 copy-done.14
  59.3 1.7 %shard_map.97 = (f32[8,8,256]{2,1,0:T(8,128)}, f32[8,8,256]{2,1,0:T(8,128)}, f32[8,8,256]{2,1,0:T(8,128)}) custom-call(s32[8,3]{1,0:T(8,128)} %copy.17.refs_0_, s32[1,3]{1,0:T(1,128)} %refs_1_.9, s32[1]{0:T(128)} %bitcast.refs_2_, f32[8,8,256]{2,1,0:T(8,128)} %shard_map.95.refs_3_, f32[8,8,256]{2,1,0:T(8,128)} %copy-done.14, f32[8,8,256]{2,1,0:T(8,128)} %copy-done.13), custom_call_target="tpu_custom_call" | custom-call | flops 524288 | bytes 393328 | tf_op jit(solution)/shard_map/pallas_call | solution.py:43
  61.0 1.3 %collective-permute-start.11 = (f32[8,8,256]{2,1,0:T(8,128)}, f32[8,8,256]{2,1,0:T(8,128)S(1)}, u32[]{:S(2)}, u32[]{:S(2)}) collective-permute-start(f32[8,8,256]{2,1,0:T(8,128)} %get-tuple-element.26), channel_id=1, source_target_pairs={{8,0},{12,4},{16,8},{20,12},{24,16},{28,20},{9,1},{13,5},{17,9},{2... | collective-permute-start | bytes 196616 | tf_op jit(solution)/shard_map/ppermute | solution.py:25
  62.3 1.7 %collective-permute-start.12 = (f32[8,8,256]{2,1,0:T(8,128)}, f32[8,8,256]{2,1,0:T(8,128)S(1)}, u32[]{:S(2)}, u32[]{:S(2)}) collective-permute-start(f32[8,8,256]{2,1,0:T(8,128)} %get-tuple-element.27), channel_id=1, source_target_pairs={{0,4},{4,0},{8,12},{12,8},{16,20},{20,16},{24,28},{28,24},{1,5},{5... | collective-permute-start | bytes 196616 | tf_op jit(solution)/shard_map/ppermute | solution.py:30
  64.0 7.3 %shard_map.98 = (f32[256,1024]{1,0:T(8,128)}, f32[256,1024]{1,0:T(8,128)}, f32[256,1024]{1,0:T(8,128)}) custom-call(bf16[256,1024]{1,0:T(8,128)(2,1)} %refs_3_.5, bf16[256,1024]{1,0:T(8,128)(2,1)} %shard_map.94.refs_4_.g, bf16[256,1024]{1,0:T(8,128)(2,1)} %refs_9_.3, bf16[256,1024]{1,0:T(8,128)(2,1)} %refs_10_.3, f32[8,8,256]{2,1,0:T(8,128)} %get-tuple-element.25.stats.refs_13_), custom_call_target="tpu_custom_call" | custom-call | flops 671088640 | bytes 5308416 | tf_op jit(solution)/shard_map/pallas_call | solution.py:43
  71.3 0.0 collective-permute-done.11.refs_14_
  71.3 0.0 collective-permute-done.12.refs_15_
  71.3 0.6 copy-done.11
  71.9 0.0 copy-done.12
  71.9 6.7 %shard_map.99 = (f32[256,1024]{1,0:T(8,128)}, bf16[256,1024]{1,0:T(8,128)(2,1)}, bf16[256,1024]{1,0:T(8,128)(2,1)}, bf16[512,512]{1,0:T(8,128)(2,1)}, f32[256,512]{1,0:T(8,128)}, /*index=5*/f32[256,512]{1,0:T(8,128)}) custom-call(s32[8,3]{1,0:T(8,128)} %copy.17.refs_0_, s32[1,3]{1,0:T(1,128)} %refs_1_.9, s32[1]{0:T(128)} %bitcast.refs_2_, ...), custom_call_target="tpu_custom_call" | custom-call | flops 1006632960 | bytes 12255344 | tf_op jit(solution)/shard_map/pallas_call | solution.py:43
  78.6 1.3 %collective-permute-start.15 = (bf16[512,512]{1,0:T(8,128)(2,1)}, bf16[512,512]{1,0:T(8,128)(2,1)S(1)}, u32[]{:S(2)}, u32[]{:S(2)}) collective-permute-start(bf16[512,512]{1,0:T(8,128)(2,1)} %get-tuple-element.38), channel_id=1, source_target_pairs={{8,0},{12,4},{16,8},{20,12},{24,16},{28,20},{9,1},{13,5},{17,9},{2... | collective-permute-start | bytes 1572872 | tf_op jit(solution)/shard_map/ppermute | solution.py:25
  79.9 6.8 %shard_map.100 = (f32[256,1024]{1,0:T(8,128)}, bf16[256,1024]{1,0:T(8,128)(2,1)}, bf16[256,1024]{1,0:T(8,128)(2,1)}, bf16[512,512]{1,0:T(8,128)(2,1)}, f32[256,512]{1,0:T(8,128)}, /*index=5*/f32[256,512]{1,0:T(8,128)}) custom-call(s32[8,3]{1,0:T(8,128)} %copy.17.refs_0_, ...), custom_call_target="tpu_custom_call", output_to_operand_aliasing={{0}: (19, {}), {1}: (20, {}), {2}: (21, {})} | custom-call | flops 1006632960 | bytes 14352496 | tf_op jit(solution)/shard_map/pallas_call | solution.py:43
  86.7 1.4 %collective-permute-start.16 = (bf16[512,512]{1,0:T(8,128)(2,1)}, bf16[512,512]{1,0:T(8,128)(2,1)S(1)}, u32[]{:S(2)}, u32[]{:S(2)}) collective-permute-start(bf16[512,512]{1,0:T(8,128)(2,1)} %get-tuple-element.40), channel_id=1, source_target_pairs={{8,0},{12,4},{16,8},{20,12},{24,16},{28,20},{9,1},{13,5},{17,9},{2... | collective-permute-start | bytes 1572872 | tf_op jit(solution)/shard_map/ppermute | solution.py:25
  88.2 5.8 %collective-permute-start.13 = (bf16[256,1024]{1,0:T(8,128)(2,1)}, bf16[256,1024]{1,0:T(8,128)(2,1)S(1)}, u32[]{:S(2)}, u32[]{:S(2)}) collective-permute-start(bf16[256,1024]{1,0:T(8,128)(2,1)} %get-tuple-element.35), channel_id=1, source_target_pairs={{0,8},{4,12},{8,16},{12,20},{16,24},{20,28},{1,9},{5,13},{9,17},{1... | collective-permute-start | bytes 1572872 | tf_op jit(solution)/shard_map/ppermute | solution.py:25
  94.0 0.5 collective-permute-start.14
  94.5 0.8 collective-permute-done.15
  95.3 0.1 convert_element_type.30
  95.5 0.3 fusion.1
  95.7 8.5 %collective-permute-done.16 = bf16[512,512]{1,0:T(8,128)(2,1)S(1)} collective-permute-done((bf16[512,512]{1,0:T(8,128)(2,1)}, bf16[512,512]{1,0:T(8,128)(2,1)S(1)}, u32[]{:S(2)}, u32[]{:S(2)}) %collective-permute-start.16) | collective-permute-done | bytes 524320 | tf_op jit(solution)/shard_map/ppermute | solution.py:25
  104.2 0.1 convert_element_type.32
  104.4 0.3 fusion
  104.6 1.1 %pad_maximum_fusion = (bf16[256,1024]{1,0:T(8,128)(2,1)}, bf16[256,1024]{1,0:T(8,128)(2,1)}) fusion(bf16[256,512]{1,0:T(8,128)(2,1)S(1)} %get-tuple-element.46, bf16[256,512]{1,0:T(8,128)(2,1)S(1)} %get-tuple-element.44, bf16[256,512]{1,0:T(8,128)(2,1)S(1)} %get-tuple-element.45, bf16[256,512]{1,0:T(8,128)(2,1)S(1)} %get-tuple-element.43), kind=kLoop, calls=%fused_computation.9 | loop fusion | flops 2097152 | bytes 2097152 | tf_op jit(solution)/shard_map/dynamic_update_slice | solution.py:364
  105.8 0.0 collective-permute-done.13
  105.8 1.0 add_convert_fusion
  (38 shorter events, 0.1 us)
Async XLA Ops:
  0.6 24.7 %copy-start.15 = (s32[8,3]{0,1:T(4,128)S(1)}, s32[8,3]{0,1:T(4,128)}, u32[]{:S(2)}) copy-start(s32[8,3]{0,1:T(4,128)} %param.12) | copy-start | bytes 292
  0.6 9.6 %collective-permute-start.1 = (bf16[256,512]{1,0:T(8,128)(2,1)}, bf16[256,512]{1,0:T(8,128)(2,1)S(1)}, u32[]{:S(2)}, u32[]{:S(2)}) collective-permute-start(bf16[256,512]{1,0:T(8,128)(2,1)} %refs_0_.6), channel_id=1, source_target_pairs={{0,2},{1,3},{2,0},{3,1},{4,6},{5,7},{6,4},{7,5},{8,10},{9,11},{10,... | collective-permute-start | bytes 786440 | tf_op jit(solution)/shard_map/ppermute | solution.py:30
  3.7 21.2 %collective-permute-start.7 = (bf16[256,1024]{1,0:T(8,128)(2,1)}, bf16[256,1024]{1,0:T(8,128)(2,1)S(1)}, u32[]{:S(2)}, u32[]{:S(2)}) collective-permute-start(bf16[256,1024]{1,0:T(8,128)(2,1)} %refs_9_.3), channel_id=1, source_target_pairs={{0,8},{4,12},{8,16},{12,20},{16,24},{20,28},{1,9},{5,13},{9,17},{1... | collective-permute-start | bytes 1572872 | tf_op jit(solution)/shard_map/ppermute | solution.py:25
  7.2 6.1 %collective-permute-start = (bf16[256,512]{1,0:T(8,128)(2,1)}, bf16[256,512]{1,0:T(8,128)(2,1)S(1)}, u32[]{:S(2)}, u32[]{:S(2)}) collective-permute-start(bf16[256,512]{1,0:T(8,128)(2,1)} %refs_0_.6), channel_id=1, source_target_pairs={{0,1},{1,0},{2,3},{3,2},{4,5},{5,4},{6,7},{7,6},{8,9},{9,8},{10,11... | collective-permute-start | bytes 786440 | tf_op jit(solution)/shard_map/ppermute | solution.py:30
  10.2 7.7 %copy-start.16 = (bf16[256,512]{1,0:T(8,128)(2,1)}, bf16[256,512]{1,0:T(8,128)(2,1)S(1)}, u32[]{:S(2)}) copy-start(bf16[256,512]{1,0:T(8,128)(2,1)S(1)} %collective-permute-done.1.refs_2_) | copy-start | bytes 786436
  10.2 7.7 %collective-permute-start.2 = (bf16[256,512]{1,0:T(8,128)(2,1)S(1)}, bf16[256,512]{1,0:T(8,128)(2,1)S(1)}, u32[]{:S(2)}, u32[]{:S(2)}) collective-permute-start(bf16[256,512]{1,0:T(8,128)(2,1)S(1)} %collective-permute-done.1.refs_2_), channel_id=1, source_target_pairs={{0,1},{1,0},{2,3},{3,2},{4,5},{5,4},{6,7},{7,6},{8,9},{9,8},{10,11... | collective-permute-start | bytes 786440 | tf_op jit(solution)/shard_map/ppermute | solution.py:30
  10.2 19.4 %collective-permute-start.3 = (bf16[256,1024]{1,0:T(8,128)(2,1)}, bf16[256,1024]{1,0:T(8,128)(2,1)S(1)}, u32[]{:S(2)}, u32[]{:S(2)}) collective-permute-start(bf16[256,1024]{1,0:T(8,128)(2,1)} %refs_3_.5), channel_id=1, source_target_pairs={{8,0},{12,4},{16,8},{20,12},{24,16},{28,20},{9,1},{13,5},{17,9},{2... | collective-permute-start | bytes 1572872 | tf_op jit(solution)/shard_map/ppermute | solution.py:25
  11.5 18.1 %collective-permute-start.5 = (bf16[256,1024]{1,0:T(8,128)(2,1)}, bf16[256,1024]{1,0:T(8,128)(2,1)S(1)}, u32[]{:S(2)}, u32[]{:S(2)}) collective-permute-start(bf16[256,1024]{1,0:T(8,128)(2,1)} %refs_3_.5), channel_id=1, source_target_pairs={{0,4},{4,0},{8,12},{12,8},{16,20},{20,16},{24,28},{28,24},{1,5},{5... | collective-permute-start | bytes 1572872 | tf_op jit(solution)/shard_map/ppermute | solution.py:30
  13.3 4.6 %copy-start.17 = (bf16[256,512]{1,0:T(8,128)(2,1)}, bf16[256,512]{1,0:T(8,128)(2,1)S(1)}, u32[]{:S(2)}) copy-start(bf16[256,512]{1,0:T(8,128)(2,1)S(1)} %collective-permute-done.refs_1_) | copy-start | bytes 786436
  13.3 16.3 %collective-permute-start.8 = (bf16[256,1024]{1,0:T(8,128)(2,1)}, bf16[256,1024]{1,0:T(8,128)(2,1)S(1)}, u32[]{:S(2)}, u32[]{:S(2)}) collective-permute-start(bf16[256,1024]{1,0:T(8,128)(2,1)} %refs_10_.3), channel_id=1, source_target_pairs={{0,8},{4,12},{8,16},{12,20},{16,24},{20,28},{1,9},{5,13},{9,17},{1... | collective-permute-start | bytes 1572872 | tf_op jit(solution)/shard_map/ppermute | solution.py:25
  17.9 0.7 copy-start.18
  23.7 15.6 %collective-permute-start.4 = (bf16[256,1024]{1,0:T(8,128)(2,1)}, bf16[256,1024]{1,0:T(8,128)(2,1)S(1)}, u32[]{:S(2)}, u32[]{:S(2)}) collective-permute-start(bf16[256,1024]{1,0:T(8,128)(2,1)} %shard_map.94.refs_4_.g), channel_id=1, source_target_pairs={{8,0},{12,4},{16,8},{20,12},{24,16},{28,20},{9,1},{13,5},{17,9},{2... | collective-permute-start | bytes 1572872 | tf_op jit(solution)/shard_map/ppermute | solution.py:25
  25.0 14.3 %copy-start = (bf16[256,1024]{1,0:T(8,128)(2,1)}, bf16[256,1024]{1,0:T(8,128)(2,1)S(1)}, u32[]{:S(2)}) copy-start(bf16[256,1024]{1,0:T(8,128)(2,1)S(1)} %collective-permute-done.7.refs_7_.refs_9_.refs_11_) | copy-start | bytes 1572868
  25.0 14.3 %collective-permute-start.6 = (bf16[256,1024]{1,0:T(8,128)(2,1)}, bf16[256,1024]{1,0:T(8,128)(2,1)S(1)}, u32[]{:S(2)}, u32[]{:S(2)}) collective-permute-start(bf16[256,1024]{1,0:T(8,128)(2,1)} %shard_map.94.refs_4_.g), channel_id=1, source_target_pairs={{0,4},{4,0},{8,12},{12,8},{16,20},{20,16},{24,28},{28,24},{1,5},{5... | collective-permute-start | bytes 1572872 | tf_op jit(solution)/shard_map/ppermute | solution.py:30
  29.6 9.6 %copy-start.3 = (bf16[256,1024]{1,0:T(8,128)(2,1)}, bf16[256,1024]{1,0:T(8,128)(2,1)S(1)}, u32[]{:S(2)}) copy-start(bf16[256,1024]{1,0:T(8,128)(2,1)S(1)} %collective-permute-done.8.refs_8_.refs_10_.refs_12_) | copy-start | bytes 1572868
  29.6 9.6 %copy-start.1 = (bf16[256,1024]{1,0:T(8,128)(2,1)}, bf16[256,1024]{1,0:T(8,128)(2,1)S(1)}, u32[]{:S(2)}) copy-start(bf16[256,1024]{1,0:T(8,128)(2,1)S(1)} %collective-permute-done.3.refs_3_.refs_5_) | copy-start | bytes 1572868
  29.6 9.6 %copy-start.2 = (bf16[256,1024]{1,0:T(8,128)(2,1)}, bf16[256,1024]{1,0:T(8,128)(2,1)S(1)}, u32[]{:S(2)}) copy-start(bf16[256,1024]{1,0:T(8,128)(2,1)S(1)} %collective-permute-done.5.refs_5_.refs_7_) | copy-start | bytes 1572868
  39.2 0.8 copy-start.4
  39.2 1.0 copy-start.5
  47.3 10.8 %collective-permute-start.10 = (f32[8,8,256]{2,1,0:T(8,128)}, f32[8,8,256]{2,1,0:T(8,128)S(1)}, u32[]{:S(2)}, u32[]{:S(2)}) collective-permute-start(f32[8,8,256]{2,1,0:T(8,128)} %get-tuple-element.24), channel_id=1, source_target_pairs={{0,4},{4,0},{8,12},{12,8},{16,20},{20,16},{24,28},{28,24},{1,5},{5... | collective-permute-start | bytes 196616 | tf_op jit(solution)/shard_map/ppermute | solution.py:30
  47.7 10.4 %collective-permute-start.9 = (f32[8,8,256]{2,1,0:T(8,128)}, f32[8,8,256]{2,1,0:T(8,128)S(1)}, u32[]{:S(2)}, u32[]{:S(2)}) collective-permute-start(f32[8,8,256]{2,1,0:T(8,128)} %get-tuple-element.23), channel_id=1, source_target_pairs={{0,8},{4,12},{8,16},{12,20},{16,24},{20,28},{1,9},{5,13},{9,17},{1... | collective-permute-start | bytes 196616 | tf_op jit(solution)/shard_map/ppermute | solution.py:25
  58.1 0.6 copy-start.13
  58.7 0.6 copy-start.14
  61.0 10.3 %collective-permute-start.11 = (f32[8,8,256]{2,1,0:T(8,128)}, f32[8,8,256]{2,1,0:T(8,128)S(1)}, u32[]{:S(2)}, u32[]{:S(2)}) collective-permute-start(f32[8,8,256]{2,1,0:T(8,128)} %get-tuple-element.26), channel_id=1, source_target_pairs={{8,0},{12,4},{16,8},{20,12},{24,16},{28,20},{9,1},{13,5},{17,9},{2... | collective-permute-start | bytes 196616 | tf_op jit(solution)/shard_map/ppermute | solution.py:25
  62.3 9.0 %collective-permute-start.12 = (f32[8,8,256]{2,1,0:T(8,128)}, f32[8,8,256]{2,1,0:T(8,128)S(1)}, u32[]{:S(2)}, u32[]{:S(2)}) collective-permute-start(f32[8,8,256]{2,1,0:T(8,128)} %get-tuple-element.27), channel_id=1, source_target_pairs={{0,4},{4,0},{8,12},{12,8},{16,20},{20,16},{24,28},{28,24},{1,5},{5... | collective-permute-start | bytes 196616 | tf_op jit(solution)/shard_map/ppermute | solution.py:30
  71.3 0.6 copy-start.11
  71.3 0.6 copy-start.12
  78.6 16.7 %collective-permute-start.15 = (bf16[512,512]{1,0:T(8,128)(2,1)}, bf16[512,512]{1,0:T(8,128)(2,1)S(1)}, u32[]{:S(2)}, u32[]{:S(2)}) collective-permute-start(bf16[512,512]{1,0:T(8,128)(2,1)} %get-tuple-element.38), channel_id=1, source_target_pairs={{8,0},{12,4},{16,8},{20,12},{24,16},{28,20},{9,1},{13,5},{17,9},{2... | collective-permute-start | bytes 1572872 | tf_op jit(solution)/shard_map/ppermute | solution.py:25
  79.9 15.6 %copy-start.9 = (f32[256,512]{1,0:T(8,128)S(1)}, f32[256,512]{1,0:T(8,128)}, u32[]{:S(2)}) copy-start(f32[256,512]{1,0:T(8,128)} %get-tuple-element.37) | copy-start | bytes 1572868
  79.9 15.6 %copy-start.10 = (f32[256,512]{1,0:T(8,128)S(1)}, f32[256,512]{1,0:T(8,128)}, u32[]{:S(2)}) copy-start(f32[256,512]{1,0:T(8,128)} %get-tuple-element.41) | copy-start | bytes 1572868
  86.7 17.6 %copy-start.7 = (f32[256,512]{1,0:T(8,128)S(1)}, f32[256,512]{1,0:T(8,128)}, u32[]{:S(2)}) copy-start(f32[256,512]{1,0:T(8,128)} %get-tuple-element.39) | copy-start | bytes 1572868
  86.7 17.6 %copy-start.8 = (f32[256,512]{1,0:T(8,128)S(1)}, f32[256,512]{1,0:T(8,128)}, u32[]{:S(2)}) copy-start(f32[256,512]{1,0:T(8,128)} %get-tuple-element.42) | copy-start | bytes 1572868
  86.7 17.5 %collective-permute-start.16 = (bf16[512,512]{1,0:T(8,128)(2,1)}, bf16[512,512]{1,0:T(8,128)(2,1)S(1)}, u32[]{:S(2)}, u32[]{:S(2)}) collective-permute-start(bf16[512,512]{1,0:T(8,128)(2,1)} %get-tuple-element.40), channel_id=1, source_target_pairs={{8,0},{12,4},{16,8},{20,12},{24,16},{28,20},{9,1},{13,5},{17,9},{2... | collective-permute-start | bytes 1572872 | tf_op jit(solution)/shard_map/ppermute | solution.py:25
  88.2 17.6 %collective-permute-start.13 = (bf16[256,1024]{1,0:T(8,128)(2,1)}, bf16[256,1024]{1,0:T(8,128)(2,1)S(1)}, u32[]{:S(2)}, u32[]{:S(2)}) collective-permute-start(bf16[256,1024]{1,0:T(8,128)(2,1)} %get-tuple-element.35), channel_id=1, source_target_pairs={{0,8},{4,12},{8,16},{12,20},{16,24},{20,28},{1,9},{5,13},{9,17},{1... | collective-permute-start | bytes 1572872 | tf_op jit(solution)/shard_map/ppermute | solution.py:25
  94.0 11.8 %collective-permute-start.14 = (bf16[256,1024]{1,0:T(8,128)(2,1)}, bf16[256,1024]{1,0:T(8,128)(2,1)S(1)}, u32[]{:S(2)}, u32[]{:S(2)}) collective-permute-start(bf16[256,1024]{1,0:T(8,128)(2,1)} %get-tuple-element.36), channel_id=1, source_target_pairs={{0,4},{4,0},{8,12},{12,8},{16,20},{20,16},{24,28},{28,24},{1,5},{5... | collective-permute-start | bytes 1572872 | tf_op jit(solution)/shard_map/ppermute | solution.py:30
  95.5 10.3 %copy-start.6 = (f32[256,1024]{1,0:T(8,128)S(1)}, f32[256,1024]{1,0:T(8,128)}, u32[]{:S(2)}) copy-start(f32[256,1024]{1,0:T(8,128)} %get-tuple-element.34) | copy-start | bytes 3145732

commit v2 on v1

v2 whole, which is shorter than its diff:
```python
import math

import jax
import jax.numpy as jnp
from jax import lax
from jax.experimental import pallas as pl
from jax.experimental.pallas import tpu as pltpu
from jax.sharding import PartitionSpec as P


HDIM = 128
FAR, MID, NEAR = range(3)
SECTIONS = 3
GROUPS = 2
HEADS_PER_STEP = 2
KERNEL_VMEM = 8 * 2**20
STAT_ROWS = 8
BIG = 1e30
SCALE = 1.0 / math.sqrt(HDIM)
LOG2E = math.log2(math.e)
EXP_SCALE = SCALE * LOG2E


def shift(value, steps):
    count = lax.axis_size("seq")
    low, high = max(0, -steps), min(count, count - steps)
    return lax.ppermute(value, "seq", [(src, src + steps) for src in range(low, high)])


def swap(value, axis, bit):
    pairs = [(src, src ^ bit) for src in range(lax.axis_size(axis))]
    return lax.ppermute(value, axis, pairs)


def dot(lhs, rhs, lhs_dim, rhs_dim):
    return lax.dot_general(
        lhs, rhs, (((lhs_dim,), (rhs_dim,)), ((), ())), preferred_element_type=jnp.float32
    )


def on_chip(array):
    return pltpu.with_memory_space_constraint(array, pltpu.VMEM)


def call(kernel, scalars, ins, outs, work, aliases=None):
    smem = pl.BlockSpec(memory_space=pltpu.SMEM)
    vmem = pl.BlockSpec(memory_space=pltpu.VMEM)
    return pl.pallas_call(
        kernel,
        in_specs=[smem] * len(scalars) + [vmem] * len(ins),
        out_specs=[vmem] * len(outs),
        out_shape=[pltpu.VMEM(shape, dtype) for shape, dtype in outs],
        input_output_aliases=aliases or {},
        compiler_params=pltpu.CompilerParams(vmem_limit_bytes=KERNEL_VMEM),
        cost_estimate=pl.CostEstimate(
            flops=2 * work, bytes_accessed=0, transcendentals=work // HDIM
        ),
    )(*scalars, *[on_chip(array) for array in ins])


def each_head(first, count, step):
    def pair(index, carry):
        for offset in range(HEADS_PER_STEP):
            step(first + index * HEADS_PER_STEP + offset)
        return carry

    lax.fori_loop(0, count // HEADS_PER_STEP, pair, None)


def columns(head):
    return pl.ds(pl.multiple_of(head * HDIM, HDIM), HDIM)


def gathered_pieces(out_grad):
    pieces = {0: out_grad}
    bit = lax.axis_size("head") // 2
    while bit:
        for offset in list(pieces):
            pieces[offset | bit] = swap(pieces[offset], "head", bit)
        bit //= 2
    return [pieces[offset] for offset in range(len(pieces))]


def grad_kernel(head_ref, *refs):
    *piece_refs, proj_ref, out_ref = refs
    width = piece_refs[0].shape[1]
    block = 2 * HDIM

    def step(index, carry):
        rows = pl.ds(pl.multiple_of(index * block, block), block)
        total = None
        for offset, piece in enumerate(piece_refs):
            start = pl.multiple_of((head_ref[0] ^ offset) * width, width)
            part = dot(piece[...], proj_ref[rows, pl.ds(start, width)], 1, 1)
            total = part if total is None else total + part
        out_ref[:, rows] = total.astype(out_ref.dtype)
        return carry

    lax.fori_loop(0, out_ref.shape[1] // block, step, None)


def attn_grad_of(out_grad, out_proj):
    pieces = gathered_pieces(out_grad)
    rows = out_grad.shape[0]
    cols, features = out_proj.shape
    head = lax.axis_index("head").astype(jnp.int32).reshape(1)
    (result,) = call(
        grad_kernel,
        [head],
        [*pieces, out_proj],
        [((rows, cols), jnp.bfloat16)],
        rows * cols * features,
    )
    return result


def causal(raw, fill):
    key_at = lax.broadcasted_iota(jnp.int32, raw.shape, 0)
    query_at = lax.broadcasted_iota(jnp.int32, raw.shape, 1)
    return jnp.where(key_at <= query_at, raw, fill)


class Flags:
    def __init__(self, spans, table_ref, active_ref, place_ref):
        self.spans, self.table = spans, table_ref
        self.active, self.place = active_ref, place_ref

    def usable(self, head, section):
        used = self.table[head, section] * self.active[0, section] > 0
        return used & (self.place[0] >= self.spans[section])

    def is_odd(self):
        return (self.place[0] // self.spans[NEAR]) % 2 == 1


def row_stats(head, raws, pgrads, probs, stats):
    top = None
    for raw in raws:
        peak = jnp.max(raw, axis=0, keepdims=True)
        top = peak if top is None else jnp.maximum(top, peak)
    norm, delta = 0.0, 0.0
    for raw, pgrad, out in zip(raws, pgrads, probs):
        prob = jnp.exp2((raw - top) * EXP_SCALE)
        out[head] = prob
        norm = norm + jnp.sum(prob, axis=0, keepdims=True)
        delta = delta + jnp.sum(prob * pgrad, axis=0, keepdims=True)
    for index, row in enumerate((top, norm, delta)):
        stats[head, index : index + 1, :] = row


def stats_own_kernel(spans, t, a, p, q, g, k, v, k_up, v_up, out, pr, pr_up, pg, pg_up):
    flags = Flags(spans, t, a, p)

    def step(head):
        at = columns(head)
        query, grad = q[:, at], g[:, at]
        bias = jnp.where(flags.usable(head, MID), 0.0, -BIG)
        raws = [causal(dot(k[:, at], query, 1, 1), -BIG), dot(k_up[:, at], query, 1, 1) + bias]
        pgrads = [dot(v[:, at], grad, 1, 1), dot(v_up[:, at], grad, 1, 1)]
        pg[head], pg_up[head] = pgrads
        row_stats(head, raws, pgrads, [pr, pr_up], out)

    each_head(0, out.shape[0], step)


def stats_guest_kernel(
    spans, t, a, p, qf, gf, qn, gn, k, v, k_up, v_up, far, near, pr_far, pr_near, pg_far, pg_near
):
    odd = Flags(spans, t, a, p).is_odd()

    def step(head):
        at = columns(head)
        key_up, value_up = k_up[:, at], v_up[:, at]
        key_near = jnp.where(odd, key_up, k[:, at])
        value_near = jnp.where(odd, value_up, v[:, at])
        for query, grad, keys, values, stats, probs, pgrads in (
            (qf, gf, key_up, value_up, far, pr_far, pg_far),
            (qn, gn, key_near, value_near, near, pr_near, pg_near),
        ):
            raw = dot(keys, query[:, at], 1, 1)
            pgrad = dot(values, grad[:, at], 1, 1)
            pgrads[head] = pgrad
            row_stats(head, [raw], [pgrad], [probs], stats)

    each_head(0, far.shape[0], step)


def combine_kernel(spans, t, a, p, own, far, near, own_out, far_out, near_out):
    flags = Flags(spans, t, a, p)
    for head in range(own.shape[0]):
        uses = (True, flags.usable(head, FAR), flags.usable(head, NEAR))
        peaks = []
        for ref, usable in zip((own, far, near), uses):
            peak = ref[head, 0:1, :]
            peaks.append(peak if usable is True else jnp.where(usable, peak, -BIG))
        top = jnp.maximum(jnp.maximum(peaks[0], peaks[1]), peaks[2])
        factors = [jnp.exp2((peak - top) * EXP_SCALE) for peak in peaks]
        norm, delta = 0.0, 0.0
        for ref, factor in zip((own, far, near), factors):
            norm = norm + factor * ref[head, 1:2, :]
            delta = delta + factor * ref[head, 2:3, :]
        inverse = 1.0 / norm
        delta = delta * inverse
        for out, factor in zip((own_out, far_out, near_out), factors):
            out[head, 0:1, :] = factor * inverse
            out[head, 1:2, :] = delta


def pair_terms(head, query, grad, keys, probs, pgrads, norm):
    prob = probs[head] * norm[head, 0:1, :]
    weight = prob.astype(jnp.bfloat16)
    dlogit = (prob * (pgrads[head] - norm[head, 1:2, :])).astype(jnp.bfloat16)
    return dot(keys, dlogit, 0, 0), dot(dlogit, query, 1, 0), dot(weight, grad, 1, 0)


def own_kernel(q, g, k, k_up, norm, pr, pr_up, pg, pg_up, dq, dk, dv, dk_up, dv_up):
    def step(head):
        at = columns(head)
        query, grad = q[:, at], g[:, at]
        dq_own, dk[:, at], dv[:, at] = pair_terms(head, query, grad, k[:, at], pr, pg, norm)
        dq_mid, dk_up[:, at], dv_up[:, at] = pair_terms(
            head, query, grad, k_up[:, at], pr_up, pg_up, norm
        )
        dq[:, at] = ((dq_own + dq_mid) * SCALE).T

    each_head(0, norm.shape[0], step)


def pairs_kernel(
    spans, first, t, a, p, qf, gf, qn, gn, k, k_up, norm_far, norm_near,
    pr_far, pr_near, pg_far, pg_near, dk_own, dv_own, dk_up, dv_up, *refs,
):
    dqf, dqn, back, dk, dv = refs[-5:]
    odd = Flags(spans, t, a, p).is_odd()
    rows = qf.shape[0]

    def step(head):
        at, out = columns(head), columns(head - first)
        key_up = k_up[:, at]
        dq, key_far, value_far = pair_terms(
            head, qf[:, at], gf[:, at], key_up, pr_far, pg_far, norm_far
        )
        dqf[:, at] = (dq * SCALE).T.astype(dqf.dtype)
        key_near = jnp.where(odd, key_up, k[:, at])
        dq, key_term, value_term = pair_terms(
            head, qn[:, at], gn[:, at], key_near, pr_near, pg_near, norm_near
        )
        dqn[:, at] = (dq * SCALE).T.astype(dqn.dtype)
        zero = jnp.zeros_like(key_term)
        key_back = dk_up[:, at] + key_far + jnp.where(odd, key_term, zero)
        value_back = dv_up[:, at] + value_far + jnp.where(odd, value_term, zero)
        back[:rows, out] = (key_back * SCALE).astype(back.dtype)
        back[rows:, out] = value_back.astype(back.dtype)
        dk[:, out] = (dk_own[:, at] + jnp.where(odd, zero, key_term)) * SCALE
        dv[:, out] = dv_own[:, at] + jnp.where(odd, zero, value_term)

    each_head(first, dk.shape[1] // HDIM, step)


def body(queries, key_rows, value_rows, out_grad, out_proj, section_table, block_active):
    seq_count = lax.axis_size("seq")
    place = lax.axis_index("seq")
    spans = [seq_count // 2 ** (index + 1) for index in range(SECTIONS)]
    mid_span, near_span = spans[MID], spans[NEAR]
    assert spans[FAR] == 2 * mid_span and mid_span == 2 * near_span
    assert block_active.shape[0] == 1
    rows, cols = queries.shape
    heads = cols // HDIM
    group = heads // GROUPS
    pair_work = rows * rows * HDIM
    flags = [section_table, block_active, place.astype(jnp.int32).reshape(1)]

    wide_f32 = ((rows, cols), jnp.float32)
    wide_bf16 = ((rows, cols), jnp.bfloat16)
    stat = ((heads, STAT_ROWS, rows), jnp.float32)
    square = ((heads, rows, rows), jnp.float32)

    def with_spans(kernel, *fixed):
        def run(*refs):
            kernel(spans, *fixed, *refs)

        return run

    key_up = shift(key_rows, mid_span)
    value_up = shift(value_rows, mid_span)
    query_far = shift(queries, -mid_span)
    query_near = swap(queries, "seq", near_span)
    grads = attn_grad_of(out_grad, out_proj)
    grad_far = shift(grads, -mid_span)
    grad_near = swap(grads, "seq", near_span)
    local = (key_rows, value_rows, key_up, value_up)
    guests = (query_far, grad_far, query_near, grad_near)

    own_stats, *own_squares = call(
        with_spans(stats_own_kernel),
        flags,
        [queries, grads, *local],
        [stat] + [square] * 4,
        heads * 4 * pair_work,
    )
    far_stats, near_stats, *guest_squares = call(
        with_spans(stats_guest_kernel),
        flags,
        [*guests, *local],
        [stat] * 2 + [square] * 4,
        heads * 4 * pair_work,
    )
    far_stats = shift(far_stats, mid_span)
    near_stats = swap(near_stats, "seq", near_span)
    own_norm, far_norm, near_norm = call(
        with_spans(combine_kernel),
        flags,
        [own_stats, far_stats, near_stats],
        [stat] * 3,
        heads * rows * HDIM,
    )
    far_norm = shift(far_norm, -mid_span)
    near_norm = swap(near_norm, "seq", near_span)
    query_part, *own_terms = call(
        own_kernel,
        [],
        [queries, grads, key_rows, key_up, own_norm, *own_squares],
        [wide_f32] * 5,
        heads * 6 * pair_work,
    )

    partial_queries = []
    key_grad = jnp.zeros((rows, cols), jnp.bfloat16)
    value_grad = jnp.zeros((rows, cols), jnp.bfloat16)
    for index in range(GROUPS):
        first = index * group
        ins = [*guests, key_rows, key_up, far_norm, near_norm, *guest_squares, *own_terms]
        start = len(flags) + len(ins)
        aliases = {start + number: number for number in range(len(partial_queries))}
        half = (rows, group * HDIM)
        *partial_queries, back, key_part, value_part = call(
            with_spans(pairs_kernel, first),
            flags,
            ins + partial_queries,
            [wide_bf16] * 2
            + [((2 * rows, group * HDIM), jnp.bfloat16), (half, jnp.float32), (half, jnp.float32)],
            group * 6 * pair_work,
            aliases,
        )
        back = shift(back, -mid_span).astype(jnp.float32)
        key_part = (key_part + back[:rows]).astype(jnp.bfloat16)
        value_part = (value_part + back[rows:]).astype(jnp.bfloat16)
        at = (0, first * HDIM)
        key_grad = lax.dynamic_update_slice(key_grad, key_part, at)
        value_grad = lax.dynamic_update_slice(value_grad, value_part, at)
    query_far_part = shift(partial_queries[0], mid_span)
    query_near_part = swap(partial_queries[1], "seq", near_span)
    query_grad = query_part + query_far_part.astype(jnp.float32)
    query_grad = query_grad + query_near_part.astype(jnp.float32)
    return query_grad.astype(jnp.bfloat16), key_grad, value_grad


def solution(mesh):
    return jax.shard_map(
        body,
        mesh=mesh,
        in_specs=(
            P("seq", "head"),
            P("seq", "head"),
            P("seq", "head"),
            P("seq", "head"),
            P("head", None),
            P("head", None),
            P("seq", None),
        ),
        out_specs=(P("seq", "head"), P("seq", "head"), P("seq", "head")),
        check_vma=False,
    )
```

time: 109 us -> 92.7 us (0.85); the launches traced: 107 us -> 92.1 us
  Pallas kernels: 41.3 us -> 17.5 us
  waiting for transfers between devices: 25.5 us -> 32 us
  local copies, waits for them, and re-layouts: 4.19 us -> 6.11 us
    pallas_call x7, Pallas kernels: 41.3 us -> 17.5 us  [call(): pl.pallas_call(kernel, in_specs=[smem] * len(scalars) + [vmem] * len(ins)...]
    ppermute x8, waiting for transfers between devices: 2.94 us -> 10.8 us  [swap(): return lax.ppermute(value, axis, pairs)]
    unnamed x39 -> x21, local copies, waits for them, and re-layouts: 4.19 us -> 6.11 us
    ppermute x9, waiting for transfers between devices: 22.5 us -> 21.2 us  [shift(): lax.ppermute(value, 'seq', [(src, src + steps) for src in range(low, high)])]
  transfers between devices with their start and end apart: 17 -> 17, of which waited for: 5 -> 8; matrix products, arithmetic and copies ran while one was open for 2% -> 2% of each run, Pallas kernels for 24% -> 11%
where the time goes in v2:
time: 92.7 us; the launch traced here: 92.1 us
  starting transfers between devices  32.8 us (35%)
  waiting for transfers between devices  32 us (35%)
  Pallas kernels  17.5 us (19%)
  local copies, waits for them, and re-layouts  6.11 us (7%)
  other arithmetic  2.9 us (3%)
    ppermute x9, starting transfers between devices, shift(): lax.ppermute(value, 'seq', [(src, src + steps) for src in range(low, high)])  23.8 us
    ppermute x9, waiting for transfers between devices, shift(): lax.ppermute(value, 'seq', [(src, src + steps) for src in range(low, high)])  21.2 us
    pallas_call x7, Pallas kernels, call(): pl.pallas_call(kernel, in_specs=[smem] * len(scalars) + [vmem] * len(ins)...  17.5 us
    ppermute x8, waiting for transfers between devices, swap(): return lax.ppermute(value, axis, pairs)  10.8 us
    ppermute x8, starting transfers between devices, swap(): return lax.ppermute(value, axis, pairs)  8.93 us
    unnamed x21, local copies, waits for them, and re-layouts  6.11 us
  transfers between devices with their start and end apart: 17, of which 8 were waited for; matrix products, arithmetic and copies ran while one was open for 2% of the time, Pallas kernels for 11%

profile of v2, /device:TPU:0, one launch (start us, length us, event | category | flops | bytes accessed | tf_op | source)
XLA Modules:
  0.0 92.1 jit_solution(1543959593849010616)
XLA Ops:
  0.6 3.1 %collective-permute-start.1 = (bf16[256,512]{1,0:T(8,128)(2,1)}, bf16[256,512]{1,0:T(8,128)(2,1)S(1)}, u32[]{:S(2)}, u32[]{:S(2)}) collective-permute-start(bf16[256,512]{1,0:T(8,128)(2,1)} %refs_0_.6), channel_id=1, source_target_pairs={{0,2},{1,3},{2,0},{3,1},{4,6},{5,7},{6,4},{7,5},{8,10},{9,11},{10,... | collective-permute-start | bytes 786440 | tf_op jit(solution)/shard_map/ppermute | solution.py:32
  3.7 3.5 %collective-permute-start.4 = (bf16[256,1024]{1,0:T(8,128)(2,1)}, bf16[256,1024]{1,0:T(8,128)(2,1)S(1)}, u32[]{:S(2)}, u32[]{:S(2)}) collective-permute-start(bf16[256,1024]{1,0:T(8,128)(2,1)} %refs_8_.1), channel_id=1, source_target_pairs={{0,8},{4,12},{8,16},{12,20},{16,24},{20,28},{1,9},{5,13},{9,17},{1... | collective-permute-start | bytes 1572872 | tf_op jit(solution)/shard_map/ppermute | solution.py:27
  7.2 0.1 collective-permute-start
  7.3 2.9 %collective-permute-done.1.refs_2_ = bf16[256,512]{1,0:T(8,128)(2,1)S(1)} collective-permute-done((bf16[256,512]{1,0:T(8,128)(2,1)}, bf16[256,512]{1,0:T(8,128)(2,1)S(1)}, u32[]{:S(2)}, u32[]{:S(2)}) %collective-permute-start.1) | collective-permute-done | bytes 262176 | tf_op jit(solution)/shard_map/ppermute | solution.py:32
  10.2 0.0 collective-permute-start.2
  10.2 1.3 %collective-permute-start.5 = (bf16[256,1024]{1,0:T(8,128)(2,1)}, bf16[256,1024]{1,0:T(8,128)(2,1)S(1)}, u32[]{:S(2)}, u32[]{:S(2)}) collective-permute-start(bf16[256,1024]{1,0:T(8,128)(2,1)} %q.1), channel_id=1, source_target_pairs={{8,0},{12,4},{16,8},{20,12},{24,16},{28,20},{9,1},{13,5},{17,9},{2... | collective-permute-start | bytes 1572872 | tf_op jit(solution)/shard_map/ppermute | solution.py:27
  11.5 1.8 %collective-permute-start.7 = (bf16[256,1024]{1,0:T(8,128)(2,1)}, bf16[256,1024]{1,0:T(8,128)(2,1)S(1)}, u32[]{:S(2)}, u32[]{:S(2)}) collective-permute-start(bf16[256,1024]{1,0:T(8,128)(2,1)} %q.1), channel_id=1, source_target_pairs={{0,4},{4,0},{8,12},{12,8},{16,20},{20,16},{24,28},{28,24},{1,5},{5... | collective-permute-start | bytes 1572872 | tf_op jit(solution)/shard_map/ppermute | solution.py:32
  13.3 0.0 collective-permute-done.refs_1_
  13.3 4.6 %collective-permute-start.3 = (bf16[256,1024]{1,0:T(8,128)(2,1)}, bf16[256,1024]{1,0:T(8,128)(2,1)S(1)}, u32[]{:S(2)}, u32[]{:S(2)}) collective-permute-start(bf16[256,1024]{1,0:T(8,128)(2,1)} %refs_7_.5), channel_id=1, source_target_pairs={{0,8},{4,12},{8,16},{12,20},{16,24},{20,28},{1,9},{5,13},{9,17},{1... | collective-permute-start | bytes 1572872 | tf_op jit(solution)/shard_map/ppermute | solution.py:27
  17.9 2.2 %copy-done.7 = bf16[1024,2048]{1,0:T(8,128)(2,1)S(1)} copy-done((bf16[1024,2048]{1,0:T(8,128)(2,1)S(1)}, bf16[1024,2048]{1,0:T(8,128)(2,1)}, u32[]{:S(2)}) %copy-start.7) | copy-done | bytes 4194328
  20.1 0.9 %copy-done.8 = bf16[256,512]{1,0:T(8,128)(2,1)S(1)} copy-done((bf16[256,512]{1,0:T(8,128)(2,1)S(1)}, bf16[256,512]{1,0:T(8,128)(2,1)}, u32[]{:S(2)}) %copy-start.8) | copy-done | bytes 262168
  21.0 2.7 %shard_map.94.refs_4_.g = bf16[256,1024]{1,0:T(8,128)(2,1)} custom-call(s32[1]{0:T(128)} %bitcast.head_ref, bf16[256,512]{1,0:T(8,128)(2,1)S(1)} %copy-done.8, bf16[256,512]{1,0:T(8,128)(2,1)S(1)} %collective-permute-done.refs_1_, bf16[256,512]{1,0:T(8,128)(2,1)S(1)} %collective-permute-done.1.refs_2_, bf16[256,512]{1,0:T(8,128)(2,1)S(1)} %collective-permute-done.2.refs_3_, ...), custom_call_target="tpu_custom_call" | custom-call | flops 1073741824 | tf_op jit(solution)/shard_map/pallas_call | solution.py:48
  23.7 0.3 collective-permute-start.8
  24.0 0.8 copy-done.4
  24.8 1.3 %collective-permute-start.6 = (bf16[256,1024]{1,0:T(8,128)(2,1)}, bf16[256,1024]{1,0:T(8,128)(2,1)S(1)}, u32[]{:S(2)}, u32[]{:S(2)}) collective-permute-start(bf16[256,1024]{1,0:T(8,128)(2,1)} %shard_map.94.refs_4_.g), channel_id=1, source_target_pairs={{8,0},{12,4},{16,8},{20,12},{24,16},{28,20},{9,1},{13,5},{17,9},{2... | collective-permute-start | bytes 1572872 | tf_op jit(solution)/shard_map/ppermute | solution.py:27
  26.1 0.1 copy.14.refs_0_
  26.2 0.5 collective-permute-done.5.refs_3_
  26.7 0.0 collective-permute-done.7.refs_5_
  26.7 2.9 %collective-permute-done.3.refs_7_.refs_9_.k_up.refs_8_ = bf16[256,1024]{1,0:T(8,128)(2,1)S(1)} collective-permute-done((bf16[256,1024]{1,0:T(8,128)(2,1)}, bf16[256,1024]{1,0:T(8,128)(2,1)S(1)}, u32[]{:S(2)}, u32[]{:S(2)}) %collective-permute-start.3) | collective-permute-done | bytes 524320 | tf_op jit(solution)/shard_map/ppermute | solution.py:27
  29.6 7.8 %collective-permute-done.8.refs_6_ = bf16[256,1024]{1,0:T(8,128)(2,1)S(1)} collective-permute-done((bf16[256,1024]{1,0:T(8,128)(2,1)}, bf16[256,1024]{1,0:T(8,128)(2,1)S(1)}, u32[]{:S(2)}, u32[]{:S(2)}) %collective-permute-start.8) | collective-permute-done | bytes 524320 | tf_op jit(solution)/shard_map/ppermute | solution.py:32
  37.4 2.8 %collective-permute-done.6.refs_4_ = bf16[256,1024]{1,0:T(8,128)(2,1)S(1)} collective-permute-done((bf16[256,1024]{1,0:T(8,128)(2,1)}, bf16[256,1024]{1,0:T(8,128)(2,1)S(1)}, u32[]{:S(2)}, u32[]{:S(2)}) %collective-permute-start.6) | collective-permute-done | bytes 524320 | tf_op jit(solution)/shard_map/ppermute | solution.py:27
  40.2 1.0 %copy-done.2 = bf16[256,1024]{1,0:T(8,128)(2,1)S(1)} copy-done((bf16[256,1024]{1,0:T(8,128)(2,1)S(1)}, bf16[256,1024]{1,0:T(8,128)(2,1)}, u32[]{:S(2)}) %copy-start.2) | copy-done | bytes 524312
  41.3 1.0 %copy-done.5 = bf16[256,1024]{1,0:T(8,128)(2,1)S(1)} copy-done((bf16[256,1024]{1,0:T(8,128)(2,1)S(1)}, bf16[256,1024]{1,0:T(8,128)(2,1)}, u32[]{:S(2)}) %copy-start.5) | copy-done | bytes 524312
  42.3 3.1 %shard_map.96 = (f32[8,8,256]{2,1,0:T(8,128)S(1)}, f32[8,8,256]{2,1,0:T(8,128)S(1)}, f32[8,256,256]{2,1,0:T(8,128)S(1)}, f32[8,256,256]{2,1,0:T(8,128)S(1)}, f32...) custom-call(s32[8,3]{1,0:T(8,128)S(1)} %copy.14.refs_0_, s32[1,3]{1,0:T(1,128)S(1)} %copy-done.6, s32[1]{0:T(128)} %bitcast.1.refs_2_, ...), custom_call_target="tpu_custom_call" | custom-call | flops 536870912 | tf_op jit(solution)/shard_map/pallas_call | solution.py:48
  45.4 3.6 %collective-permute-start.9 = (f32[8,8,256]{2,1,0:T(8,128)S(1)}, f32[8,8,256]{2,1,0:T(8,128)S(1)}, u32[]{:S(2)}, u32[]{:S(2)}) collective-permute-start(f32[8,8,256]{2,1,0:T(8,128)S(1)} %get-tuple-element.33), channel_id=1, source_target_pairs={{0,8},{4,12},{8,16},{12,20},{16,24},{20,28},{1,9},{5,13},{9,17},{1... | collective-permute-start | bytes 196616 | tf_op jit(solution)/shard_map/ppermute | solution.py:27
  49.1 1.6 %collective-permute-start.10 = (f32[8,8,256]{2,1,0:T(8,128)S(1)}, f32[8,8,256]{2,1,0:T(8,128)S(1)}, u32[]{:S(2)}, u32[]{:S(2)}) collective-permute-start(f32[8,8,256]{2,1,0:T(8,128)S(1)} %get-tuple-element.34), channel_id=1, source_target_pairs={{0,4},{4,0},{8,12},{12,8},{16,20},{20,16},{24,28},{28,24},{1,5},{5... | collective-permute-start | bytes 196616 | tf_op jit(solution)/shard_map/ppermute | solution.py:32
  50.6 3.3 %shard_map.95 = (f32[8,8,256]{2,1,0:T(8,128)S(1)}, f32[8,256,256]{2,1,0:T(8,128)S(1)}, f32[8,256,256]{2,1,0:T(8,128)S(1)}, f32[8,256,256]{2,1,0:T(8,128)S(1)}, f32[8,256,256]{2,1,0:T(8,128)S(1)}) custom-call(s32[8,3]{1,0:T(8,128)S(1)} %copy.14.refs_0_, s32[1,3]{1,0:T(1,128)S(1)} %copy-done.6, s32[1]{0:T(128)} %bitcast.1.refs_2_, ...), custom_call_target="tpu_custom_call" | custom-call | flops 536870912 | tf_op jit(solution)/shard_map/pallas_call | solution.py:48
  53.9 0.0 collective-permute-done.10.refs_5_
  53.9 0.7 shard_map.97
  54.6 1.3 %collective-permute-start.11 = (f32[8,8,256]{2,1,0:T(8,128)S(1)}, f32[8,8,256]{2,1,0:T(8,128)S(1)}, u32[]{:S(2)}, u32[]{:S(2)}) collective-permute-start(f32[8,8,256]{2,1,0:T(8,128)S(1)} %get-tuple-element.41), channel_id=1, source_target_pairs={{8,0},{12,4},{16,8},{20,12},{24,16},{28,20},{9,1},{13,5},{17,9},{2... | collective-permute-start | bytes 196616 | tf_op jit(solution)/shard_map/ppermute | solution.py:27
  55.9 1.0 %collective-permute-start.12 = (f32[8,8,256]{2,1,0:T(8,128)S(1)}, f32[8,8,256]{2,1,0:T(8,128)S(1)}, u32[]{:S(2)}, u32[]{:S(2)}) collective-permute-start(f32[8,8,256]{2,1,0:T(8,128)S(1)} %get-tuple-element.42), channel_id=1, source_target_pairs={{0,4},{4,0},{8,12},{12,8},{16,20},{20,16},{24,28},{28,24},{1,5},{5... | collective-permute-start | bytes 196616 | tf_op jit(solution)/shard_map/ppermute | solution.py:32
  56.9 3.7 %shard_map.98 = (f32[256,1024]{1,0:T(8,128)S(1)}, f32[256,1024]{1,0:T(8,128)S(1)}, f32[256,1024]{1,0:T(8,128)S(1)}, f32[256,1024]{1,0:T(8,128)S(1)}, f32[256,1024]{1,0:T(8,128)S(1)}) custom-call(bf16[256,1024]{1,0:T(8,128)(2,1)S(1)} %copy-done.1, bf16[256,1024]{1,0:T(8,128)(2,1)} %shard_map.94.refs_4_.g, bf16[256,1024]{1,0:T(8,128)(2,1)S(1)} %copy-done, ...), custom_call_target="tpu_custom_call" | custom-call | flops 805306368 | tf_op jit(solution)/shard_map/pallas_call | solution.py:48
  60.6 0.2 collective-permute-done.11.refs_9_
  60.8 0.0 collective-permute-done.12.refs_10_
  60.8 2.0 %shard_map.99 = (bf16[256,1024]{1,0:T(8,128)(2,1)S(1)}, bf16[256,1024]{1,0:T(8,128)(2,1)S(1)}, bf16[512,512]{1,0:T(8,128)(2,1)S(1)}, f32[256,512]{1,0:T(8,128)S(1)}, f32[256,512]{1,0:T(8,128)S(1)}) custom-call(s32[8,3]{1,0:T(8,128)S(1)} %copy.14.refs_0_, s32[1,3]{1,0:T(1,128)S(1)} %copy-done.6, s32[1]{0:T(128)} %bitcast.1.refs_2_, ...), custom_call_target="tpu_custom_call" | custom-call | flops 402653184 | tf_op jit(solution)/shard_map/pallas_call | solution.py:48
  62.8 2.0 %shard_map.100 = (bf16[256,1024]{1,0:T(8,128)(2,1)S(1)}, bf16[256,1024]{1,0:T(8,128)(2,1)S(1)}, bf16[512,512]{1,0:T(8,128)(2,1)S(1)}, f32[256,512]{1,0:T(8,128)S(1)}, f32[256,512]{1,0:T(8,128)S(1)}) custom-call(s32[8,3]{1,0:T(8,128)S(1)} %copy.14.refs_0_, s32[1,3]{1,0:T(1,128)S(1)} %copy-done.6, ...), custom_call_target="tpu_custom_call", output_to_operand_aliasing={{0}: (19, {}), {1}: (20, {})} | custom-call | flops 402653184 | tf_op jit(solution)/shard_map/pallas_call | solution.py:48
  64.8 1.3 %collective-permute-start.16 = (bf16[512,512]{1,0:T(8,128)(2,1)S(1)}, bf16[512,512]{1,0:T(8,128)(2,1)S(1)}, u32[]{:S(2)}, u32[]{:S(2)}) collective-permute-start(bf16[512,512]{1,0:T(8,128)(2,1)S(1)} %get-tuple-element.58), channel_id=1, source_target_pairs={{8,0},{12,4},{16,8},{20,12},{24,16},{28,20},{9,1},{13,5},{17,9},{2... | collective-permute-start | bytes 1572872 | tf_op jit(solution)/shard_map/ppermute | solution.py:27
  66.1 1.3 %collective-permute-start.15 = (bf16[512,512]{1,0:T(8,128)(2,1)S(1)}, bf16[512,512]{1,0:T(8,128)(2,1)S(1)}, u32[]{:S(2)}, u32[]{:S(2)}) collective-permute-start(bf16[512,512]{1,0:T(8,128)(2,1)S(1)} %get-tuple-element.56), channel_id=1, source_target_pairs={{8,0},{12,4},{16,8},{20,12},{24,16},{28,20},{9,1},{13,5},{17,9},{2... | collective-permute-start | bytes 1572872 | tf_op jit(solution)/shard_map/ppermute | solution.py:27
  67.4 5.7 %collective-permute-start.13 = (bf16[256,1024]{1,0:T(8,128)(2,1)S(1)}, bf16[256,1024]{1,0:T(8,128)(2,1)S(1)}, u32[]{:S(2)}, u32[]{:S(2)}) collective-permute-start(bf16[256,1024]{1,0:T(8,128)(2,1)S(1)} %get-tuple-element.53), channel_id=1, source_target_pairs={{0,8},{4,12},{8,16},{12,20},{16,24},{20,28},{1,9},{5,13},{9,17},{1... | collective-permute-start | bytes 1572872 | tf_op jit(solution)/shard_map/ppermute | solution.py:27
  73.1 1.1 %collective-permute-start.14 = (bf16[256,1024]{1,0:T(8,128)(2,1)S(1)}, bf16[256,1024]{1,0:T(8,128)(2,1)S(1)}, u32[]{:S(2)}, u32[]{:S(2)}) collective-permute-start(bf16[256,1024]{1,0:T(8,128)(2,1)S(1)} %get-tuple-element.54), channel_id=1, source_target_pairs={{0,4},{4,0},{8,12},{12,8},{16,20},{20,16},{24,28},{28,24},{1,5},{5... | collective-permute-start | bytes 1572872 | tf_op jit(solution)/shard_map/ppermute | solution.py:32
  74.3 7.7 %collective-permute-done.16 = bf16[512,512]{1,0:T(8,128)(2,1)S(1)} collective-permute-done((bf16[512,512]{1,0:T(8,128)(2,1)S(1)}, bf16[512,512]{1,0:T(8,128)(2,1)S(1)}, u32[]{:S(2)}, u32[]{:S(2)}) %collective-permute-start.16) | collective-permute-done | bytes 524320 | tf_op jit(solution)/shard_map/ppermute | solution.py:27
  82.0 0.1 convert_element_type.32
  82.1 0.3 fusion
  82.4 7.2 %collective-permute-done.15 = bf16[512,512]{1,0:T(8,128)(2,1)S(1)} collective-permute-done((bf16[512,512]{1,0:T(8,128)(2,1)S(1)}, bf16[512,512]{1,0:T(8,128)(2,1)S(1)}, u32[]{:S(2)}, u32[]{:S(2)}) %collective-permute-start.15) | collective-permute-done | bytes 524320 | tf_op jit(solution)/shard_map/ppermute | solution.py:27
  89.6 0.1 convert_element_type.30
  89.7 0.3 fusion.1
  89.9 1.1 %pad_maximum_fusion = (bf16[256,1024]{1,0:T(8,128)(2,1)}, bf16[256,1024]{1,0:T(8,128)(2,1)}) fusion(bf16[256,512]{1,0:T(8,128)(2,1)S(1)} %get-tuple-element.64, bf16[256,512]{1,0:T(8,128)(2,1)S(1)} %get-tuple-element.62, bf16[256,512]{1,0:T(8,128)(2,1)S(1)} %get-tuple-element.63, bf16[256,512]{1,0:T(8,128)(2,1)S(1)} %get-tuple-element.61), kind=kLoop, calls=%fused_computation.9 | loop fusion | flops 2097152 | bytes 2097152 | tf_op jit(solution)/shard_map/dynamic_update_slice | solution.py:349
  91.1 1.0 %add_convert_fusion = bf16[256,1024]{1,0:T(8,128)(2,1)} fusion(bf16[256,1024]{1,0:T(8,128)(2,1)S(1)} %collective-permute-done.14, f32[256,1024]{1,0:T(8,128)S(1)} %get-tuple-element.40, bf16[256,1024]{1,0:T(8,128)(2,1)S(1)} %collective-permute-done.13), kind=kLoop, calls=%fused_computation | loop fusion | flops 1310720 | bytes 2621440 | tf_op jit(solution)/shard_map/convert_element_type | solution.py:355
  (20 shorter events, 0.0 us)
Async XLA Ops:
  0.6 9.6 %collective-permute-start.1 = (bf16[256,512]{1,0:T(8,128)(2,1)}, bf16[256,512]{1,0:T(8,128)(2,1)S(1)}, u32[]{:S(2)}, u32[]{:S(2)}) collective-permute-start(bf16[256,512]{1,0:T(8,128)(2,1)} %refs_0_.6), channel_id=1, source_target_pairs={{0,2},{1,3},{2,0},{3,1},{4,6},{5,7},{6,4},{7,5},{8,10},{9,11},{10,... | collective-permute-start | bytes 786440 | tf_op jit(solution)/shard_map/ppermute | solution.py:32
  3.7 20.4 %collective-permute-start.4 = (bf16[256,1024]{1,0:T(8,128)(2,1)}, bf16[256,1024]{1,0:T(8,128)(2,1)S(1)}, u32[]{:S(2)}, u32[]{:S(2)}) collective-permute-start(bf16[256,1024]{1,0:T(8,128)(2,1)} %refs_8_.1), channel_id=1, source_target_pairs={{0,8},{4,12},{8,16},{12,20},{16,24},{20,28},{1,9},{5,13},{9,17},{1... | collective-permute-start | bytes 1572872 | tf_op jit(solution)/shard_map/ppermute | solution.py:27
  7.2 6.1 %collective-permute-start = (bf16[256,512]{1,0:T(8,128)(2,1)}, bf16[256,512]{1,0:T(8,128)(2,1)S(1)}, u32[]{:S(2)}, u32[]{:S(2)}) collective-permute-start(bf16[256,512]{1,0:T(8,128)(2,1)} %refs_0_.6), channel_id=1, source_target_pairs={{0,1},{1,0},{2,3},{3,2},{4,5},{5,4},{6,7},{7,6},{8,9},{9,8},{10,11... | collective-permute-start | bytes 786440 | tf_op jit(solution)/shard_map/ppermute | solution.py:32
  10.2 7.7 %collective-permute-start.2 = (bf16[256,512]{1,0:T(8,128)(2,1)S(1)}, bf16[256,512]{1,0:T(8,128)(2,1)S(1)}, u32[]{:S(2)}, u32[]{:S(2)}) collective-permute-start(bf16[256,512]{1,0:T(8,128)(2,1)S(1)} %collective-permute-done.1.refs_2_), channel_id=1, source_target_pairs={{0,1},{1,0},{2,3},{3,2},{4,5},{5,4},{6,7},{7,6},{8,9},{9,8},{10,11... | collective-permute-start | bytes 786440 | tf_op jit(solution)/shard_map/ppermute | solution.py:32
  10.2 16.5 %collective-permute-start.5 = (bf16[256,1024]{1,0:T(8,128)(2,1)}, bf16[256,1024]{1,0:T(8,128)(2,1)S(1)}, u32[]{:S(2)}, u32[]{:S(2)}) collective-permute-start(bf16[256,1024]{1,0:T(8,128)(2,1)} %q.1), channel_id=1, source_target_pairs={{8,0},{12,4},{16,8},{20,12},{24,16},{28,20},{9,1},{13,5},{17,9},{2... | collective-permute-start | bytes 1572872 | tf_op jit(solution)/shard_map/ppermute | solution.py:27
  11.5 15.2 %collective-permute-start.7 = (bf16[256,1024]{1,0:T(8,128)(2,1)}, bf16[256,1024]{1,0:T(8,128)(2,1)S(1)}, u32[]{:S(2)}, u32[]{:S(2)}) collective-permute-start(bf16[256,1024]{1,0:T(8,128)(2,1)} %q.1), channel_id=1, source_target_pairs={{0,4},{4,0},{8,12},{12,8},{16,20},{20,16},{24,28},{28,24},{1,5},{5... | collective-permute-start | bytes 1572872 | tf_op jit(solution)/shard_map/ppermute | solution.py:32
  13.3 16.3 %collective-permute-start.3 = (bf16[256,1024]{1,0:T(8,128)(2,1)}, bf16[256,1024]{1,0:T(8,128)(2,1)S(1)}, u32[]{:S(2)}, u32[]{:S(2)}) collective-permute-start(bf16[256,1024]{1,0:T(8,128)(2,1)} %refs_7_.5), channel_id=1, source_target_pairs={{0,8},{4,12},{8,16},{12,20},{16,24},{20,28},{1,9},{5,13},{9,17},{1... | collective-permute-start | bytes 1572872 | tf_op jit(solution)/shard_map/ppermute | solution.py:27
  17.9 2.2 %copy-start.7 = (bf16[1024,2048]{1,0:T(8,128)(2,1)S(1)}, bf16[1024,2048]{1,0:T(8,128)(2,1)}, u32[]{:S(2)}) copy-start(bf16[1024,2048]{1,0:T(8,128)(2,1)} %refs_4_.1) | copy-start | bytes 12582916
  20.1 0.9 %copy-start.8 = (bf16[256,512]{1,0:T(8,128)(2,1)S(1)}, bf16[256,512]{1,0:T(8,128)(2,1)}, u32[]{:S(2)}) copy-start(bf16[256,512]{1,0:T(8,128)(2,1)} %refs_0_.6) | copy-start | bytes 786436
  21.0 5.1 %copy-start.9 = (s32[8,3]{0,1:T(4,128)S(1)}, s32[8,3]{0,1:T(4,128)}, u32[]{:S(2)}) copy-start(s32[8,3]{0,1:T(4,128)} %param.12) | copy-start | bytes 292
  21.0 19.2 %copy-start = (bf16[256,1024]{1,0:T(8,128)(2,1)S(1)}, bf16[256,1024]{1,0:T(8,128)(2,1)}, u32[]{:S(2)}) copy-start(bf16[256,1024]{1,0:T(8,128)(2,1)} %refs_7_.5) | copy-start | bytes 1572868
  21.0 19.2 %copy-start.6 = (s32[1,3]{1,0:T(1,128)S(1)}, s32[1,3]{1,0:T(1,128)}, u32[]{:S(2)}) copy-start(s32[1,3]{1,0:T(1,128)} %refs_1_.9) | copy-start | bytes 40
  23.7 13.7 %collective-permute-start.8 = (bf16[256,1024]{1,0:T(8,128)(2,1)}, bf16[256,1024]{1,0:T(8,128)(2,1)S(1)}, u32[]{:S(2)}, u32[]{:S(2)}) collective-permute-start(bf16[256,1024]{1,0:T(8,128)(2,1)} %shard_map.94.refs_4_.g), channel_id=1, source_target_pairs={{0,4},{4,0},{8,12},{12,8},{16,20},{20,16},{24,28},{28,24},{1,5},{5... | collective-permute-start | bytes 1572872 | tf_op jit(solution)/shard_map/ppermute | solution.py:32
  24.0 0.8 copy-start.4
  24.8 15.4 %collective-permute-start.6 = (bf16[256,1024]{1,0:T(8,128)(2,1)}, bf16[256,1024]{1,0:T(8,128)(2,1)S(1)}, u32[]{:S(2)}, u32[]{:S(2)}) collective-permute-start(bf16[256,1024]{1,0:T(8,128)(2,1)} %shard_map.94.refs_4_.g), channel_id=1, source_target_pairs={{8,0},{12,4},{16,8},{20,12},{24,16},{28,20},{9,1},{13,5},{17,9},{2... | collective-permute-start | bytes 1572872 | tf_op jit(solution)/shard_map/ppermute | solution.py:27
  40.2 1.0 %copy-start.2 = (bf16[256,1024]{1,0:T(8,128)(2,1)S(1)}, bf16[256,1024]{1,0:T(8,128)(2,1)}, u32[]{:S(2)}) copy-start(bf16[256,1024]{1,0:T(8,128)(2,1)} %refs_8_.1) | copy-start | bytes 1572868
  41.3 1.0 %copy-start.5 = (bf16[256,1024]{1,0:T(8,128)(2,1)S(1)}, bf16[256,1024]{1,0:T(8,128)(2,1)}, u32[]{:S(2)}) copy-start(bf16[256,1024]{1,0:T(8,128)(2,1)} %copy-done.4) | copy-start | bytes 1572868
  42.3 8.3 %copy-start.1 = (bf16[256,1024]{1,0:T(8,128)(2,1)S(1)}, bf16[256,1024]{1,0:T(8,128)(2,1)}, u32[]{:S(2)}) copy-start(bf16[256,1024]{1,0:T(8,128)(2,1)} %q.1) | copy-start | bytes 1572868
  42.3 8.3 %copy-start.3 = (bf16[256,1024]{1,0:T(8,128)(2,1)S(1)}, bf16[256,1024]{1,0:T(8,128)(2,1)}, u32[]{:S(2)}) copy-start(bf16[256,1024]{1,0:T(8,128)(2,1)} %refs_8_.1) | copy-start | bytes 1572868
  45.4 8.5 %collective-permute-start.9 = (f32[8,8,256]{2,1,0:T(8,128)S(1)}, f32[8,8,256]{2,1,0:T(8,128)S(1)}, u32[]{:S(2)}, u32[]{:S(2)}) collective-permute-start(f32[8,8,256]{2,1,0:T(8,128)S(1)} %get-tuple-element.33), channel_id=1, source_target_pairs={{0,8},{4,12},{8,16},{12,20},{16,24},{20,28},{1,9},{5,13},{9,17},{1... | collective-permute-start | bytes 196616 | tf_op jit(solution)/shard_map/ppermute | solution.py:27
  49.1 4.9 %collective-permute-start.10 = (f32[8,8,256]{2,1,0:T(8,128)S(1)}, f32[8,8,256]{2,1,0:T(8,128)S(1)}, u32[]{:S(2)}, u32[]{:S(2)}) collective-permute-start(f32[8,8,256]{2,1,0:T(8,128)S(1)} %get-tuple-element.34), channel_id=1, source_target_pairs={{0,4},{4,0},{8,12},{12,8},{16,20},{20,16},{24,28},{28,24},{1,5},{5... | collective-permute-start | bytes 196616 | tf_op jit(solution)/shard_map/ppermute | solution.py:32
  54.6 6.2 %collective-permute-start.11 = (f32[8,8,256]{2,1,0:T(8,128)S(1)}, f32[8,8,256]{2,1,0:T(8,128)S(1)}, u32[]{:S(2)}, u32[]{:S(2)}) collective-permute-start(f32[8,8,256]{2,1,0:T(8,128)S(1)} %get-tuple-element.41), channel_id=1, source_target_pairs={{8,0},{12,4},{16,8},{20,12},{24,16},{28,20},{9,1},{13,5},{17,9},{2... | collective-permute-start | bytes 196616 | tf_op jit(solution)/shard_map/ppermute | solution.py:27
  55.9 4.9 %collective-permute-start.12 = (f32[8,8,256]{2,1,0:T(8,128)S(1)}, f32[8,8,256]{2,1,0:T(8,128)S(1)}, u32[]{:S(2)}, u32[]{:S(2)}) collective-permute-start(f32[8,8,256]{2,1,0:T(8,128)S(1)} %get-tuple-element.42), channel_id=1, source_target_pairs={{0,4},{4,0},{8,12},{12,8},{16,20},{20,16},{24,28},{28,24},{1,5},{5... | collective-permute-start | bytes 196616 | tf_op jit(solution)/shard_map/ppermute | solution.py:32
  64.8 17.2 %collective-permute-start.16 = (bf16[512,512]{1,0:T(8,128)(2,1)S(1)}, bf16[512,512]{1,0:T(8,128)(2,1)S(1)}, u32[]{:S(2)}, u32[]{:S(2)}) collective-permute-start(bf16[512,512]{1,0:T(8,128)(2,1)S(1)} %get-tuple-element.58), channel_id=1, source_target_pairs={{8,0},{12,4},{16,8},{20,12},{24,16},{28,20},{9,1},{13,5},{17,9},{2... | collective-permute-start | bytes 1572872 | tf_op jit(solution)/shard_map/ppermute | solution.py:27
  66.1 23.5 %collective-permute-start.15 = (bf16[512,512]{1,0:T(8,128)(2,1)S(1)}, bf16[512,512]{1,0:T(8,128)(2,1)S(1)}, u32[]{:S(2)}, u32[]{:S(2)}) collective-permute-start(bf16[512,512]{1,0:T(8,128)(2,1)S(1)} %get-tuple-element.56), channel_id=1, source_target_pairs={{8,0},{12,4},{16,8},{20,12},{24,16},{28,20},{9,1},{13,5},{17,9},{2... | collective-permute-start | bytes 1572872 | tf_op jit(solution)/shard_map/ppermute | solution.py:27
  67.4 23.7 %collective-permute-start.13 = (bf16[256,1024]{1,0:T(8,128)(2,1)S(1)}, bf16[256,1024]{1,0:T(8,128)(2,1)S(1)}, u32[]{:S(2)}, u32[]{:S(2)}) collective-permute-start(bf16[256,1024]{1,0:T(8,128)(2,1)S(1)} %get-tuple-element.53), channel_id=1, source_target_pairs={{0,8},{4,12},{8,16},{12,20},{16,24},{20,28},{1,9},{5,13},{9,17},{1... | collective-permute-start | bytes 1572872 | tf_op jit(solution)/shard_map/ppermute | solution.py:27
  73.1 17.9 %collective-permute-start.14 = (bf16[256,1024]{1,0:T(8,128)(2,1)S(1)}, bf16[256,1024]{1,0:T(8,128)(2,1)S(1)}, u32[]{:S(2)}, u32[]{:S(2)}) collective-permute-start(bf16[256,1024]{1,0:T(8,128)(2,1)S(1)} %get-tuple-element.54), channel_id=1, source_target_pairs={{0,4},{4,0},{8,12},{12,8},{16,20},{20,16},{24,28},{28,24},{1,5},{5... | collective-permute-start | bytes 1572872 | tf_op jit(solution)/shard_map/ppermute | solution.py:32

commit v3 on v2

v3 whole, which is shorter than its diff:
```python
import math

import jax
import jax.numpy as jnp
from jax import lax
from jax.experimental import pallas as pl
from jax.experimental.pallas import tpu as pltpu
from jax.sharding import PartitionSpec as P


HDIM = 128
FAR, MID, NEAR = range(3)
SECTIONS = 3
GROUPS = (2, 4, 2)
HEADS_PER_STEP = 2
KERNEL_VMEM = 8 * 2**20
BIG = 1e30
SCALE = 1.0 / math.sqrt(HDIM)
LOG2E = math.log2(math.e)
EXP_SCALE = SCALE * LOG2E


def shift(value, steps):
    count = lax.axis_size("seq")
    low, high = max(0, -steps), min(count, count - steps)
    return lax.ppermute(value, "seq", [(src, src + steps) for src in range(low, high)])


def swap(value, axis, bit):
    pairs = [(src, src ^ bit) for src in range(lax.axis_size(axis))]
    return lax.ppermute(value, axis, pairs)


def dot(lhs, rhs, lhs_dim, rhs_dim):
    return lax.dot_general(
        lhs, rhs, (((lhs_dim,), (rhs_dim,)), ((), ())), preferred_element_type=jnp.float32
    )


def on_chip(array):
    return pltpu.with_memory_space_constraint(array, pltpu.VMEM)


def in_hbm(array):
    return pltpu.with_memory_space_constraint(array, pltpu.HBM)


def call(kernel, scalars, ins, outs, work, aliases=None, grid=None, streams=(), blocks=None):
    smem = pl.BlockSpec(memory_space=pltpu.SMEM)
    vmem = pl.BlockSpec(memory_space=pltpu.VMEM)
    return pl.pallas_call(
        kernel,
        grid=grid or (),
        in_specs=[smem] * len(scalars) + [vmem] * len(ins) + [spec for _, spec in streams],
        out_specs=blocks or [vmem] * len(outs),
        out_shape=[
            (jax.ShapeDtypeStruct if blocks else pltpu.VMEM)(shape, dtype)
            for shape, dtype in outs
        ],
        input_output_aliases=aliases or {},
        compiler_params=pltpu.CompilerParams(vmem_limit_bytes=KERNEL_VMEM),
        cost_estimate=pl.CostEstimate(
            flops=2 * work, bytes_accessed=0, transcendentals=work // HDIM
        ),
    )(*scalars, *[on_chip(array) for array in ins], *[array for array, _ in streams])


def each_head(first, count, step):
    def pair(index, carry):
        for offset in range(HEADS_PER_STEP):
            step(first + index * HEADS_PER_STEP + offset)
        return carry

    lax.fori_loop(0, count // HEADS_PER_STEP, pair, None)


def columns(head):
    return pl.ds(pl.multiple_of(head * HDIM, HDIM), HDIM)


def gathered_pieces(out_grad):
    pieces = {0: out_grad}
    bit = lax.axis_size("head") // 2
    while bit:
        for offset in list(pieces):
            pieces[offset | bit] = swap(pieces[offset], "head", bit)
        bit //= 2
    return [pieces[offset] for offset in range(len(pieces))]


def grad_kernel(head_ref, *refs):
    *piece_refs, own_ref, proj_ref, out_ref = refs
    piece_refs = [own_ref, *piece_refs]
    width = own_ref.shape[1]
    block = proj_ref.shape[0]
    total = None
    for offset, piece in enumerate(piece_refs):
        start = pl.multiple_of((head_ref[0] ^ offset) * width, width)
        part = dot(piece[...], proj_ref[:, pl.ds(start, width)], 1, 1)
        total = part if total is None else total + part
    at = pl.ds(pl.multiple_of(pl.program_id(0) * block, block), block)
    out_ref[:, at] = total.astype(out_ref.dtype)


def attn_grad_of(out_grad, out_proj):
    pieces = gathered_pieces(out_grad)
    rows, width = out_grad.shape
    cols, features = out_proj.shape
    block = 2 * HDIM
    head = lax.axis_index("head").astype(jnp.int32).reshape(1)
    (result,) = call(
        grad_kernel,
        [head],
        pieces[1:],
        [((rows, cols), jnp.bfloat16)],
        rows * cols * features,
        grid=(cols // block,),
        streams=[
            (in_hbm(out_grad), pl.BlockSpec((rows, width), lambda i: (0, 0))),
            (in_hbm(out_proj), pl.BlockSpec((block, features), lambda i: (i, 0))),
        ],
    )
    return result


def stage_kernel(*refs):
    count = len(refs) // 3
    sources, targets, sems = refs[:count], refs[count : 2 * count], refs[2 * count :]
    copies = [pltpu.make_async_copy(*each) for each in zip(sources, targets, sems)]
    for copy in copies:
        copy.start()
    for copy in copies:
        copy.wait()


def staged(*arrays):
    return pl.pallas_call(
        stage_kernel,
        in_specs=[pl.BlockSpec(memory_space=pltpu.HBM)] * len(arrays),
        out_specs=[pl.BlockSpec(memory_space=pltpu.VMEM)] * len(arrays),
        out_shape=[pltpu.VMEM(array.shape, array.dtype) for array in arrays],
        scratch_shapes=[pltpu.SemaphoreType.DMA] * len(arrays),
        compiler_params=pltpu.CompilerParams(vmem_limit_bytes=KERNEL_VMEM),
        cost_estimate=pl.CostEstimate(flops=10**6, bytes_accessed=0, transcendentals=0),
        name="stage",
    )(*[in_hbm(array) for array in arrays])


def causal(raw, fill):
    key_at = lax.broadcasted_iota(jnp.int32, raw.shape, 0)
    query_at = lax.broadcasted_iota(jnp.int32, raw.shape, 1)
    return jnp.where(key_at <= query_at, raw, fill)


class Flags:
    def __init__(self, spans, table_ref, active_ref, place_ref):
        self.spans, self.table = spans, table_ref
        self.active, self.place = active_ref, place_ref

    def usable(self, head, section):
        used = self.table[head, section] * self.active[0, section] > 0
        return used & (self.place[0] >= self.spans[section])

    def is_odd(self):
        return (self.place[0] // self.spans[NEAR]) % 2 == 1


def set_stats(head, raw, pgrad, probs, pgrads, stats):
    top = jnp.max(raw, axis=0, keepdims=True)
    prob = jnp.exp2((raw - top) * EXP_SCALE)
    probs[head] = prob
    pgrads[head] = pgrad
    norm = jnp.sum(prob, axis=0, keepdims=True)
    delta = jnp.sum(prob * pgrad, axis=0, keepdims=True)
    for index, row in enumerate((top, norm, delta)):
        stats[index, pl.ds(head, 1), :] = row


def stats_kernel(diagonal, q, g, k, v, stats, probs, pgrads):
    def step(head):
        at = columns(head)
        raw = dot(k[:, at], q[:, at], 1, 1)
        if diagonal:
            raw = causal(raw, -BIG)
        set_stats(head, raw, dot(v[:, at], g[:, at], 1, 1), probs, pgrads, stats)

    each_head(0, probs.shape[0], step)


def stats_near_kernel(spans, t, a, p, q, g, k, v, k_up, v_up, stats, probs, pgrads):
    odd = Flags(spans, t, a, p).is_odd()

    def step(head):
        at = columns(head)
        keys = jnp.where(odd, k_up[:, at], k[:, at])
        values = jnp.where(odd, v_up[:, at], v[:, at])
        raw = dot(keys, q[:, at], 1, 1)
        set_stats(head, raw, dot(values, g[:, at], 1, 1), probs, pgrads, stats)

    each_head(0, probs.shape[0], step)


def combine_kernel(spans, t, a, p, *refs):
    flags = Flags(spans, t, a, p)
    ins, outs = refs[:4], refs[4:]
    for head in range(ins[0].shape[1]):
        at = slice(head, head + 1)
        peaks = [ins[0][0, at, :]]
        for ref, section in zip(ins[1:], (MID, FAR, NEAR)):
            peaks.append(jnp.where(flags.usable(head, section), ref[0, at, :], -BIG))
        top = jnp.maximum(jnp.maximum(peaks[0], peaks[1]), jnp.maximum(peaks[2], peaks[3]))
        factors = [jnp.exp2((peak - top) * EXP_SCALE) for peak in peaks]
        norm, delta = 0.0, 0.0
        for ref, factor in zip(ins, factors):
            norm = norm + factor * ref[1, at, :]
            delta = delta + factor * ref[2, at, :]
        inverse = 1.0 / norm
        delta = delta * inverse
        for out, factor in zip(outs, factors):
            out[0, at, :] = factor * inverse
            out[1, at, :] = delta


def pair_terms(head, query, grad, keys, probs, pgrads, norm):
    factor, delta = norm[0, pl.ds(head, 1), :], norm[1, pl.ds(head, 1), :]
    prob = probs[head] * factor
    weight = prob.astype(jnp.bfloat16)
    dlogit = (prob * (pgrads[head] - delta)).astype(jnp.bfloat16)
    return dot(keys, dlogit, 0, 0), dot(dlogit, query, 1, 0), dot(weight, grad, 1, 0)


def terms_kernel(q, g, k, norm, probs, pgrads, *refs):
    dq, dk, dv = refs[-3:]

    def step(head):
        at = columns(head)
        query_term, dk[:, at], dv[:, at] = pair_terms(
            head, q[:, at], g[:, at], k[:, at], probs, pgrads, norm
        )
        query_term = query_term.T
        dq[:, at] = query_term + refs[0][:, at] if len(refs) > 3 else query_term

    each_head(0, probs.shape[0], step)


def pairs_kernel(
    spans, first, t, a, p, qf, gf, qn, gn, k, k_up, norm_far, norm_near,
    pr_far, pg_far, pr_near, pg_near, dk_mid, dv_mid, *refs,
):
    dqf, dqn, back, dk, dv = refs[-5:]
    odd = Flags(spans, t, a, p).is_odd()
    rows = qf.shape[0]

    def step(head):
        at, out = columns(head), columns(head - first)
        key_up = k_up[:, at]
        dq, key_far, value_far = pair_terms(
            head, qf[:, at], gf[:, at], key_up, pr_far, pg_far, norm_far
        )
        dqf[:, at] = (dq * SCALE).T.astype(dqf.dtype)
        key_near = jnp.where(odd, key_up, k[:, at])
        dq, key_term, value_term = pair_terms(
            head, qn[:, at], gn[:, at], key_near, pr_near, pg_near, norm_near
        )
        dqn[:, at] = (dq * SCALE).T.astype(dqn.dtype)
        zero = jnp.zeros_like(key_term)
        key_back = dk_mid[:, at] + key_far + jnp.where(odd, key_term, zero)
        value_back = dv_mid[:, at] + value_far + jnp.where(odd, value_term, zero)
        back[:rows, out] = (key_back * SCALE).astype(back.dtype)
        back[rows:, out] = value_back.astype(back.dtype)
        dk[:, out] = jnp.where(odd, zero, key_term)
        dv[:, out] = jnp.where(odd, zero, value_term)

    each_head(first, dk.shape[1] // HDIM, step)


def step_columns(block, first=0):
    return pl.ds(pl.multiple_of(pl.program_id(0) * block + first, block), block)


def finish_kernel(first, dk, dv, near_k, near_v, back, *refs):
    key_out, value_out = refs[-2:]
    rows, block = key_out.shape
    here, at = step_columns(block), step_columns(block, first)
    key_out[...] = (
        (dk[:, at] + near_k[:, here]) * SCALE + back[:rows, here].astype(jnp.float32)
    ).astype(key_out.dtype)
    value_out[...] = (
        dv[:, at] + near_v[:, here] + back[rows:, here].astype(jnp.float32)
    ).astype(value_out.dtype)


def finish_query_kernel(dq, far, near, out):
    at = step_columns(out.shape[1])
    total = dq[:, at] * SCALE + far[:, at].astype(jnp.float32) + near[:, at].astype(jnp.float32)
    out[...] = total.astype(out.dtype)


def body(queries, key_rows, value_rows, out_grad, out_proj, section_table, block_active):
    seq_count = lax.axis_size("seq")
    place = lax.axis_index("seq")
    spans = [seq_count // 2 ** (index + 1) for index in range(SECTIONS)]
    mid_span, near_span = spans[MID], spans[NEAR]
    assert spans[FAR] == 2 * mid_span and mid_span == 2 * near_span
    assert block_active.shape[0] == 1
    rows, cols = queries.shape
    heads = cols // HDIM
    assert heads == sum(GROUPS)
    pair_work = rows * rows * HDIM
    flags = [section_table, block_active, place.astype(jnp.int32).reshape(1)]

    wide_f32 = ((rows, cols), jnp.float32)
    wide_bf16 = ((rows, cols), jnp.bfloat16)
    stat = ((3, heads, rows), jnp.float32)
    norm = ((2, heads, rows), jnp.float32)
    square = ((heads, rows, rows), jnp.float32)

    def bound(kernel, *fixed):
        def run(*refs):
            kernel(*fixed, *refs)

        return run

    key_up = shift(key_rows, mid_span)
    value_up = shift(value_rows, mid_span)
    query_far = shift(queries, -mid_span)
    query_near = swap(queries, "seq", near_span)
    grads = attn_grad_of(out_grad, out_proj)
    grad_far = shift(grads, -mid_span)
    grad_near = swap(grads, "seq", near_span)
    query, key, value = staged(queries, key_rows, value_rows)

    def stats(kernel, scalars, *ins):
        outs = [stat, square, square]
        return call(kernel, scalars, ins, outs, heads * 2 * pair_work)

    self_stats, *self_squares = stats(bound(stats_kernel, True), [], query, grads, key, value)
    mid_stats, *mid_squares = stats(bound(stats_kernel, False), [], query, grads, key_up, value_up)
    near_stats, *near_squares = stats(
        bound(stats_near_kernel, spans), flags,
        query_near, grad_near, key, value, key_up, value_up,
    )
    near_stats = swap(near_stats, "seq", near_span)
    far_stats, *far_squares = stats(
        bound(stats_kernel, False), [], query_far, grad_far, key_up, value_up
    )
    far_stats = shift(far_stats, mid_span)
    self_norm, mid_norm, far_norm, near_norm = call(
        bound(combine_kernel, spans),
        flags,
        [self_stats, mid_stats, far_stats, near_stats],
        [norm] * 4,
        heads * rows * HDIM,
    )
    far_norm = shift(far_norm, -mid_span)
    near_norm = swap(near_norm, "seq", near_span)

    def terms(keys, row_norm, squares, *added):
        ins = [query, grads, keys, row_norm, *squares, *added]
        return call(terms_kernel, [], ins, [wide_f32] * 3, heads * 3 * pair_work)

    mid_query, *mid_terms = terms(key_up, mid_norm, mid_squares)
    guests = [query_far, grad_far, query_near, grad_near, key, key_up, far_norm, near_norm]
    guests += [*far_squares, *near_squares, *mid_terms]
    partial_queries, returned = [], []
    first = 0
    for group in GROUPS:
        width = group * HDIM
        start = len(flags) + len(guests)
        aliases = {start + number: number for number in range(len(partial_queries))}
        *partial_queries, back, near_key, near_value = call(
            bound(pairs_kernel, spans, first),
            flags,
            guests + partial_queries,
            [wide_bf16] * 2 + [((2 * rows, width), jnp.bfloat16)]
            + [((rows, width), jnp.float32)] * 2,
            group * 6 * pair_work,
            aliases,
        )
        returned.append((near_key, near_value, shift(back, -mid_span)))
        first += group
    query_far_part = shift(partial_queries[0], mid_span)
    query_near_part = swap(partial_queries[1], "seq", near_span)
    query_sum, *self_terms = terms(key, self_norm, self_squares, mid_query)

    block = 2 * HDIM
    outputs = []
    first = 0
    for index, group in enumerate(GROUPS):
        start = first * HDIM
        place_of = start // block
        ins = [*self_terms, *returned[index]]
        outputs = call(
            bound(finish_kernel, start),
            [],
            ins,
            [wide_bf16] * 2,
            group * rows * HDIM * HDIM,
            {len(ins) + number: number for number in range(len(outputs))},
            grid=(group * HDIM // block,),
            streams=[(array, pl.BlockSpec(memory_space=pl.ANY)) for array in outputs],
            blocks=[pl.BlockSpec((rows, block), lambda i, j=place_of: (0, i + j))] * 2,
        )
        first += group
    (query_grad,) = call(
        finish_query_kernel,
        [],
        [query_sum, query_far_part, query_near_part],
        [wide_bf16],
        heads * rows * HDIM,
        grid=(cols // block,),
        blocks=[pl.BlockSpec((rows, block), lambda i: (0, i))],
    )
    return query_grad, *outputs


def solution(mesh):
    return jax.shard_map(
        body,
        mesh=mesh,
        in_specs=(
            P("seq", "head"),
            P("seq", "head"),
            P("seq", "head"),
            P("seq", "head"),
            P("head", None),
            P("head", None),
            P("seq", None),
        ),
        out_specs=(P("seq", "head"), P("seq", "head"), P("seq", "head")),
        check_vma=False,
    )
```

time: 92.7 us -> 97.6 us (1.053)
  Pallas kernels: 17.5 us -> 27.7 us
  local copies, waits for them, and re-layouts: 6.11 us -> 0.09 us
  waiting for transfers between devices: 32 us -> 36.1 us
  other arithmetic: 2.9 us -> 0 us
    pallas_call x7 -> x16, Pallas kernels: 17.5 us -> 27.7 us  [the longest x15 26.3 us: call(): pl.pallas_call(kernel, grid=grid or (), in_specs=[smem] * len(scalars) +...]
    unnamed x21 -> x5, local copies, waits for them, and re-layouts: 6.11 us -> 0.09 us
    ppermute x8, waiting for transfers between devices: 10.8 us -> 13.5 us  [swap(): return lax.ppermute(value, axis, pairs)]
    convert_element_type x5 -> x0, other arithmetic: 1.79 us -> none  [the longest x1 1.03 us: body(): return (query_grad.astype(jnp.bfloat16), key_grad, value_grad)]
    ppermute x9 -> x10, waiting for transfers between devices: 21.2 us -> 22.5 us  [shift(): lax.ppermute(value, 'seq', [(src, src + steps) for src in range(low, high)])]
    ppermute x9 -> x10, starting transfers between devices: 23.8 us -> 22.5 us  [shift(): lax.ppermute(value, 'seq', [(src, src + steps) for src in range(low, high)])]
    dynamic_update_slice x1 -> x0, other arithmetic: 1.11 us -> none  [body(): key_grad = lax.dynamic_update_slice(key_grad, key_part, at)]
  transfers between devices with their start and end apart: 17 -> 18, of which waited for: 8 -> 7; matrix products, arithmetic and copies ran while one was open for 2% -> 0% of each run, Pallas kernels for 11% -> 22%
where the time goes in v3:
time: 97.6 us; the launch traced here: 97.1 us
  waiting for transfers between devices  36.1 us (37%)
  starting transfers between devices  32.4 us (33%)
  Pallas kernels  27.7 us (28%)
    pallas_call x15, Pallas kernels, call(): pl.pallas_call(kernel, grid=grid or (), in_specs=[smem] * len(scalars) +...  26.3 us
    ppermute x10, starting transfers between devices, shift(): lax.ppermute(value, 'seq', [(src, src + steps) for src in range(low, high)])  22.5 us
    ppermute x10, waiting for transfers between devices, shift(): lax.ppermute(value, 'seq', [(src, src + steps) for src in range(low, high)])  22.5 us
    ppermute x8, waiting for transfers between devices, swap(): return lax.ppermute(value, axis, pairs)  13.5 us
    ppermute x8, starting transfers between devices, swap(): return lax.ppermute(value, axis, pairs)  9.89 us
  transfers between devices with their start and end apart: 18, of which 7 were waited for; matrix products, arithmetic and copies ran while one was open for 0% of the time, Pallas kernels for 22%

profile of v3, /device:TPU:0, one launch (start us, length us, event | category | flops | bytes accessed | tf_op | source)
XLA Modules:
  0.0 97.1 jit_solution(6340663001435121060)
XLA Ops:
  0.6 3.1 %collective-permute-start.1 = (bf16[256,512]{1,0:T(8,128)(2,1)}, bf16[256,512]{1,0:T(8,128)(2,1)S(1)}, u32[]{:S(2)}, u32[]{:S(2)}) collective-permute-start(bf16[256,512]{1,0:T(8,128)(2,1)} %refs_3_.1), channel_id=1, source_target_pairs={{0,2},{1,3},{2,0},{3,1},{4,6},{5,7},{6,4},{7,5},{8,10},{9,11},{10,... | collective-permute-start | bytes 786440 | tf_op jit(solution)/shard_map/ppermute | solution.py:31
  3.7 3.5 %collective-permute-start.3 = (bf16[256,1024]{1,0:T(8,128)(2,1)}, bf16[256,1024]{1,0:T(8,128)(2,1)S(1)}, u32[]{:S(2)}, u32[]{:S(2)}) collective-permute-start(bf16[256,1024]{1,0:T(8,128)(2,1)} %refs_1_.6), channel_id=1, source_target_pairs={{0,8},{4,12},{8,16},{12,20},{16,24},{20,28},{1,9},{5,13},{9,17},{1... | collective-permute-start | bytes 1572872 | tf_op jit(solution)/shard_map/ppermute | solution.py:26
  7.2 0.1 collective-permute-start
  7.3 2.9 %collective-permute-done.1.refs_1_ = bf16[256,512]{1,0:T(8,128)(2,1)S(1)} collective-permute-done((bf16[256,512]{1,0:T(8,128)(2,1)}, bf16[256,512]{1,0:T(8,128)(2,1)S(1)}, u32[]{:S(2)}, u32[]{:S(2)}) %collective-permute-start.1) | collective-permute-done | bytes 262176 | tf_op jit(solution)/shard_map/ppermute | solution.py:31
  10.2 4.5 %collective-permute-start.4 = (bf16[256,1024]{1,0:T(8,128)(2,1)}, bf16[256,1024]{1,0:T(8,128)(2,1)}, u32[]{:S(2)}, u32[]{:S(2)}) collective-permute-start(bf16[256,1024]{1,0:T(8,128)(2,1)} %refs_2_.1), channel_id=1, source_target_pairs={{0,8},{4,12},{8,16},{12,20},{16,24},{20,28},{1,9},{5,13},{9,17},{1... | collective-permute-start | bytes 1572872 | tf_op jit(solution)/shard_map/ppermute | solution.py:26
  14.7 1.5 %collective-permute-start.8 = (bf16[256,1024]{1,0:T(8,128)(2,1)}, bf16[256,1024]{1,0:T(8,128)(2,1)S(1)}, u32[]{:S(2)}, u32[]{:S(2)}) collective-permute-start(bf16[256,1024]{1,0:T(8,128)(2,1)} %refs_0_.6), channel_id=1, source_target_pairs={{0,4},{4,0},{8,12},{12,8},{16,20},{20,16},{24,28},{28,24},{1,5},{5... | collective-permute-start | bytes 1572872 | tf_op jit(solution)/shard_map/ppermute | solution.py:31
  16.2 0.0 collective-permute-done.refs_0_
  16.2 0.0 collective-permute-done.2.refs_2_
  16.2 4.0 %shard_map.94.refs_1_.g = bf16[256,1024]{1,0:T(8,128)(2,1)S(1)} custom-call(s32[1]{0:T(128)} %bitcast.head_ref, bf16[256,512]{1,0:T(8,128)(2,1)S(1)} %collective-permute-done.refs_0_, bf16[256,512]{1,0:T(8,128)(2,1)S(1)} %collective-permute-done.1.refs_1_, bf16[256,512]{1,0:T(8,128)(2,1)S(1)} %collective-permute-done.2.refs_2_, bf16[256,512]{1,0:T(8,128)(2,1)} %refs_3_.1, ...), custom_call_target="tpu_custom_call" | custom-call | flops 1073741824 | tf_op jit(solution)/shard_map/pallas_call | solution.py:51
  20.3 0.0 copy-start
  20.3 0.6 collective-permute-start.9
  20.9 1.3 %collective-permute-start.5 = (bf16[256,1024]{1,0:T(8,128)(2,1)}, bf16[256,1024]{1,0:T(8,128)(2,1)S(1)}, u32[]{:S(2)}, u32[]{:S(2)}) collective-permute-start(bf16[256,1024]{1,0:T(8,128)(2,1)} %refs_0_.6), channel_id=1, source_target_pairs={{8,0},{12,4},{16,8},{20,12},{24,16},{28,20},{9,1},{13,5},{17,9},{2... | collective-permute-start | bytes 1572872 | tf_op jit(solution)/shard_map/ppermute | solution.py:26
  22.2 0.0 collective-permute-done.3.refs_2_.refs_7_.k.refs_8_
  22.2 1.3 %collective-permute-start.6 = (bf16[256,1024]{1,0:T(8,128)(2,1)S(1)}, bf16[256,1024]{1,0:T(8,128)(2,1)S(1)}, u32[]{:S(2)}, u32[]{:S(2)}) collective-permute-start(bf16[256,1024]{1,0:T(8,128)(2,1)S(1)} %shard_map.94.refs_1_.g), channel_id=1, source_target_pairs={{8,0},{12,4},{16,8},{20,12},{24,16},{28,20},{9,1},{13,5},{17,9},{2... | collective-permute-start | bytes 1572872 | tf_op jit(solution)/shard_map/ppermute | solution.py:26
  23.5 0.1 copy.19.refs_0_
  23.6 1.4 %stage.1 = (bf16[256,1024]{1,0:T(8,128)(2,1)S(1)}, bf16[256,1024]{1,0:T(8,128)(2,1)S(1)}, bf16[256,1024]{1,0:T(8,128)(2,1)S(1)}) custom-call(bf16[256,1024]{1,0:T(8,128)(2,1)} %refs_0_.6, bf16[256,1024]{1,0:T(8,128)(2,1)} %refs_1_.6, bf16[256,1024]{1,0:T(8,128)(2,1)} %refs_2_.1), custom_call_target="tpu_custom_call" | custom-call | flops 1000000 | tf_op jit(solution)/shard_map/stage/pallas_call | solution.py:137
  25.0 1.6 %shard_map.95 = (f32[3,8,256]{2,1,0:T(8,128)S(1)}, f32[8,256,256]{2,1,0:T(8,128)S(1)}, f32[8,256,256]{2,1,0:T(8,128)S(1)}) custom-call(bf16[256,1024]{1,0:T(8,128)(2,1)S(1)} %get-tuple-element.49.refs_0_.q, bf16[256,1024]{1,0:T(8,128)(2,1)S(1)} %shard_map.94.refs_1_.g, bf16[256,1024]{1,0:T(8,128)(2,1)S(1)} %get-tuple-element.50.refs_2_.refs_5_.k.refs_7_, ...), custom_call_target="tpu_custom_call" | custom-call | flops 268435456 | tf_op jit(solution)/shard_map/pallas_call | solution.py:51
  26.6 3.0 %collective-permute-done.4.refs_3_.refs_8_ = bf16[256,1024]{1,0:T(8,128)(2,1)} collective-permute-done((bf16[256,1024]{1,0:T(8,128)(2,1)}, bf16[256,1024]{1,0:T(8,128)(2,1)}, u32[]{:S(2)}, u32[]{:S(2)}) %collective-permute-start.4) | collective-permute-done | bytes 524320 | tf_op jit(solution)/shard_map/ppermute | solution.py:26
  29.6 0.1 collective-permute-done.8.refs_3_.refs_5_
  29.7 10.5 %collective-permute-done.9.refs_4_.refs_6_ = bf16[256,1024]{1,0:T(8,128)(2,1)S(1)} collective-permute-done((bf16[256,1024]{1,0:T(8,128)(2,1)S(1)}, bf16[256,1024]{1,0:T(8,128)(2,1)S(1)}, u32[]{:S(2)}, u32[]{:S(2)}) %collective-permute-start.9) | collective-permute-done | bytes 524320 | tf_op jit(solution)/shard_map/ppermute | solution.py:31
  40.2 2.8 %shard_map.98 = (f32[3,8,256]{2,1,0:T(8,128)S(1)}, f32[8,256,256]{2,1,0:T(8,128)S(1)}, f32[8,256,256]{2,1,0:T(8,128)S(1)}) custom-call(s32[8,3]{1,0:T(8,128)S(1)} %copy.19.refs_0_, s32[1,3]{1,0:T(1,128)S(1)} %copy-done, s32[1]{0:T(128)} %bitcast.1.refs_2_, bf16[256,1024]{1,0:T(8,128)(2,1)S(1)} %collective-permute-done.8.refs_3_.refs_5_, ...), custom_call_target="tpu_custom_call" | custom-call | flops 268435456 | tf_op jit(solution)/shard_map/pallas_call | solution.py:51
  43.0 1.6 %collective-permute-start.10 = (f32[3,8,256]{2,1,0:T(8,128)S(1)}, f32[3,8,256]{2,1,0:T(8,128)S(1)}, u32[]{:S(2)}, u32[]{:S(2)}) collective-permute-start(f32[3,8,256]{2,1,0:T(8,128)S(1)} %get-tuple-element.55), channel_id=1, source_target_pairs={{0,4},{4,0},{8,12},{12,8},{16,20},{20,16},{24,28},{28,24},{1,5},{5... | collective-permute-start | bytes 73736 | tf_op jit(solution)/shard_map/ppermute | solution.py:31
  44.6 0.0 collective-permute-done.5.refs_0_.refs_3_
  44.6 3.1 %collective-permute-done.6.refs_1_.refs_4_ = bf16[256,1024]{1,0:T(8,128)(2,1)S(1)} collective-permute-done((bf16[256,1024]{1,0:T(8,128)(2,1)S(1)}, bf16[256,1024]{1,0:T(8,128)(2,1)S(1)}, u32[]{:S(2)}, u32[]{:S(2)}) %collective-permute-start.6) | collective-permute-done | bytes 524320 | tf_op jit(solution)/shard_map/ppermute | solution.py:26
  47.7 2.7 %shard_map.97 = (f32[3,8,256]{2,1,0:T(8,128)S(1)}, f32[8,256,256]{2,1,0:T(8,128)S(1)}, f32[8,256,256]{2,1,0:T(8,128)S(1)}) custom-call(bf16[256,1024]{1,0:T(8,128)(2,1)S(1)} %collective-permute-done.5.refs_0_.refs_3_, bf16[256,1024]{1,0:T(8,128)(2,1)S(1)} %collective-permute-done.6.refs_1_.refs_4_, ...), custom_call_target="tpu_custom_call" | custom-call | flops 268435456 | tf_op jit(solution)/shard_map/pallas_call | solution.py:51
  50.4 2.8 %collective-permute-start.7 = (f32[3,8,256]{2,1,0:T(8,128)S(1)}, f32[3,8,256]{2,1,0:T(8,128)S(1)}, u32[]{:S(2)}, u32[]{:S(2)}) collective-permute-start(f32[3,8,256]{2,1,0:T(8,128)S(1)} %get-tuple-element.54), channel_id=1, source_target_pairs={{0,8},{4,12},{8,16},{12,20},{16,24},{20,28},{1,9},{5,13},{9,17},{1... | collective-permute-start | bytes 73736 | tf_op jit(solution)/shard_map/ppermute | solution.py:26
  53.2 2.7 %shard_map.96 = (f32[3,8,256]{2,1,0:T(8,128)S(1)}, f32[8,256,256]{2,1,0:T(8,128)S(1)}, f32[8,256,256]{2,1,0:T(8,128)S(1)}) custom-call(bf16[256,1024]{1,0:T(8,128)(2,1)S(1)} %get-tuple-element.49.refs_0_.q, bf16[256,1024]{1,0:T(8,128)(2,1)S(1)} %shard_map.94.refs_1_.g, bf16[256,1024]{1,0:T(8,128)(2,1)S(1)} %collective-permute-done.3.refs_2_.refs_7_.k.refs_8_, ...), custom_call_target="tpu_custom_call" | custom-call | flops 268435456 | tf_op jit(solution)/shard_map/pallas_call | solution.py:51
  55.9 0.0 collective-permute-done.7.refs_5_
  55.9 0.7 shard_map.99
  56.6 1.3 %collective-permute-start.11 = (f32[2,8,256]{2,1,0:T(8,128)S(1)}, f32[2,8,256]{2,1,0:T(8,128)S(1)}, u32[]{:S(2)}, u32[]{:S(2)}) collective-permute-start(f32[2,8,256]{2,1,0:T(8,128)S(1)} %get-tuple-element.64), channel_id=1, source_target_pairs={{8,0},{12,4},{16,8},{20,12},{24,16},{28,20},{9,1},{13,5},{17,9},{2... | collective-permute-start | bytes 49160 | tf_op jit(solution)/shard_map/ppermute | solution.py:26
  57.9 1.6 %collective-permute-start.12 = (f32[2,8,256]{2,1,0:T(8,128)S(1)}, f32[2,8,256]{2,1,0:T(8,128)S(1)}, u32[]{:S(2)}, u32[]{:S(2)}) collective-permute-start(f32[2,8,256]{2,1,0:T(8,128)S(1)} %get-tuple-element.65), channel_id=1, source_target_pairs={{0,4},{4,0},{8,12},{12,8},{16,20},{20,16},{24,28},{28,24},{1,5},{5... | collective-permute-start | bytes 49160 | tf_op jit(solution)/shard_map/ppermute | solution.py:31
  59.5 1.6 %shard_map.100 = (f32[256,1024]{1,0:T(8,128)S(1)}, f32[256,1024]{1,0:T(8,128)S(1)}, f32[256,1024]{1,0:T(8,128)S(1)}) custom-call(bf16[256,1024]{1,0:T(8,128)(2,1)S(1)} %get-tuple-element.49.refs_0_.q, bf16[256,1024]{1,0:T(8,128)(2,1)S(1)} %shard_map.94.refs_1_.g, bf16[256,1024]{1,0:T(8,128)(2,1)S(1)} %collective-permute-done.3.refs_2_.refs_7_.k.refs_8_, ...), custom_call_target="tpu_custom_call" | custom-call | flops 402653184 | tf_op jit(solution)/shard_map/pallas_call | solution.py:51
  61.1 1.2 %collective-permute-done.11.refs_9_ = f32[2,8,256]{2,1,0:T(8,128)S(1)} collective-permute-done((f32[2,8,256]{2,1,0:T(8,128)S(1)}, f32[2,8,256]{2,1,0:T(8,128)S(1)}, u32[]{:S(2)}, u32[]{:S(2)}) %collective-permute-start.11) | collective-permute-done | bytes 16416 | tf_op jit(solution)/shard_map/ppermute | solution.py:26
  62.3 1.3 %shard_map.102 = (bf16[256,1024]{1,0:T(8,128)(2,1)S(1)}, bf16[256,1024]{1,0:T(8,128)(2,1)S(1)}, bf16[512,256]{1,0:T(8,128)(2,1)S(1)}, f32[256,256]{1,0:T(8,128)S(1)}, f32[256,256]{1,0:T(8,128)S(1)}) custom-call(s32[8,3]{1,0:T(8,128)S(1)} %copy.19.refs_0_, s32[1,3]{1,0:T(1,128)S(1)} %copy-done, s32[1]{0:T(128)} %bitcast.1.refs_2_, ...), custom_call_target="tpu_custom_call" | custom-call | flops 201326592 | tf_op jit(solution)/shard_map/pallas_call | solution.py:51
  63.5 2.0 %shard_map.103 = (bf16[256,1024]{1,0:T(8,128)(2,1)S(1)}, bf16[256,1024]{1,0:T(8,128)(2,1)S(1)}, bf16[512,512]{1,0:T(8,128)(2,1)S(1)}, f32[256,512]{1,0:T(8,128)S(1)}, f32[256,512]{1,0:T(8,128)S(1)}) custom-call(s32[8,3]{1,0:T(8,128)S(1)} %copy.19.refs_0_, s32[1,3]{1,0:T(1,128)S(1)} %copy-done, ...), custom_call_target="tpu_custom_call", output_to_operand_aliasing={{0}: (17, {}), {1}: (18, {})} | custom-call | flops 402653184 | tf_op jit(solution)/shard_map/pallas_call | solution.py:51
  65.5 1.2 %shard_map.104 = (bf16[256,1024]{1,0:T(8,128)(2,1)S(1)}, bf16[256,1024]{1,0:T(8,128)(2,1)S(1)}, bf16[512,256]{1,0:T(8,128)(2,1)S(1)}, f32[256,256]{1,0:T(8,128)S(1)}, f32[256,256]{1,0:T(8,128)S(1)}) custom-call(s32[8,3]{1,0:T(8,128)S(1)} %copy.19.refs_0_, s32[1,3]{1,0:T(1,128)S(1)} %copy-done, ...), custom_call_target="tpu_custom_call", output_to_operand_aliasing={{0}: (17, {}), {1}: (18, {})} | custom-call | flops 201326592 | tf_op jit(solution)/shard_map/pallas_call | solution.py:51
  66.8 4.0 %collective-permute-start.13 = (bf16[256,1024]{1,0:T(8,128)(2,1)S(1)}, bf16[256,1024]{1,0:T(8,128)(2,1)S(1)}, u32[]{:S(2)}, u32[]{:S(2)}) collective-permute-start(bf16[256,1024]{1,0:T(8,128)(2,1)S(1)} %get-tuple-element.76), channel_id=1, source_target_pairs={{0,8},{4,12},{8,16},{12,20},{16,24},{20,28},{1,9},{5,13},{9,17},{1... | collective-permute-start | bytes 1572872 | tf_op jit(solution)/shard_map/ppermute | solution.py:26
  70.8 1.6 %collective-permute-start.14 = (bf16[256,1024]{1,0:T(8,128)(2,1)S(1)}, bf16[256,1024]{1,0:T(8,128)(2,1)S(1)}, u32[]{:S(2)}, u32[]{:S(2)}) collective-permute-start(bf16[256,1024]{1,0:T(8,128)(2,1)S(1)} %get-tuple-element.77), channel_id=1, source_target_pairs={{0,4},{4,0},{8,12},{12,8},{16,20},{20,16},{24,28},{28,24},{1,5},{5... | collective-permute-start | bytes 1572872 | tf_op jit(solution)/shard_map/ppermute | solution.py:31
  72.4 1.3 %collective-permute-start.16 = (bf16[512,512]{1,0:T(8,128)(2,1)S(1)}, bf16[512,512]{1,0:T(8,128)(2,1)S(1)}, u32[]{:S(2)}, u32[]{:S(2)}) collective-permute-start(bf16[512,512]{1,0:T(8,128)(2,1)S(1)} %get-tuple-element.85), channel_id=1, source_target_pairs={{8,0},{12,4},{16,8},{20,12},{24,16},{28,20},{9,1},{13,5},{17,9},{2... | collective-permute-start | bytes 1572872 | tf_op jit(solution)/shard_map/ppermute | solution.py:26
  73.7 1.3 %collective-permute-start.17 = (bf16[512,256]{1,0:T(8,128)(2,1)S(1)}, bf16[512,256]{1,0:T(8,128)(2,1)S(1)}, u32[]{:S(2)}, u32[]{:S(2)}) collective-permute-start(bf16[512,256]{1,0:T(8,128)(2,1)S(1)} %get-tuple-element.88), channel_id=1, source_target_pairs={{8,0},{12,4},{16,8},{20,12},{24,16},{28,20},{9,1},{13,5},{17,9},{2... | collective-permute-start | bytes 786440 | tf_op jit(solution)/shard_map/ppermute | solution.py:26
  75.0 1.3 %collective-permute-start.15 = (bf16[512,256]{1,0:T(8,128)(2,1)S(1)}, bf16[512,256]{1,0:T(8,128)(2,1)S(1)}, u32[]{:S(2)}, u32[]{:S(2)}) collective-permute-start(bf16[512,256]{1,0:T(8,128)(2,1)S(1)} %get-tuple-element.82), channel_id=1, source_target_pairs={{8,0},{12,4},{16,8},{20,12},{24,16},{28,20},{9,1},{13,5},{17,9},{2... | collective-permute-start | bytes 786440 | tf_op jit(solution)/shard_map/ppermute | solution.py:26
  76.3 1.6 %shard_map.101 = (f32[256,1024]{1,0:T(8,128)S(1)}, f32[256,1024]{1,0:T(8,128)S(1)}, f32[256,1024]{1,0:T(8,128)S(1)}) custom-call(bf16[256,1024]{1,0:T(8,128)(2,1)S(1)} %get-tuple-element.49.refs_0_.q, bf16[256,1024]{1,0:T(8,128)(2,1)S(1)} %shard_map.94.refs_1_.g, bf16[256,1024]{1,0:T(8,128)(2,1)S(1)} %get-tuple-element.50.refs_2_.refs_5_.k.refs_7_, ...), custom_call_target="tpu_custom_call" | custom-call | flops 402653184 | tf_op jit(solution)/shard_map/pallas_call | solution.py:51
  77.8 15.2 %collective-permute-done.17.refs_4_ = bf16[512,256]{1,0:T(8,128)(2,1)S(1)} collective-permute-done((bf16[512,256]{1,0:T(8,128)(2,1)S(1)}, bf16[512,256]{1,0:T(8,128)(2,1)S(1)}, u32[]{:S(2)}, u32[]{:S(2)}) %collective-permute-start.17) | collective-permute-done | bytes 262176 | tf_op jit(solution)/shard_map/ppermute | solution.py:26
  93.0 0.8 shard_map.106
  93.8 0.0 collective-permute-done.13.far
  93.8 1.5 %shard_map.105 = bf16[256,1024]{1,0:T(8,128)(2,1)} custom-call(f32[256,1024]{1,0:T(8,128)S(1)} %get-tuple-element.63.dq, bf16[256,1024]{1,0:T(8,128)(2,1)S(1)} %collective-permute-done.13.far, bf16[256,1024]{1,0:T(8,128)(2,1)S(1)} %collective-permute-done.14.near), custom_call_target="tpu_custom_call" | custom-call | flops 524288 | tf_op jit(solution)/shard_map/pallas_call | solution.py:51
  95.3 0.9 shard_map.107
  96.3 0.8 shard_map.108
  (9 shorter events, 0.0 us)
Async XLA Ops:
  0.6 9.6 %collective-permute-start.1 = (bf16[256,512]{1,0:T(8,128)(2,1)}, bf16[256,512]{1,0:T(8,128)(2,1)S(1)}, u32[]{:S(2)}, u32[]{:S(2)}) collective-permute-start(bf16[256,512]{1,0:T(8,128)(2,1)} %refs_3_.1), channel_id=1, source_target_pairs={{0,2},{1,3},{2,0},{3,1},{4,6},{5,7},{6,4},{7,5},{8,10},{9,11},{10,... | collective-permute-start | bytes 786440 | tf_op jit(solution)/shard_map/ppermute | solution.py:31
  3.7 18.5 %collective-permute-start.3 = (bf16[256,1024]{1,0:T(8,128)(2,1)}, bf16[256,1024]{1,0:T(8,128)(2,1)S(1)}, u32[]{:S(2)}, u32[]{:S(2)}) collective-permute-start(bf16[256,1024]{1,0:T(8,128)(2,1)} %refs_1_.6), channel_id=1, source_target_pairs={{0,8},{4,12},{8,16},{12,20},{16,24},{20,28},{1,9},{5,13},{9,17},{1... | collective-permute-start | bytes 1572872 | tf_op jit(solution)/shard_map/ppermute | solution.py:26
  7.2 9.0 %collective-permute-start = (bf16[256,512]{1,0:T(8,128)(2,1)}, bf16[256,512]{1,0:T(8,128)(2,1)S(1)}, u32[]{:S(2)}, u32[]{:S(2)}) collective-permute-start(bf16[256,512]{1,0:T(8,128)(2,1)} %refs_3_.1), channel_id=1, source_target_pairs={{0,1},{1,0},{2,3},{3,2},{4,5},{5,4},{6,7},{7,6},{8,9},{9,8},{10,11... | collective-permute-start | bytes 786440 | tf_op jit(solution)/shard_map/ppermute | solution.py:31
  10.2 6.0 %collective-permute-start.2 = (bf16[256,512]{1,0:T(8,128)(2,1)S(1)}, bf16[256,512]{1,0:T(8,128)(2,1)S(1)}, u32[]{:S(2)}, u32[]{:S(2)}) collective-permute-start(bf16[256,512]{1,0:T(8,128)(2,1)S(1)} %collective-permute-done.1.refs_1_), channel_id=1, source_target_pairs={{0,1},{1,0},{2,3},{3,2},{4,5},{5,4},{6,7},{7,6},{8,9},{9,8},{10,11... | collective-permute-start | bytes 786440 | tf_op jit(solution)/shard_map/ppermute | solution.py:31
  10.2 19.4 %collective-permute-start.4 = (bf16[256,1024]{1,0:T(8,128)(2,1)}, bf16[256,1024]{1,0:T(8,128)(2,1)}, u32[]{:S(2)}, u32[]{:S(2)}) collective-permute-start(bf16[256,1024]{1,0:T(8,128)(2,1)} %refs_2_.1), channel_id=1, source_target_pairs={{0,8},{4,12},{8,16},{12,20},{16,24},{20,28},{1,9},{5,13},{9,17},{1... | collective-permute-start | bytes 1572872 | tf_op jit(solution)/shard_map/ppermute | solution.py:26
  14.7 15.0 %collective-permute-start.8 = (bf16[256,1024]{1,0:T(8,128)(2,1)}, bf16[256,1024]{1,0:T(8,128)(2,1)S(1)}, u32[]{:S(2)}, u32[]{:S(2)}) collective-permute-start(bf16[256,1024]{1,0:T(8,128)(2,1)} %refs_0_.6), channel_id=1, source_target_pairs={{0,4},{4,0},{8,12},{12,8},{16,20},{20,16},{24,28},{28,24},{1,5},{5... | collective-permute-start | bytes 1572872 | tf_op jit(solution)/shard_map/ppermute | solution.py:31
  16.2 7.3 %copy-start.1 = (s32[8,3]{0,1:T(4,128)S(1)}, s32[8,3]{0,1:T(4,128)}, u32[]{:S(2)}) copy-start(s32[8,3]{0,1:T(4,128)} %param.12) | copy-start | bytes 292
  20.3 19.9 %copy-start = (s32[1,3]{1,0:T(1,128)S(1)}, s32[1,3]{1,0:T(1,128)}, u32[]{:S(2)}) copy-start(s32[1,3]{1,0:T(1,128)} %refs_1_.11) | copy-start | bytes 40
  20.3 19.9 %collective-permute-start.9 = (bf16[256,1024]{1,0:T(8,128)(2,1)S(1)}, bf16[256,1024]{1,0:T(8,128)(2,1)S(1)}, u32[]{:S(2)}, u32[]{:S(2)}) collective-permute-start(bf16[256,1024]{1,0:T(8,128)(2,1)S(1)} %shard_map.94.refs_1_.g), channel_id=1, source_target_pairs={{0,4},{4,0},{8,12},{12,8},{16,20},{20,16},{24,28},{28,24},{1,5},{5... | collective-permute-start | bytes 1572872 | tf_op jit(solution)/shard_map/ppermute | solution.py:31
  20.9 23.7 %collective-permute-start.5 = (bf16[256,1024]{1,0:T(8,128)(2,1)}, bf16[256,1024]{1,0:T(8,128)(2,1)S(1)}, u32[]{:S(2)}, u32[]{:S(2)}) collective-permute-start(bf16[256,1024]{1,0:T(8,128)(2,1)} %refs_0_.6), channel_id=1, source_target_pairs={{8,0},{12,4},{16,8},{20,12},{24,16},{28,20},{9,1},{13,5},{17,9},{2... | collective-permute-start | bytes 1572872 | tf_op jit(solution)/shard_map/ppermute | solution.py:26
  22.2 25.5 %collective-permute-start.6 = (bf16[256,1024]{1,0:T(8,128)(2,1)S(1)}, bf16[256,1024]{1,0:T(8,128)(2,1)S(1)}, u32[]{:S(2)}, u32[]{:S(2)}) collective-permute-start(bf16[256,1024]{1,0:T(8,128)(2,1)S(1)} %shard_map.94.refs_1_.g), channel_id=1, source_target_pairs={{8,0},{12,4},{16,8},{20,12},{24,16},{28,20},{9,1},{13,5},{17,9},{2... | collective-permute-start | bytes 1572872 | tf_op jit(solution)/shard_map/ppermute | solution.py:26
  43.0 12.9 %collective-permute-start.10 = (f32[3,8,256]{2,1,0:T(8,128)S(1)}, f32[3,8,256]{2,1,0:T(8,128)S(1)}, u32[]{:S(2)}, u32[]{:S(2)}) collective-permute-start(f32[3,8,256]{2,1,0:T(8,128)S(1)} %get-tuple-element.55), channel_id=1, source_target_pairs={{0,4},{4,0},{8,12},{12,8},{16,20},{20,16},{24,28},{28,24},{1,5},{5... | collective-permute-start | bytes 73736 | tf_op jit(solution)/shard_map/ppermute | solution.py:31
  50.4 5.5 %collective-permute-start.7 = (f32[3,8,256]{2,1,0:T(8,128)S(1)}, f32[3,8,256]{2,1,0:T(8,128)S(1)}, u32[]{:S(2)}, u32[]{:S(2)}) collective-permute-start(f32[3,8,256]{2,1,0:T(8,128)S(1)} %get-tuple-element.54), channel_id=1, source_target_pairs={{0,8},{4,12},{8,16},{12,20},{16,24},{20,28},{1,9},{5,13},{9,17},{1... | collective-permute-start | bytes 73736 | tf_op jit(solution)/shard_map/ppermute | solution.py:26
  56.6 5.6 %collective-permute-start.11 = (f32[2,8,256]{2,1,0:T(8,128)S(1)}, f32[2,8,256]{2,1,0:T(8,128)S(1)}, u32[]{:S(2)}, u32[]{:S(2)}) collective-permute-start(f32[2,8,256]{2,1,0:T(8,128)S(1)} %get-tuple-element.64), channel_id=1, source_target_pairs={{8,0},{12,4},{16,8},{20,12},{24,16},{28,20},{9,1},{13,5},{17,9},{2... | collective-permute-start | bytes 49160 | tf_op jit(solution)/shard_map/ppermute | solution.py:26
  57.9 4.3 %collective-permute-start.12 = (f32[2,8,256]{2,1,0:T(8,128)S(1)}, f32[2,8,256]{2,1,0:T(8,128)S(1)}, u32[]{:S(2)}, u32[]{:S(2)}) collective-permute-start(f32[2,8,256]{2,1,0:T(8,128)S(1)} %get-tuple-element.65), channel_id=1, source_target_pairs={{0,4},{4,0},{8,12},{12,8},{16,20},{20,16},{24,28},{28,24},{1,5},{5... | collective-permute-start | bytes 49160 | tf_op jit(solution)/shard_map/ppermute | solution.py:31
  66.8 27.1 %collective-permute-start.13 = (bf16[256,1024]{1,0:T(8,128)(2,1)S(1)}, bf16[256,1024]{1,0:T(8,128)(2,1)S(1)}, u32[]{:S(2)}, u32[]{:S(2)}) collective-permute-start(bf16[256,1024]{1,0:T(8,128)(2,1)S(1)} %get-tuple-element.76), channel_id=1, source_target_pairs={{0,8},{4,12},{8,16},{12,20},{16,24},{20,28},{1,9},{5,13},{9,17},{1... | collective-permute-start | bytes 1572872 | tf_op jit(solution)/shard_map/ppermute | solution.py:26
  70.8 23.0 %collective-permute-start.14 = (bf16[256,1024]{1,0:T(8,128)(2,1)S(1)}, bf16[256,1024]{1,0:T(8,128)(2,1)S(1)}, u32[]{:S(2)}, u32[]{:S(2)}) collective-permute-start(bf16[256,1024]{1,0:T(8,128)(2,1)S(1)} %get-tuple-element.77), channel_id=1, source_target_pairs={{0,4},{4,0},{8,12},{12,8},{16,20},{20,16},{24,28},{28,24},{1,5},{5... | collective-permute-start | bytes 1572872 | tf_op jit(solution)/shard_map/ppermute | solution.py:31
  72.4 23.0 %collective-permute-start.16 = (bf16[512,512]{1,0:T(8,128)(2,1)S(1)}, bf16[512,512]{1,0:T(8,128)(2,1)S(1)}, u32[]{:S(2)}, u32[]{:S(2)}) collective-permute-start(bf16[512,512]{1,0:T(8,128)(2,1)S(1)} %get-tuple-element.85), channel_id=1, source_target_pairs={{8,0},{12,4},{16,8},{20,12},{24,16},{28,20},{9,1},{13,5},{17,9},{2... | collective-permute-start | bytes 1572872 | tf_op jit(solution)/shard_map/ppermute | solution.py:26
  73.7 19.4 %collective-permute-start.17 = (bf16[512,256]{1,0:T(8,128)(2,1)S(1)}, bf16[512,256]{1,0:T(8,128)(2,1)S(1)}, u32[]{:S(2)}, u32[]{:S(2)}) collective-permute-start(bf16[512,256]{1,0:T(8,128)(2,1)S(1)} %get-tuple-element.88), channel_id=1, source_target_pairs={{8,0},{12,4},{16,8},{20,12},{24,16},{28,20},{9,1},{13,5},{17,9},{2... | collective-permute-start | bytes 786440 | tf_op jit(solution)/shard_map/ppermute | solution.py:26
  75.0 21.3 %collective-permute-start.15 = (bf16[512,256]{1,0:T(8,128)(2,1)S(1)}, bf16[512,256]{1,0:T(8,128)(2,1)S(1)}, u32[]{:S(2)}, u32[]{:S(2)}) collective-permute-start(bf16[512,256]{1,0:T(8,128)(2,1)S(1)} %get-tuple-element.82), channel_id=1, source_target_pairs={{8,0},{12,4},{16,8},{20,12},{24,16},{28,20},{9,1},{13,5},{17,9},{2... | collective-permute-start | bytes 786440 | tf_op jit(solution)/shard_map/ppermute | solution.py:26

commit v4 on v3

--- a/solution.py
+++ b/solution.py
@@ -45,7 +45,7 @@
     return pltpu.with_memory_space_constraint(array, pltpu.HBM)
 
 
-def call(kernel, scalars, ins, outs, work, aliases=None, grid=None, streams=(), blocks=None):
+def call(kernel, scalars, ins, outs, work, aliases=None, grid=None, streams=(), blocks=None, scratch=()):
     smem = pl.BlockSpec(memory_space=pltpu.SMEM)
     vmem = pl.BlockSpec(memory_space=pltpu.VMEM)
     return pl.pallas_call(
@@ -57,6 +57,7 @@
             (jax.ShapeDtypeStruct if blocks else pltpu.VMEM)(shape, dtype)
             for shape, dtype in outs
         ],
+        scratch_shapes=scratch,
         input_output_aliases=aliases or {},
         compiler_params=pltpu.CompilerParams(vmem_limit_bytes=KERNEL_VMEM),
         cost_estimate=pl.CostEstimate(
@@ -89,24 +90,35 @@
 
 
 def grad_kernel(head_ref, *refs):
-    *piece_refs, own_ref, proj_ref, out_ref = refs
-    piece_refs = [own_ref, *piece_refs]
+    *piece_refs, own_hbm, proj_hbm, out_ref, own_ref, proj, sems, own_sem = refs
+    pieces = [own_ref, *piece_refs]
     width = own_ref.shape[1]
-    block = proj_ref.shape[0]
-    total = None
-    for offset, piece in enumerate(piece_refs):
-        start = pl.multiple_of((head_ref[0] ^ offset) * width, width)
-        part = dot(piece[...], proj_ref[:, pl.ds(start, width)], 1, 1)
-        total = part if total is None else total + part
-    at = pl.ds(pl.multiple_of(pl.program_id(0) * block, block), block)
-    out_ref[:, at] = total.astype(out_ref.dtype)
+    count = sems.shape[0]
+    block = proj.shape[0] // count
+    own_copy = pltpu.make_async_copy(own_hbm, own_ref, own_sem)
+    own_copy.start()
+    copies = []
+    for index in range(count):
+        at = pl.ds(index * block, block)
+        copies.append(pltpu.make_async_copy(proj_hbm.at[at], proj.at[at], sems.at[index]))
+        copies[-1].start()
+    own_copy.wait()
+    for index, copy in enumerate(copies):
+        copy.wait()
+        at = slice(index * block, (index + 1) * block)
+        total = None
+        for offset, piece in enumerate(pieces):
+            start = pl.multiple_of((head_ref[0] ^ offset) * width, width)
+            part = dot(piece[...], proj[at, pl.ds(start, width)], 1, 1)
+            total = part if total is None else total + part
+        out_ref[:, at] = total.astype(out_ref.dtype)
 
 
 def attn_grad_of(out_grad, out_proj):
     pieces = gathered_pieces(out_grad)
     rows, width = out_grad.shape
     cols, features = out_proj.shape
-    block = 2 * HDIM
+    count = cols // (2 * HDIM)
     head = lax.axis_index("head").astype(jnp.int32).reshape(1)
     (result,) = call(
         grad_kernel,
@@ -114,10 +126,14 @@
         pieces[1:],
         [((rows, cols), jnp.bfloat16)],
         rows * cols * features,
-        grid=(cols // block,),
         streams=[
-            (in_hbm(out_grad), pl.BlockSpec((rows, width), lambda i: (0, 0))),
-            (in_hbm(out_proj), pl.BlockSpec((block, features), lambda i: (i, 0))),
+            (in_hbm(array), pl.BlockSpec(memory_space=pltpu.HBM)) for array in (out_grad, out_proj)
+        ],
+        scratch=[
+            pltpu.VMEM((rows, width), out_grad.dtype),
+            pltpu.VMEM((cols, features), out_proj.dtype),
+            pltpu.SemaphoreType.DMA((count,)),
+            pltpu.SemaphoreType.DMA,
         ],
     )
     return result
@@ -165,37 +181,59 @@
         return (self.place[0] // self.spans[NEAR]) % 2 == 1
 
 
-def set_stats(head, raw, pgrad, probs, pgrads, stats):
+def soft_set(head, keys, query, probs, stats, diagonal=False):
+    raw = dot(keys, query, 1, 1)
+    if diagonal:
+        raw = causal(raw, -BIG)
     top = jnp.max(raw, axis=0, keepdims=True)
     prob = jnp.exp2((raw - top) * EXP_SCALE)
     probs[head] = prob
+    stats[0, pl.ds(head, 1), :] = top
+    stats[1, pl.ds(head, 1), :] = jnp.sum(prob, axis=0, keepdims=True)
+
+
+def delta_set(head, values, grad, probs, pgrads, stats):
+    pgrad = dot(values, grad, 1, 1)
     pgrads[head] = pgrad
-    norm = jnp.sum(prob, axis=0, keepdims=True)
-    delta = jnp.sum(prob * pgrad, axis=0, keepdims=True)
-    for index, row in enumerate((top, norm, delta)):
-        stats[index, pl.ds(head, 1), :] = row
-
-
-def stats_kernel(diagonal, q, g, k, v, stats, probs, pgrads):
+    stats[2, pl.ds(head, 1), :] = jnp.sum(probs[head] * pgrad, axis=0, keepdims=True)
+
+
+def soft_kernel(
+    spans, t, a, p, q, g, k, v, qf, qn, k_up, *refs,
+):
+    odd = Flags(spans, t, a, p).is_odd()
+    own, mid, far, near, pr_own, pr_mid, pr_far, pr_near, pg_own = refs
+
     def step(head):
         at = columns(head)
-        raw = dot(k[:, at], q[:, at], 1, 1)
-        if diagonal:
-            raw = causal(raw, -BIG)
-        set_stats(head, raw, dot(v[:, at], g[:, at], 1, 1), probs, pgrads, stats)
-
-    each_head(0, probs.shape[0], step)
-
-
-def stats_near_kernel(spans, t, a, p, q, g, k, v, k_up, v_up, stats, probs, pgrads):
-    odd = Flags(spans, t, a, p).is_odd()
+        key_up, key, query = k_up[:, at], k[:, at], q[:, at]
+        soft_set(head, key, query, pr_own, own, True)
+        delta_set(head, v[:, at], g[:, at], pr_own, pg_own, own)
+        soft_set(head, key_up, query, pr_mid, mid)
+        soft_set(head, key_up, qf[:, at], pr_far, far)
+        soft_set(head, jnp.where(odd, key_up, key), qn[:, at], pr_near, near)
+
+    each_head(0, pg_own.shape[0], step)
+
+
+def delta_kernel(g, v_up, probs, soft, stats, pgrads):
+    stats[0:2] = soft[0:2]
 
     def step(head):
         at = columns(head)
-        keys = jnp.where(odd, k_up[:, at], k[:, at])
+        delta_set(head, v_up[:, at], g[:, at], probs, pgrads, stats)
+
+    each_head(0, probs.shape[0], step)
+
+
+def delta_near_kernel(spans, t, a, p, g, v, v_up, probs, soft, stats, pgrads):
+    odd = Flags(spans, t, a, p).is_odd()
+    stats[0:2] = soft[0:2]
+
+    def step(head):
+        at = columns(head)
         values = jnp.where(odd, v_up[:, at], v[:, at])
-        raw = dot(keys, q[:, at], 1, 1)
-        set_stats(head, raw, dot(values, g[:, at], 1, 1), probs, pgrads, stats)
+        delta_set(head, values, g[:, at], probs, pgrads, stats)
 
     each_head(0, probs.shape[0], step)
 
@@ -244,7 +282,7 @@
 
 
 def pairs_kernel(
-    spans, first, t, a, p, qf, gf, qn, gn, k, k_up, norm_far, norm_near,
+    spans, first, t, a, p, qf, gf, qn, gn, k, k_up, _, norm_far, norm_near,
     pr_far, pg_far, pr_near, pg_near, dk_mid, dv_mid, *refs,
 ):
     dqf, dqn, back, dk, dv = refs[-5:]
@@ -330,21 +368,28 @@
     grad_near = swap(grads, "seq", near_span)
     query, key, value = staged(queries, key_rows, value_rows)
 
-    def stats(kernel, scalars, *ins):
-        outs = [stat, square, square]
-        return call(kernel, scalars, ins, outs, heads * 2 * pair_work)
-
-    self_stats, *self_squares = stats(bound(stats_kernel, True), [], query, grads, key, value)
-    mid_stats, *mid_squares = stats(bound(stats_kernel, False), [], query, grads, key_up, value_up)
-    near_stats, *near_squares = stats(
-        bound(stats_near_kernel, spans), flags,
-        query_near, grad_near, key, value, key_up, value_up,
+    self_stats, mid_soft, far_soft, near_soft, *probs, self_pgrad = call(
+        bound(soft_kernel, spans),
+        flags,
+        [query, grads, key, value, query_far, query_near, key_up],
+        [stat] * 4 + [square] * 5,
+        heads * 5 * pair_work,
+    )
+    self_prob, mid_prob, far_prob, near_prob = probs
+
+    def deltas(kernel, scalars, *ins):
+        return call(kernel, scalars, ins, [stat, square], heads * pair_work)
+
+    near_stats, near_pgrad = deltas(
+        bound(delta_near_kernel, spans), flags,
+        grad_near, value, value_up, near_prob, near_soft,
     )
     near_stats = swap(near_stats, "seq", near_span)
-    far_stats, *far_squares = stats(
-        bound(stats_kernel, False), [], query_far, grad_far, key_up, value_up
-    )
+    far_stats, far_pgrad = deltas(delta_kernel, [], grad_far, value_up, far_prob, far_soft)
     far_stats = shift(far_stats, mid_span)
+    mid_stats, mid_pgrad = deltas(delta_kernel, [], grads, value_up, mid_prob, mid_soft)
+    self_squares, mid_squares = (self_prob, self_pgrad), (mid_prob, mid_pgrad)
+    far_squares, near_squares = (far_prob, far_pgrad), (near_prob, near_pgrad)
     self_norm, mid_norm, far_norm, near_norm = call(
         bound(combine_kernel, spans),
         flags,
@@ -360,7 +405,7 @@
         return call(terms_kernel, [], ins, [wide_f32] * 3, heads * 3 * pair_work)
 
     mid_query, *mid_terms = terms(key_up, mid_norm, mid_squares)
-    guests = [query_far, grad_far, query_near, grad_near, key, key_up, far_norm, near_norm]
+    guests = [query_far, grad_far, query_near, grad_near, key, key_up, value_up, far_norm, near_norm]
     guests += [*far_squares, *near_squares, *mid_terms]
     partial_queries, returned = [], []
     first = 0

time: 97.6 us -> 88.3 us (0.905)
  waiting for transfers between devices: 36.1 us -> 23.8 us
  Pallas kernels: 27.7 us -> 30.8 us
    ppermute x10, waiting for transfers between devices: 22.5 us -> 16.3 us  [shift(): lax.ppermute(value, 'seq', [(src, src + steps) for src in range(low, high)])]
    ppermute x8, waiting for transfers between devices: 13.5 us -> 7.51 us  [swap(): return lax.ppermute(value, axis, pairs)]
    pallas_call x15, Pallas kernels: 26.3 us -> 29.4 us  [call(): pl.pallas_call(kernel, grid=grid or (), in_specs=[smem] * len(scalars) +...]
    ppermute x8, starting transfers between devices: 9.89 us -> 8.45 us  [swap(): return lax.ppermute(value, axis, pairs)]
    ppermute x10, starting transfers between devices: 22.5 us -> 23.8 us  [shift(): lax.ppermute(value, 'seq', [(src, src + steps) for src in range(low, high)])]
  transfers between devices with their start and end apart: 18 -> 18, of which waited for: 7 -> 5; matrix products, arithmetic and copies ran while one was open for 0% -> 0% of each run, Pallas kernels for 22% -> 28%
where the time goes in v4:
time: 88.3 us; the launch traced here: 87.8 us
  starting transfers between devices  32.3 us (37%)
  Pallas kernels  30.8 us (35%)
  waiting for transfers between devices  23.8 us (27%)
  between operations  0.89 us (1%)
    pallas_call x15, Pallas kernels, call(): pl.pallas_call(kernel, grid=grid or (), in_specs=[smem] * len(scalars) +...  29.4 us
    ppermute x10, starting transfers between devices, shift(): lax.ppermute(value, 'seq', [(src, src + steps) for src in range(low, high)])  23.8 us
    ppermute x10, waiting for transfers between devices, shift(): lax.ppermute(value, 'seq', [(src, src + steps) for src in range(low, high)])  16.3 us
    ppermute x8, starting transfers between devices, swap(): return lax.ppermute(value, axis, pairs)  8.45 us
    ppermute x8, waiting for transfers between devices, swap(): return lax.ppermute(value, axis, pairs)  7.51 us
  transfers between devices with their start and end apart: 18, of which 5 were waited for; matrix products, arithmetic and copies ran while one was open for 0% of the time, Pallas kernels for 28%

profile of v4, /device:TPU:0, one launch (start us, length us, event | category | flops | bytes accessed | tf_op | source)
XLA Modules:
  0.0 87.8 jit_solution(2676442597062226192)
XLA Ops:
  0.6 3.1 %collective-permute-start.1 = (bf16[256,512]{1,0:T(8,128)(2,1)}, bf16[256,512]{1,0:T(8,128)(2,1)S(1)}, u32[]{:S(2)}, u32[]{:S(2)}) collective-permute-start(bf16[256,512]{1,0:T(8,128)(2,1)} %refs_3_.1), channel_id=1, source_target_pairs={{0,2},{1,3},{2,0},{3,1},{4,6},{5,7},{6,4},{7,5},{8,10},{9,11},{10,... | collective-permute-start | bytes 786440 | tf_op jit(solution)/shard_map/ppermute | solution.py:31
  3.7 3.5 %collective-permute-start.5 = (bf16[256,1024]{1,0:T(8,128)(2,1)}, bf16[256,1024]{1,0:T(8,128)(2,1)S(1)}, u32[]{:S(2)}, u32[]{:S(2)}) collective-permute-start(bf16[256,1024]{1,0:T(8,128)(2,1)} %refs_1_.7), channel_id=1, source_target_pairs={{0,8},{4,12},{8,16},{12,20},{16,24},{20,28},{1,9},{5,13},{9,17},{1... | collective-permute-start | bytes 1572872 | tf_op jit(solution)/shard_map/ppermute | solution.py:26
  7.2 0.1 collective-permute-start
  7.3 2.9 %collective-permute-done.1.refs_1_ = bf16[256,512]{1,0:T(8,128)(2,1)S(1)} collective-permute-done((bf16[256,512]{1,0:T(8,128)(2,1)}, bf16[256,512]{1,0:T(8,128)(2,1)S(1)}, u32[]{:S(2)}, u32[]{:S(2)}) %collective-permute-start.1) | collective-permute-done | bytes 262176 | tf_op jit(solution)/shard_map/ppermute | solution.py:31
  10.2 1.7 %collective-permute-start.4 = (bf16[256,1024]{1,0:T(8,128)(2,1)}, bf16[256,1024]{1,0:T(8,128)(2,1)S(1)}, u32[]{:S(2)}, u32[]{:S(2)}) collective-permute-start(bf16[256,1024]{1,0:T(8,128)(2,1)} %refs_0_.7), channel_id=1, source_target_pairs={{0,4},{4,0},{8,12},{12,8},{16,20},{20,16},{24,28},{28,24},{1,5},{5... | collective-permute-start | bytes 1572872 | tf_op jit(solution)/shard_map/ppermute | solution.py:31
  11.9 1.3 %collective-permute-start.3 = (bf16[256,1024]{1,0:T(8,128)(2,1)}, bf16[256,1024]{1,0:T(8,128)(2,1)S(1)}, u32[]{:S(2)}, u32[]{:S(2)}) collective-permute-start(bf16[256,1024]{1,0:T(8,128)(2,1)} %refs_0_.7), channel_id=1, source_target_pairs={{8,0},{12,4},{16,8},{20,12},{24,16},{28,20},{9,1},{13,5},{17,9},{2... | collective-permute-start | bytes 1572872 | tf_op jit(solution)/shard_map/ppermute | solution.py:26
  13.2 0.0 collective-permute-done.refs_0_
  13.2 4.6 %collective-permute-start.6 = (bf16[256,1024]{1,0:T(8,128)(2,1)}, bf16[256,1024]{1,0:T(8,128)(2,1)S(1)}, u32[]{:S(2)}, u32[]{:S(2)}) collective-permute-start(bf16[256,1024]{1,0:T(8,128)(2,1)} %refs_2_.1), channel_id=1, source_target_pairs={{0,8},{4,12},{8,16},{12,20},{16,24},{20,28},{1,9},{5,13},{9,17},{1... | collective-permute-start | bytes 1572872 | tf_op jit(solution)/shard_map/ppermute | solution.py:26
  17.8 0.0 collective-permute-done.2.refs_2_
  17.8 5.6 %shard_map.94.refs_4_.g = bf16[256,1024]{1,0:T(8,128)(2,1)} custom-call(s32[1]{0:T(128)} %bitcast.head_ref, bf16[256,512]{1,0:T(8,128)(2,1)S(1)} %collective-permute-done.refs_0_, bf16[256,512]{1,0:T(8,128)(2,1)S(1)} %collective-permute-done.1.refs_1_, bf16[256,512]{1,0:T(8,128)(2,1)S(1)} %collective-permute-done.2.refs_2_, bf16[256,512]{1,0:T(8,128)(2,1)} %refs_3_.1, ...), custom_call_target="tpu_custom_call" | custom-call | flops 1073741824 | tf_op jit(solution)/shard_map/pallas_call | solution.py:51
  23.5 0.4 collective-permute-start.9
  23.9 1.3 %collective-permute-start.7 = (bf16[256,1024]{1,0:T(8,128)(2,1)}, bf16[256,1024]{1,0:T(8,128)(2,1)S(1)}, u32[]{:S(2)}, u32[]{:S(2)}) collective-permute-start(bf16[256,1024]{1,0:T(8,128)(2,1)} %shard_map.94.refs_4_.g), channel_id=1, source_target_pairs={{8,0},{12,4},{16,8},{20,12},{24,16},{28,20},{9,1},{13,5},{17,9},{2... | collective-permute-start | bytes 1572872 | tf_op jit(solution)/shard_map/ppermute | solution.py:26
  25.2 0.1 copy.20.refs_0_
  25.3 1.4 %stage.1 = (bf16[256,1024]{1,0:T(8,128)(2,1)S(1)}, bf16[256,1024]{1,0:T(8,128)(2,1)S(1)}, bf16[256,1024]{1,0:T(8,128)(2,1)S(1)}) custom-call(bf16[256,1024]{1,0:T(8,128)(2,1)} %refs_0_.7, bf16[256,1024]{1,0:T(8,128)(2,1)} %refs_1_.7, bf16[256,1024]{1,0:T(8,128)(2,1)} %refs_2_.1), custom_call_target="tpu_custom_call" | custom-call | flops 1000000 | tf_op jit(solution)/shard_map/stage/pallas_call | solution.py:153
  26.7 0.0 collective-permute-done.4.refs_8_.refs_5_
  26.7 1.5 %collective-permute-done.3.refs_7_.refs_3_ = bf16[256,1024]{1,0:T(8,128)(2,1)S(1)} collective-permute-done((bf16[256,1024]{1,0:T(8,128)(2,1)}, bf16[256,1024]{1,0:T(8,128)(2,1)S(1)}, u32[]{:S(2)}, u32[]{:S(2)}) %collective-permute-start.3) | collective-permute-done | bytes 524320 | tf_op jit(solution)/shard_map/ppermute | solution.py:26
  28.1 4.6 %shard_map.95 = (f32[3,8,256]{2,1,0:T(8,128)S(1)}, f32[3,8,256]{2,1,0:T(8,128)S(1)}, f32[3,8,256]{2,1,0:T(8,128)S(1)}, f32[3,8,256]{2,1,0:T(8,128)S(1)}, f32[8,2...) custom-call(s32[8,3]{1,0:T(8,128)S(1)} %copy.20.refs_0_, ...), custom_call_target="tpu_custom_call" | custom-call | flops 671088640 | tf_op jit(solution)/shard_map/pallas_call | solution.py:51
  32.7 0.0 collective-permute-done.6.v_up.refs_5_.refs_9_
  32.7 4.6 %collective-permute-done.9.refs_3_.refs_6_ = bf16[256,1024]{1,0:T(8,128)(2,1)S(1)} collective-permute-done((bf16[256,1024]{1,0:T(8,128)(2,1)}, bf16[256,1024]{1,0:T(8,128)(2,1)S(1)}, u32[]{:S(2)}, u32[]{:S(2)}) %collective-permute-start.9) | collective-permute-done | bytes 524320 | tf_op jit(solution)/shard_map/ppermute | solution.py:31
  37.3 1.8 %shard_map.98 = (f32[3,8,256]{2,1,0:T(8,128)S(1)}, f32[8,256,256]{2,1,0:T(8,128)S(1)}) custom-call(s32[8,3]{1,0:T(8,128)S(1)} %copy.20.refs_0_, s32[1,3]{1,0:T(1,128)S(1)} %copy-done, s32[1]{0:T(128)} %bitcast.1.refs_2_, bf16[256,1024]{1,0:T(8,128)(2,1)S(1)} %collective-permute-done.9.refs_3_.refs_6_, ...), custom_call_target="tpu_custom_call" | custom-call | flops 134217728 | tf_op jit(solution)/shard_map/pallas_call | solution.py:51
  39.1 0.5 collective-permute-start.10
  39.6 0.0 collective-permute-done.7.g.refs_4_
  39.6 1.0 %shard_map.97 = (f32[3,8,256]{2,1,0:T(8,128)S(1)}, f32[8,256,256]{2,1,0:T(8,128)S(1)}) custom-call(bf16[256,1024]{1,0:T(8,128)(2,1)S(1)} %collective-permute-done.7.g.refs_4_, bf16[256,1024]{1,0:T(8,128)(2,1)S(1)} %collective-permute-done.6.v_up.refs_5_.refs_9_, f32[8,256,256]{2,1,0:T(8,128)S(1)} %get-tuple-element.59.probs.refs_12_, ...), custom_call_target="tpu_custom_call" | custom-call | flops 134217728 | tf_op jit(solution)/shard_map/pallas_call | solution.py:51
  40.6 3.5 %collective-permute-start.8 = (f32[3,8,256]{2,1,0:T(8,128)S(1)}, f32[3,8,256]{2,1,0:T(8,128)S(1)}, u32[]{:S(2)}, u32[]{:S(2)}) collective-permute-start(f32[3,8,256]{2,1,0:T(8,128)S(1)} %get-tuple-element.61), channel_id=1, source_target_pairs={{0,8},{4,12},{8,16},{12,20},{16,24},{20,28},{1,9},{5,13},{9,17},{1... | collective-permute-start | bytes 73736 | tf_op jit(solution)/shard_map/ppermute | solution.py:26
  44.1 2.0 %shard_map.96 = (f32[3,8,256]{2,1,0:T(8,128)S(1)}, f32[8,256,256]{2,1,0:T(8,128)S(1)}) custom-call(bf16[256,1024]{1,0:T(8,128)(2,1)} %shard_map.94.refs_4_.g, bf16[256,1024]{1,0:T(8,128)(2,1)S(1)} %collective-permute-done.6.v_up.refs_5_.refs_9_, f32[8,256,256]{2,1,0:T(8,128)S(1)} %get-tuple-element.56.probs, f32[3,8,256]{2,1,0:T(8,128)S(1)} %get-tuple-element.57.soft), custom_call_target="tpu_custom_call" | custom-call | flops 134217728 | tf_op jit(solution)/shard_map/pallas_call | solution.py:51
  46.2 0.0 collective-permute-done.8.refs_5_
  46.2 0.7 shard_map.99
  46.9 1.3 %collective-permute-start.11 = (f32[2,8,256]{2,1,0:T(8,128)S(1)}, f32[2,8,256]{2,1,0:T(8,128)S(1)}, u32[]{:S(2)}, u32[]{:S(2)}) collective-permute-start(f32[2,8,256]{2,1,0:T(8,128)S(1)} %get-tuple-element.72), channel_id=1, source_target_pairs={{8,0},{12,4},{16,8},{20,12},{24,16},{28,20},{9,1},{13,5},{17,9},{2... | collective-permute-start | bytes 49160 | tf_op jit(solution)/shard_map/ppermute | solution.py:26
  48.2 1.6 %collective-permute-start.12 = (f32[2,8,256]{2,1,0:T(8,128)S(1)}, f32[2,8,256]{2,1,0:T(8,128)S(1)}, u32[]{:S(2)}, u32[]{:S(2)}) collective-permute-start(f32[2,8,256]{2,1,0:T(8,128)S(1)} %get-tuple-element.73), channel_id=1, source_target_pairs={{0,4},{4,0},{8,12},{12,8},{16,20},{20,16},{24,28},{28,24},{1,5},{5... | collective-permute-start | bytes 49160 | tf_op jit(solution)/shard_map/ppermute | solution.py:31
  49.8 2.6 %shard_map.100 = (f32[256,1024]{1,0:T(8,128)S(1)}, f32[256,1024]{1,0:T(8,128)S(1)}, f32[256,1024]{1,0:T(8,128)S(1)}) custom-call(bf16[256,1024]{1,0:T(8,128)(2,1)S(1)} %get-tuple-element.52.refs_3_.q, bf16[256,1024]{1,0:T(8,128)(2,1)} %shard_map.94.refs_4_.g, bf16[256,1024]{1,0:T(8,128)(2,1)S(1)} %collective-permute-done.5.refs_9_.k.refs_8_, ...), custom_call_target="tpu_custom_call" | custom-call | flops 402653184 | tf_op jit(solution)/shard_map/pallas_call | solution.py:51
  52.4 0.2 collective-permute-done.11.refs_10_
  52.5 1.2 %shard_map.102 = (bf16[256,1024]{1,0:T(8,128)(2,1)S(1)}, bf16[256,1024]{1,0:T(8,128)(2,1)S(1)}, bf16[512,256]{1,0:T(8,128)(2,1)S(1)}, f32[256,256]{1,0:T(8,128)S(1)}, f32[256,256]{1,0:T(8,128)S(1)}) custom-call(s32[8,3]{1,0:T(8,128)S(1)} %copy.20.refs_0_, s32[1,3]{1,0:T(1,128)S(1)} %copy-done, s32[1]{0:T(128)} %bitcast.1.refs_2_, ...), custom_call_target="tpu_custom_call" | custom-call | flops 201326592 | tf_op jit(solution)/shard_map/pallas_call | solution.py:51
  53.8 2.0 %shard_map.103 = (bf16[256,1024]{1,0:T(8,128)(2,1)S(1)}, bf16[256,1024]{1,0:T(8,128)(2,1)S(1)}, bf16[512,512]{1,0:T(8,128)(2,1)S(1)}, f32[256,512]{1,0:T(8,128)S(1)}, f32[256,512]{1,0:T(8,128)S(1)}) custom-call(s32[8,3]{1,0:T(8,128)S(1)} %copy.20.refs_0_, s32[1,3]{1,0:T(1,128)S(1)} %copy-done, ...), custom_call_target="tpu_custom_call", output_to_operand_aliasing={{0}: (18, {}), {1}: (19, {})} | custom-call | flops 402653184 | tf_op jit(solution)/shard_map/pallas_call | solution.py:51
  55.8 1.2 %shard_map.104 = (bf16[256,1024]{1,0:T(8,128)(2,1)S(1)}, bf16[256,1024]{1,0:T(8,128)(2,1)S(1)}, bf16[512,256]{1,0:T(8,128)(2,1)S(1)}, f32[256,256]{1,0:T(8,128)S(1)}, f32[256,256]{1,0:T(8,128)S(1)}) custom-call(s32[8,3]{1,0:T(8,128)S(1)} %copy.20.refs_0_, s32[1,3]{1,0:T(1,128)S(1)} %copy-done, ...), custom_call_target="tpu_custom_call", output_to_operand_aliasing={{0}: (18, {}), {1}: (19, {})} | custom-call | flops 201326592 | tf_op jit(solution)/shard_map/pallas_call | solution.py:51
  57.0 4.5 %collective-permute-start.13 = (bf16[256,1024]{1,0:T(8,128)(2,1)S(1)}, bf16[256,1024]{1,0:T(8,128)(2,1)S(1)}, u32[]{:S(2)}, u32[]{:S(2)}) collective-permute-start(bf16[256,1024]{1,0:T(8,128)(2,1)S(1)} %get-tuple-element.82), channel_id=1, source_target_pairs={{0,8},{4,12},{8,16},{12,20},{16,24},{20,28},{1,9},{5,13},{9,17},{1... | collective-permute-start | bytes 1572872 | tf_op jit(solution)/shard_map/ppermute | solution.py:26
  61.5 1.2 %collective-permute-start.14 = (bf16[256,1024]{1,0:T(8,128)(2,1)S(1)}, bf16[256,1024]{1,0:T(8,128)(2,1)S(1)}, u32[]{:S(2)}, u32[]{:S(2)}) collective-permute-start(bf16[256,1024]{1,0:T(8,128)(2,1)S(1)} %get-tuple-element.83), channel_id=1, source_target_pairs={{0,4},{4,0},{8,12},{12,8},{16,20},{20,16},{24,28},{28,24},{1,5},{5... | collective-permute-start | bytes 1572872 | tf_op jit(solution)/shard_map/ppermute | solution.py:31
  62.6 1.3 %collective-permute-start.16 = (bf16[512,512]{1,0:T(8,128)(2,1)S(1)}, bf16[512,512]{1,0:T(8,128)(2,1)S(1)}, u32[]{:S(2)}, u32[]{:S(2)}) collective-permute-start(bf16[512,512]{1,0:T(8,128)(2,1)S(1)} %get-tuple-element.91), channel_id=1, source_target_pairs={{8,0},{12,4},{16,8},{20,12},{24,16},{28,20},{9,1},{13,5},{17,9},{2... | collective-permute-start | bytes 1572872 | tf_op jit(solution)/shard_map/ppermute | solution.py:26
  63.9 1.3 %collective-permute-start.17 = (bf16[512,256]{1,0:T(8,128)(2,1)S(1)}, bf16[512,256]{1,0:T(8,128)(2,1)S(1)}, u32[]{:S(2)}, u32[]{:S(2)}) collective-permute-start(bf16[512,256]{1,0:T(8,128)(2,1)S(1)} %get-tuple-element.94), channel_id=1, source_target_pairs={{8,0},{12,4},{16,8},{20,12},{24,16},{28,20},{9,1},{13,5},{17,9},{2... | collective-permute-start | bytes 786440 | tf_op jit(solution)/shard_map/ppermute | solution.py:26
  65.2 1.3 %collective-permute-start.15 = (bf16[512,256]{1,0:T(8,128)(2,1)S(1)}, bf16[512,256]{1,0:T(8,128)(2,1)S(1)}, u32[]{:S(2)}, u32[]{:S(2)}) collective-permute-start(bf16[512,256]{1,0:T(8,128)(2,1)S(1)} %get-tuple-element.88), channel_id=1, source_target_pairs={{8,0},{12,4},{16,8},{20,12},{24,16},{28,20},{9,1},{13,5},{17,9},{2... | collective-permute-start | bytes 786440 | tf_op jit(solution)/shard_map/ppermute | solution.py:26
  66.5 2.6 %shard_map.101 = (f32[256,1024]{1,0:T(8,128)S(1)}, f32[256,1024]{1,0:T(8,128)S(1)}, f32[256,1024]{1,0:T(8,128)S(1)}) custom-call(bf16[256,1024]{1,0:T(8,128)(2,1)S(1)} %get-tuple-element.52.refs_3_.q, bf16[256,1024]{1,0:T(8,128)(2,1)} %shard_map.94.refs_4_.g, bf16[256,1024]{1,0:T(8,128)(2,1)S(1)} %get-tuple-element.53.refs_5_.k.refs_7_, ...), custom_call_target="tpu_custom_call" | custom-call | flops 402653184 | tf_op jit(solution)/shard_map/pallas_call | solution.py:51
  69.1 14.6 %collective-permute-done.17.refs_4_ = bf16[512,256]{1,0:T(8,128)(2,1)S(1)} collective-permute-done((bf16[512,256]{1,0:T(8,128)(2,1)S(1)}, bf16[512,256]{1,0:T(8,128)(2,1)S(1)}, u32[]{:S(2)}, u32[]{:S(2)}) %collective-permute-start.17) | collective-permute-done | bytes 262176 | tf_op jit(solution)/shard_map/ppermute | solution.py:26
  83.8 0.8 shard_map.106
  84.5 0.0 collective-permute-done.13.far
  84.5 0.0 collective-permute-done.14.near
  84.5 1.5 %shard_map.105 = bf16[256,1024]{1,0:T(8,128)(2,1)} custom-call(f32[256,1024]{1,0:T(8,128)S(1)} %get-tuple-element.71.dq, bf16[256,1024]{1,0:T(8,128)(2,1)S(1)} %collective-permute-done.13.far, bf16[256,1024]{1,0:T(8,128)(2,1)S(1)} %collective-permute-done.14.near), custom_call_target="tpu_custom_call" | custom-call | flops 524288 | tf_op jit(solution)/shard_map/pallas_call | solution.py:51
  86.1 0.9 %shard_map.107 = (bf16[256,1024]{1,0:T(8,128)(2,1)}, bf16[256,1024]{1,0:T(8,128)(2,1)}) custom-call(f32[256,1024]{1,0:T(8,128)S(1)} %get-tuple-element.84.refs_0_, f32[256,1024]{1,0:T(8,128)S(1)} %get-tuple-element.85.refs_1_, f32[256,512]{1,0:T(8,128)S(1)} %get-tuple-element.89.refs_2_, ...), custom_call_target="tpu_custom_call", output_to_operand_aliasing={{0}: (5, {}), {1}: (6, {})} | custom-call | flops 33554432 | tf_op jit(solution)/shard_map/pallas_call | solution.py:51
  87.0 0.0 collective-permute-done.15.refs_4_
  87.0 0.8 shard_map.108
  (9 shorter events, 0.0 us)
Async XLA Ops:
  0.6 9.6 %collective-permute-start.1 = (bf16[256,512]{1,0:T(8,128)(2,1)}, bf16[256,512]{1,0:T(8,128)(2,1)S(1)}, u32[]{:S(2)}, u32[]{:S(2)}) collective-permute-start(bf16[256,512]{1,0:T(8,128)(2,1)} %refs_3_.1), channel_id=1, source_target_pairs={{0,2},{1,3},{2,0},{3,1},{4,6},{5,7},{6,4},{7,5},{8,10},{9,11},{10,... | collective-permute-start | bytes 786440 | tf_op jit(solution)/shard_map/ppermute | solution.py:31
  3.7 20.2 %collective-permute-start.5 = (bf16[256,1024]{1,0:T(8,128)(2,1)}, bf16[256,1024]{1,0:T(8,128)(2,1)S(1)}, u32[]{:S(2)}, u32[]{:S(2)}) collective-permute-start(bf16[256,1024]{1,0:T(8,128)(2,1)} %refs_1_.7), channel_id=1, source_target_pairs={{0,8},{4,12},{8,16},{12,20},{16,24},{20,28},{1,9},{5,13},{9,17},{1... | collective-permute-start | bytes 1572872 | tf_op jit(solution)/shard_map/ppermute | solution.py:26
  7.2 6.0 %collective-permute-start = (bf16[256,512]{1,0:T(8,128)(2,1)}, bf16[256,512]{1,0:T(8,128)(2,1)S(1)}, u32[]{:S(2)}, u32[]{:S(2)}) collective-permute-start(bf16[256,512]{1,0:T(8,128)(2,1)} %refs_3_.1), channel_id=1, source_target_pairs={{0,1},{1,0},{2,3},{3,2},{4,5},{5,4},{6,7},{7,6},{8,9},{9,8},{10,11... | collective-permute-start | bytes 786440 | tf_op jit(solution)/shard_map/ppermute | solution.py:31
  10.2 7.6 %collective-permute-start.2 = (bf16[256,512]{1,0:T(8,128)(2,1)S(1)}, bf16[256,512]{1,0:T(8,128)(2,1)S(1)}, u32[]{:S(2)}, u32[]{:S(2)}) collective-permute-start(bf16[256,512]{1,0:T(8,128)(2,1)S(1)} %collective-permute-done.1.refs_1_), channel_id=1, source_target_pairs={{0,1},{1,0},{2,3},{3,2},{4,5},{5,4},{6,7},{7,6},{8,9},{9,8},{10,11... | collective-permute-start | bytes 786440 | tf_op jit(solution)/shard_map/ppermute | solution.py:31
  10.2 16.4 %collective-permute-start.4 = (bf16[256,1024]{1,0:T(8,128)(2,1)}, bf16[256,1024]{1,0:T(8,128)(2,1)S(1)}, u32[]{:S(2)}, u32[]{:S(2)}) collective-permute-start(bf16[256,1024]{1,0:T(8,128)(2,1)} %refs_0_.7), channel_id=1, source_target_pairs={{0,4},{4,0},{8,12},{12,8},{16,20},{20,16},{24,28},{28,24},{1,5},{5... | collective-permute-start | bytes 1572872 | tf_op jit(solution)/shard_map/ppermute | solution.py:31
  11.9 16.2 %collective-permute-start.3 = (bf16[256,1024]{1,0:T(8,128)(2,1)}, bf16[256,1024]{1,0:T(8,128)(2,1)S(1)}, u32[]{:S(2)}, u32[]{:S(2)}) collective-permute-start(bf16[256,1024]{1,0:T(8,128)(2,1)} %refs_0_.7), channel_id=1, source_target_pairs={{8,0},{12,4},{16,8},{20,12},{24,16},{28,20},{9,1},{13,5},{17,9},{2... | collective-permute-start | bytes 1572872 | tf_op jit(solution)/shard_map/ppermute | solution.py:26
  13.2 19.5 %collective-permute-start.6 = (bf16[256,1024]{1,0:T(8,128)(2,1)}, bf16[256,1024]{1,0:T(8,128)(2,1)S(1)}, u32[]{:S(2)}, u32[]{:S(2)}) collective-permute-start(bf16[256,1024]{1,0:T(8,128)(2,1)} %refs_2_.1), channel_id=1, source_target_pairs={{0,8},{4,12},{8,16},{12,20},{16,24},{20,28},{1,9},{5,13},{9,17},{1... | collective-permute-start | bytes 1572872 | tf_op jit(solution)/shard_map/ppermute | solution.py:26
  17.8 7.3 %copy-start.1 = (s32[8,3]{0,1:T(4,128)S(1)}, s32[8,3]{0,1:T(4,128)}, u32[]{:S(2)}) copy-start(s32[8,3]{0,1:T(4,128)} %param.12) | copy-start | bytes 292
  17.8 10.3 %copy-start = (s32[1,3]{1,0:T(1,128)S(1)}, s32[1,3]{1,0:T(1,128)}, u32[]{:S(2)}) copy-start(s32[1,3]{1,0:T(1,128)} %refs_1_.13) | copy-start | bytes 40
  23.5 13.8 %collective-permute-start.9 = (bf16[256,1024]{1,0:T(8,128)(2,1)}, bf16[256,1024]{1,0:T(8,128)(2,1)S(1)}, u32[]{:S(2)}, u32[]{:S(2)}) collective-permute-start(bf16[256,1024]{1,0:T(8,128)(2,1)} %shard_map.94.refs_4_.g), channel_id=1, source_target_pairs={{0,4},{4,0},{8,12},{12,8},{16,20},{20,16},{24,28},{28,24},{1,5},{5... | collective-permute-start | bytes 1572872 | tf_op jit(solution)/shard_map/ppermute | solution.py:31
  23.9 15.7 %collective-permute-start.7 = (bf16[256,1024]{1,0:T(8,128)(2,1)}, bf16[256,1024]{1,0:T(8,128)(2,1)S(1)}, u32[]{:S(2)}, u32[]{:S(2)}) collective-permute-start(bf16[256,1024]{1,0:T(8,128)(2,1)} %shard_map.94.refs_4_.g), channel_id=1, source_target_pairs={{8,0},{12,4},{16,8},{20,12},{24,16},{28,20},{9,1},{13,5},{17,9},{2... | collective-permute-start | bytes 1572872 | tf_op jit(solution)/shard_map/ppermute | solution.py:26
  39.1 7.1 %collective-permute-start.10 = (f32[3,8,256]{2,1,0:T(8,128)S(1)}, f32[3,8,256]{2,1,0:T(8,128)S(1)}, u32[]{:S(2)}, u32[]{:S(2)}) collective-permute-start(f32[3,8,256]{2,1,0:T(8,128)S(1)} %get-tuple-element.64), channel_id=1, source_target_pairs={{0,4},{4,0},{8,12},{12,8},{16,20},{20,16},{24,28},{28,24},{1,5},{5... | collective-permute-start | bytes 73736 | tf_op jit(solution)/shard_map/ppermute | solution.py:31
  40.6 5.6 %collective-permute-start.8 = (f32[3,8,256]{2,1,0:T(8,128)S(1)}, f32[3,8,256]{2,1,0:T(8,128)S(1)}, u32[]{:S(2)}, u32[]{:S(2)}) collective-permute-start(f32[3,8,256]{2,1,0:T(8,128)S(1)} %get-tuple-element.61), channel_id=1, source_target_pairs={{0,8},{4,12},{8,16},{12,20},{16,24},{20,28},{1,9},{5,13},{9,17},{1... | collective-permute-start | bytes 73736 | tf_op jit(solution)/shard_map/ppermute | solution.py:26
  46.9 5.6 %collective-permute-start.11 = (f32[2,8,256]{2,1,0:T(8,128)S(1)}, f32[2,8,256]{2,1,0:T(8,128)S(1)}, u32[]{:S(2)}, u32[]{:S(2)}) collective-permute-start(f32[2,8,256]{2,1,0:T(8,128)S(1)} %get-tuple-element.72), channel_id=1, source_target_pairs={{8,0},{12,4},{16,8},{20,12},{24,16},{28,20},{9,1},{13,5},{17,9},{2... | collective-permute-start | bytes 49160 | tf_op jit(solution)/shard_map/ppermute | solution.py:26
  48.2 4.3 %collective-permute-start.12 = (f32[2,8,256]{2,1,0:T(8,128)S(1)}, f32[2,8,256]{2,1,0:T(8,128)S(1)}, u32[]{:S(2)}, u32[]{:S(2)}) collective-permute-start(f32[2,8,256]{2,1,0:T(8,128)S(1)} %get-tuple-element.73), channel_id=1, source_target_pairs={{0,4},{4,0},{8,12},{12,8},{16,20},{20,16},{24,28},{28,24},{1,5},{5... | collective-permute-start | bytes 49160 | tf_op jit(solution)/shard_map/ppermute | solution.py:31
  57.0 27.5 %collective-permute-start.13 = (bf16[256,1024]{1,0:T(8,128)(2,1)S(1)}, bf16[256,1024]{1,0:T(8,128)(2,1)S(1)}, u32[]{:S(2)}, u32[]{:S(2)}) collective-permute-start(bf16[256,1024]{1,0:T(8,128)(2,1)S(1)} %get-tuple-element.82), channel_id=1, source_target_pairs={{0,8},{4,12},{8,16},{12,20},{16,24},{20,28},{1,9},{5,13},{9,17},{1... | collective-permute-start | bytes 1572872 | tf_op jit(solution)/shard_map/ppermute | solution.py:26
  61.5 23.1 %collective-permute-start.14 = (bf16[256,1024]{1,0:T(8,128)(2,1)S(1)}, bf16[256,1024]{1,0:T(8,128)(2,1)S(1)}, u32[]{:S(2)}, u32[]{:S(2)}) collective-permute-start(bf16[256,1024]{1,0:T(8,128)(2,1)S(1)} %get-tuple-element.83), channel_id=1, source_target_pairs={{0,4},{4,0},{8,12},{12,8},{16,20},{20,16},{24,28},{28,24},{1,5},{5... | collective-permute-start | bytes 1572872 | tf_op jit(solution)/shard_map/ppermute | solution.py:31
  62.6 23.4 %collective-permute-start.16 = (bf16[512,512]{1,0:T(8,128)(2,1)S(1)}, bf16[512,512]{1,0:T(8,128)(2,1)S(1)}, u32[]{:S(2)}, u32[]{:S(2)}) collective-permute-start(bf16[512,512]{1,0:T(8,128)(2,1)S(1)} %get-tuple-element.91), channel_id=1, source_target_pairs={{8,0},{12,4},{16,8},{20,12},{24,16},{28,20},{9,1},{13,5},{17,9},{2... | collective-permute-start | bytes 1572872 | tf_op jit(solution)/shard_map/ppermute | solution.py:26
  63.9 19.8 %collective-permute-start.17 = (bf16[512,256]{1,0:T(8,128)(2,1)S(1)}, bf16[512,256]{1,0:T(8,128)(2,1)S(1)}, u32[]{:S(2)}, u32[]{:S(2)}) collective-permute-start(bf16[512,256]{1,0:T(8,128)(2,1)S(1)} %get-tuple-element.94), channel_id=1, source_target_pairs={{8,0},{12,4},{16,8},{20,12},{24,16},{28,20},{9,1},{13,5},{17,9},{2... | collective-permute-start | bytes 786440 | tf_op jit(solution)/shard_map/ppermute | solution.py:26
  65.2 21.8 %collective-permute-start.15 = (bf16[512,256]{1,0:T(8,128)(2,1)S(1)}, bf16[512,256]{1,0:T(8,128)(2,1)S(1)}, u32[]{:S(2)}, u32[]{:S(2)}) collective-permute-start(bf16[512,256]{1,0:T(8,128)(2,1)S(1)} %get-tuple-element.88), channel_id=1, source_target_pairs={{8,0},{12,4},{16,8},{20,12},{24,16},{28,20},{9,1},{13,5},{17,9},{2... | collective-permute-start | bytes 786440 | tf_op jit(solution)/shard_map/ppermute | solution.py:26

commit v5 on v4

--- a/solution.py
+++ b/solution.py
@@ -89,7 +89,8 @@
     return [pieces[offset] for offset in range(len(pieces))]
 
 
-def grad_kernel(head_ref, *refs):
+def grad_kernel(*refs):
+    head = lax.axis_index("head")
     *piece_refs, own_hbm, proj_hbm, out_ref, own_ref, proj, sems, own_sem = refs
     pieces = [own_ref, *piece_refs]
     width = own_ref.shape[1]
@@ -108,7 +109,7 @@
         at = slice(index * block, (index + 1) * block)
         total = None
         for offset, piece in enumerate(pieces):
-            start = pl.multiple_of((head_ref[0] ^ offset) * width, width)
+            start = pl.multiple_of((head ^ offset) * width, width)
             part = dot(piece[...], proj[at, pl.ds(start, width)], 1, 1)
             total = part if total is None else total + part
         out_ref[:, at] = total.astype(out_ref.dtype)
@@ -119,10 +120,9 @@
     rows, width = out_grad.shape
     cols, features = out_proj.shape
     count = cols // (2 * HDIM)
-    head = lax.axis_index("head").astype(jnp.int32).reshape(1)
     (result,) = call(
         grad_kernel,
-        [head],
+        [],
         pieces[1:],
         [((rows, cols), jnp.bfloat16)],
         rows * cols * features,
@@ -169,16 +169,19 @@
 
 
 class Flags:
-    def __init__(self, spans, table_ref, active_ref, place_ref):
-        self.spans, self.table = spans, table_ref
-        self.active, self.place = active_ref, place_ref
+    def __init__(self, spans, table_ref, active_ref):
+        self.spans, self.table, self.active = spans, table_ref, active_ref
+        self.place = lax.axis_index("seq")
 
     def usable(self, head, section):
-        used = self.table[head, section] * self.active[0, section] > 0
-        return used & (self.place[0] >= self.spans[section])
-
-    def is_odd(self):
-        return (self.place[0] // self.spans[NEAR]) % 2 == 1
+        used = self.table[section, head] * self.active[0, section] > 0
+        return used & (self.place >= self.spans[section])
+
+
+def by_parity(near_span, run):
+    odd = (lax.axis_index("seq") // near_span) % 2 == 1
+    pl.when(odd)(lambda: run(True))
+    pl.when(jnp.logical_not(odd))(lambda: run(False))
 
 
 def soft_set(head, keys, query, probs, stats, diagonal=False):
@@ -198,22 +201,22 @@
     stats[2, pl.ds(head, 1), :] = jnp.sum(probs[head] * pgrad, axis=0, keepdims=True)
 
 
-def soft_kernel(
-    spans, t, a, p, q, g, k, v, qf, qn, k_up, *refs,
-):
-    odd = Flags(spans, t, a, p).is_odd()
+def soft_kernel(near_span, q, g, k, v, qf, qn, k_up, *refs):
     own, mid, far, near, pr_own, pr_mid, pr_far, pr_near, pg_own = refs
 
-    def step(head):
-        at = columns(head)
-        key_up, key, query = k_up[:, at], k[:, at], q[:, at]
-        soft_set(head, key, query, pr_own, own, True)
-        delta_set(head, v[:, at], g[:, at], pr_own, pg_own, own)
-        soft_set(head, key_up, query, pr_mid, mid)
-        soft_set(head, key_up, qf[:, at], pr_far, far)
-        soft_set(head, jnp.where(odd, key_up, key), qn[:, at], pr_near, near)
-
-    each_head(0, pg_own.shape[0], step)
+    def run(odd):
+        def step(head):
+            at = columns(head)
+            key_up, key, query = k_up[:, at], k[:, at], q[:, at]
+            soft_set(head, key, query, pr_own, own, True)
+            delta_set(head, v[:, at], g[:, at], pr_own, pg_own, own)
+            soft_set(head, key_up, query, pr_mid, mid)
+            soft_set(head, key_up, qf[:, at], pr_far, far)
+            soft_set(head, key_up if odd else key, qn[:, at], pr_near, near)
+
+        each_head(0, pg_own.shape[0], step)
+
+    by_parity(near_span, run)
 
 
 def delta_kernel(g, v_up, probs, soft, stats, pgrads):
@@ -226,20 +229,12 @@
     each_head(0, probs.shape[0], step)
 
 
-def delta_near_kernel(spans, t, a, p, g, v, v_up, probs, soft, stats, pgrads):
-    odd = Flags(spans, t, a, p).is_odd()
-    stats[0:2] = soft[0:2]
-
-    def step(head):
-        at = columns(head)
-        values = jnp.where(odd, v_up[:, at], v[:, at])
-        delta_set(head, values, g[:, at], probs, pgrads, stats)
-
-    each_head(0, probs.shape[0], step)
-
-
-def combine_kernel(spans, t, a, p, *refs):
-    flags = Flags(spans, t, a, p)
+def delta_near_kernel(near_span, g, v, v_up, *refs):
+    by_parity(near_span, lambda odd: delta_kernel(g, v_up if odd else v, *refs))
+
+
+def combine_kernel(spans, t, a, *refs):
+    flags = Flags(spans, t, a)
     ins, outs = refs[:4], refs[4:]
     for head in range(ins[0].shape[1]):
         at = slice(head, head + 1)
@@ -282,34 +277,37 @@
 
 
 def pairs_kernel(
-    spans, first, t, a, p, qf, gf, qn, gn, k, k_up, _, norm_far, norm_near,
+    near_span, first, qf, gf, qn, gn, k, k_up, norm_far, norm_near,
     pr_far, pg_far, pr_near, pg_near, dk_mid, dv_mid, *refs,
 ):
     dqf, dqn, back, dk, dv = refs[-5:]
-    odd = Flags(spans, t, a, p).is_odd()
     rows = qf.shape[0]
 
-    def step(head):
-        at, out = columns(head), columns(head - first)
-        key_up = k_up[:, at]
-        dq, key_far, value_far = pair_terms(
-            head, qf[:, at], gf[:, at], key_up, pr_far, pg_far, norm_far
-        )
-        dqf[:, at] = (dq * SCALE).T.astype(dqf.dtype)
-        key_near = jnp.where(odd, key_up, k[:, at])
-        dq, key_term, value_term = pair_terms(
-            head, qn[:, at], gn[:, at], key_near, pr_near, pg_near, norm_near
-        )
-        dqn[:, at] = (dq * SCALE).T.astype(dqn.dtype)
-        zero = jnp.zeros_like(key_term)
-        key_back = dk_mid[:, at] + key_far + jnp.where(odd, key_term, zero)
-        value_back = dv_mid[:, at] + value_far + jnp.where(odd, value_term, zero)
-        back[:rows, out] = (key_back * SCALE).astype(back.dtype)
-        back[rows:, out] = value_back.astype(back.dtype)
-        dk[:, out] = jnp.where(odd, zero, key_term)
-        dv[:, out] = jnp.where(odd, zero, value_term)
-
-    each_head(first, dk.shape[1] // HDIM, step)
+    def run(odd):
+        def step(head):
+            at, out = columns(head), columns(head - first)
+            key_up = k_up[:, at]
+            dq, key_back, value_back = pair_terms(
+                head, qf[:, at], gf[:, at], key_up, pr_far, pg_far, norm_far
+            )
+            dqf[:, at] = (dq * SCALE).T.astype(dqf.dtype)
+            key_near = key_up if odd else k[:, at]
+            dq, key_term, value_term = pair_terms(
+                head, qn[:, at], gn[:, at], key_near, pr_near, pg_near, norm_near
+            )
+            dqn[:, at] = (dq * SCALE).T.astype(dqn.dtype)
+            key_back, value_back = dk_mid[:, at] + key_back, dv_mid[:, at] + value_back
+            if odd:
+                key_back, value_back = key_back + key_term, value_back + value_term
+                key_term, value_term = jnp.zeros_like(key_term), jnp.zeros_like(value_term)
+            back[:rows, out] = (key_back * SCALE).astype(back.dtype)
+            back[rows:, out] = value_back.astype(back.dtype)
+            dk[:, out] = key_term
+            dv[:, out] = value_term
+
+        each_head(first, dk.shape[1] // HDIM, step)
+
+    by_parity(near_span, run)
 
 
 def step_columns(block, first=0):
@@ -336,7 +334,6 @@
 
 def body(queries, key_rows, value_rows, out_grad, out_proj, section_table, block_active):
     seq_count = lax.axis_size("seq")
-    place = lax.axis_index("seq")
     spans = [seq_count // 2 ** (index + 1) for index in range(SECTIONS)]
     mid_span, near_span = spans[MID], spans[NEAR]
     assert spans[FAR] == 2 * mid_span and mid_span == 2 * near_span
@@ -345,7 +342,7 @@
     heads = cols // HDIM
     assert heads == sum(GROUPS)
     pair_work = rows * rows * HDIM
-    flags = [section_table, block_active, place.astype(jnp.int32).reshape(1)]
+    flags = [section_table.T, block_active]
 
     wide_f32 = ((rows, cols), jnp.float32)
     wide_bf16 = ((rows, cols), jnp.bfloat16)
@@ -369,8 +366,8 @@
     query, key, value = staged(queries, key_rows, value_rows)
 
     self_stats, mid_soft, far_soft, near_soft, *probs, self_pgrad = call(
-        bound(soft_kernel, spans),
-        flags,
+        bound(soft_kernel, near_span),
+        [],
         [query, grads, key, value, query_far, query_near, key_up],
         [stat] * 4 + [square] * 5,
         heads * 5 * pair_work,
@@ -381,7 +378,7 @@
         return call(kernel, scalars, ins, [stat, square], heads * pair_work)
 
     near_stats, near_pgrad = deltas(
-        bound(delta_near_kernel, spans), flags,
+        bound(delta_near_kernel, near_span), [],
         grad_near, value, value_up, near_prob, near_soft,
     )
     near_stats = swap(near_stats, "seq", near_span)
@@ -405,17 +402,17 @@
         return call(terms_kernel, [], ins, [wide_f32] * 3, heads * 3 * pair_work)
 
     mid_query, *mid_terms = terms(key_up, mid_norm, mid_squares)
-    guests = [query_far, grad_far, query_near, grad_near, key, key_up, value_up, far_norm, near_norm]
+    guests = [query_far, grad_far, query_near, grad_near, key, key_up, far_norm, near_norm]
     guests += [*far_squares, *near_squares, *mid_terms]
     partial_queries, returned = [], []
     first = 0
     for group in GROUPS:
         width = group * HDIM
-        start = len(flags) + len(guests)
+        start = len(guests)
         aliases = {start + number: number for number in range(len(partial_queries))}
         *partial_queries, back, near_key, near_value = call(
-            bound(pairs_kernel, spans, first),
-            flags,
+            bound(pairs_kernel, near_span, first),
+            [],
             guests + partial_queries,
             [wide_bf16] * 2 + [((2 * rows, width), jnp.bfloat16)]
             + [((rows, width), jnp.float32)] * 2,

time: 88.3 us -> 84.4 us (0.956)
  Pallas kernels: 30.8 us -> 22.8 us
  waiting for transfers between devices: 23.8 us -> 28.9 us
  starting transfers between devices: 32.3 us -> 31.4 us
    pallas_call x15, Pallas kernels: 29.4 us -> 21.4 us  [call(): pl.pallas_call(kernel, grid=grid or (), in_specs=[smem] * len(scalars) +...]
    ppermute x10, waiting for transfers between devices: 16.3 us -> 21.9 us  [shift(): lax.ppermute(value, 'seq', [(src, src + steps) for src in range(low, high)])]
  transfers between devices with their start and end apart: 18 -> 18, of which waited for: 5 -> 7; matrix products, arithmetic and copies ran while one was open for 0% -> 0% of each run, Pallas kernels for 28% -> 22%
where the time goes in v5:
time: 84.4 us; the launch traced here: 84 us
  starting transfers between devices  31.4 us (37%)
  waiting for transfers between devices  28.9 us (34%)
  Pallas kernels  22.8 us (27%)
  between operations  0.86 us (1%)
    ppermute x10, starting transfers between devices, shift(): lax.ppermute(value, 'seq', [(src, src + steps) for src in range(low, high)])  23.3 us
    ppermute x10, waiting for transfers between devices, shift(): lax.ppermute(value, 'seq', [(src, src + steps) for src in range(low, high)])  21.9 us
    pallas_call x15, Pallas kernels, call(): pl.pallas_call(kernel, grid=grid or (), in_specs=[smem] * len(scalars) +...  21.4 us
    ppermute x8, starting transfers between devices, swap(): return lax.ppermute(value, axis, pairs)  8.04 us
    ppermute x8, waiting for transfers between devices, swap(): return lax.ppermute(value, axis, pairs)  7 us
  transfers between devices with their start and end apart: 18, of which 7 were waited for; matrix products, arithmetic and copies ran while one was open for 0% of the time, Pallas kernels for 22%

profile of v5, /device:TPU:0, one launch (start us, length us, event | category | flops | bytes accessed | tf_op | source)
XLA Modules:
  0.0 84.0 jit_solution(9015849598903115325)
XLA Ops:
  0.6 3.1 %collective-permute-start.1 = (bf16[256,512]{1,0:T(8,128)(2,1)}, bf16[256,512]{1,0:T(8,128)(2,1)S(1)}, u32[]{:S(2)}, u32[]{:S(2)}) collective-permute-start(bf16[256,512]{1,0:T(8,128)(2,1)} %refs_3_.1), channel_id=1, source_target_pairs={{0,2},{1,3},{2,0},{3,1},{4,6},{5,7},{6,4},{7,5},{8,10},{9,11},{10,... | collective-permute-start | bytes 786440 | tf_op jit(solution)/shard_map/ppermute | solution.py:31
  3.7 3.5 %collective-permute-start.5 = (bf16[256,1024]{1,0:T(8,128)(2,1)}, bf16[256,1024]{1,0:T(8,128)(2,1)S(1)}, u32[]{:S(2)}, u32[]{:S(2)}) collective-permute-start(bf16[256,1024]{1,0:T(8,128)(2,1)} %refs_1_.2), channel_id=1, source_target_pairs={{0,8},{4,12},{8,16},{12,20},{16,24},{20,28},{1,9},{5,13},{9,17},{1... | collective-permute-start | bytes 1572872 | tf_op jit(solution)/shard_map/ppermute | solution.py:26
  7.2 0.1 collective-permute-start
  7.3 2.9 %collective-permute-done.1.refs_1_ = bf16[256,512]{1,0:T(8,128)(2,1)S(1)} collective-permute-done((bf16[256,512]{1,0:T(8,128)(2,1)}, bf16[256,512]{1,0:T(8,128)(2,1)S(1)}, u32[]{:S(2)}, u32[]{:S(2)}) %collective-permute-start.1) | collective-permute-done | bytes 262176 | tf_op jit(solution)/shard_map/ppermute | solution.py:31
  10.2 0.0 collective-permute-start.2
  10.2 1.7 %collective-permute-start.4 = (bf16[256,1024]{1,0:T(8,128)(2,1)}, bf16[256,1024]{1,0:T(8,128)(2,1)S(1)}, u32[]{:S(2)}, u32[]{:S(2)}) collective-permute-start(bf16[256,1024]{1,0:T(8,128)(2,1)} %refs_0_.1), channel_id=1, source_target_pairs={{0,4},{4,0},{8,12},{12,8},{16,20},{20,16},{24,28},{28,24},{1,5},{5... | collective-permute-start | bytes 1572872 | tf_op jit(solution)/shard_map/ppermute | solution.py:31
  11.9 1.3 %collective-permute-start.3 = (bf16[256,1024]{1,0:T(8,128)(2,1)}, bf16[256,1024]{1,0:T(8,128)(2,1)S(1)}, u32[]{:S(2)}, u32[]{:S(2)}) collective-permute-start(bf16[256,1024]{1,0:T(8,128)(2,1)} %refs_0_.1), channel_id=1, source_target_pairs={{8,0},{12,4},{16,8},{20,12},{24,16},{28,20},{9,1},{13,5},{17,9},{2... | collective-permute-start | bytes 1572872 | tf_op jit(solution)/shard_map/ppermute | solution.py:26
  13.2 4.6 %collective-permute-start.6 = (bf16[256,1024]{1,0:T(8,128)(2,1)}, bf16[256,1024]{1,0:T(8,128)(2,1)S(1)}, u32[]{:S(2)}, u32[]{:S(2)}) collective-permute-start(bf16[256,1024]{1,0:T(8,128)(2,1)} %refs_2_.1), channel_id=1, source_target_pairs={{0,8},{4,12},{8,16},{12,20},{16,24},{20,28},{1,9},{5,13},{9,17},{1... | collective-permute-start | bytes 1572872 | tf_op jit(solution)/shard_map/ppermute | solution.py:26
  17.8 4.8 %shard_map.94.refs_1_.g = bf16[256,1024]{1,0:T(8,128)(2,1)S(1)} custom-call(bf16[256,512]{1,0:T(8,128)(2,1)S(1)} %collective-permute-done.refs_0_, bf16[256,512]{1,0:T(8,128)(2,1)S(1)} %collective-permute-done.1.refs_1_, bf16[256,512]{1,0:T(8,128)(2,1)S(1)} %collective-permute-done.2.refs_2_, bf16[256,512]{1,0:T(8,128)(2,1)} %refs_3_.1, ...), custom_call_target="tpu_custom_call" | custom-call | flops 1073741824 | tf_op jit(solution)/shard_map/pallas_call | solution.py:51
  22.7 0.4 collective-permute-start.9
  23.1 0.0 collective-permute-done.5.refs_6_.k.refs_5_
  23.1 1.3 %collective-permute-start.7 = (bf16[256,1024]{1,0:T(8,128)(2,1)S(1)}, bf16[256,1024]{1,0:T(8,128)(2,1)S(1)}, u32[]{:S(2)}, u32[]{:S(2)}) collective-permute-start(bf16[256,1024]{1,0:T(8,128)(2,1)S(1)} %shard_map.94.refs_1_.g), channel_id=1, source_target_pairs={{8,0},{12,4},{16,8},{20,12},{24,16},{28,20},{9,1},{13,5},{17,9},{2... | collective-permute-start | bytes 1572872 | tf_op jit(solution)/shard_map/ppermute | solution.py:26
  24.3 1.4 %stage.1 = (bf16[256,1024]{1,0:T(8,128)(2,1)S(1)}, bf16[256,1024]{1,0:T(8,128)(2,1)S(1)}, bf16[256,1024]{1,0:T(8,128)(2,1)S(1)}) custom-call(bf16[256,1024]{1,0:T(8,128)(2,1)} %refs_0_.1, bf16[256,1024]{1,0:T(8,128)(2,1)} %refs_1_.2, bf16[256,1024]{1,0:T(8,128)(2,1)} %refs_2_.1), custom_call_target="tpu_custom_call" | custom-call | flops 1000000 | tf_op jit(solution)/shard_map/stage/pallas_call | solution.py:153
  25.7 3.1 %collective-permute-done.3.refs_4_.refs_0_ = bf16[256,1024]{1,0:T(8,128)(2,1)S(1)} collective-permute-done((bf16[256,1024]{1,0:T(8,128)(2,1)}, bf16[256,1024]{1,0:T(8,128)(2,1)S(1)}, u32[]{:S(2)}, u32[]{:S(2)}) %collective-permute-start.3) | collective-permute-done | bytes 524320 | tf_op jit(solution)/shard_map/ppermute | solution.py:26
  28.8 3.3 %shard_map.95 = (f32[3,8,256]{2,1,0:T(8,128)S(1)}, f32[3,8,256]{2,1,0:T(8,128)S(1)}, f32[3,8,256]{2,1,0:T(8,128)S(1)}, f32[3,8,256]{2,1,0:T(8,128)S(1)}, f32[8,2...) custom-call(bf16[256,1024]{1,0:T(8,128)(2,1)S(1)} %get-tuple-element, ...), custom_call_target="tpu_custom_call" | custom-call | flops 671088640 | tf_op jit(solution)/shard_map/pallas_call | solution.py:51
  32.2 0.0 collective-permute-done.6.v_up.refs_2_
  32.2 4.1 %collective-permute-done.9.refs_0_.refs_3_ = bf16[256,1024]{1,0:T(8,128)(2,1)S(1)} collective-permute-done((bf16[256,1024]{1,0:T(8,128)(2,1)S(1)}, bf16[256,1024]{1,0:T(8,128)(2,1)S(1)}, u32[]{:S(2)}, u32[]{:S(2)}) %collective-permute-start.9) | collective-permute-done | bytes 524320 | tf_op jit(solution)/shard_map/ppermute | solution.py:31
  36.2 1.0 %shard_map.98 = (f32[3,8,256]{2,1,0:T(8,128)S(1)}, f32[8,256,256]{2,1,0:T(8,128)S(1)}) custom-call(bf16[256,1024]{1,0:T(8,128)(2,1)S(1)} %collective-permute-done.9.refs_0_.refs_3_, bf16[256,1024]{1,0:T(8,128)(2,1)S(1)} %get-tuple-element.54.refs_3_.refs_1_, bf16[256,1024]{1,0:T(8,128)(2,1)S(1)} %collective-permute-done.6.v_up.refs_2_, ...), custom_call_target="tpu_custom_call" | custom-call | flops 134217728 | tf_op jit(solution)/shard_map/pallas_call | solution.py:51
  37.2 1.6 %collective-permute-start.10 = (f32[3,8,256]{2,1,0:T(8,128)S(1)}, f32[3,8,256]{2,1,0:T(8,128)S(1)}, u32[]{:S(2)}, u32[]{:S(2)}) collective-permute-start(f32[3,8,256]{2,1,0:T(8,128)S(1)} %get-tuple-element.64), channel_id=1, source_target_pairs={{0,4},{4,0},{8,12},{12,8},{16,20},{20,16},{24,28},{28,24},{1,5},{5... | collective-permute-start | bytes 73736 | tf_op jit(solution)/shard_map/ppermute | solution.py:31
  38.8 0.5 collective-permute-done.7.g.refs_1_
  39.3 1.0 %shard_map.97 = (f32[3,8,256]{2,1,0:T(8,128)S(1)}, f32[8,256,256]{2,1,0:T(8,128)S(1)}) custom-call(bf16[256,1024]{1,0:T(8,128)(2,1)S(1)} %collective-permute-done.7.g.refs_1_, bf16[256,1024]{1,0:T(8,128)(2,1)S(1)} %collective-permute-done.6.v_up.refs_2_, f32[8,256,256]{2,1,0:T(8,128)S(1)} %get-tuple-element.59.probs.refs_8_, ...), custom_call_target="tpu_custom_call" | custom-call | flops 134217728 | tf_op jit(solution)/shard_map/pallas_call | solution.py:51
  40.3 0.0 copy-start
  40.3 0.0 copy-start.1
  40.3 3.5 %collective-permute-start.8 = (f32[3,8,256]{2,1,0:T(8,128)S(1)}, f32[3,8,256]{2,1,0:T(8,128)S(1)}, u32[]{:S(2)}, u32[]{:S(2)}) collective-permute-start(f32[3,8,256]{2,1,0:T(8,128)S(1)} %get-tuple-element.61), channel_id=1, source_target_pairs={{0,8},{4,12},{8,16},{12,20},{16,24},{20,28},{1,9},{5,13},{9,17},{1... | collective-permute-start | bytes 73736 | tf_op jit(solution)/shard_map/ppermute | solution.py:26
  43.8 1.0 %shard_map.96 = (f32[3,8,256]{2,1,0:T(8,128)S(1)}, f32[8,256,256]{2,1,0:T(8,128)S(1)}) custom-call(bf16[256,1024]{1,0:T(8,128)(2,1)S(1)} %shard_map.94.refs_1_.g, bf16[256,1024]{1,0:T(8,128)(2,1)S(1)} %collective-permute-done.6.v_up.refs_2_, f32[8,256,256]{2,1,0:T(8,128)S(1)} %get-tuple-element.56.probs, f32[3,8,256]{2,1,0:T(8,128)S(1)} %get-tuple-element.57.soft), custom_call_target="tpu_custom_call" | custom-call | flops 134217728 | tf_op jit(solution)/shard_map/pallas_call | solution.py:51
  44.9 0.0 collective-permute-done.10.refs_5_
  44.9 0.5 collective-permute-done.8.refs_4_
  45.3 0.7 shard_map.99
  46.0 1.3 %collective-permute-start.11 = (f32[2,8,256]{2,1,0:T(8,128)S(1)}, f32[2,8,256]{2,1,0:T(8,128)S(1)}, u32[]{:S(2)}, u32[]{:S(2)}) collective-permute-start(f32[2,8,256]{2,1,0:T(8,128)S(1)} %get-tuple-element.72), channel_id=1, source_target_pairs={{8,0},{12,4},{16,8},{20,12},{24,16},{28,20},{9,1},{13,5},{17,9},{2... | collective-permute-start | bytes 49160 | tf_op jit(solution)/shard_map/ppermute | solution.py:26
  47.3 0.6 collective-permute-start.12
  47.9 1.5 %shard_map.100 = (f32[256,1024]{1,0:T(8,128)S(1)}, f32[256,1024]{1,0:T(8,128)S(1)}, f32[256,1024]{1,0:T(8,128)S(1)}) custom-call(bf16[256,1024]{1,0:T(8,128)(2,1)S(1)} %get-tuple-element.52.refs_0_.q, bf16[256,1024]{1,0:T(8,128)(2,1)S(1)} %shard_map.94.refs_1_.g, bf16[256,1024]{1,0:T(8,128)(2,1)S(1)} %collective-permute-done.5.refs_6_.k.refs_5_, ...), custom_call_target="tpu_custom_call" | custom-call | flops 402653184 | tf_op jit(solution)/shard_map/pallas_call | solution.py:51
  49.4 2.5 %collective-permute-done.11.refs_6_ = f32[2,8,256]{2,1,0:T(8,128)S(1)} collective-permute-done((f32[2,8,256]{2,1,0:T(8,128)S(1)}, f32[2,8,256]{2,1,0:T(8,128)S(1)}, u32[]{:S(2)}, u32[]{:S(2)}) %collective-permute-start.11) | collective-permute-done | bytes 16416 | tf_op jit(solution)/shard_map/ppermute | solution.py:26
  51.9 0.6 shard_map.102
  52.5 1.3 %shard_map.103 = (bf16[256,1024]{1,0:T(8,128)(2,1)S(1)}, bf16[256,1024]{1,0:T(8,128)(2,1)S(1)}, bf16[512,512]{1,0:T(8,128)(2,1)S(1)}, f32[256,512]{1,0:T(8,128)S(1)}, f32[256,512]{1,0:T(8,128)S(1)}) custom-call(bf16[256,1024]{1,0:T(8,128)(2,1)S(1)} %collective-permute-done.3.refs_4_.refs_0_, ...), custom_call_target="tpu_custom_call", output_to_operand_aliasing={{0}: (14, {}), {1}: (15, {})} | custom-call | flops 402653184 | tf_op jit(solution)/shard_map/pallas_call | solution.py:51
  53.8 0.6 shard_map.104
  54.4 4.0 %collective-permute-start.13 = (bf16[256,1024]{1,0:T(8,128)(2,1)S(1)}, bf16[256,1024]{1,0:T(8,128)(2,1)S(1)}, u32[]{:S(2)}, u32[]{:S(2)}) collective-permute-start(bf16[256,1024]{1,0:T(8,128)(2,1)S(1)} %get-tuple-element.82), channel_id=1, source_target_pairs={{0,8},{4,12},{8,16},{12,20},{16,24},{20,28},{1,9},{5,13},{9,17},{1... | collective-permute-start | bytes 1572872 | tf_op jit(solution)/shard_map/ppermute | solution.py:26
  58.5 0.7 collective-permute-start.14
  59.2 1.3 %collective-permute-start.16 = (bf16[512,512]{1,0:T(8,128)(2,1)S(1)}, bf16[512,512]{1,0:T(8,128)(2,1)S(1)}, u32[]{:S(2)}, u32[]{:S(2)}) collective-permute-start(bf16[512,512]{1,0:T(8,128)(2,1)S(1)} %get-tuple-element.91), channel_id=1, source_target_pairs={{8,0},{12,4},{16,8},{20,12},{24,16},{28,20},{9,1},{13,5},{17,9},{2... | collective-permute-start | bytes 1572872 | tf_op jit(solution)/shard_map/ppermute | solution.py:26
  60.5 1.3 %collective-permute-start.17 = (bf16[512,256]{1,0:T(8,128)(2,1)S(1)}, bf16[512,256]{1,0:T(8,128)(2,1)S(1)}, u32[]{:S(2)}, u32[]{:S(2)}) collective-permute-start(bf16[512,256]{1,0:T(8,128)(2,1)S(1)} %get-tuple-element.94), channel_id=1, source_target_pairs={{8,0},{12,4},{16,8},{20,12},{24,16},{28,20},{9,1},{13,5},{17,9},{2... | collective-permute-start | bytes 786440 | tf_op jit(solution)/shard_map/ppermute | solution.py:26
  61.8 1.3 %collective-permute-start.15 = (bf16[512,256]{1,0:T(8,128)(2,1)S(1)}, bf16[512,256]{1,0:T(8,128)(2,1)S(1)}, u32[]{:S(2)}, u32[]{:S(2)}) collective-permute-start(bf16[512,256]{1,0:T(8,128)(2,1)S(1)} %get-tuple-element.88), channel_id=1, source_target_pairs={{8,0},{12,4},{16,8},{20,12},{24,16},{28,20},{9,1},{13,5},{17,9},{2... | collective-permute-start | bytes 786440 | tf_op jit(solution)/shard_map/ppermute | solution.py:26
  63.1 1.6 %shard_map.101 = (f32[256,1024]{1,0:T(8,128)S(1)}, f32[256,1024]{1,0:T(8,128)S(1)}, f32[256,1024]{1,0:T(8,128)S(1)}) custom-call(bf16[256,1024]{1,0:T(8,128)(2,1)S(1)} %get-tuple-element.52.refs_0_.q, bf16[256,1024]{1,0:T(8,128)(2,1)S(1)} %shard_map.94.refs_1_.g, bf16[256,1024]{1,0:T(8,128)(2,1)S(1)} %get-tuple-element.53.refs_2_.k.refs_4_, ...), custom_call_target="tpu_custom_call" | custom-call | flops 402653184 | tf_op jit(solution)/shard_map/pallas_call | solution.py:51
  64.6 15.4 %collective-permute-done.17.refs_4_ = bf16[512,256]{1,0:T(8,128)(2,1)S(1)} collective-permute-done((bf16[512,256]{1,0:T(8,128)(2,1)S(1)}, bf16[512,256]{1,0:T(8,128)(2,1)S(1)}, u32[]{:S(2)}, u32[]{:S(2)}) %collective-permute-start.17) | collective-permute-done | bytes 262176 | tf_op jit(solution)/shard_map/ppermute | solution.py:26
  80.0 0.8 shard_map.106
  80.8 0.0 collective-permute-done.13.far
  80.8 0.0 collective-permute-done.14.near
  80.8 1.5 %shard_map.105 = bf16[256,1024]{1,0:T(8,128)(2,1)} custom-call(f32[256,1024]{1,0:T(8,128)S(1)} %get-tuple-element.71.dq, bf16[256,1024]{1,0:T(8,128)(2,1)S(1)} %collective-permute-done.13.far, bf16[256,1024]{1,0:T(8,128)(2,1)S(1)} %collective-permute-done.14.near), custom_call_target="tpu_custom_call" | custom-call | flops 524288 | tf_op jit(solution)/shard_map/pallas_call | solution.py:51
  82.3 0.9 %shard_map.107 = (bf16[256,1024]{1,0:T(8,128)(2,1)}, bf16[256,1024]{1,0:T(8,128)(2,1)}) custom-call(f32[256,1024]{1,0:T(8,128)S(1)} %get-tuple-element.84.refs_0_, f32[256,1024]{1,0:T(8,128)S(1)} %get-tuple-element.85.refs_1_, f32[256,512]{1,0:T(8,128)S(1)} %get-tuple-element.89.refs_2_, ...), custom_call_target="tpu_custom_call", output_to_operand_aliasing={{0}: (5, {}), {1}: (6, {})} | custom-call | flops 33554432 | tf_op jit(solution)/shard_map/pallas_call | solution.py:51
  83.2 0.8 shard_map.108
  (8 shorter events, 0.0 us)
Async XLA Ops:
  0.6 9.6 %collective-permute-start.1 = (bf16[256,512]{1,0:T(8,128)(2,1)}, bf16[256,512]{1,0:T(8,128)(2,1)S(1)}, u32[]{:S(2)}, u32[]{:S(2)}) collective-permute-start(bf16[256,512]{1,0:T(8,128)(2,1)} %refs_3_.1), channel_id=1, source_target_pairs={{0,2},{1,3},{2,0},{3,1},{4,6},{5,7},{6,4},{7,5},{8,10},{9,11},{10,... | collective-permute-start | bytes 786440 | tf_op jit(solution)/shard_map/ppermute | solution.py:31
  3.7 19.4 %collective-permute-start.5 = (bf16[256,1024]{1,0:T(8,128)(2,1)}, bf16[256,1024]{1,0:T(8,128)(2,1)S(1)}, u32[]{:S(2)}, u32[]{:S(2)}) collective-permute-start(bf16[256,1024]{1,0:T(8,128)(2,1)} %refs_1_.2), channel_id=1, source_target_pairs={{0,8},{4,12},{8,16},{12,20},{16,24},{20,28},{1,9},{5,13},{9,17},{1... | collective-permute-start | bytes 1572872 | tf_op jit(solution)/shard_map/ppermute | solution.py:26
  7.2 6.0 %collective-permute-start = (bf16[256,512]{1,0:T(8,128)(2,1)}, bf16[256,512]{1,0:T(8,128)(2,1)S(1)}, u32[]{:S(2)}, u32[]{:S(2)}) collective-permute-start(bf16[256,512]{1,0:T(8,128)(2,1)} %refs_3_.1), channel_id=1, source_target_pairs={{0,1},{1,0},{2,3},{3,2},{4,5},{5,4},{6,7},{7,6},{8,9},{9,8},{10,11... | collective-permute-start | bytes 786440 | tf_op jit(solution)/shard_map/ppermute | solution.py:31
  10.2 7.6 %collective-permute-start.2 = (bf16[256,512]{1,0:T(8,128)(2,1)S(1)}, bf16[256,512]{1,0:T(8,128)(2,1)S(1)}, u32[]{:S(2)}, u32[]{:S(2)}) collective-permute-start(bf16[256,512]{1,0:T(8,128)(2,1)S(1)} %collective-permute-done.1.refs_1_), channel_id=1, source_target_pairs={{0,1},{1,0},{2,3},{3,2},{4,5},{5,4},{6,7},{7,6},{8,9},{9,8},{10,11... | collective-permute-start | bytes 786440 | tf_op jit(solution)/shard_map/ppermute | solution.py:31
  10.2 15.5 %collective-permute-start.4 = (bf16[256,1024]{1,0:T(8,128)(2,1)}, bf16[256,1024]{1,0:T(8,128)(2,1)S(1)}, u32[]{:S(2)}, u32[]{:S(2)}) collective-permute-start(bf16[256,1024]{1,0:T(8,128)(2,1)} %refs_0_.1), channel_id=1, source_target_pairs={{0,4},{4,0},{8,12},{12,8},{16,20},{20,16},{24,28},{28,24},{1,5},{5... | collective-permute-start | bytes 1572872 | tf_op jit(solution)/shard_map/ppermute | solution.py:31
  11.9 16.9 %collective-permute-start.3 = (bf16[256,1024]{1,0:T(8,128)(2,1)}, bf16[256,1024]{1,0:T(8,128)(2,1)S(1)}, u32[]{:S(2)}, u32[]{:S(2)}) collective-permute-start(bf16[256,1024]{1,0:T(8,128)(2,1)} %refs_0_.1), channel_id=1, source_target_pairs={{8,0},{12,4},{16,8},{20,12},{24,16},{28,20},{9,1},{13,5},{17,9},{2... | collective-permute-start | bytes 1572872 | tf_op jit(solution)/shard_map/ppermute | solution.py:26
  13.2 18.9 %collective-permute-start.6 = (bf16[256,1024]{1,0:T(8,128)(2,1)}, bf16[256,1024]{1,0:T(8,128)(2,1)S(1)}, u32[]{:S(2)}, u32[]{:S(2)}) collective-permute-start(bf16[256,1024]{1,0:T(8,128)(2,1)} %refs_2_.1), channel_id=1, source_target_pairs={{0,8},{4,12},{8,16},{12,20},{16,24},{20,28},{1,9},{5,13},{9,17},{1... | collective-permute-start | bytes 1572872 | tf_op jit(solution)/shard_map/ppermute | solution.py:26
  22.7 13.6 %collective-permute-start.9 = (bf16[256,1024]{1,0:T(8,128)(2,1)S(1)}, bf16[256,1024]{1,0:T(8,128)(2,1)S(1)}, u32[]{:S(2)}, u32[]{:S(2)}) collective-permute-start(bf16[256,1024]{1,0:T(8,128)(2,1)S(1)} %shard_map.94.refs_1_.g), channel_id=1, source_target_pairs={{0,4},{4,0},{8,12},{12,8},{16,20},{20,16},{24,28},{28,24},{1,5},{5... | collective-permute-start | bytes 1572872 | tf_op jit(solution)/shard_map/ppermute | solution.py:31
  23.1 16.3 %collective-permute-start.7 = (bf16[256,1024]{1,0:T(8,128)(2,1)S(1)}, bf16[256,1024]{1,0:T(8,128)(2,1)S(1)}, u32[]{:S(2)}, u32[]{:S(2)}) collective-permute-start(bf16[256,1024]{1,0:T(8,128)(2,1)S(1)} %shard_map.94.refs_1_.g), channel_id=1, source_target_pairs={{8,0},{12,4},{16,8},{20,12},{24,16},{28,20},{9,1},{13,5},{17,9},{2... | collective-permute-start | bytes 1572872 | tf_op jit(solution)/shard_map/ppermute | solution.py:26
  37.2 7.6 %collective-permute-start.10 = (f32[3,8,256]{2,1,0:T(8,128)S(1)}, f32[3,8,256]{2,1,0:T(8,128)S(1)}, u32[]{:S(2)}, u32[]{:S(2)}) collective-permute-start(f32[3,8,256]{2,1,0:T(8,128)S(1)} %get-tuple-element.64), channel_id=1, source_target_pairs={{0,4},{4,0},{8,12},{12,8},{16,20},{20,16},{24,28},{28,24},{1,5},{5... | collective-permute-start | bytes 73736 | tf_op jit(solution)/shard_map/ppermute | solution.py:31
  40.3 5.0 %copy-start = (s32[8,3]{0,1:T(4,128)S(1)}, s32[8,3]{0,1:T(4,128)}, u32[]{:S(2)}) copy-start(s32[8,3]{0,1:T(4,128)} %param.12) | copy-start | bytes 292
  40.3 5.0 %copy-start.1 = (s32[1,3]{1,0:T(1,128)S(1)}, s32[1,3]{1,0:T(1,128)}, u32[]{:S(2)}) copy-start(s32[1,3]{1,0:T(1,128)} %refs_1_.3) | copy-start | bytes 40
  40.3 5.0 %collective-permute-start.8 = (f32[3,8,256]{2,1,0:T(8,128)S(1)}, f32[3,8,256]{2,1,0:T(8,128)S(1)}, u32[]{:S(2)}, u32[]{:S(2)}) collective-permute-start(f32[3,8,256]{2,1,0:T(8,128)S(1)} %get-tuple-element.61), channel_id=1, source_target_pairs={{0,8},{4,12},{8,16},{12,20},{16,24},{20,28},{1,9},{5,13},{9,17},{1... | collective-permute-start | bytes 73736 | tf_op jit(solution)/shard_map/ppermute | solution.py:26
  46.0 5.9 %collective-permute-start.11 = (f32[2,8,256]{2,1,0:T(8,128)S(1)}, f32[2,8,256]{2,1,0:T(8,128)S(1)}, u32[]{:S(2)}, u32[]{:S(2)}) collective-permute-start(f32[2,8,256]{2,1,0:T(8,128)S(1)} %get-tuple-element.72), channel_id=1, source_target_pairs={{8,0},{12,4},{16,8},{20,12},{24,16},{28,20},{9,1},{13,5},{17,9},{2... | collective-permute-start | bytes 49160 | tf_op jit(solution)/shard_map/ppermute | solution.py:26
  47.3 4.6 %collective-permute-start.12 = (f32[2,8,256]{2,1,0:T(8,128)S(1)}, f32[2,8,256]{2,1,0:T(8,128)S(1)}, u32[]{:S(2)}, u32[]{:S(2)}) collective-permute-start(f32[2,8,256]{2,1,0:T(8,128)S(1)} %get-tuple-element.73), channel_id=1, source_target_pairs={{0,4},{4,0},{8,12},{12,8},{16,20},{20,16},{24,28},{28,24},{1,5},{5... | collective-permute-start | bytes 49160 | tf_op jit(solution)/shard_map/ppermute | solution.py:31
  54.4 26.3 %collective-permute-start.13 = (bf16[256,1024]{1,0:T(8,128)(2,1)S(1)}, bf16[256,1024]{1,0:T(8,128)(2,1)S(1)}, u32[]{:S(2)}, u32[]{:S(2)}) collective-permute-start(bf16[256,1024]{1,0:T(8,128)(2,1)S(1)} %get-tuple-element.82), channel_id=1, source_target_pairs={{0,8},{4,12},{8,16},{12,20},{16,24},{20,28},{1,9},{5,13},{9,17},{1... | collective-permute-start | bytes 1572872 | tf_op jit(solution)/shard_map/ppermute | solution.py:26
  58.5 22.3 %collective-permute-start.14 = (bf16[256,1024]{1,0:T(8,128)(2,1)S(1)}, bf16[256,1024]{1,0:T(8,128)(2,1)S(1)}, u32[]{:S(2)}, u32[]{:S(2)}) collective-permute-start(bf16[256,1024]{1,0:T(8,128)(2,1)S(1)} %get-tuple-element.83), channel_id=1, source_target_pairs={{0,4},{4,0},{8,12},{12,8},{16,20},{20,16},{24,28},{28,24},{1,5},{5... | collective-permute-start | bytes 1572872 | tf_op jit(solution)/shard_map/ppermute | solution.py:31
  59.2 23.1 %collective-permute-start.16 = (bf16[512,512]{1,0:T(8,128)(2,1)S(1)}, bf16[512,512]{1,0:T(8,128)(2,1)S(1)}, u32[]{:S(2)}, u32[]{:S(2)}) collective-permute-start(bf16[512,512]{1,0:T(8,128)(2,1)S(1)} %get-tuple-element.91), channel_id=1, source_target_pairs={{8,0},{12,4},{16,8},{20,12},{24,16},{28,20},{9,1},{13,5},{17,9},{2... | collective-permute-start | bytes 1572872 | tf_op jit(solution)/shard_map/ppermute | solution.py:26
  60.5 19.6 %collective-permute-start.17 = (bf16[512,256]{1,0:T(8,128)(2,1)S(1)}, bf16[512,256]{1,0:T(8,128)(2,1)S(1)}, u32[]{:S(2)}, u32[]{:S(2)}) collective-permute-start(bf16[512,256]{1,0:T(8,128)(2,1)S(1)} %get-tuple-element.94), channel_id=1, source_target_pairs={{8,0},{12,4},{16,8},{20,12},{24,16},{28,20},{9,1},{13,5},{17,9},{2... | collective-permute-start | bytes 786440 | tf_op jit(solution)/shard_map/ppermute | solution.py:26
  61.8 21.5 %collective-permute-start.15 = (bf16[512,256]{1,0:T(8,128)(2,1)S(1)}, bf16[512,256]{1,0:T(8,128)(2,1)S(1)}, u32[]{:S(2)}, u32[]{:S(2)}) collective-permute-start(bf16[512,256]{1,0:T(8,128)(2,1)S(1)} %get-tuple-element.88), channel_id=1, source_target_pairs={{8,0},{12,4},{16,8},{20,12},{24,16},{28,20},{9,1},{13,5},{17,9},{2... | collective-permute-start | bytes 786440 | tf_op jit(solution)/shard_map/ppermute | solution.py:26

commit v6 on v5

--- a/solution.py
+++ b/solution.py
@@ -102,10 +102,13 @@
     for index in range(count):
         at = pl.ds(index * block, block)
         copies.append(pltpu.make_async_copy(proj_hbm.at[at], proj.at[at], sems.at[index]))
-        copies[-1].start()
+    for copy in copies[:2]:
+        copy.start()
     own_copy.wait()
     for index, copy in enumerate(copies):
         copy.wait()
+        if index + 2 < count:
+            copies[index + 2].start()
         at = slice(index * block, (index + 1) * block)
         total = None
         for offset, piece in enumerate(pieces):
@@ -233,25 +236,66 @@
     by_parity(near_span, lambda odd: delta_kernel(g, v_up if odd else v, *refs))
 
 
-def combine_kernel(spans, t, a, *refs):
+def merge(parts):
+    top = parts[0][0]
+    for part in parts[1:]:
+        top = jnp.maximum(top, part[0])
+    factors = [jnp.exp2((part[0] - top) * EXP_SCALE) for part in parts]
+    norm, delta = 0.0, 0.0
+    for part, factor in zip(parts, factors):
+        norm = norm + factor * part[1]
+        delta = delta + factor * part[2]
+    return (top, norm, delta), factors
+
+
+def rows_of(ref, at):
+    return ref[0, at, :], ref[1, at, :], ref[2, at, :]
+
+
+def masked_rows(ref, at, usable):
+    top, norm, delta = rows_of(ref, at)
+    return jnp.where(usable, top, -BIG), norm, delta
+
+
+def put_norm(outs, at, factors, merged):
+    inverse = 1.0 / merged[1]
+    for out, factor in zip(outs, factors):
+        out[0, at, :] = factor * inverse
+        out[1, at, :] = merged[2] * inverse
+
+
+def combine_local_kernel(spans, t, a, own, mid, near, out):
     flags = Flags(spans, t, a)
-    ins, outs = refs[:4], refs[4:]
-    for head in range(ins[0].shape[1]):
+    for head in range(own.shape[1]):
         at = slice(head, head + 1)
-        peaks = [ins[0][0, at, :]]
-        for ref, section in zip(ins[1:], (MID, FAR, NEAR)):
-            peaks.append(jnp.where(flags.usable(head, section), ref[0, at, :], -BIG))
-        top = jnp.maximum(jnp.maximum(peaks[0], peaks[1]), jnp.maximum(peaks[2], peaks[3]))
-        factors = [jnp.exp2((peak - top) * EXP_SCALE) for peak in peaks]
-        norm, delta = 0.0, 0.0
-        for ref, factor in zip(ins, factors):
-            norm = norm + factor * ref[1, at, :]
-            delta = delta + factor * ref[2, at, :]
-        inverse = 1.0 / norm
-        delta = delta * inverse
-        for out, factor in zip(outs, factors):
-            out[0, at, :] = factor * inverse
-            out[1, at, :] = delta
+        parts = [rows_of(own, at)]
+        parts.append(masked_rows(mid, at, flags.usable(head, MID)))
+        parts.append(masked_rows(near, at, flags.usable(head, NEAR)))
+        merged, _ = merge(parts)
+        bias = jnp.full_like(merged[0], 0.0)
+        bias = jnp.where(flags.usable(head, FAR), bias, -BIG)
+        for index, row in enumerate((*merged, bias)):
+            out[index, at, :] = row
+
+
+def combine_own_kernel(spans, t, a, own, mid, near, far, *outs):
+    flags = Flags(spans, t, a)
+    for head in range(own.shape[1]):
+        at = slice(head, head + 1)
+        parts = [rows_of(own, at)]
+        for ref, section in ((mid, MID), (near, NEAR), (far, FAR)):
+            parts.append(masked_rows(ref, at, flags.usable(head, section)))
+        merged, factors = merge(parts)
+        put_norm(outs, at, factors[:3], merged)
+
+
+def combine_far_kernel(guest, far, out):
+    for head in range(far.shape[1]):
+        at = slice(head, head + 1)
+        top, norm, delta = rows_of(far, at)
+        parts = [(top + guest[3, at, :], norm, delta), rows_of(guest, at)]
+        merged, factors = merge(parts)
+        put_norm([out], at, factors[:1], merged)
 
 
 def pair_terms(head, query, grad, keys, probs, pgrads, norm):
@@ -377,25 +421,35 @@
     def deltas(kernel, scalars, *ins):
         return call(kernel, scalars, ins, [stat, square], heads * pair_work)
 
-    near_stats, near_pgrad = deltas(
+    mid_stats, mid_pgrad = deltas(delta_kernel, [], grads, value_up, mid_prob, mid_soft)
+    near_part, near_pgrad = deltas(
         bound(delta_near_kernel, near_span), [],
         grad_near, value, value_up, near_prob, near_soft,
     )
-    near_stats = swap(near_stats, "seq", near_span)
-    far_stats, far_pgrad = deltas(delta_kernel, [], grad_far, value_up, far_prob, far_soft)
-    far_stats = shift(far_stats, mid_span)
-    mid_stats, mid_pgrad = deltas(delta_kernel, [], grads, value_up, mid_prob, mid_soft)
+    near_stats = swap(near_part, "seq", near_span)
+    far_part, far_pgrad = deltas(delta_kernel, [], grad_far, value_up, far_prob, far_soft)
+    far_stats = shift(far_part, mid_span)
     self_squares, mid_squares = (self_prob, self_pgrad), (mid_prob, mid_pgrad)
     far_squares, near_squares = (far_prob, far_pgrad), (near_prob, near_pgrad)
-    self_norm, mid_norm, far_norm, near_norm = call(
-        bound(combine_kernel, spans),
+
+    row_work = heads * rows * HDIM
+    (merged,) = call(
+        bound(combine_local_kernel, spans),
         flags,
-        [self_stats, mid_stats, far_stats, near_stats],
-        [norm] * 4,
-        heads * rows * HDIM,
-    )
-    far_norm = shift(far_norm, -mid_span)
+        [self_stats, mid_stats, near_stats],
+        [((4, heads, rows), jnp.float32)],
+        row_work,
+    )
+    guest_stats = shift(merged, -mid_span)
+    self_norm, mid_norm, near_norm = call(
+        bound(combine_own_kernel, spans),
+        flags,
+        [self_stats, mid_stats, near_stats, far_stats],
+        [norm] * 3,
+        row_work,
+    )
     near_norm = swap(near_norm, "seq", near_span)
+    (far_norm,) = call(combine_far_kernel, [], [guest_stats, far_part], [norm], row_work)
 
     def terms(keys, row_norm, squares, *added):
         ins = [query, grads, keys, row_norm, *squares, *added]

time: 84.4 us -> 84.9 us (level)
    pallas_call x15 -> x17, Pallas kernels: 21.4 us -> 21.5 us  [call(): pl.pallas_call(kernel, grid=grid or (), in_specs=[smem] * len(scalars) +...]
  transfers between devices with their start and end apart: 18 -> 18, of which waited for: 7 -> 6; matrix products, arithmetic and copies ran while one was open for 0% -> 0% of each run, Pallas kernels for 22% -> 23%
where the time goes in v6:
time: 84.9 us; the launch traced here: 84.5 us
  starting transfers between devices  32 us (38%)
  waiting for transfers between devices  28.7 us (34%)
  Pallas kernels  22.9 us (27%)
  between operations  0.89 us (1%)
    ppermute x10, starting transfers between devices, shift(): lax.ppermute(value, 'seq', [(src, src + steps) for src in range(low, high)])  23.8 us
    ppermute x10, waiting for transfers between devices, shift(): lax.ppermute(value, 'seq', [(src, src + steps) for src in range(low, high)])  21.9 us
    pallas_call x17, Pallas kernels, call(): pl.pallas_call(kernel, grid=grid or (), in_specs=[smem] * len(scalars) +...  21.5 us
    ppermute x8, starting transfers between devices, swap(): return lax.ppermute(value, axis, pairs)  8.27 us
    ppermute x8, waiting for transfers between devices, swap(): return lax.ppermute(value, axis, pairs)  6.79 us
  transfers between devices with their start and end apart: 18, of which 6 were waited for; matrix products, arithmetic and copies ran while one was open for 0% of the time, Pallas kernels for 23%

profile of v6, /device:TPU:0, one launch (start us, length us, event | category | flops | bytes accessed | tf_op | source)
XLA Modules:
  0.0 84.5 jit_solution(7284008041771035194)
XLA Ops:
  0.6 3.1 %collective-permute-start.1 = (bf16[256,512]{1,0:T(8,128)(2,1)}, bf16[256,512]{1,0:T(8,128)(2,1)S(1)}, u32[]{:S(2)}, u32[]{:S(2)}) collective-permute-start(bf16[256,512]{1,0:T(8,128)(2,1)} %refs_3_.1), channel_id=1, source_target_pairs={{0,2},{1,3},{2,0},{3,1},{4,6},{5,7},{6,4},{7,5},{8,10},{9,11},{10,... | collective-permute-start | bytes 786440 | tf_op jit(solution)/shard_map/ppermute | solution.py:31
  3.7 3.5 %collective-permute-start.5 = (bf16[256,1024]{1,0:T(8,128)(2,1)}, bf16[256,1024]{1,0:T(8,128)(2,1)S(1)}, u32[]{:S(2)}, u32[]{:S(2)}) collective-permute-start(bf16[256,1024]{1,0:T(8,128)(2,1)} %refs_1_.3), channel_id=1, source_target_pairs={{0,8},{4,12},{8,16},{12,20},{16,24},{20,28},{1,9},{5,13},{9,17},{1... | collective-permute-start | bytes 1572872 | tf_op jit(solution)/shard_map/ppermute | solution.py:26
  7.2 0.1 collective-permute-start
  7.3 2.9 %collective-permute-done.1.refs_1_ = bf16[256,512]{1,0:T(8,128)(2,1)S(1)} collective-permute-done((bf16[256,512]{1,0:T(8,128)(2,1)}, bf16[256,512]{1,0:T(8,128)(2,1)S(1)}, u32[]{:S(2)}, u32[]{:S(2)}) %collective-permute-start.1) | collective-permute-done | bytes 262176 | tf_op jit(solution)/shard_map/ppermute | solution.py:31
  10.2 0.0 collective-permute-start.2
  10.2 1.7 %collective-permute-start.4 = (bf16[256,1024]{1,0:T(8,128)(2,1)}, bf16[256,1024]{1,0:T(8,128)(2,1)S(1)}, u32[]{:S(2)}, u32[]{:S(2)}) collective-permute-start(bf16[256,1024]{1,0:T(8,128)(2,1)} %refs_0_.1), channel_id=1, source_target_pairs={{0,4},{4,0},{8,12},{12,8},{16,20},{20,16},{24,28},{28,24},{1,5},{5... | collective-permute-start | bytes 1572872 | tf_op jit(solution)/shard_map/ppermute | solution.py:31
  11.9 1.3 %collective-permute-start.3 = (bf16[256,1024]{1,0:T(8,128)(2,1)}, bf16[256,1024]{1,0:T(8,128)(2,1)S(1)}, u32[]{:S(2)}, u32[]{:S(2)}) collective-permute-start(bf16[256,1024]{1,0:T(8,128)(2,1)} %refs_0_.1), channel_id=1, source_target_pairs={{8,0},{12,4},{16,8},{20,12},{24,16},{28,20},{9,1},{13,5},{17,9},{2... | collective-permute-start | bytes 1572872 | tf_op jit(solution)/shard_map/ppermute | solution.py:26
  13.2 4.6 %collective-permute-start.6 = (bf16[256,1024]{1,0:T(8,128)(2,1)}, bf16[256,1024]{1,0:T(8,128)(2,1)S(1)}, u32[]{:S(2)}, u32[]{:S(2)}) collective-permute-start(bf16[256,1024]{1,0:T(8,128)(2,1)} %refs_2_.1), channel_id=1, source_target_pairs={{0,8},{4,12},{8,16},{12,20},{16,24},{20,28},{1,9},{5,13},{9,17},{1... | collective-permute-start | bytes 1572872 | tf_op jit(solution)/shard_map/ppermute | solution.py:26
  17.8 4.2 %shard_map.94.refs_1_.g = bf16[256,1024]{1,0:T(8,128)(2,1)S(1)} custom-call(bf16[256,512]{1,0:T(8,128)(2,1)S(1)} %collective-permute-done.refs_0_, bf16[256,512]{1,0:T(8,128)(2,1)S(1)} %collective-permute-done.1.refs_1_, bf16[256,512]{1,0:T(8,128)(2,1)S(1)} %collective-permute-done.2.refs_2_, bf16[256,512]{1,0:T(8,128)(2,1)} %refs_3_.1, ...), custom_call_target="tpu_custom_call" | custom-call | flops 1073741824 | tf_op jit(solution)/shard_map/pallas_call | solution.py:51
  22.0 0.4 collective-permute-start.7
  22.4 0.0 collective-permute-done.5.refs_6_.k.refs_5_
  22.4 1.3 %collective-permute-start.9 = (bf16[256,1024]{1,0:T(8,128)(2,1)S(1)}, bf16[256,1024]{1,0:T(8,128)(2,1)S(1)}, u32[]{:S(2)}, u32[]{:S(2)}) collective-permute-start(bf16[256,1024]{1,0:T(8,128)(2,1)S(1)} %shard_map.94.refs_1_.g), channel_id=1, source_target_pairs={{8,0},{12,4},{16,8},{20,12},{24,16},{28,20},{9,1},{13,5},{17,9},{2... | collective-permute-start | bytes 1572872 | tf_op jit(solution)/shard_map/ppermute | solution.py:26
  23.7 1.4 %stage.1 = (bf16[256,1024]{1,0:T(8,128)(2,1)S(1)}, bf16[256,1024]{1,0:T(8,128)(2,1)S(1)}, bf16[256,1024]{1,0:T(8,128)(2,1)S(1)}) custom-call(bf16[256,1024]{1,0:T(8,128)(2,1)} %refs_0_.1, bf16[256,1024]{1,0:T(8,128)(2,1)} %refs_1_.3, bf16[256,1024]{1,0:T(8,128)(2,1)} %refs_2_.1), custom_call_target="tpu_custom_call" | custom-call | flops 1000000 | tf_op jit(solution)/shard_map/stage/pallas_call | solution.py:156
  25.1 0.0 collective-permute-done.4.refs_5_.refs_2_
  25.1 3.7 %collective-permute-done.3.refs_4_.refs_0_ = bf16[256,1024]{1,0:T(8,128)(2,1)S(1)} collective-permute-done((bf16[256,1024]{1,0:T(8,128)(2,1)}, bf16[256,1024]{1,0:T(8,128)(2,1)S(1)}, u32[]{:S(2)}, u32[]{:S(2)}) %collective-permute-start.3) | collective-permute-done | bytes 524320 | tf_op jit(solution)/shard_map/ppermute | solution.py:26
  28.8 3.4 %shard_map.95 = (f32[3,8,256]{2,1,0:T(8,128)S(1)}, f32[3,8,256]{2,1,0:T(8,128)S(1)}, f32[3,8,256]{2,1,0:T(8,128)S(1)}, f32[3,8,256]{2,1,0:T(8,128)S(1)}, f32[8,2...) custom-call(bf16[256,1024]{1,0:T(8,128)(2,1)S(1)} %get-tuple-element, ...), custom_call_target="tpu_custom_call" | custom-call | flops 671088640 | tf_op jit(solution)/shard_map/pallas_call | solution.py:51
  32.2 0.0 collective-permute-done.6.v_up.refs_2_
  32.2 3.8 %collective-permute-done.7.refs_0_.refs_3_ = bf16[256,1024]{1,0:T(8,128)(2,1)S(1)} collective-permute-done((bf16[256,1024]{1,0:T(8,128)(2,1)S(1)}, bf16[256,1024]{1,0:T(8,128)(2,1)S(1)}, u32[]{:S(2)}, u32[]{:S(2)}) %collective-permute-start.7) | collective-permute-done | bytes 524320 | tf_op jit(solution)/shard_map/ppermute | solution.py:31
  36.0 1.0 %shard_map.97 = (f32[3,8,256]{2,1,0:T(8,128)S(1)}, f32[8,256,256]{2,1,0:T(8,128)S(1)}) custom-call(bf16[256,1024]{1,0:T(8,128)(2,1)S(1)} %collective-permute-done.7.refs_0_.refs_3_, bf16[256,1024]{1,0:T(8,128)(2,1)S(1)} %get-tuple-element.53.refs_3_.refs_1_, bf16[256,1024]{1,0:T(8,128)(2,1)S(1)} %collective-permute-done.6.v_up.refs_2_, ...), custom_call_target="tpu_custom_call" | custom-call | flops 134217728 | tf_op jit(solution)/shard_map/pallas_call | solution.py:51
  37.0 1.8 %collective-permute-start.8 = (f32[3,8,256]{2,1,0:T(8,128)S(1)}, f32[3,8,256]{2,1,0:T(8,128)S(1)}, u32[]{:S(2)}, u32[]{:S(2)}) collective-permute-start(f32[3,8,256]{2,1,0:T(8,128)S(1)} %get-tuple-element.60), channel_id=1, source_target_pairs={{0,4},{4,0},{8,12},{12,8},{16,20},{20,16},{24,28},{28,24},{1,5},{5... | collective-permute-start | bytes 73736 | tf_op jit(solution)/shard_map/ppermute | solution.py:31
  38.8 0.5 collective-permute-done.9.g.refs_1_
  39.3 1.0 %shard_map.98 = (f32[3,8,256]{2,1,0:T(8,128)S(1)}, f32[8,256,256]{2,1,0:T(8,128)S(1)}) custom-call(bf16[256,1024]{1,0:T(8,128)(2,1)S(1)} %collective-permute-done.9.g.refs_1_, bf16[256,1024]{1,0:T(8,128)(2,1)S(1)} %collective-permute-done.6.v_up.refs_2_, f32[8,256,256]{2,1,0:T(8,128)S(1)} %get-tuple-element.61.probs.refs_8_, ...), custom_call_target="tpu_custom_call" | custom-call | flops 134217728 | tf_op jit(solution)/shard_map/pallas_call | solution.py:51
  40.3 0.0 copy-start
  40.3 0.0 copy-start.1
  40.3 3.5 %collective-permute-start.10 = (f32[3,8,256]{2,1,0:T(8,128)S(1)}, f32[3,8,256]{2,1,0:T(8,128)S(1)}, u32[]{:S(2)}, u32[]{:S(2)}) collective-permute-start(f32[3,8,256]{2,1,0:T(8,128)S(1)} %get-tuple-element.63.far), channel_id=1, source_target_pairs={{0,8},{4,12},{8,16},{12,20},{16,24},{20,28},{1,9},{5,13},{9,17},{1... | collective-permute-start | bytes 73736 | tf_op jit(solution)/shard_map/ppermute | solution.py:26
  43.8 1.0 %shard_map.96 = (f32[3,8,256]{2,1,0:T(8,128)S(1)}, f32[8,256,256]{2,1,0:T(8,128)S(1)}) custom-call(bf16[256,1024]{1,0:T(8,128)(2,1)S(1)} %shard_map.94.refs_1_.g, bf16[256,1024]{1,0:T(8,128)(2,1)S(1)} %collective-permute-done.6.v_up.refs_2_, f32[8,256,256]{2,1,0:T(8,128)S(1)} %get-tuple-element.55.probs, f32[3,8,256]{2,1,0:T(8,128)S(1)} %get-tuple-element.56.soft), custom_call_target="tpu_custom_call" | custom-call | flops 134217728 | tf_op jit(solution)/shard_map/pallas_call | solution.py:51
  44.9 0.0 collective-permute-done.8.refs_4_
  44.9 0.6 shard_map.102
  45.5 1.3 %collective-permute-start.11 = (f32[4,8,256]{2,1,0:T(8,128)S(1)}, f32[4,8,256]{2,1,0:T(8,128)S(1)}, u32[]{:S(2)}, u32[]{:S(2)}) collective-permute-start(f32[4,8,256]{2,1,0:T(8,128)S(1)} %shard_map.102), channel_id=1, source_target_pairs={{8,0},{12,4},{16,8},{20,12},{24,16},{28,20},{9,1},{13,5},{17,9},{2... | collective-permute-start | bytes 98312 | tf_op jit(solution)/shard_map/ppermute | solution.py:26
  46.8 0.0 collective-permute-done.10.refs_5_
  46.8 0.7 shard_map.99
  47.5 0.6 collective-permute-start.12
  48.1 1.5 %shard_map.100 = (f32[256,1024]{1,0:T(8,128)S(1)}, f32[256,1024]{1,0:T(8,128)S(1)}, f32[256,1024]{1,0:T(8,128)S(1)}) custom-call(bf16[256,1024]{1,0:T(8,128)(2,1)S(1)} %get-tuple-element.51.refs_0_.q, bf16[256,1024]{1,0:T(8,128)(2,1)S(1)} %shard_map.94.refs_1_.g, bf16[256,1024]{1,0:T(8,128)(2,1)S(1)} %collective-permute-done.5.refs_6_.k.refs_5_, ...), custom_call_target="tpu_custom_call" | custom-call | flops 402653184 | tf_op jit(solution)/shard_map/pallas_call | solution.py:51
  49.6 1.7 %collective-permute-done.11.guest = f32[4,8,256]{2,1,0:T(8,128)S(1)} collective-permute-done((f32[4,8,256]{2,1,0:T(8,128)S(1)}, f32[4,8,256]{2,1,0:T(8,128)S(1)}, u32[]{:S(2)}, u32[]{:S(2)}) %collective-permute-start.11) | collective-permute-done | bytes 32800 | tf_op jit(solution)/shard_map/ppermute | solution.py:26
  51.4 0.6 shard_map.104
  52.0 1.3 %shard_map.105 = (bf16[256,1024]{1,0:T(8,128)(2,1)S(1)}, bf16[256,1024]{1,0:T(8,128)(2,1)S(1)}, bf16[512,512]{1,0:T(8,128)(2,1)S(1)}, f32[256,512]{1,0:T(8,128)S(1)}, f32[256,512]{1,0:T(8,128)S(1)}) custom-call(bf16[256,1024]{1,0:T(8,128)(2,1)S(1)} %collective-permute-done.3.refs_4_.refs_0_, ...), custom_call_target="tpu_custom_call", output_to_operand_aliasing={{0}: (14, {}), {1}: (15, {})} | custom-call | flops 402653184 | tf_op jit(solution)/shard_map/pallas_call | solution.py:51
  53.3 0.6 shard_map.106
  53.9 4.5 %collective-permute-start.13 = (bf16[256,1024]{1,0:T(8,128)(2,1)S(1)}, bf16[256,1024]{1,0:T(8,128)(2,1)S(1)}, u32[]{:S(2)}, u32[]{:S(2)}) collective-permute-start(bf16[256,1024]{1,0:T(8,128)(2,1)S(1)} %get-tuple-element.80), channel_id=1, source_target_pairs={{0,8},{4,12},{8,16},{12,20},{16,24},{20,28},{1,9},{5,13},{9,17},{1... | collective-permute-start | bytes 1572872 | tf_op jit(solution)/shard_map/ppermute | solution.py:26
  58.4 0.7 collective-permute-start.14
  59.1 1.3 %collective-permute-start.16 = (bf16[512,512]{1,0:T(8,128)(2,1)S(1)}, bf16[512,512]{1,0:T(8,128)(2,1)S(1)}, u32[]{:S(2)}, u32[]{:S(2)}) collective-permute-start(bf16[512,512]{1,0:T(8,128)(2,1)S(1)} %get-tuple-element.89), channel_id=1, source_target_pairs={{8,0},{12,4},{16,8},{20,12},{24,16},{28,20},{9,1},{13,5},{17,9},{2... | collective-permute-start | bytes 1572872 | tf_op jit(solution)/shard_map/ppermute | solution.py:26
  60.3 1.3 %collective-permute-start.17 = (bf16[512,256]{1,0:T(8,128)(2,1)S(1)}, bf16[512,256]{1,0:T(8,128)(2,1)S(1)}, u32[]{:S(2)}, u32[]{:S(2)}) collective-permute-start(bf16[512,256]{1,0:T(8,128)(2,1)S(1)} %get-tuple-element.92), channel_id=1, source_target_pairs={{8,0},{12,4},{16,8},{20,12},{24,16},{28,20},{9,1},{13,5},{17,9},{2... | collective-permute-start | bytes 786440 | tf_op jit(solution)/shard_map/ppermute | solution.py:26
  61.6 1.3 %collective-permute-start.15 = (bf16[512,256]{1,0:T(8,128)(2,1)S(1)}, bf16[512,256]{1,0:T(8,128)(2,1)S(1)}, u32[]{:S(2)}, u32[]{:S(2)}) collective-permute-start(bf16[512,256]{1,0:T(8,128)(2,1)S(1)} %get-tuple-element.86), channel_id=1, source_target_pairs={{8,0},{12,4},{16,8},{20,12},{24,16},{28,20},{9,1},{13,5},{17,9},{2... | collective-permute-start | bytes 786440 | tf_op jit(solution)/shard_map/ppermute | solution.py:26
  62.9 1.6 %shard_map.101 = (f32[256,1024]{1,0:T(8,128)S(1)}, f32[256,1024]{1,0:T(8,128)S(1)}, f32[256,1024]{1,0:T(8,128)S(1)}) custom-call(bf16[256,1024]{1,0:T(8,128)(2,1)S(1)} %get-tuple-element.51.refs_0_.q, bf16[256,1024]{1,0:T(8,128)(2,1)S(1)} %shard_map.94.refs_1_.g, bf16[256,1024]{1,0:T(8,128)(2,1)S(1)} %get-tuple-element.52.refs_2_.k.refs_4_, ...), custom_call_target="tpu_custom_call" | custom-call | flops 402653184 | tf_op jit(solution)/shard_map/pallas_call | solution.py:51
  64.5 16.0 %collective-permute-done.17.refs_4_ = bf16[512,256]{1,0:T(8,128)(2,1)S(1)} collective-permute-done((bf16[512,256]{1,0:T(8,128)(2,1)S(1)}, bf16[512,256]{1,0:T(8,128)(2,1)S(1)}, u32[]{:S(2)}, u32[]{:S(2)}) %collective-permute-start.17) | collective-permute-done | bytes 262176 | tf_op jit(solution)/shard_map/ppermute | solution.py:26
  80.6 0.8 shard_map.108
  81.3 1.5 %shard_map.107 = bf16[256,1024]{1,0:T(8,128)(2,1)} custom-call(f32[256,1024]{1,0:T(8,128)S(1)} %get-tuple-element.70.dq, bf16[256,1024]{1,0:T(8,128)(2,1)S(1)} %collective-permute-done.13.far, bf16[256,1024]{1,0:T(8,128)(2,1)S(1)} %collective-permute-done.14.near), custom_call_target="tpu_custom_call" | custom-call | flops 524288 | tf_op jit(solution)/shard_map/pallas_call | solution.py:51
  82.8 0.9 %shard_map.109 = (bf16[256,1024]{1,0:T(8,128)(2,1)}, bf16[256,1024]{1,0:T(8,128)(2,1)}) custom-call(f32[256,1024]{1,0:T(8,128)S(1)} %get-tuple-element.82.refs_0_, f32[256,1024]{1,0:T(8,128)S(1)} %get-tuple-element.83.refs_1_, f32[256,512]{1,0:T(8,128)S(1)} %get-tuple-element.87.refs_2_, ...), custom_call_target="tpu_custom_call", output_to_operand_aliasing={{0}: (5, {}), {1}: (6, {})} | custom-call | flops 33554432 | tf_op jit(solution)/shard_map/pallas_call | solution.py:51
  83.7 0.8 shard_map.110
  (10 shorter events, 0.1 us)
Async XLA Ops:
  0.6 9.6 %collective-permute-start.1 = (bf16[256,512]{1,0:T(8,128)(2,1)}, bf16[256,512]{1,0:T(8,128)(2,1)S(1)}, u32[]{:S(2)}, u32[]{:S(2)}) collective-permute-start(bf16[256,512]{1,0:T(8,128)(2,1)} %refs_3_.1), channel_id=1, source_target_pairs={{0,2},{1,3},{2,0},{3,1},{4,6},{5,7},{6,4},{7,5},{8,10},{9,11},{10,... | collective-permute-start | bytes 786440 | tf_op jit(solution)/shard_map/ppermute | solution.py:31
  3.7 18.7 %collective-permute-start.5 = (bf16[256,1024]{1,0:T(8,128)(2,1)}, bf16[256,1024]{1,0:T(8,128)(2,1)S(1)}, u32[]{:S(2)}, u32[]{:S(2)}) collective-permute-start(bf16[256,1024]{1,0:T(8,128)(2,1)} %refs_1_.3), channel_id=1, source_target_pairs={{0,8},{4,12},{8,16},{12,20},{16,24},{20,28},{1,9},{5,13},{9,17},{1... | collective-permute-start | bytes 1572872 | tf_op jit(solution)/shard_map/ppermute | solution.py:26
  7.2 6.0 %collective-permute-start = (bf16[256,512]{1,0:T(8,128)(2,1)}, bf16[256,512]{1,0:T(8,128)(2,1)S(1)}, u32[]{:S(2)}, u32[]{:S(2)}) collective-permute-start(bf16[256,512]{1,0:T(8,128)(2,1)} %refs_3_.1), channel_id=1, source_target_pairs={{0,1},{1,0},{2,3},{3,2},{4,5},{5,4},{6,7},{7,6},{8,9},{9,8},{10,11... | collective-permute-start | bytes 786440 | tf_op jit(solution)/shard_map/ppermute | solution.py:31
  10.2 7.6 %collective-permute-start.2 = (bf16[256,512]{1,0:T(8,128)(2,1)S(1)}, bf16[256,512]{1,0:T(8,128)(2,1)S(1)}, u32[]{:S(2)}, u32[]{:S(2)}) collective-permute-start(bf16[256,512]{1,0:T(8,128)(2,1)S(1)} %collective-permute-done.1.refs_1_), channel_id=1, source_target_pairs={{0,1},{1,0},{2,3},{3,2},{4,5},{5,4},{6,7},{7,6},{8,9},{9,8},{10,11... | collective-permute-start | bytes 786440 | tf_op jit(solution)/shard_map/ppermute | solution.py:31
  10.2 14.9 %collective-permute-start.4 = (bf16[256,1024]{1,0:T(8,128)(2,1)}, bf16[256,1024]{1,0:T(8,128)(2,1)S(1)}, u32[]{:S(2)}, u32[]{:S(2)}) collective-permute-start(bf16[256,1024]{1,0:T(8,128)(2,1)} %refs_0_.1), channel_id=1, source_target_pairs={{0,4},{4,0},{8,12},{12,8},{16,20},{20,16},{24,28},{28,24},{1,5},{5... | collective-permute-start | bytes 1572872 | tf_op jit(solution)/shard_map/ppermute | solution.py:31
  11.9 16.9 %collective-permute-start.3 = (bf16[256,1024]{1,0:T(8,128)(2,1)}, bf16[256,1024]{1,0:T(8,128)(2,1)S(1)}, u32[]{:S(2)}, u32[]{:S(2)}) collective-permute-start(bf16[256,1024]{1,0:T(8,128)(2,1)} %refs_0_.1), channel_id=1, source_target_pairs={{8,0},{12,4},{16,8},{20,12},{24,16},{28,20},{9,1},{13,5},{17,9},{2... | collective-permute-start | bytes 1572872 | tf_op jit(solution)/shard_map/ppermute | solution.py:26
  13.2 19.0 %collective-permute-start.6 = (bf16[256,1024]{1,0:T(8,128)(2,1)}, bf16[256,1024]{1,0:T(8,128)(2,1)S(1)}, u32[]{:S(2)}, u32[]{:S(2)}) collective-permute-start(bf16[256,1024]{1,0:T(8,128)(2,1)} %refs_2_.1), channel_id=1, source_target_pairs={{0,8},{4,12},{8,16},{12,20},{16,24},{20,28},{1,9},{5,13},{9,17},{1... | collective-permute-start | bytes 1572872 | tf_op jit(solution)/shard_map/ppermute | solution.py:26
  22.0 13.9 %collective-permute-start.7 = (bf16[256,1024]{1,0:T(8,128)(2,1)S(1)}, bf16[256,1024]{1,0:T(8,128)(2,1)S(1)}, u32[]{:S(2)}, u32[]{:S(2)}) collective-permute-start(bf16[256,1024]{1,0:T(8,128)(2,1)S(1)} %shard_map.94.refs_1_.g), channel_id=1, source_target_pairs={{0,4},{4,0},{8,12},{12,8},{16,20},{20,16},{24,28},{28,24},{1,5},{5... | collective-permute-start | bytes 1572872 | tf_op jit(solution)/shard_map/ppermute | solution.py:31
  22.4 16.9 %collective-permute-start.9 = (bf16[256,1024]{1,0:T(8,128)(2,1)S(1)}, bf16[256,1024]{1,0:T(8,128)(2,1)S(1)}, u32[]{:S(2)}, u32[]{:S(2)}) collective-permute-start(bf16[256,1024]{1,0:T(8,128)(2,1)S(1)} %shard_map.94.refs_1_.g), channel_id=1, source_target_pairs={{8,0},{12,4},{16,8},{20,12},{24,16},{28,20},{9,1},{13,5},{17,9},{2... | collective-permute-start | bytes 1572872 | tf_op jit(solution)/shard_map/ppermute | solution.py:26
  37.0 7.9 %collective-permute-start.8 = (f32[3,8,256]{2,1,0:T(8,128)S(1)}, f32[3,8,256]{2,1,0:T(8,128)S(1)}, u32[]{:S(2)}, u32[]{:S(2)}) collective-permute-start(f32[3,8,256]{2,1,0:T(8,128)S(1)} %get-tuple-element.60), channel_id=1, source_target_pairs={{0,4},{4,0},{8,12},{12,8},{16,20},{20,16},{24,28},{28,24},{1,5},{5... | collective-permute-start | bytes 73736 | tf_op jit(solution)/shard_map/ppermute | solution.py:31
  40.3 4.5 %copy-start = (s32[8,3]{0,1:T(4,128)S(1)}, s32[8,3]{0,1:T(4,128)}, u32[]{:S(2)}) copy-start(s32[8,3]{0,1:T(4,128)} %param.12) | copy-start | bytes 292
  40.3 4.5 %copy-start.1 = (s32[1,3]{1,0:T(1,128)S(1)}, s32[1,3]{1,0:T(1,128)}, u32[]{:S(2)}) copy-start(s32[1,3]{1,0:T(1,128)} %refs_1_.5) | copy-start | bytes 40
  40.3 6.5 %collective-permute-start.10 = (f32[3,8,256]{2,1,0:T(8,128)S(1)}, f32[3,8,256]{2,1,0:T(8,128)S(1)}, u32[]{:S(2)}, u32[]{:S(2)}) collective-permute-start(f32[3,8,256]{2,1,0:T(8,128)S(1)} %get-tuple-element.63.far), channel_id=1, source_target_pairs={{0,8},{4,12},{8,16},{12,20},{16,24},{20,28},{1,9},{5,13},{9,17},{1... | collective-permute-start | bytes 73736 | tf_op jit(solution)/shard_map/ppermute | solution.py:26
  45.5 5.8 %collective-permute-start.11 = (f32[4,8,256]{2,1,0:T(8,128)S(1)}, f32[4,8,256]{2,1,0:T(8,128)S(1)}, u32[]{:S(2)}, u32[]{:S(2)}) collective-permute-start(f32[4,8,256]{2,1,0:T(8,128)S(1)} %shard_map.102), channel_id=1, source_target_pairs={{8,0},{12,4},{16,8},{20,12},{24,16},{28,20},{9,1},{13,5},{17,9},{2... | collective-permute-start | bytes 98312 | tf_op jit(solution)/shard_map/ppermute | solution.py:26
  47.5 3.9 %collective-permute-start.12 = (f32[2,8,256]{2,1,0:T(8,128)S(1)}, f32[2,8,256]{2,1,0:T(8,128)S(1)}, u32[]{:S(2)}, u32[]{:S(2)}) collective-permute-start(f32[2,8,256]{2,1,0:T(8,128)S(1)} %get-tuple-element.71), channel_id=1, source_target_pairs={{0,4},{4,0},{8,12},{12,8},{16,20},{20,16},{24,28},{28,24},{1,5},{5... | collective-permute-start | bytes 49160 | tf_op jit(solution)/shard_map/ppermute | solution.py:31
  53.9 27.4 %collective-permute-start.13 = (bf16[256,1024]{1,0:T(8,128)(2,1)S(1)}, bf16[256,1024]{1,0:T(8,128)(2,1)S(1)}, u32[]{:S(2)}, u32[]{:S(2)}) collective-permute-start(bf16[256,1024]{1,0:T(8,128)(2,1)S(1)} %get-tuple-element.80), channel_id=1, source_target_pairs={{0,8},{4,12},{8,16},{12,20},{16,24},{20,28},{1,9},{5,13},{9,17},{1... | collective-permute-start | bytes 1572872 | tf_op jit(solution)/shard_map/ppermute | solution.py:26
  58.4 22.9 %collective-permute-start.14 = (bf16[256,1024]{1,0:T(8,128)(2,1)S(1)}, bf16[256,1024]{1,0:T(8,128)(2,1)S(1)}, u32[]{:S(2)}, u32[]{:S(2)}) collective-permute-start(bf16[256,1024]{1,0:T(8,128)(2,1)S(1)} %get-tuple-element.81), channel_id=1, source_target_pairs={{0,4},{4,0},{8,12},{12,8},{16,20},{20,16},{24,28},{28,24},{1,5},{5... | collective-permute-start | bytes 1572872 | tf_op jit(solution)/shard_map/ppermute | solution.py:31
  59.1 23.8 %collective-permute-start.16 = (bf16[512,512]{1,0:T(8,128)(2,1)S(1)}, bf16[512,512]{1,0:T(8,128)(2,1)S(1)}, u32[]{:S(2)}, u32[]{:S(2)}) collective-permute-start(bf16[512,512]{1,0:T(8,128)(2,1)S(1)} %get-tuple-element.89), channel_id=1, source_target_pairs={{8,0},{12,4},{16,8},{20,12},{24,16},{28,20},{9,1},{13,5},{17,9},{2... | collective-permute-start | bytes 1572872 | tf_op jit(solution)/shard_map/ppermute | solution.py:26
  60.3 20.2 %collective-permute-start.17 = (bf16[512,256]{1,0:T(8,128)(2,1)S(1)}, bf16[512,256]{1,0:T(8,128)(2,1)S(1)}, u32[]{:S(2)}, u32[]{:S(2)}) collective-permute-start(bf16[512,256]{1,0:T(8,128)(2,1)S(1)} %get-tuple-element.92), channel_id=1, source_target_pairs={{8,0},{12,4},{16,8},{20,12},{24,16},{28,20},{9,1},{13,5},{17,9},{2... | collective-permute-start | bytes 786440 | tf_op jit(solution)/shard_map/ppermute | solution.py:26
  61.6 22.1 %collective-permute-start.15 = (bf16[512,256]{1,0:T(8,128)(2,1)S(1)}, bf16[512,256]{1,0:T(8,128)(2,1)S(1)}, u32[]{:S(2)}, u32[]{:S(2)}) collective-permute-start(bf16[512,256]{1,0:T(8,128)(2,1)S(1)} %get-tuple-element.86), channel_id=1, source_target_pairs={{8,0},{12,4},{16,8},{20,12},{24,16},{28,20},{9,1},{13,5},{17,9},{2... | collective-permute-start | bytes 786440 | tf_op jit(solution)/shard_map/ppermute | solution.py:26

commit v7 on v6

--- a/solution.py
+++ b/solution.py
@@ -180,6 +180,14 @@
         used = self.table[section, head] * self.active[0, section] > 0
         return used & (self.place >= self.spans[section])
 
+    def bias(self, section, shape):
+        head_at = lax.broadcasted_iota(jnp.int32, shape, 0)
+        total = jnp.zeros(shape, jnp.float32)
+        for head in range(shape[0]):
+            value = jnp.where(self.usable(head, section), 0.0, -BIG)
+            total = jnp.where(head_at == head, value, total)
+        return total
+
 
 def by_parity(near_span, run):
     odd = (lax.axis_index("seq") // near_span) % 2 == 1
@@ -187,42 +195,43 @@
     pl.when(jnp.logical_not(odd))(lambda: run(False))
 
 
-def soft_set(head, keys, query, probs, stats, diagonal=False):
+def soft_set(head, keys, query, probs, stats, base=0, diagonal=False):
     raw = dot(keys, query, 1, 1)
     if diagonal:
         raw = causal(raw, -BIG)
     top = jnp.max(raw, axis=0, keepdims=True)
     prob = jnp.exp2((raw - top) * EXP_SCALE)
     probs[head] = prob
-    stats[0, pl.ds(head, 1), :] = top
-    stats[1, pl.ds(head, 1), :] = jnp.sum(prob, axis=0, keepdims=True)
-
-
-def delta_set(head, values, grad, probs, pgrads, stats):
+    stats[base, pl.ds(head, 1), :] = top
+    stats[base + 1, pl.ds(head, 1), :] = jnp.sum(prob, axis=0, keepdims=True)
+
+
+def delta_set(head, values, grad, probs, pgrads, stats, base=0):
     pgrad = dot(values, grad, 1, 1)
     pgrads[head] = pgrad
-    stats[2, pl.ds(head, 1), :] = jnp.sum(probs[head] * pgrad, axis=0, keepdims=True)
-
-
-def soft_kernel(near_span, q, g, k, v, qf, qn, k_up, *refs):
+    row = jnp.sum(probs[head] * pgrad, axis=0, keepdims=True)
+    stats[base + 2, pl.ds(head, 1), :] = row
+
+
+def soft_kernel(near_span, q, g, k, v, qf, k_up, k_x, *refs):
     own, mid, far, near, pr_own, pr_mid, pr_far, pr_near, pg_own = refs
 
     def run(odd):
         def step(head):
             at = columns(head)
-            key_up, key, query = k_up[:, at], k[:, at], q[:, at]
-            soft_set(head, key, query, pr_own, own, True)
+            key_up, query, guest = k_up[:, at], q[:, at], qf[:, at]
+            soft_set(head, k[:, at], query, pr_own, own, diagonal=True)
             delta_set(head, v[:, at], g[:, at], pr_own, pg_own, own)
             soft_set(head, key_up, query, pr_mid, mid)
-            soft_set(head, key_up, qf[:, at], pr_far, far)
-            soft_set(head, key_up if odd else key, qn[:, at], pr_near, near)
+            soft_set(head, key_up, guest, pr_far, far)
+            soft_set(head, k_x[:, at], query if odd else guest, pr_near, near)
 
         each_head(0, pg_own.shape[0], step)
 
     by_parity(near_span, run)
 
 
-def delta_kernel(g, v_up, probs, soft, stats, pgrads):
+def delta_mid_kernel(g, v_up, probs, soft, stats, pgrads):
     stats[0:2] = soft[0:2]
 
     def step(head):
@@ -232,8 +241,29 @@
     each_head(0, probs.shape[0], step)
 
 
-def delta_near_kernel(near_span, g, v, v_up, *refs):
-    by_parity(near_span, lambda odd: delta_kernel(g, v_up if odd else v, *refs))
+def delta_near_kernel(near_span, g, v_x, probs, soft, stats, pgrads):
+    def run(odd):
+        if odd:
+            delta_mid_kernel(g, v_x, probs, soft, stats, pgrads)
+
+    by_parity(near_span, run)
+
+
+def delta_guest_kernel(near_span, gf, v_up, v_x, pr_far, far, pr_near, near, _, up, pg_far, pg_near):
+    up[0:2] = far[0:2]
+    up[3:5] = near[0:2]
+
+    def run(odd):
+        def step(head):
+            at = columns(head)
+            grad = gf[:, at]
+            delta_set(head, v_up[:, at], grad, pr_far, pg_far, up)
+            if not odd:
+                delta_set(head, v_x[:, at], grad, pr_near, pg_near, up, 3)
+
+        each_head(0, pr_far.shape[0], step)
+
+    by_parity(near_span, run)
 
 
 def merge(parts):
@@ -248,54 +278,60 @@
     return (top, norm, delta), factors
 
 
-def rows_of(ref, at):
-    return ref[0, at, :], ref[1, at, :], ref[2, at, :]
-
-
-def masked_rows(ref, at, usable):
-    top, norm, delta = rows_of(ref, at)
-    return jnp.where(usable, top, -BIG), norm, delta
-
-
-def put_norm(outs, at, factors, merged):
+def part_of(ref, bias=0.0, base=0):
+    return ref[base] + bias, ref[base + 1], ref[base + 2]
+
+
+def put_norm(outs, factors, merged):
     inverse = 1.0 / merged[1]
+    delta = merged[2] * inverse
     for out, factor in zip(outs, factors):
-        out[0, at, :] = factor * inverse
-        out[1, at, :] = merged[2] * inverse
+        out[0] = factor * inverse
+        out[1] = delta
 
 
 def combine_local_kernel(spans, t, a, own, mid, near, out):
     flags = Flags(spans, t, a)
-    for head in range(own.shape[1]):
-        at = slice(head, head + 1)
-        parts = [rows_of(own, at)]
-        parts.append(masked_rows(mid, at, flags.usable(head, MID)))
-        parts.append(masked_rows(near, at, flags.usable(head, NEAR)))
+
+    def run(odd):
+        shape = own.shape[1:]
+        near_bias = flags.bias(NEAR, shape)
+        parts = [part_of(own), part_of(mid, flags.bias(MID, shape))]
+        if odd:
+            parts.append(part_of(near, near_bias))
+            near_bias = jnp.full(shape, -BIG, jnp.float32)
         merged, _ = merge(parts)
-        bias = jnp.full_like(merged[0], 0.0)
-        bias = jnp.where(flags.usable(head, FAR), bias, -BIG)
-        for index, row in enumerate((*merged, bias)):
-            out[index, at, :] = row
-
-
-def combine_own_kernel(spans, t, a, own, mid, near, far, *outs):
+        for index, row in enumerate((*merged, flags.bias(FAR, shape), near_bias)):
+            out[index] = row
+
+    by_parity(spans[NEAR], run)
+
+
+def combine_own_kernel(spans, t, a, own, mid, near, up, *outs):
     flags = Flags(spans, t, a)
-    for head in range(own.shape[1]):
-        at = slice(head, head + 1)
-        parts = [rows_of(own, at)]
-        for ref, section in ((mid, MID), (near, NEAR), (far, FAR)):
-            parts.append(masked_rows(ref, at, flags.usable(head, section)))
+
+    def run(odd):
+        shape = own.shape[1:]
+        near_bias = flags.bias(NEAR, shape)
+        parts = [part_of(own), part_of(mid, flags.bias(MID, shape))]
+        parts.append(part_of(near, near_bias) if odd else part_of(up, near_bias, 3))
+        parts.append(part_of(up, flags.bias(FAR, shape)))
         merged, factors = merge(parts)
-        put_norm(outs, at, factors[:3], merged)
-
-
-def combine_far_kernel(guest, far, out):
-    for head in range(far.shape[1]):
-        at = slice(head, head + 1)
-        top, norm, delta = rows_of(far, at)
-        parts = [(top + guest[3, at, :], norm, delta), rows_of(guest, at)]
+        put_norm(outs if odd else outs[:2], factors, merged)
+
+    by_parity(spans[NEAR], run)
+
+
+def combine_guest_kernel(near_span, guest, up, far_out, near_out):
+    def run(odd):
+        parts = [part_of(up, guest[3])]
+        if not odd:
+            parts.append(part_of(up, guest[4], 3))
+        parts.append(part_of(guest))
         merged, factors = merge(parts)
-        put_norm([out], at, factors[:1], merged)
+        put_norm((far_out, near_out), factors[:-1], merged)
+
+    by_parity(near_span, run)
 
 
 def pair_terms(head, query, grad, keys, probs, pgrads, norm):
@@ -306,50 +342,68 @@
     return dot(keys, dlogit, 0, 0), dot(dlogit, query, 1, 0), dot(weight, grad, 1, 0)
 
 
-def terms_kernel(q, g, k, norm, probs, pgrads, *refs):
-    dq, dk, dv = refs[-3:]
-
+def self_kernel(q, g, k, norm, probs, pgrads, dq_part, dq, dk, dv):
     def step(head):
         at = columns(head)
         query_term, dk[:, at], dv[:, at] = pair_terms(
             head, q[:, at], g[:, at], k[:, at], probs, pgrads, norm
         )
-        query_term = query_term.T
-        dq[:, at] = query_term + refs[0][:, at] if len(refs) > 3 else query_term
+        dq[:, at] = query_term.T + dq_part[:, at]
 
     each_head(0, probs.shape[0], step)
 
 
-def pairs_kernel(
-    near_span, first, qf, gf, qn, gn, k, k_up, norm_far, norm_near,
-    pr_far, pg_far, pr_near, pg_near, dk_mid, dv_mid, *refs,
+def guest_terms_kernel(
+    near_span, q, g, k_up, k_x, norm_far, norm_near, pr_far, pg_far, pr_near, pg_near,
+    dq, dk_far, dv_far, dk_near, dv_near,
 ):
-    dqf, dqn, back, dk, dv = refs[-5:]
-    rows = qf.shape[0]
+    def run(odd):
+        def step(head):
+            at = columns(head)
+            query, grad = q[:, at], g[:, at]
+            query_term, dk_far[:, at], dv_far[:, at] = pair_terms(
+                head, query, grad, k_up[:, at], pr_far, pg_far, norm_far
+            )
+            if not odd:
+                more, dk_near[:, at], dv_near[:, at] = pair_terms(
+                    head, query, grad, k_x[:, at], pr_near, pg_near, norm_near
+                )
+                query_term = query_term + more
+            dq[:, at] = (query_term * SCALE).T.astype(dq.dtype)
+
+        each_head(0, pr_far.shape[0], step)
+
+    by_parity(near_span, run)
+
+
+def own_terms_kernel(
+    near_span, first, q, g, k_up, k_x, norm_mid, norm_near, pr_mid, pg_mid, pr_near, pg_near,
+    dk_far, dv_far, dk_near, dv_near, *refs,
+):
+    dq, back, cross = refs[-3:]
+    rows = q.shape[0]
 
     def run(odd):
         def step(head):
             at, out = columns(head), columns(head - first)
-            key_up = k_up[:, at]
-            dq, key_back, value_back = pair_terms(
-                head, qf[:, at], gf[:, at], key_up, pr_far, pg_far, norm_far
+            query, grad = q[:, at], g[:, at]
+            query_term, key_term, value_term = pair_terms(
+                head, query, grad, k_up[:, at], pr_mid, pg_mid, norm_mid
             )
-            dqf[:, at] = (dq * SCALE).T.astype(dqf.dtype)
-            key_near = key_up if odd else k[:, at]
-            dq, key_term, value_term = pair_terms(
-                head, qn[:, at], gn[:, at], key_near, pr_near, pg_near, norm_near
-            )
-            dqn[:, at] = (dq * SCALE).T.astype(dqn.dtype)
-            key_back, value_back = dk_mid[:, at] + key_back, dv_mid[:, at] + value_back
+            back[:rows, out] = ((key_term + dk_far[:, at]) * SCALE).astype(back.dtype)
+            back[rows:, out] = (value_term + dv_far[:, at]).astype(back.dtype)
             if odd:
-                key_back, value_back = key_back + key_term, value_back + value_term
-                key_term, value_term = jnp.zeros_like(key_term), jnp.zeros_like(value_term)
-            back[:rows, out] = (key_back * SCALE).astype(back.dtype)
-            back[rows:, out] = value_back.astype(back.dtype)
-            dk[:, out] = key_term
-            dv[:, out] = value_term
-
-        each_head(first, dk.shape[1] // HDIM, step)
+                more, key_term, value_term = pair_terms(
+                    head, query, grad, k_x[:, at], pr_near, pg_near, norm_near
+                )
+                query_term = query_term + more
+            else:
+                key_term, value_term = dk_near[:, at], dv_near[:, at]
+            cross[:rows, out] = (key_term * SCALE).astype(cross.dtype)
+            cross[rows:, out] = value_term.astype(cross.dtype)
+            dq[:, at] = query_term.T
+
+        each_head(first, cross.shape[1] // HDIM, step)
 
     by_parity(near_span, run)
 
@@ -358,21 +412,22 @@
     return pl.ds(pl.multiple_of(pl.program_id(0) * block + first, block), block)
 
 
-def finish_kernel(first, dk, dv, near_k, near_v, back, *refs):
+def finish_kernel(first, dk, dv, back, cross, *refs):
     key_out, value_out = refs[-2:]
     rows, block = key_out.shape
     here, at = step_columns(block), step_columns(block, first)
-    key_out[...] = (
-        (dk[:, at] + near_k[:, here]) * SCALE + back[:rows, here].astype(jnp.float32)
-    ).astype(key_out.dtype)
-    value_out[...] = (
-        dv[:, at] + near_v[:, here] + back[rows:, here].astype(jnp.float32)
-    ).astype(value_out.dtype)
-
-
-def finish_query_kernel(dq, far, near, out):
+    for rows_at, total, out in (
+        (slice(0, rows), dk[:, at] * SCALE, key_out),
+        (slice(rows, 2 * rows), dv[:, at], value_out),
+    ):
+        for ref in (back, cross):
+            total = total + ref[rows_at, here].astype(jnp.float32)
+        out[...] = total.astype(out.dtype)
+
+
+def finish_query_kernel(dq, guest, out):
     at = step_columns(out.shape[1])
-    total = dq[:, at] * SCALE + far[:, at].astype(jnp.float32) + near[:, at].astype(jnp.float32)
+    total = dq[:, at] * SCALE + guest[:, at].astype(jnp.float32)
     out[...] = total.astype(out.dtype)
 
 
@@ -390,9 +445,13 @@
 
     wide_f32 = ((rows, cols), jnp.float32)
     wide_bf16 = ((rows, cols), jnp.bfloat16)
-    stat = ((3, heads, rows), jnp.float32)
-    norm = ((2, heads, rows), jnp.float32)
+
+    def table(count):
+        return ((count, heads, rows), jnp.float32)
+
+    stat, norm = table(3), table(2)
     square = ((heads, rows, rows), jnp.float32)
+    row_work = heads * rows * HDIM
 
     def bound(kernel, *fixed):
         def run(*refs):
@@ -402,82 +461,91 @@
 
     key_up = shift(key_rows, mid_span)
     value_up = shift(value_rows, mid_span)
-    query_far = shift(queries, -mid_span)
-    query_near = swap(queries, "seq", near_span)
+    key_x = swap(key_rows, "seq", near_span)
+    value_x = swap(value_rows, "seq", near_span)
+    guest_query = shift(queries, -mid_span)
     grads = attn_grad_of(out_grad, out_proj)
-    grad_far = shift(grads, -mid_span)
-    grad_near = swap(grads, "seq", near_span)
+    guest_grad = shift(grads, -mid_span)
     query, key, value = staged(queries, key_rows, value_rows)
 
     self_stats, mid_soft, far_soft, near_soft, *probs, self_pgrad = call(
         bound(soft_kernel, near_span),
         [],
-        [query, grads, key, value, query_far, query_near, key_up],
+        [query, grads, key, value, guest_query, key_up, key_x],
         [stat] * 4 + [square] * 5,
         heads * 5 * pair_work,
     )
     self_prob, mid_prob, far_prob, near_prob = probs
 
-    def deltas(kernel, scalars, *ins):
-        return call(kernel, scalars, ins, [stat, square], heads * pair_work)
-
-    mid_stats, mid_pgrad = deltas(delta_kernel, [], grads, value_up, mid_prob, mid_soft)
-    near_part, near_pgrad = deltas(
-        bound(delta_near_kernel, near_span), [],
-        grad_near, value, value_up, near_prob, near_soft,
-    )
-    near_stats = swap(near_part, "seq", near_span)
-    far_part, far_pgrad = deltas(delta_kernel, [], grad_far, value_up, far_prob, far_soft)
-    far_stats = shift(far_part, mid_span)
-    self_squares, mid_squares = (self_prob, self_pgrad), (mid_prob, mid_pgrad)
-    far_squares, near_squares = (far_prob, far_pgrad), (near_prob, near_pgrad)
-
-    row_work = heads * rows * HDIM
+    def deltas(kernel, *ins):
+        return call(kernel, [], ins, [stat, square], heads * pair_work)
+
+    mid_stats, mid_pgrad = deltas(delta_mid_kernel, grads, value_up, mid_prob, mid_soft)
+    near_stats, near_pgrad = deltas(
+        bound(delta_near_kernel, near_span), grads, value_x, near_prob, near_soft
+    )
     (merged,) = call(
         bound(combine_local_kernel, spans),
         flags,
         [self_stats, mid_stats, near_stats],
-        [((4, heads, rows), jnp.float32)],
+        [table(5)],
         row_work,
     )
     guest_stats = shift(merged, -mid_span)
+    ins = [guest_grad, value_up, value_x, far_prob, far_soft, near_prob, near_soft, near_pgrad]
+    up_part, far_pgrad, near_pgrad = call(
+        bound(delta_guest_kernel, near_span),
+        [],
+        ins,
+        [table(6), square, square],
+        heads * 2 * pair_work,
+        {len(ins) - 1: 2},
+    )
+    up_stats = shift(up_part, mid_span)
+    far_norm, near_norm_guest = call(
+        bound(combine_guest_kernel, near_span), [], [guest_stats, up_part], [norm] * 2, row_work
+    )
+    near_squares = [near_prob, near_pgrad]
+    ins = [guest_query, guest_grad, key_up, key_x, far_norm, near_norm_guest]
+    guest_part, *guest_terms = call(
+        bound(guest_terms_kernel, near_span),
+        [],
+        [*ins, far_prob, far_pgrad, *near_squares],
+        [wide_bf16] + [wide_f32] * 4,
+        heads * 6 * pair_work,
+    )
     self_norm, mid_norm, near_norm = call(
         bound(combine_own_kernel, spans),
         flags,
-        [self_stats, mid_stats, near_stats, far_stats],
+        [self_stats, mid_stats, near_stats, up_stats],
         [norm] * 3,
         row_work,
     )
-    near_norm = swap(near_norm, "seq", near_span)
-    (far_norm,) = call(combine_far_kernel, [], [guest_stats, far_part], [norm], row_work)
-
-    def terms(keys, row_norm, squares, *added):
-        ins = [query, grads, keys, row_norm, *squares, *added]
-        return call(terms_kernel, [], ins, [wide_f32] * 3, heads * 3 * pair_work)
-
-    mid_query, *mid_terms = terms(key_up, mid_norm, mid_squares)
-    guests = [query_far, grad_far, query_near, grad_near, key, key_up, far_norm, near_norm]
-    guests += [*far_squares, *near_squares, *mid_terms]
-    partial_queries, returned = [], []
+    query_part, returned = [], []
     first = 0
     for group in GROUPS:
-        width = group * HDIM
-        start = len(guests)
-        aliases = {start + number: number for number in range(len(partial_queries))}
-        *partial_queries, back, near_key, near_value = call(
-            bound(pairs_kernel, near_span, first),
+        ins = [query, grads, key_up, key_x, mid_norm, near_norm, mid_prob, mid_pgrad]
+        ins += [*near_squares, *guest_terms]
+        half = ((2 * rows, group * HDIM), jnp.bfloat16)
+        *query_part, back, cross = call(
+            bound(own_terms_kernel, near_span, first),
             [],
-            guests + partial_queries,
-            [wide_bf16] * 2 + [((2 * rows, width), jnp.bfloat16)]
-            + [((rows, width), jnp.float32)] * 2,
+            ins + query_part,
+            [wide_f32, half, half],
             group * 6 * pair_work,
-            aliases,
+            {len(ins): 0} if query_part else {},
         )
-        returned.append((near_key, near_value, shift(back, -mid_span)))
+        cross = swap(cross, "seq", near_span)
+        returned.append((shift(back, -mid_span), cross))
         first += group
-    query_far_part = shift(partial_queries[0], mid_span)
-    query_near_part = swap(partial_queries[1], "seq", near_span)
-    query_sum, *self_terms = terms(key, self_norm, self_squares, mid_query)
+    guest_part = shift(guest_part, mid_span)
+    query_sum, *self_terms = call(
+        self_kernel,
+        [],
+        [query, grads, key, self_norm, self_prob, self_pgrad, *query_part],
+        [wide_f32] * 3,
+        heads * 3 * pair_work,
+    )
 
     block = 2 * HDIM
     outputs = []
@@ -501,7 +569,7 @@
     (query_grad,) = call(
         finish_query_kernel,
         [],
-        [query_sum, query_far_part, query_near_part],
+        [query_sum, guest_part],
         [wide_bf16],
         heads * rows * HDIM,
         grid=(cols // block,),

time: 84.9 us -> 85.5 us (level)
  waiting for transfers between devices: 28.7 us -> 29.9 us
    ppermute x8, waiting for transfers between devices: 6.79 us -> 8.82 us  [swap(): return lax.ppermute(value, axis, pairs)]
  transfers between devices with their start and end apart: 18 -> 18, of which waited for: 6 -> 6; matrix products, arithmetic and copies ran while one was open for 0% -> 0% of each run, Pallas kernels for 23% -> 25%
where the time goes in v7:
time: 85.5 us; the launch traced here: 85 us
  starting transfers between devices  32 us (37%)
  waiting for transfers between devices  29.9 us (35%)
  Pallas kernels  22.2 us (26%)
  between operations  0.89 us (1%)
    ppermute x10, starting transfers between devices, shift(): lax.ppermute(value, 'seq', [(src, src + steps) for src in range(low, high)])  23.3 us
    ppermute x10, waiting for transfers between devices, shift(): lax.ppermute(value, 'seq', [(src, src + steps) for src in range(low, high)])  21.1 us
    pallas_call x17, Pallas kernels, call(): pl.pallas_call(kernel, grid=grid or (), in_specs=[smem] * len(scalars) +...  20.9 us
    ppermute x8, waiting for transfers between devices, swap(): return lax.ppermute(value, axis, pairs)  8.82 us
    ppermute x8, starting transfers between devices, swap(): return lax.ppermute(value, axis, pairs)  8.73 us
  transfers between devices with their start and end apart: 18, of which 6 were waited for; matrix products, arithmetic and copies ran while one was open for 0% of the time, Pallas kernels for 25%

profile of v7, /device:TPU:0, one launch (start us, length us, event | category | flops | bytes accessed | tf_op | source)
XLA Modules:
  0.0 85.0 jit_solution(680102820280503127)
XLA Ops:
  0.6 3.1 %collective-permute-start.1 = (bf16[256,512]{1,0:T(8,128)(2,1)}, bf16[256,512]{1,0:T(8,128)(2,1)S(1)}, u32[]{:S(2)}, u32[]{:S(2)}) collective-permute-start(bf16[256,512]{1,0:T(8,128)(2,1)} %refs_3_.1), channel_id=1, source_target_pairs={{0,2},{1,3},{2,0},{3,1},{4,6},{5,7},{6,4},{7,5},{8,10},{9,11},{10,... | collective-permute-start | bytes 786440 | tf_op jit(solution)/shard_map/ppermute | solution.py:31
  3.7 1.3 %collective-permute-start.3 = (bf16[256,1024]{1,0:T(8,128)(2,1)}, bf16[256,1024]{1,0:T(8,128)(2,1)S(1)}, u32[]{:S(2)}, u32[]{:S(2)}) collective-permute-start(bf16[256,1024]{1,0:T(8,128)(2,1)} %refs_0_.1), channel_id=1, source_target_pairs={{8,0},{12,4},{16,8},{20,12},{24,16},{28,20},{9,1},{13,5},{17,9},{2... | collective-permute-start | bytes 1572872 | tf_op jit(solution)/shard_map/ppermute | solution.py:26
  5.0 0.1 collective-permute-start
  5.1 5.1 %collective-permute-done.1.refs_1_ = bf16[256,512]{1,0:T(8,128)(2,1)S(1)} collective-permute-done((bf16[256,512]{1,0:T(8,128)(2,1)}, bf16[256,512]{1,0:T(8,128)(2,1)S(1)}, u32[]{:S(2)}, u32[]{:S(2)}) %collective-permute-start.1) | collective-permute-done | bytes 262176 | tf_op jit(solution)/shard_map/ppermute | solution.py:31
  10.2 0.0 collective-permute-start.2
  10.2 3.7 %collective-permute-start.4 = (bf16[256,1024]{1,0:T(8,128)(2,1)}, bf16[256,1024]{1,0:T(8,128)(2,1)S(1)}, u32[]{:S(2)}, u32[]{:S(2)}) collective-permute-start(bf16[256,1024]{1,0:T(8,128)(2,1)} %refs_1_.3), channel_id=1, source_target_pairs={{0,8},{4,12},{8,16},{12,20},{16,24},{20,28},{1,9},{5,13},{9,17},{1... | collective-permute-start | bytes 1572872 | tf_op jit(solution)/shard_map/ppermute | solution.py:26
  13.9 1.6 %collective-permute-start.5 = (bf16[256,1024]{1,0:T(8,128)(2,1)}, bf16[256,1024]{1,0:T(8,128)(2,1)S(1)}, u32[]{:S(2)}, u32[]{:S(2)}) collective-permute-start(bf16[256,1024]{1,0:T(8,128)(2,1)} %refs_1_.3), channel_id=1, source_target_pairs={{0,4},{4,0},{8,12},{12,8},{16,20},{20,16},{24,28},{28,24},{1,5},{5... | collective-permute-start | bytes 1572872 | tf_op jit(solution)/shard_map/ppermute | solution.py:31
  15.5 0.0 collective-permute-done.refs_0_
  15.5 3.5 %collective-permute-start.6 = (bf16[256,1024]{1,0:T(8,128)(2,1)}, bf16[256,1024]{1,0:T(8,128)(2,1)S(1)}, u32[]{:S(2)}, u32[]{:S(2)}) collective-permute-start(bf16[256,1024]{1,0:T(8,128)(2,1)} %refs_2_.1), channel_id=1, source_target_pairs={{0,8},{4,12},{8,16},{12,20},{16,24},{20,28},{1,9},{5,13},{9,17},{1... | collective-permute-start | bytes 1572872 | tf_op jit(solution)/shard_map/ppermute | solution.py:26
  19.0 0.0 collective-permute-done.2.refs_2_
  19.0 0.6 collective-permute-start.7
  19.6 4.2 %shard_map.94.refs_1_.g.refs_0_ = bf16[256,1024]{1,0:T(8,128)(2,1)S(1)} custom-call(bf16[256,512]{1,0:T(8,128)(2,1)S(1)} %collective-permute-done.refs_0_, bf16[256,512]{1,0:T(8,128)(2,1)S(1)} %collective-permute-done.1.refs_1_, bf16[256,512]{1,0:T(8,128)(2,1)S(1)} %collective-permute-done.2.refs_2_, bf16[256,512]{1,0:T(8,128)(2,1)} %refs_3_.1, ...), custom_call_target="tpu_custom_call" | custom-call | flops 1073741824 | tf_op jit(solution)/shard_map/pallas_call | solution.py:51
  23.8 1.3 %collective-permute-start.8 = (bf16[256,1024]{1,0:T(8,128)(2,1)S(1)}, bf16[256,1024]{1,0:T(8,128)(2,1)S(1)}, u32[]{:S(2)}, u32[]{:S(2)}) collective-permute-start(bf16[256,1024]{1,0:T(8,128)(2,1)S(1)} %shard_map.94.refs_1_.g.refs_0_), channel_id=1, source_target_pairs={{8,0},{12,4},{16,8},{20,12},{24,16},{28,20},{9,1},{13,5},{17,9},{2... | collective-permute-start | bytes 1572872 | tf_op jit(solution)/shard_map/ppermute | solution.py:26
  25.1 1.4 %stage.1 = (bf16[256,1024]{1,0:T(8,128)(2,1)S(1)}, bf16[256,1024]{1,0:T(8,128)(2,1)S(1)}, bf16[256,1024]{1,0:T(8,128)(2,1)S(1)}) custom-call(bf16[256,1024]{1,0:T(8,128)(2,1)} %refs_0_.1, bf16[256,1024]{1,0:T(8,128)(2,1)} %refs_1_.3, bf16[256,1024]{1,0:T(8,128)(2,1)} %refs_2_.1), custom_call_target="tpu_custom_call" | custom-call | flops 1000000 | tf_op jit(solution)/shard_map/stage/pallas_call | solution.py:156
  26.5 0.0 collective-permute-done.4.refs_5_.refs_2_
  26.5 2.5 %collective-permute-done.5.refs_6_.refs_3_ = bf16[256,1024]{1,0:T(8,128)(2,1)S(1)} collective-permute-done((bf16[256,1024]{1,0:T(8,128)(2,1)}, bf16[256,1024]{1,0:T(8,128)(2,1)S(1)}, u32[]{:S(2)}, u32[]{:S(2)}) %collective-permute-start.5) | collective-permute-done | bytes 524320 | tf_op jit(solution)/shard_map/ppermute | solution.py:31
  29.0 3.2 %shard_map.95 = (f32[3,8,256]{2,1,0:T(8,128)S(1)}, f32[3,8,256]{2,1,0:T(8,128)S(1)}, f32[3,8,256]{2,1,0:T(8,128)S(1)}, f32[3,8,256]{2,1,0:T(8,128)S(1)}, f32[8,2...) custom-call(bf16[256,1024]{1,0:T(8,128)(2,1)S(1)} %get-tuple-element, ...), custom_call_target="tpu_custom_call" | custom-call | flops 671088640 | tf_op jit(solution)/shard_map/pallas_call | solution.py:51
  32.2 5.1 %collective-permute-done.6.v_up.refs_1_ = bf16[256,1024]{1,0:T(8,128)(2,1)S(1)} collective-permute-done((bf16[256,1024]{1,0:T(8,128)(2,1)}, bf16[256,1024]{1,0:T(8,128)(2,1)S(1)}, u32[]{:S(2)}, u32[]{:S(2)}) %collective-permute-start.6) | collective-permute-done | bytes 524320 | tf_op jit(solution)/shard_map/ppermute | solution.py:26
  37.3 1.0 %shard_map.96 = (f32[3,8,256]{2,1,0:T(8,128)S(1)}, f32[8,256,256]{2,1,0:T(8,128)S(1)}) custom-call(bf16[256,1024]{1,0:T(8,128)(2,1)S(1)} %shard_map.94.refs_1_.g.refs_0_, bf16[256,1024]{1,0:T(8,128)(2,1)S(1)} %collective-permute-done.6.v_up.refs_1_, f32[8,256,256]{2,1,0:T(8,128)S(1)} %get-tuple-element.54.probs.refs_6_, f32[3,8,256]{2,1,0:T(8,128)S(1)} %get-tuple-element.55.soft), custom_call_target="tpu_custom_call" | custom-call | flops 134217728 | tf_op jit(solution)/shard_map/pallas_call | solution.py:51
  38.3 0.0 copy-start
  38.3 0.0 copy-start.1
  38.3 1.2 %collective-permute-done.7.refs_1_.refs_2_ = bf16[256,1024]{1,0:T(8,128)(2,1)S(1)} collective-permute-done((bf16[256,1024]{1,0:T(8,128)(2,1)}, bf16[256,1024]{1,0:T(8,128)(2,1)S(1)}, u32[]{:S(2)}, u32[]{:S(2)}) %collective-permute-start.7) | collective-permute-done | bytes 524320 | tf_op jit(solution)/shard_map/ppermute | solution.py:31
  39.5 0.6 shard_map.100
  40.2 1.3 %collective-permute-start.10 = (f32[5,8,256]{2,1,0:T(8,128)S(1)}, f32[5,8,256]{2,1,0:T(8,128)S(1)}, u32[]{:S(2)}, u32[]{:S(2)}) collective-permute-start(f32[5,8,256]{2,1,0:T(8,128)S(1)} %shard_map.100), channel_id=1, source_target_pairs={{8,0},{12,4},{16,8},{20,12},{24,16},{28,20},{9,1},{13,5},{17,9},{2... | collective-permute-start | bytes 122888 | tf_op jit(solution)/shard_map/ppermute | solution.py:26
  41.5 0.0 collective-permute-done.8.refs_0_.refs_1_
  41.5 1.3 %shard_map.98 = (f32[6,8,256]{2,1,0:T(8,128)S(1)}, f32[8,256,256]{2,1,0:T(8,128)S(1)}, f32[8,256,256]{2,1,0:T(8,128)S(1)}) custom-call(bf16[256,1024]{1,0:T(8,128)(2,1)S(1)} %collective-permute-done.8.refs_0_.refs_1_, bf16[256,1024]{1,0:T(8,128)(2,1)S(1)} %collective-permute-done.6.v_up.refs_1_, ...), custom_call_target="tpu_custom_call", output_to_operand_aliasing={{2}: (7, {})} | custom-call | flops 268435456 | tf_op jit(solution)/shard_map/pallas_call | solution.py:51
  42.8 4.5 %collective-permute-start.9 = (f32[6,8,256]{2,1,0:T(8,128)S(1)}, f32[6,8,256]{2,1,0:T(8,128)S(1)}, u32[]{:S(2)}, u32[]{:S(2)}) collective-permute-start(f32[6,8,256]{2,1,0:T(8,128)S(1)} %get-tuple-element.63.refs_1_), channel_id=1, source_target_pairs={{0,8},{4,12},{8,16},{12,20},{16,24},{20,28},{1,9},{5,13},{9,17},{1... | collective-permute-start | bytes 147464 | tf_op jit(solution)/shard_map/ppermute | solution.py:26
  47.4 0.0 collective-permute-done.10.refs_0_
  47.4 2.6 %shard_map.102 = (bf16[256,1024]{1,0:T(8,128)(2,1)S(1)}, f32[256,1024]{1,0:T(8,128)S(1)}, f32[256,1024]{1,0:T(8,128)S(1)}, f32[256,1024]{1,0:T(8,128)S(1)}, f32[256,1024]{1,0:T(8,128)S(1)}) custom-call(bf16[256,1024]{1,0:T(8,128)(2,1)S(1)} %collective-permute-done.3.refs_4_.refs_0_, bf16[256,1024]{1,0:T(8,128)(2,1)S(1)} %collective-permute-done.8.refs_0_.refs_1_, ...), custom_call_target="tpu_custom_call" | custom-call | flops 805306368 | tf_op jit(solution)/shard_map/pallas_call | solution.py:51
  50.0 3.8 %collective-permute-start.11 = (bf16[256,1024]{1,0:T(8,128)(2,1)S(1)}, bf16[256,1024]{1,0:T(8,128)(2,1)S(1)}, u32[]{:S(2)}, u32[]{:S(2)}) collective-permute-start(bf16[256,1024]{1,0:T(8,128)(2,1)S(1)} %get-tuple-element.82), channel_id=1, source_target_pairs={{0,8},{4,12},{8,16},{12,20},{16,24},{20,28},{1,9},{5,13},{9,17},{1... | collective-permute-start | bytes 1572872 | tf_op jit(solution)/shard_map/ppermute | solution.py:26
  53.8 0.0 collective-permute-done.9.refs_5_
  53.8 0.7 shard_map.99
  54.5 0.4 shard_map.103
  54.9 0.9 %shard_map.104 = (f32[256,1024]{1,0:T(8,128)S(1)}, bf16[512,512]{1,0:T(8,128)(2,1)S(1)}, bf16[512,512]{1,0:T(8,128)(2,1)S(1)}) custom-call(bf16[256,1024]{1,0:T(8,128)(2,1)S(1)} %get-tuple-element.50.refs_0_.q, bf16[256,1024]{1,0:T(8,128)(2,1)S(1)} %shard_map.94.refs_1_.g.refs_0_, ...), custom_call_target="tpu_custom_call", output_to_operand_aliasing={{0}: (14, {})} | custom-call | flops 402653184 | tf_op jit(solution)/shard_map/pallas_call | solution.py:51
  55.9 1.3 %collective-permute-start.14 = (bf16[512,512]{1,0:T(8,128)(2,1)S(1)}, bf16[512,512]{1,0:T(8,128)(2,1)S(1)}, u32[]{:S(2)}, u32[]{:S(2)}) collective-permute-start(bf16[512,512]{1,0:T(8,128)(2,1)S(1)} %get-tuple-element.87), channel_id=1, source_target_pairs={{8,0},{12,4},{16,8},{20,12},{24,16},{28,20},{9,1},{13,5},{17,9},{2... | collective-permute-start | bytes 1572872 | tf_op jit(solution)/shard_map/ppermute | solution.py:26
  57.2 1.6 %collective-permute-start.15 = (bf16[512,512]{1,0:T(8,128)(2,1)S(1)}, bf16[512,512]{1,0:T(8,128)(2,1)S(1)}, u32[]{:S(2)}, u32[]{:S(2)}) collective-permute-start(bf16[512,512]{1,0:T(8,128)(2,1)S(1)} %get-tuple-element.88), channel_id=1, source_target_pairs={{0,4},{4,0},{8,12},{12,8},{16,20},{20,16},{24,28},{28,24},{1,5},{5... | collective-permute-start | bytes 1572872 | tf_op jit(solution)/shard_map/ppermute | solution.py:31
  58.7 1.3 %collective-permute-start.16 = (bf16[512,256]{1,0:T(8,128)(2,1)S(1)}, bf16[512,256]{1,0:T(8,128)(2,1)S(1)}, u32[]{:S(2)}, u32[]{:S(2)}) collective-permute-start(bf16[512,256]{1,0:T(8,128)(2,1)S(1)} %get-tuple-element.89), channel_id=1, source_target_pairs={{8,0},{12,4},{16,8},{20,12},{24,16},{28,20},{9,1},{13,5},{17,9},{2... | collective-permute-start | bytes 786440 | tf_op jit(solution)/shard_map/ppermute | solution.py:26
  60.0 0.6 collective-permute-start.17
  60.6 0.4 shard_map.105
  61.0 15.0 %collective-permute-done.16.refs_2_ = bf16[512,256]{1,0:T(8,128)(2,1)S(1)} collective-permute-done((bf16[512,256]{1,0:T(8,128)(2,1)S(1)}, bf16[512,256]{1,0:T(8,128)(2,1)S(1)}, u32[]{:S(2)}, u32[]{:S(2)}) %collective-permute-start.16) | collective-permute-done | bytes 262176 | tf_op jit(solution)/shard_map/ppermute | solution.py:26
  76.0 1.3 %collective-permute-start.12 = (bf16[512,256]{1,0:T(8,128)(2,1)S(1)}, bf16[512,256]{1,0:T(8,128)(2,1)S(1)}, u32[]{:S(2)}, u32[]{:S(2)}) collective-permute-start(bf16[512,256]{1,0:T(8,128)(2,1)S(1)} %get-tuple-element.85), channel_id=1, source_target_pairs={{8,0},{12,4},{16,8},{20,12},{24,16},{28,20},{9,1},{13,5},{17,9},{2... | collective-permute-start | bytes 786440 | tf_op jit(solution)/shard_map/ppermute | solution.py:26
  77.3 1.3 %collective-permute-start.13 = (bf16[512,256]{1,0:T(8,128)(2,1)S(1)}, bf16[512,256]{1,0:T(8,128)(2,1)S(1)}, u32[]{:S(2)}, u32[]{:S(2)}) collective-permute-start(bf16[512,256]{1,0:T(8,128)(2,1)S(1)} %get-tuple-element.86), channel_id=1, source_target_pairs={{0,4},{4,0},{8,12},{12,8},{16,20},{20,16},{24,28},{28,24},{1,5},{5... | collective-permute-start | bytes 786440 | tf_op jit(solution)/shard_map/ppermute | solution.py:31
  78.6 1.6 %shard_map.106 = (f32[256,1024]{1,0:T(8,128)S(1)}, f32[256,1024]{1,0:T(8,128)S(1)}, f32[256,1024]{1,0:T(8,128)S(1)}) custom-call(bf16[256,1024]{1,0:T(8,128)(2,1)S(1)} %get-tuple-element.50.refs_0_.q, bf16[256,1024]{1,0:T(8,128)(2,1)S(1)} %shard_map.94.refs_1_.g.refs_0_, bf16[256,1024]{1,0:T(8,128)(2,1)S(1)} %get-tuple-element.51.refs_2_.k, ...), custom_call_target="tpu_custom_call" | custom-call | flops 402653184 | tf_op jit(solution)/shard_map/pallas_call | solution.py:51
  80.2 0.8 shard_map.108
  80.9 1.4 %shard_map.107 = bf16[256,1024]{1,0:T(8,128)(2,1)} custom-call(f32[256,1024]{1,0:T(8,128)S(1)} %get-tuple-element.81.dq, bf16[256,1024]{1,0:T(8,128)(2,1)S(1)} %collective-permute-done.11.guest), custom_call_target="tpu_custom_call" | custom-call | flops 524288 | tf_op jit(solution)/shard_map/pallas_call | solution.py:51
  82.4 0.9 %shard_map.109 = (bf16[256,1024]{1,0:T(8,128)(2,1)}, bf16[256,1024]{1,0:T(8,128)(2,1)}) custom-call(f32[256,1024]{1,0:T(8,128)S(1)} %get-tuple-element.83.refs_0_, f32[256,1024]{1,0:T(8,128)S(1)} %get-tuple-element.84.refs_1_, bf16[512,512]{1,0:T(8,128)(2,1)S(1)} %collective-permute-done.14.refs_2_, ...), custom_call_target="tpu_custom_call", output_to_operand_aliasing={{0}: (4, {}), {1}: (5, {})} | custom-call | flops 33554432 | tf_op jit(solution)/shard_map/pallas_call | solution.py:51
  83.3 1.0 %collective-permute-done.12.refs_2_ = bf16[512,256]{1,0:T(8,128)(2,1)S(1)} collective-permute-done((bf16[512,256]{1,0:T(8,128)(2,1)S(1)}, bf16[512,256]{1,0:T(8,128)(2,1)S(1)}, u32[]{:S(2)}, u32[]{:S(2)}) %collective-permute-start.12) | collective-permute-done | bytes 262176 | tf_op jit(solution)/shard_map/ppermute | solution.py:26
  84.3 0.7 shard_map.110
  (10 shorter events, 0.1 us)
Async XLA Ops:
  0.6 9.6 %collective-permute-start.1 = (bf16[256,512]{1,0:T(8,128)(2,1)}, bf16[256,512]{1,0:T(8,128)(2,1)S(1)}, u32[]{:S(2)}, u32[]{:S(2)}) collective-permute-start(bf16[256,512]{1,0:T(8,128)(2,1)} %refs_3_.1), channel_id=1, source_target_pairs={{0,2},{1,3},{2,0},{3,1},{4,6},{5,7},{6,4},{7,5},{8,10},{9,11},{10,... | collective-permute-start | bytes 786440 | tf_op jit(solution)/shard_map/ppermute | solution.py:31
  3.7 20.1 %collective-permute-start.3 = (bf16[256,1024]{1,0:T(8,128)(2,1)}, bf16[256,1024]{1,0:T(8,128)(2,1)S(1)}, u32[]{:S(2)}, u32[]{:S(2)}) collective-permute-start(bf16[256,1024]{1,0:T(8,128)(2,1)} %refs_0_.1), channel_id=1, source_target_pairs={{8,0},{12,4},{16,8},{20,12},{24,16},{28,20},{9,1},{13,5},{17,9},{2... | collective-permute-start | bytes 1572872 | tf_op jit(solution)/shard_map/ppermute | solution.py:26
  5.0 10.5 %collective-permute-start = (bf16[256,512]{1,0:T(8,128)(2,1)}, bf16[256,512]{1,0:T(8,128)(2,1)S(1)}, u32[]{:S(2)}, u32[]{:S(2)}) collective-permute-start(bf16[256,512]{1,0:T(8,128)(2,1)} %refs_3_.1), channel_id=1, source_target_pairs={{0,1},{1,0},{2,3},{3,2},{4,5},{5,4},{6,7},{7,6},{8,9},{9,8},{10,11... | collective-permute-start | bytes 786440 | tf_op jit(solution)/shard_map/ppermute | solution.py:31
  10.2 8.8 %collective-permute-start.2 = (bf16[256,512]{1,0:T(8,128)(2,1)S(1)}, bf16[256,512]{1,0:T(8,128)(2,1)S(1)}, u32[]{:S(2)}, u32[]{:S(2)}) collective-permute-start(bf16[256,512]{1,0:T(8,128)(2,1)S(1)} %collective-permute-done.1.refs_1_), channel_id=1, source_target_pairs={{0,1},{1,0},{2,3},{3,2},{4,5},{5,4},{6,7},{7,6},{8,9},{9,8},{10,11... | collective-permute-start | bytes 786440 | tf_op jit(solution)/shard_map/ppermute | solution.py:31
  10.2 16.3 %collective-permute-start.4 = (bf16[256,1024]{1,0:T(8,128)(2,1)}, bf16[256,1024]{1,0:T(8,128)(2,1)S(1)}, u32[]{:S(2)}, u32[]{:S(2)}) collective-permute-start(bf16[256,1024]{1,0:T(8,128)(2,1)} %refs_1_.3), channel_id=1, source_target_pairs={{0,8},{4,12},{8,16},{12,20},{16,24},{20,28},{1,9},{5,13},{9,17},{1... | collective-permute-start | bytes 1572872 | tf_op jit(solution)/shard_map/ppermute | solution.py:26
  13.9 15.1 %collective-permute-start.5 = (bf16[256,1024]{1,0:T(8,128)(2,1)}, bf16[256,1024]{1,0:T(8,128)(2,1)S(1)}, u32[]{:S(2)}, u32[]{:S(2)}) collective-permute-start(bf16[256,1024]{1,0:T(8,128)(2,1)} %refs_1_.3), channel_id=1, source_target_pairs={{0,4},{4,0},{8,12},{12,8},{16,20},{20,16},{24,28},{28,24},{1,5},{5... | collective-permute-start | bytes 1572872 | tf_op jit(solution)/shard_map/ppermute | solution.py:31
  15.5 21.8 %collective-permute-start.6 = (bf16[256,1024]{1,0:T(8,128)(2,1)}, bf16[256,1024]{1,0:T(8,128)(2,1)S(1)}, u32[]{:S(2)}, u32[]{:S(2)}) collective-permute-start(bf16[256,1024]{1,0:T(8,128)(2,1)} %refs_2_.1), channel_id=1, source_target_pairs={{0,8},{4,12},{8,16},{12,20},{16,24},{20,28},{1,9},{5,13},{9,17},{1... | collective-permute-start | bytes 1572872 | tf_op jit(solution)/shard_map/ppermute | solution.py:26
  19.0 20.5 %collective-permute-start.7 = (bf16[256,1024]{1,0:T(8,128)(2,1)}, bf16[256,1024]{1,0:T(8,128)(2,1)S(1)}, u32[]{:S(2)}, u32[]{:S(2)}) collective-permute-start(bf16[256,1024]{1,0:T(8,128)(2,1)} %refs_2_.1), channel_id=1, source_target_pairs={{0,4},{4,0},{8,12},{12,8},{16,20},{20,16},{24,28},{28,24},{1,5},{5... | collective-permute-start | bytes 1572872 | tf_op jit(solution)/shard_map/ppermute | solution.py:31
  23.8 17.6 %collective-permute-start.8 = (bf16[256,1024]{1,0:T(8,128)(2,1)S(1)}, bf16[256,1024]{1,0:T(8,128)(2,1)S(1)}, u32[]{:S(2)}, u32[]{:S(2)}) collective-permute-start(bf16[256,1024]{1,0:T(8,128)(2,1)S(1)} %shard_map.94.refs_1_.g.refs_0_), channel_id=1, source_target_pairs={{8,0},{12,4},{16,8},{20,12},{24,16},{28,20},{9,1},{13,5},{17,9},{2... | collective-permute-start | bytes 1572872 | tf_op jit(solution)/shard_map/ppermute | solution.py:26
  38.3 1.2 %copy-start = (s32[8,3]{0,1:T(4,128)S(1)}, s32[8,3]{0,1:T(4,128)}, u32[]{:S(2)}) copy-start(s32[8,3]{0,1:T(4,128)} %param.12) | copy-start | bytes 292
  38.3 1.2 %copy-start.1 = (s32[1,3]{1,0:T(1,128)S(1)}, s32[1,3]{1,0:T(1,128)}, u32[]{:S(2)}) copy-start(s32[1,3]{1,0:T(1,128)} %refs_1_.5) | copy-start | bytes 40
  40.2 7.2 %collective-permute-start.10 = (f32[5,8,256]{2,1,0:T(8,128)S(1)}, f32[5,8,256]{2,1,0:T(8,128)S(1)}, u32[]{:S(2)}, u32[]{:S(2)}) collective-permute-start(f32[5,8,256]{2,1,0:T(8,128)S(1)} %shard_map.100), channel_id=1, source_target_pairs={{8,0},{12,4},{16,8},{20,12},{24,16},{28,20},{9,1},{13,5},{17,9},{2... | collective-permute-start | bytes 122888 | tf_op jit(solution)/shard_map/ppermute | solution.py:26
  42.8 11.0 %collective-permute-start.9 = (f32[6,8,256]{2,1,0:T(8,128)S(1)}, f32[6,8,256]{2,1,0:T(8,128)S(1)}, u32[]{:S(2)}, u32[]{:S(2)}) collective-permute-start(f32[6,8,256]{2,1,0:T(8,128)S(1)} %get-tuple-element.63.refs_1_), channel_id=1, source_target_pairs={{0,8},{4,12},{8,16},{12,20},{16,24},{20,28},{1,9},{5,13},{9,17},{1... | collective-permute-start | bytes 147464 | tf_op jit(solution)/shard_map/ppermute | solution.py:26
  50.0 30.9 %collective-permute-start.11 = (bf16[256,1024]{1,0:T(8,128)(2,1)S(1)}, bf16[256,1024]{1,0:T(8,128)(2,1)S(1)}, u32[]{:S(2)}, u32[]{:S(2)}) collective-permute-start(bf16[256,1024]{1,0:T(8,128)(2,1)S(1)} %get-tuple-element.82), channel_id=1, source_target_pairs={{0,8},{4,12},{8,16},{12,20},{16,24},{20,28},{1,9},{5,13},{9,17},{1... | collective-permute-start | bytes 1572872 | tf_op jit(solution)/shard_map/ppermute | solution.py:26
  55.9 26.5 %collective-permute-start.14 = (bf16[512,512]{1,0:T(8,128)(2,1)S(1)}, bf16[512,512]{1,0:T(8,128)(2,1)S(1)}, u32[]{:S(2)}, u32[]{:S(2)}) collective-permute-start(bf16[512,512]{1,0:T(8,128)(2,1)S(1)} %get-tuple-element.87), channel_id=1, source_target_pairs={{8,0},{12,4},{16,8},{20,12},{24,16},{28,20},{9,1},{13,5},{17,9},{2... | collective-permute-start | bytes 1572872 | tf_op jit(solution)/shard_map/ppermute | solution.py:26
  57.2 25.2 %collective-permute-start.15 = (bf16[512,512]{1,0:T(8,128)(2,1)S(1)}, bf16[512,512]{1,0:T(8,128)(2,1)S(1)}, u32[]{:S(2)}, u32[]{:S(2)}) collective-permute-start(bf16[512,512]{1,0:T(8,128)(2,1)S(1)} %get-tuple-element.88), channel_id=1, source_target_pairs={{0,4},{4,0},{8,12},{12,8},{16,20},{20,16},{24,28},{28,24},{1,5},{5... | collective-permute-start | bytes 1572872 | tf_op jit(solution)/shard_map/ppermute | solution.py:31
  58.7 17.3 %collective-permute-start.16 = (bf16[512,256]{1,0:T(8,128)(2,1)S(1)}, bf16[512,256]{1,0:T(8,128)(2,1)S(1)}, u32[]{:S(2)}, u32[]{:S(2)}) collective-permute-start(bf16[512,256]{1,0:T(8,128)(2,1)S(1)} %get-tuple-element.89), channel_id=1, source_target_pairs={{8,0},{12,4},{16,8},{20,12},{24,16},{28,20},{9,1},{13,5},{17,9},{2... | collective-permute-start | bytes 786440 | tf_op jit(solution)/shard_map/ppermute | solution.py:26
  60.0 17.3 %collective-permute-start.17 = (bf16[512,256]{1,0:T(8,128)(2,1)S(1)}, bf16[512,256]{1,0:T(8,128)(2,1)S(1)}, u32[]{:S(2)}, u32[]{:S(2)}) collective-permute-start(bf16[512,256]{1,0:T(8,128)(2,1)S(1)} %get-tuple-element.90), channel_id=1, source_target_pairs={{0,4},{4,0},{8,12},{12,8},{16,20},{20,16},{24,28},{28,24},{1,5},{5... | collective-permute-start | bytes 786440 | tf_op jit(solution)/shard_map/ppermute | solution.py:31
  76.0 8.3 %collective-permute-start.12 = (bf16[512,256]{1,0:T(8,128)(2,1)S(1)}, bf16[512,256]{1,0:T(8,128)(2,1)S(1)}, u32[]{:S(2)}, u32[]{:S(2)}) collective-permute-start(bf16[512,256]{1,0:T(8,128)(2,1)S(1)} %get-tuple-element.85), channel_id=1, source_target_pairs={{8,0},{12,4},{16,8},{20,12},{24,16},{28,20},{9,1},{13,5},{17,9},{2... | collective-permute-start | bytes 786440 | tf_op jit(solution)/shard_map/ppermute | solution.py:26
  77.3 7.0 %collective-permute-start.13 = (bf16[512,256]{1,0:T(8,128)(2,1)S(1)}, bf16[512,256]{1,0:T(8,128)(2,1)S(1)}, u32[]{:S(2)}, u32[]{:S(2)}) collective-permute-start(bf16[512,256]{1,0:T(8,128)(2,1)S(1)} %get-tuple-element.86), channel_id=1, source_target_pairs={{0,4},{4,0},{8,12},{12,8},{16,20},{20,16},{24,28},{28,24},{1,5},{5... | collective-permute-start | bytes 786440 | tf_op jit(solution)/shard_map/ppermute | solution.py:31

commit v8 on v7

--- a/solution.py
+++ b/solution.py
@@ -290,36 +290,35 @@
         out[1] = delta
 
 
-def combine_local_kernel(spans, t, a, own, mid, near, out):
+def bias_kernel(spans, t, a, out):
     flags = Flags(spans, t, a)
-
-    def run(odd):
-        shape = own.shape[1:]
-        near_bias = flags.bias(NEAR, shape)
-        parts = [part_of(own), part_of(mid, flags.bias(MID, shape))]
+    for section in range(SECTIONS):
+        out[section] = flags.bias(section, out.shape[1:])
+
+
+def combine_local_kernel(near_span, bias, own, mid, near, out):
+    def run(odd):
+        near_bias = bias[NEAR]
+        parts = [part_of(own), part_of(mid, bias[MID])]
         if odd:
             parts.append(part_of(near, near_bias))
-            near_bias = jnp.full(shape, -BIG, jnp.float32)
+            near_bias = jnp.full(near_bias.shape, -BIG, jnp.float32)
         merged, _ = merge(parts)
-        for index, row in enumerate((*merged, flags.bias(FAR, shape), near_bias)):
+        for index, row in enumerate((*merged, bias[FAR], near_bias)):
             out[index] = row
 
-    by_parity(spans[NEAR], run)
-
-
-def combine_own_kernel(spans, t, a, own, mid, near, up, *outs):
-    flags = Flags(spans, t, a)
-
-    def run(odd):
-        shape = own.shape[1:]
-        near_bias = flags.bias(NEAR, shape)
-        parts = [part_of(own), part_of(mid, flags.bias(MID, shape))]
-        parts.append(part_of(near, near_bias) if odd else part_of(up, near_bias, 3))
-        parts.append(part_of(up, flags.bias(FAR, shape)))
+    by_parity(near_span, run)
+
+
+def combine_own_kernel(near_span, bias, own, mid, near, up, *outs):
+    def run(odd):
+        parts = [part_of(own), part_of(mid, bias[MID])]
+        parts.append(part_of(near, bias[NEAR]) if odd else part_of(up, bias[NEAR], 3))
+        parts.append(part_of(up, bias[FAR]))
         merged, factors = merge(parts)
         put_norm(outs if odd else outs[:2], factors, merged)
 
-    by_parity(spans[NEAR], run)
+    by_parity(near_span, run)
 
 
 def combine_guest_kernel(near_span, guest, up, far_out, near_out):
@@ -354,24 +353,25 @@
 
 
 def guest_terms_kernel(
-    near_span, q, g, k_up, k_x, norm_far, norm_near, pr_far, pg_far, pr_near, pg_near,
-    dq, dk_far, dv_far, dk_near, dv_near,
+    near_span, first, q, g, k_up, k_x, norm_far, norm_near, pr_far, pg_far, pr_near, pg_near, *refs
 ):
+    dq, dk_far, dv_far, dk_near, dv_near = refs[-5:]
+
     def run(odd):
         def step(head):
-            at = columns(head)
+            at, out = columns(head), columns(head - first)
             query, grad = q[:, at], g[:, at]
-            query_term, dk_far[:, at], dv_far[:, at] = pair_terms(
+            query_term, dk_far[:, out], dv_far[:, out] = pair_terms(
                 head, query, grad, k_up[:, at], pr_far, pg_far, norm_far
             )
             if not odd:
-                more, dk_near[:, at], dv_near[:, at] = pair_terms(
+                more, dk_near[:, out], dv_near[:, out] = pair_terms(
                     head, query, grad, k_x[:, at], pr_near, pg_near, norm_near
                 )
                 query_term = query_term + more
             dq[:, at] = (query_term * SCALE).T.astype(dq.dtype)
 
-        each_head(0, pr_far.shape[0], step)
+        each_head(first, dk_far.shape[1] // HDIM, step)
 
     by_parity(near_span, run)
 
@@ -390,15 +390,15 @@
             query_term, key_term, value_term = pair_terms(
                 head, query, grad, k_up[:, at], pr_mid, pg_mid, norm_mid
             )
-            back[:rows, out] = ((key_term + dk_far[:, at]) * SCALE).astype(back.dtype)
-            back[rows:, out] = (value_term + dv_far[:, at]).astype(back.dtype)
+            back[:rows, out] = ((key_term + dk_far[:, out]) * SCALE).astype(back.dtype)
+            back[rows:, out] = (value_term + dv_far[:, out]).astype(back.dtype)
             if odd:
                 more, key_term, value_term = pair_terms(
                     head, query, grad, k_x[:, at], pr_near, pg_near, norm_near
                 )
                 query_term = query_term + more
             else:
-                key_term, value_term = dk_near[:, at], dv_near[:, at]
+                key_term, value_term = dk_near[:, out], dv_near[:, out]
             cross[:rows, out] = (key_term * SCALE).astype(cross.dtype)
             cross[rows:, out] = value_term.astype(cross.dtype)
             dq[:, at] = query_term.T
@@ -468,6 +468,7 @@
     guest_grad = shift(grads, -mid_span)
     query, key, value = staged(queries, key_rows, value_rows)
 
+    (bias,) = call(bound(bias_kernel, spans), flags, [], [stat], row_work)
     self_stats, mid_soft, far_soft, near_soft, *probs, self_pgrad = call(
         bound(soft_kernel, near_span),
         [],
@@ -485,9 +486,9 @@
         bound(delta_near_kernel, near_span), grads, value_x, near_prob, near_soft
     )
     (merged,) = call(
-        bound(combine_local_kernel, spans),
-        flags,
-        [self_stats, mid_stats, near_stats],
+        bound(combine_local_kernel, near_span),
+        [],
+        [bias, self_stats, mid_stats, near_stats],
         [table(5)],
         row_work,
     )
@@ -506,26 +507,29 @@
         bound(combine_guest_kernel, near_span), [], [guest_stats, up_part], [norm] * 2, row_work
     )
     near_squares = [near_prob, near_pgrad]
-    ins = [guest_query, guest_grad, key_up, key_x, far_norm, near_norm_guest]
-    guest_part, *guest_terms = call(
-        bound(guest_terms_kernel, near_span),
+    self_norm, mid_norm, near_norm = call(
+        bound(combine_own_kernel, near_span),
         [],
-        [*ins, far_prob, far_pgrad, *near_squares],
-        [wide_bf16] + [wide_f32] * 4,
-        heads * 6 * pair_work,
-    )
-    self_norm, mid_norm, near_norm = call(
-        bound(combine_own_kernel, spans),
-        flags,
-        [self_stats, mid_stats, near_stats, up_stats],
+        [bias, self_stats, mid_stats, near_stats, up_stats],
         [norm] * 3,
         row_work,
     )
-    query_part, returned = [], []
+    guest_part, query_part, returned = [], [], []
     first = 0
     for group in GROUPS:
+        narrow = (rows, group * HDIM)
+        ins = [guest_query, guest_grad, key_up, key_x, far_norm, near_norm_guest]
+        ins += [far_prob, far_pgrad, *near_squares]
+        *guest_part, far_key, far_value, near_key, near_value = call(
+            bound(guest_terms_kernel, near_span, first),
+            [],
+            ins + guest_part,
+            [wide_bf16] + [(narrow, jnp.float32)] * 4,
+            group * 6 * pair_work,
+            {len(ins): 0} if guest_part else {},
+        )
         ins = [query, grads, key_up, key_x, mid_norm, near_norm, mid_prob, mid_pgrad]
-        ins += [*near_squares, *guest_terms]
+        ins += [*near_squares, far_key, far_value, near_key, near_value]
         half = ((2 * rows, group * HDIM), jnp.bfloat16)
         *query_part, back, cross = call(
             bound(own_terms_kernel, near_span, first),
@@ -535,9 +539,10 @@
             group * 6 * pair_work,
             {len(ins): 0} if query_part else {},
         )
-        cross = swap(cross, "seq", near_span)
-        returned.append((shift(back, -mid_span), cross))
+        back = shift(back, -mid_span)
+        returned.append((back, swap(cross, "seq", near_span)))
         first += group
+    (guest_part,) = guest_part
     guest_part = shift(guest_part, mid_span)
     query_sum, *self_terms = call(
         self_kernel,

time: 85.5 us -> 83.5 us (0.977)
  waiting for transfers between devices: 29.9 us -> 28.3 us
    ppermute x10, waiting for transfers between devices: 21.1 us -> 20.1 us  [shift(): lax.ppermute(value, 'seq', [(src, src + steps) for src in range(low, high)])]
    pallas_call x17 -> x20, Pallas kernels: 20.9 us -> 20.1 us  [call(): pl.pallas_call(kernel, grid=grid or (), in_specs=[smem] * len(scalars) +...]
where the time goes in v8:
time: 83.5 us; the launch traced here: 83.1 us
  starting transfers between devices  32.4 us (39%)
  waiting for transfers between devices  28.3 us (34%)
  Pallas kernels  21.5 us (26%)
  between operations  0.92 us (1%)
    ppermute x10, starting transfers between devices, shift(): lax.ppermute(value, 'seq', [(src, src + steps) for src in range(low, high)])  23 us
    pallas_call x20, Pallas kernels, call(): pl.pallas_call(kernel, grid=grid or (), in_specs=[smem] * len(scalars) +...  20.1 us
    ppermute x10, waiting for transfers between devices, shift(): lax.ppermute(value, 'seq', [(src, src + steps) for src in range(low, high)])  20.1 us
    ppermute x8, starting transfers between devices, swap(): return lax.ppermute(value, axis, pairs)  9.48 us
    ppermute x8, waiting for transfers between devices, swap(): return lax.ppermute(value, axis, pairs)  8.2 us
  transfers between devices with their start and end apart: 18, of which 6 were waited for; matrix products, arithmetic and copies ran while one was open for 0% of the time, Pallas kernels for 25%

profile of v8, /device:TPU:0, one launch (start us, length us, event | category | flops | bytes accessed | tf_op | source)
XLA Modules:
  0.0 83.1 jit_solution(9347913411291736437)
XLA Ops:
  0.7 3.1 %collective-permute-start.1 = (bf16[256,512]{1,0:T(8,128)(2,1)}, bf16[256,512]{1,0:T(8,128)(2,1)S(1)}, u32[]{:S(2)}, u32[]{:S(2)}) collective-permute-start(bf16[256,512]{1,0:T(8,128)(2,1)} %refs_3_.1), channel_id=1, source_target_pairs={{0,2},{1,3},{2,0},{3,1},{4,6},{5,7},{6,4},{7,5},{8,10},{9,11},{10,... | collective-permute-start | bytes 786440 | tf_op jit(solution)/shard_map/ppermute | solution.py:31
  3.7 1.3 %collective-permute-start.3 = (bf16[256,1024]{1,0:T(8,128)(2,1)}, bf16[256,1024]{1,0:T(8,128)(2,1)S(1)}, u32[]{:S(2)}, u32[]{:S(2)}) collective-permute-start(bf16[256,1024]{1,0:T(8,128)(2,1)} %refs_0_.1), channel_id=1, source_target_pairs={{8,0},{12,4},{16,8},{20,12},{24,16},{28,20},{9,1},{13,5},{17,9},{2... | collective-permute-start | bytes 1572872 | tf_op jit(solution)/shard_map/ppermute | solution.py:26
  5.0 0.1 collective-permute-start
  5.1 5.1 %collective-permute-done.1.refs_1_ = bf16[256,512]{1,0:T(8,128)(2,1)S(1)} collective-permute-done((bf16[256,512]{1,0:T(8,128)(2,1)}, bf16[256,512]{1,0:T(8,128)(2,1)S(1)}, u32[]{:S(2)}, u32[]{:S(2)}) %collective-permute-start.1) | collective-permute-done | bytes 262176 | tf_op jit(solution)/shard_map/ppermute | solution.py:31
  10.2 3.7 %collective-permute-start.4 = (bf16[256,1024]{1,0:T(8,128)(2,1)}, bf16[256,1024]{1,0:T(8,128)(2,1)S(1)}, u32[]{:S(2)}, u32[]{:S(2)}) collective-permute-start(bf16[256,1024]{1,0:T(8,128)(2,1)} %refs_1_.2), channel_id=1, source_target_pairs={{0,8},{4,12},{8,16},{12,20},{16,24},{20,28},{1,9},{5,13},{9,17},{1... | collective-permute-start | bytes 1572872 | tf_op jit(solution)/shard_map/ppermute | solution.py:26
  14.0 1.6 %collective-permute-start.5 = (bf16[256,1024]{1,0:T(8,128)(2,1)}, bf16[256,1024]{1,0:T(8,128)(2,1)S(1)}, u32[]{:S(2)}, u32[]{:S(2)}) collective-permute-start(bf16[256,1024]{1,0:T(8,128)(2,1)} %refs_1_.2), channel_id=1, source_target_pairs={{0,4},{4,0},{8,12},{12,8},{16,20},{20,16},{24,28},{28,24},{1,5},{5... | collective-permute-start | bytes 1572872 | tf_op jit(solution)/shard_map/ppermute | solution.py:31
  15.5 3.5 %collective-permute-start.6 = (bf16[256,1024]{1,0:T(8,128)(2,1)}, bf16[256,1024]{1,0:T(8,128)(2,1)S(1)}, u32[]{:S(2)}, u32[]{:S(2)}) collective-permute-start(bf16[256,1024]{1,0:T(8,128)(2,1)} %refs_2_.1), channel_id=1, source_target_pairs={{0,8},{4,12},{8,16},{12,20},{16,24},{20,28},{1,9},{5,13},{9,17},{1... | collective-permute-start | bytes 1572872 | tf_op jit(solution)/shard_map/ppermute | solution.py:26
  19.0 0.6 collective-permute-start.7
  19.6 4.2 %shard_map.94.refs_1_.g.refs_0_ = bf16[256,1024]{1,0:T(8,128)(2,1)S(1)} custom-call(bf16[256,512]{1,0:T(8,128)(2,1)S(1)} %collective-permute-done.refs_0_, bf16[256,512]{1,0:T(8,128)(2,1)S(1)} %collective-permute-done.1.refs_1_, bf16[256,512]{1,0:T(8,128)(2,1)S(1)} %collective-permute-done.2.refs_2_, bf16[256,512]{1,0:T(8,128)(2,1)} %refs_3_.1, ...), custom_call_target="tpu_custom_call" | custom-call | flops 1073741824 | tf_op jit(solution)/shard_map/pallas_call | solution.py:51
  23.8 0.0 collective-permute-done.3.refs_4_.refs_0_
  23.8 1.3 %collective-permute-start.8 = (bf16[256,1024]{1,0:T(8,128)(2,1)S(1)}, bf16[256,1024]{1,0:T(8,128)(2,1)S(1)}, u32[]{:S(2)}, u32[]{:S(2)}) collective-permute-start(bf16[256,1024]{1,0:T(8,128)(2,1)S(1)} %shard_map.94.refs_1_.g.refs_0_), channel_id=1, source_target_pairs={{8,0},{12,4},{16,8},{20,12},{24,16},{28,20},{9,1},{13,5},{17,9},{2... | collective-permute-start | bytes 1572872 | tf_op jit(solution)/shard_map/ppermute | solution.py:26
  25.2 0.6 shard_map.95.refs_0_
  25.8 1.4 %stage.1 = (bf16[256,1024]{1,0:T(8,128)(2,1)S(1)}, bf16[256,1024]{1,0:T(8,128)(2,1)S(1)}, bf16[256,1024]{1,0:T(8,128)(2,1)S(1)}) custom-call(bf16[256,1024]{1,0:T(8,128)(2,1)} %refs_0_.1, bf16[256,1024]{1,0:T(8,128)(2,1)} %refs_1_.2, bf16[256,1024]{1,0:T(8,128)(2,1)} %refs_2_.1), custom_call_target="tpu_custom_call" | custom-call | flops 1000000 | tf_op jit(solution)/shard_map/stage/pallas_call | solution.py:156
  27.2 0.0 collective-permute-done.4.refs_5_.refs_2_
  27.2 1.8 %collective-permute-done.5.refs_6_.refs_3_ = bf16[256,1024]{1,0:T(8,128)(2,1)S(1)} collective-permute-done((bf16[256,1024]{1,0:T(8,128)(2,1)}, bf16[256,1024]{1,0:T(8,128)(2,1)S(1)}, u32[]{:S(2)}, u32[]{:S(2)}) %collective-permute-start.5) | collective-permute-done | bytes 524320 | tf_op jit(solution)/shard_map/ppermute | solution.py:31
  29.0 3.2 %shard_map.96 = (f32[3,8,256]{2,1,0:T(8,128)S(1)}, f32[3,8,256]{2,1,0:T(8,128)S(1)}, f32[3,8,256]{2,1,0:T(8,128)S(1)}, f32[3,8,256]{2,1,0:T(8,128)S(1)}, f32[8,2...) custom-call(bf16[256,1024]{1,0:T(8,128)(2,1)S(1)} %get-tuple-element, ...), custom_call_target="tpu_custom_call" | custom-call | flops 671088640 | tf_op jit(solution)/shard_map/pallas_call | solution.py:51
  32.3 5.1 %collective-permute-done.6.v_up.refs_1_ = bf16[256,1024]{1,0:T(8,128)(2,1)S(1)} collective-permute-done((bf16[256,1024]{1,0:T(8,128)(2,1)}, bf16[256,1024]{1,0:T(8,128)(2,1)S(1)}, u32[]{:S(2)}, u32[]{:S(2)}) %collective-permute-start.6) | collective-permute-done | bytes 524320 | tf_op jit(solution)/shard_map/ppermute | solution.py:26
  37.3 1.0 %shard_map.97 = (f32[3,8,256]{2,1,0:T(8,128)S(1)}, f32[8,256,256]{2,1,0:T(8,128)S(1)}) custom-call(bf16[256,1024]{1,0:T(8,128)(2,1)S(1)} %shard_map.94.refs_1_.g.refs_0_, bf16[256,1024]{1,0:T(8,128)(2,1)S(1)} %collective-permute-done.6.v_up.refs_1_, f32[8,256,256]{2,1,0:T(8,128)S(1)} %get-tuple-element.64.probs.refs_6_, f32[3,8,256]{2,1,0:T(8,128)S(1)} %get-tuple-element.65.soft), custom_call_target="tpu_custom_call" | custom-call | flops 134217728 | tf_op jit(solution)/shard_map/pallas_call | solution.py:51
  38.3 1.2 %collective-permute-done.7.refs_1_.refs_2_ = bf16[256,1024]{1,0:T(8,128)(2,1)S(1)} collective-permute-done((bf16[256,1024]{1,0:T(8,128)(2,1)}, bf16[256,1024]{1,0:T(8,128)(2,1)S(1)}, u32[]{:S(2)}, u32[]{:S(2)}) %collective-permute-start.7) | collective-permute-done | bytes 524320 | tf_op jit(solution)/shard_map/ppermute | solution.py:31
  39.5 1.3 %collective-permute-start.10 = (f32[5,8,256]{2,1,0:T(8,128)S(1)}, f32[5,8,256]{2,1,0:T(8,128)S(1)}, u32[]{:S(2)}, u32[]{:S(2)}) collective-permute-start(f32[5,8,256]{2,1,0:T(8,128)S(1)} %shard_map.101), channel_id=1, source_target_pairs={{8,0},{12,4},{16,8},{20,12},{24,16},{28,20},{9,1},{13,5},{17,9},{2... | collective-permute-start | bytes 122888 | tf_op jit(solution)/shard_map/ppermute | solution.py:26
  40.8 0.0 collective-permute-done.8.refs_0_.refs_1_
  40.9 1.3 %shard_map.99 = (f32[6,8,256]{2,1,0:T(8,128)S(1)}, f32[8,256,256]{2,1,0:T(8,128)S(1)}, f32[8,256,256]{2,1,0:T(8,128)S(1)}) custom-call(bf16[256,1024]{1,0:T(8,128)(2,1)S(1)} %collective-permute-done.8.refs_0_.refs_1_, bf16[256,1024]{1,0:T(8,128)(2,1)S(1)} %collective-permute-done.6.v_up.refs_1_, ...), custom_call_target="tpu_custom_call", output_to_operand_aliasing={{2}: (7, {})} | custom-call | flops 268435456 | tf_op jit(solution)/shard_map/pallas_call | solution.py:51
  42.2 4.5 %collective-permute-start.9 = (f32[6,8,256]{2,1,0:T(8,128)S(1)}, f32[6,8,256]{2,1,0:T(8,128)S(1)}, u32[]{:S(2)}, u32[]{:S(2)}) collective-permute-start(f32[6,8,256]{2,1,0:T(8,128)S(1)} %get-tuple-element.73.refs_1_), channel_id=1, source_target_pairs={{0,8},{4,12},{8,16},{12,20},{16,24},{20,28},{1,9},{5,13},{9,17},{1... | collective-permute-start | bytes 147464 | tf_op jit(solution)/shard_map/ppermute | solution.py:26
  46.7 0.0 collective-permute-done.10.refs_0_
  46.8 0.6 shard_map.103
  47.5 1.3 %shard_map.104 = (bf16[256,1024]{1,0:T(8,128)(2,1)S(1)}, f32[256,512]{1,0:T(8,128)S(1)}, f32[256,512]{1,0:T(8,128)S(1)}, f32[256,512]{1,0:T(8,128)S(1)}, f32[256,512]{1,0:T(8,128)S(1)}) custom-call(bf16[256,1024]{1,0:T(8,128)(2,1)S(1)} %collective-permute-done.3.refs_4_.refs_0_, ...), custom_call_target="tpu_custom_call", output_to_operand_aliasing={{0}: (10, {})} | custom-call | flops 402653184 | tf_op jit(solution)/shard_map/pallas_call | solution.py:51
  48.8 0.6 shard_map.105
  49.4 3.5 %collective-permute-start.11 = (bf16[256,1024]{1,0:T(8,128)(2,1)S(1)}, bf16[256,1024]{1,0:T(8,128)(2,1)S(1)}, u32[]{:S(2)}, u32[]{:S(2)}) collective-permute-start(bf16[256,1024]{1,0:T(8,128)(2,1)S(1)} %get-tuple-element.102), channel_id=1, source_target_pairs={{0,8},{4,12},{8,16},{12,20},{16,24},{20,28},{1,9},{5,13},{9,17},{1... | collective-permute-start | bytes 1572872 | tf_op jit(solution)/shard_map/ppermute | solution.py:26
  52.9 0.0 collective-permute-done.9.refs_4_
  53.0 0.4 shard_map.106
  53.4 0.8 %shard_map.107 = (f32[256,1024]{1,0:T(8,128)S(1)}, bf16[512,512]{1,0:T(8,128)(2,1)S(1)}, bf16[512,512]{1,0:T(8,128)(2,1)S(1)}) custom-call(bf16[256,1024]{1,0:T(8,128)(2,1)S(1)} %get-tuple-element.60.refs_0_.q, bf16[256,1024]{1,0:T(8,128)(2,1)S(1)} %shard_map.94.refs_1_.g.refs_0_, ...), custom_call_target="tpu_custom_call", output_to_operand_aliasing={{0}: (14, {})} | custom-call | flops 402653184 | tf_op jit(solution)/shard_map/pallas_call | solution.py:51
  54.2 1.3 %collective-permute-start.14 = (bf16[512,512]{1,0:T(8,128)(2,1)S(1)}, bf16[512,512]{1,0:T(8,128)(2,1)S(1)}, u32[]{:S(2)}, u32[]{:S(2)}) collective-permute-start(bf16[512,512]{1,0:T(8,128)(2,1)S(1)} %get-tuple-element.107), channel_id=1, source_target_pairs={{8,0},{12,4},{16,8},{20,12},{24,16},{28,20},{9,1},{13,5},{17,9},{2... | collective-permute-start | bytes 1572872 | tf_op jit(solution)/shard_map/ppermute | solution.py:26
  55.5 2.0 %collective-permute-start.15 = (bf16[512,512]{1,0:T(8,128)(2,1)S(1)}, bf16[512,512]{1,0:T(8,128)(2,1)S(1)}, u32[]{:S(2)}, u32[]{:S(2)}) collective-permute-start(bf16[512,512]{1,0:T(8,128)(2,1)S(1)} %get-tuple-element.108), channel_id=1, source_target_pairs={{0,4},{4,0},{8,12},{12,8},{16,20},{20,16},{24,28},{28,24},{1,5},{5... | collective-permute-start | bytes 1572872 | tf_op jit(solution)/shard_map/ppermute | solution.py:31
  57.6 1.3 %collective-permute-start.16 = (bf16[512,256]{1,0:T(8,128)(2,1)S(1)}, bf16[512,256]{1,0:T(8,128)(2,1)S(1)}, u32[]{:S(2)}, u32[]{:S(2)}) collective-permute-start(bf16[512,256]{1,0:T(8,128)(2,1)S(1)} %get-tuple-element.109), channel_id=1, source_target_pairs={{8,0},{12,4},{16,8},{20,12},{24,16},{28,20},{9,1},{13,5},{17,9},{2... | collective-permute-start | bytes 786440 | tf_op jit(solution)/shard_map/ppermute | solution.py:26
  58.8 0.1 collective-permute-start.17
  59.0 0.4 shard_map.108
  59.4 14.7 %collective-permute-done.16.refs_2_ = bf16[512,256]{1,0:T(8,128)(2,1)S(1)} collective-permute-done((bf16[512,256]{1,0:T(8,128)(2,1)S(1)}, bf16[512,256]{1,0:T(8,128)(2,1)S(1)}, u32[]{:S(2)}, u32[]{:S(2)}) %collective-permute-start.16) | collective-permute-done | bytes 262176 | tf_op jit(solution)/shard_map/ppermute | solution.py:26
  74.1 1.3 %collective-permute-start.12 = (bf16[512,256]{1,0:T(8,128)(2,1)S(1)}, bf16[512,256]{1,0:T(8,128)(2,1)S(1)}, u32[]{:S(2)}, u32[]{:S(2)}) collective-permute-start(bf16[512,256]{1,0:T(8,128)(2,1)S(1)} %get-tuple-element.105), channel_id=1, source_target_pairs={{8,0},{12,4},{16,8},{20,12},{24,16},{28,20},{9,1},{13,5},{17,9},{2... | collective-permute-start | bytes 786440 | tf_op jit(solution)/shard_map/ppermute | solution.py:26
  75.4 0.0 collective-permute-done.17.refs_3_
  75.4 2.0 %collective-permute-start.13 = (bf16[512,256]{1,0:T(8,128)(2,1)S(1)}, bf16[512,256]{1,0:T(8,128)(2,1)S(1)}, u32[]{:S(2)}, u32[]{:S(2)}) collective-permute-start(bf16[512,256]{1,0:T(8,128)(2,1)S(1)} %get-tuple-element.106), channel_id=1, source_target_pairs={{0,4},{4,0},{8,12},{12,8},{16,20},{20,16},{24,28},{28,24},{1,5},{5... | collective-permute-start | bytes 786440 | tf_op jit(solution)/shard_map/ppermute | solution.py:31
  77.4 1.6 %shard_map.109 = (f32[256,1024]{1,0:T(8,128)S(1)}, f32[256,1024]{1,0:T(8,128)S(1)}, f32[256,1024]{1,0:T(8,128)S(1)}) custom-call(bf16[256,1024]{1,0:T(8,128)(2,1)S(1)} %get-tuple-element.60.refs_0_.q, bf16[256,1024]{1,0:T(8,128)(2,1)S(1)} %shard_map.94.refs_1_.g.refs_0_, bf16[256,1024]{1,0:T(8,128)(2,1)S(1)} %get-tuple-element.61.refs_2_.k, ...), custom_call_target="tpu_custom_call" | custom-call | flops 402653184 | tf_op jit(solution)/shard_map/pallas_call | solution.py:51
  79.0 0.8 shard_map.111
  79.8 0.0 collective-permute-done.11.guest
  79.8 1.4 %shard_map.110 = bf16[256,1024]{1,0:T(8,128)(2,1)} custom-call(f32[256,1024]{1,0:T(8,128)S(1)} %get-tuple-element.101.dq, bf16[256,1024]{1,0:T(8,128)(2,1)S(1)} %collective-permute-done.11.guest), custom_call_target="tpu_custom_call" | custom-call | flops 524288 | tf_op jit(solution)/shard_map/pallas_call | solution.py:51
  81.2 0.9 %shard_map.112 = (bf16[256,1024]{1,0:T(8,128)(2,1)}, bf16[256,1024]{1,0:T(8,128)(2,1)}) custom-call(f32[256,1024]{1,0:T(8,128)S(1)} %get-tuple-element.103.refs_0_, f32[256,1024]{1,0:T(8,128)S(1)} %get-tuple-element.104.refs_1_, bf16[512,512]{1,0:T(8,128)(2,1)S(1)} %collective-permute-done.14.refs_2_, ...), custom_call_target="tpu_custom_call", output_to_operand_aliasing={{0}: (4, {}), {1}: (5, {})} | custom-call | flops 33554432 | tf_op jit(solution)/shard_map/pallas_call | solution.py:51
  82.1 0.3 collective-permute-done.12.refs_2_
  82.4 0.0 collective-permute-done.13.refs_3_
  82.4 0.7 shard_map.113
  (13 shorter events, 0.1 us)
Async XLA Ops:
  0.6 24.5 %copy-start = (s32[8,3]{0,1:T(4,128)S(1)}, s32[8,3]{0,1:T(4,128)}, u32[]{:S(2)}) copy-start(s32[8,3]{0,1:T(4,128)} %param.12) | copy-start | bytes 292
  0.6 24.5 %copy-start.1 = (s32[1,3]{1,0:T(1,128)S(1)}, s32[1,3]{1,0:T(1,128)}, u32[]{:S(2)}) copy-start(s32[1,3]{1,0:T(1,128)} %refs_1_.3) | copy-start | bytes 40
  0.7 9.6 %collective-permute-start.1 = (bf16[256,512]{1,0:T(8,128)(2,1)}, bf16[256,512]{1,0:T(8,128)(2,1)S(1)}, u32[]{:S(2)}, u32[]{:S(2)}) collective-permute-start(bf16[256,512]{1,0:T(8,128)(2,1)} %refs_3_.1), channel_id=1, source_target_pairs={{0,2},{1,3},{2,0},{3,1},{4,6},{5,7},{6,4},{7,5},{8,10},{9,11},{10,... | collective-permute-start | bytes 786440 | tf_op jit(solution)/shard_map/ppermute | solution.py:31
  3.7 20.1 %collective-permute-start.3 = (bf16[256,1024]{1,0:T(8,128)(2,1)}, bf16[256,1024]{1,0:T(8,128)(2,1)S(1)}, u32[]{:S(2)}, u32[]{:S(2)}) collective-permute-start(bf16[256,1024]{1,0:T(8,128)(2,1)} %refs_0_.1), channel_id=1, source_target_pairs={{8,0},{12,4},{16,8},{20,12},{24,16},{28,20},{9,1},{13,5},{17,9},{2... | collective-permute-start | bytes 1572872 | tf_op jit(solution)/shard_map/ppermute | solution.py:26
  5.0 10.5 %collective-permute-start = (bf16[256,512]{1,0:T(8,128)(2,1)}, bf16[256,512]{1,0:T(8,128)(2,1)S(1)}, u32[]{:S(2)}, u32[]{:S(2)}) collective-permute-start(bf16[256,512]{1,0:T(8,128)(2,1)} %refs_3_.1), channel_id=1, source_target_pairs={{0,1},{1,0},{2,3},{3,2},{4,5},{5,4},{6,7},{7,6},{8,9},{9,8},{10,11... | collective-permute-start | bytes 786440 | tf_op jit(solution)/shard_map/ppermute | solution.py:31
  10.2 8.8 %collective-permute-start.2 = (bf16[256,512]{1,0:T(8,128)(2,1)S(1)}, bf16[256,512]{1,0:T(8,128)(2,1)S(1)}, u32[]{:S(2)}, u32[]{:S(2)}) collective-permute-start(bf16[256,512]{1,0:T(8,128)(2,1)S(1)} %collective-permute-done.1.refs_1_), channel_id=1, source_target_pairs={{0,1},{1,0},{2,3},{3,2},{4,5},{5,4},{6,7},{7,6},{8,9},{9,8},{10,11... | collective-permute-start | bytes 786440 | tf_op jit(solution)/shard_map/ppermute | solution.py:31
  10.2 17.0 %collective-permute-start.4 = (bf16[256,1024]{1,0:T(8,128)(2,1)}, bf16[256,1024]{1,0:T(8,128)(2,1)S(1)}, u32[]{:S(2)}, u32[]{:S(2)}) collective-permute-start(bf16[256,1024]{1,0:T(8,128)(2,1)} %refs_1_.2), channel_id=1, source_target_pairs={{0,8},{4,12},{8,16},{12,20},{16,24},{20,28},{1,9},{5,13},{9,17},{1... | collective-permute-start | bytes 1572872 | tf_op jit(solution)/shard_map/ppermute | solution.py:26
  14.0 15.1 %collective-permute-start.5 = (bf16[256,1024]{1,0:T(8,128)(2,1)}, bf16[256,1024]{1,0:T(8,128)(2,1)S(1)}, u32[]{:S(2)}, u32[]{:S(2)}) collective-permute-start(bf16[256,1024]{1,0:T(8,128)(2,1)} %refs_1_.2), channel_id=1, source_target_pairs={{0,4},{4,0},{8,12},{12,8},{16,20},{20,16},{24,28},{28,24},{1,5},{5... | collective-permute-start | bytes 1572872 | tf_op jit(solution)/shard_map/ppermute | solution.py:31
  15.5 21.8 %collective-permute-start.6 = (bf16[256,1024]{1,0:T(8,128)(2,1)}, bf16[256,1024]{1,0:T(8,128)(2,1)S(1)}, u32[]{:S(2)}, u32[]{:S(2)}) collective-permute-start(bf16[256,1024]{1,0:T(8,128)(2,1)} %refs_2_.1), channel_id=1, source_target_pairs={{0,8},{4,12},{8,16},{12,20},{16,24},{20,28},{1,9},{5,13},{9,17},{1... | collective-permute-start | bytes 1572872 | tf_op jit(solution)/shard_map/ppermute | solution.py:26
  19.0 20.5 %collective-permute-start.7 = (bf16[256,1024]{1,0:T(8,128)(2,1)}, bf16[256,1024]{1,0:T(8,128)(2,1)S(1)}, u32[]{:S(2)}, u32[]{:S(2)}) collective-permute-start(bf16[256,1024]{1,0:T(8,128)(2,1)} %refs_2_.1), channel_id=1, source_target_pairs={{0,4},{4,0},{8,12},{12,8},{16,20},{20,16},{24,28},{28,24},{1,5},{5... | collective-permute-start | bytes 1572872 | tf_op jit(solution)/shard_map/ppermute | solution.py:31
  23.8 17.0 %collective-permute-start.8 = (bf16[256,1024]{1,0:T(8,128)(2,1)S(1)}, bf16[256,1024]{1,0:T(8,128)(2,1)S(1)}, u32[]{:S(2)}, u32[]{:S(2)}) collective-permute-start(bf16[256,1024]{1,0:T(8,128)(2,1)S(1)} %shard_map.94.refs_1_.g.refs_0_), channel_id=1, source_target_pairs={{8,0},{12,4},{16,8},{20,12},{24,16},{28,20},{9,1},{13,5},{17,9},{2... | collective-permute-start | bytes 1572872 | tf_op jit(solution)/shard_map/ppermute | solution.py:26
  39.5 7.2 %collective-permute-start.10 = (f32[5,8,256]{2,1,0:T(8,128)S(1)}, f32[5,8,256]{2,1,0:T(8,128)S(1)}, u32[]{:S(2)}, u32[]{:S(2)}) collective-permute-start(f32[5,8,256]{2,1,0:T(8,128)S(1)} %shard_map.101), channel_id=1, source_target_pairs={{8,0},{12,4},{16,8},{20,12},{24,16},{28,20},{9,1},{13,5},{17,9},{2... | collective-permute-start | bytes 122888 | tf_op jit(solution)/shard_map/ppermute | solution.py:26
  42.2 10.7 %collective-permute-start.9 = (f32[6,8,256]{2,1,0:T(8,128)S(1)}, f32[6,8,256]{2,1,0:T(8,128)S(1)}, u32[]{:S(2)}, u32[]{:S(2)}) collective-permute-start(f32[6,8,256]{2,1,0:T(8,128)S(1)} %get-tuple-element.73.refs_1_), channel_id=1, source_target_pairs={{0,8},{4,12},{8,16},{12,20},{16,24},{20,28},{1,9},{5,13},{9,17},{1... | collective-permute-start | bytes 147464 | tf_op jit(solution)/shard_map/ppermute | solution.py:26
  49.4 30.4 %collective-permute-start.11 = (bf16[256,1024]{1,0:T(8,128)(2,1)S(1)}, bf16[256,1024]{1,0:T(8,128)(2,1)S(1)}, u32[]{:S(2)}, u32[]{:S(2)}) collective-permute-start(bf16[256,1024]{1,0:T(8,128)(2,1)S(1)} %get-tuple-element.102), channel_id=1, source_target_pairs={{0,8},{4,12},{8,16},{12,20},{16,24},{20,28},{1,9},{5,13},{9,17},{1... | collective-permute-start | bytes 1572872 | tf_op jit(solution)/shard_map/ppermute | solution.py:26
  54.2 27.0 %collective-permute-start.14 = (bf16[512,512]{1,0:T(8,128)(2,1)S(1)}, bf16[512,512]{1,0:T(8,128)(2,1)S(1)}, u32[]{:S(2)}, u32[]{:S(2)}) collective-permute-start(bf16[512,512]{1,0:T(8,128)(2,1)S(1)} %get-tuple-element.107), channel_id=1, source_target_pairs={{8,0},{12,4},{16,8},{20,12},{24,16},{28,20},{9,1},{13,5},{17,9},{2... | collective-permute-start | bytes 1572872 | tf_op jit(solution)/shard_map/ppermute | solution.py:26
  55.5 25.7 %collective-permute-start.15 = (bf16[512,512]{1,0:T(8,128)(2,1)S(1)}, bf16[512,512]{1,0:T(8,128)(2,1)S(1)}, u32[]{:S(2)}, u32[]{:S(2)}) collective-permute-start(bf16[512,512]{1,0:T(8,128)(2,1)S(1)} %get-tuple-element.108), channel_id=1, source_target_pairs={{0,4},{4,0},{8,12},{12,8},{16,20},{20,16},{24,28},{28,24},{1,5},{5... | collective-permute-start | bytes 1572872 | tf_op jit(solution)/shard_map/ppermute | solution.py:31
  57.6 16.5 %collective-permute-start.16 = (bf16[512,256]{1,0:T(8,128)(2,1)S(1)}, bf16[512,256]{1,0:T(8,128)(2,1)S(1)}, u32[]{:S(2)}, u32[]{:S(2)}) collective-permute-start(bf16[512,256]{1,0:T(8,128)(2,1)S(1)} %get-tuple-element.109), channel_id=1, source_target_pairs={{8,0},{12,4},{16,8},{20,12},{24,16},{28,20},{9,1},{13,5},{17,9},{2... | collective-permute-start | bytes 786440 | tf_op jit(solution)/shard_map/ppermute | solution.py:26
  58.8 16.5 %collective-permute-start.17 = (bf16[512,256]{1,0:T(8,128)(2,1)S(1)}, bf16[512,256]{1,0:T(8,128)(2,1)S(1)}, u32[]{:S(2)}, u32[]{:S(2)}) collective-permute-start(bf16[512,256]{1,0:T(8,128)(2,1)S(1)} %get-tuple-element.110), channel_id=1, source_target_pairs={{0,4},{4,0},{8,12},{12,8},{16,20},{20,16},{24,28},{28,24},{1,5},{5... | collective-permute-start | bytes 786440 | tf_op jit(solution)/shard_map/ppermute | solution.py:31
  74.1 8.3 %collective-permute-start.12 = (bf16[512,256]{1,0:T(8,128)(2,1)S(1)}, bf16[512,256]{1,0:T(8,128)(2,1)S(1)}, u32[]{:S(2)}, u32[]{:S(2)}) collective-permute-start(bf16[512,256]{1,0:T(8,128)(2,1)S(1)} %get-tuple-element.105), channel_id=1, source_target_pairs={{8,0},{12,4},{16,8},{20,12},{24,16},{28,20},{9,1},{13,5},{17,9},{2... | collective-permute-start | bytes 786440 | tf_op jit(solution)/shard_map/ppermute | solution.py:26
  75.4 7.0 %collective-permute-start.13 = (bf16[512,256]{1,0:T(8,128)(2,1)S(1)}, bf16[512,256]{1,0:T(8,128)(2,1)S(1)}, u32[]{:S(2)}, u32[]{:S(2)}) collective-permute-start(bf16[512,256]{1,0:T(8,128)(2,1)S(1)} %get-tuple-element.106), channel_id=1, source_target_pairs={{0,4},{4,0},{8,12},{12,8},{16,20},{20,16},{24,28},{28,24},{1,5},{5... | collective-permute-start | bytes 786440 | tf_op jit(solution)/shard_map/ppermute | solution.py:31

commit v9 on v8

--- a/solution.py
+++ b/solution.py
@@ -12,7 +12,7 @@
 FAR, MID, NEAR = range(3)
 SECTIONS = 3
 GROUPS = (2, 4, 2)
-HEADS_PER_STEP = 2
+HEADS_PER_STEP = 4
 KERNEL_VMEM = 8 * 2**20
 BIG = 1e30
 SCALE = 1.0 / math.sqrt(HDIM)
@@ -67,12 +67,14 @@
 
 
 def each_head(first, count, step):
-    def pair(index, carry):
-        for offset in range(HEADS_PER_STEP):
-            step(first + index * HEADS_PER_STEP + offset)
+    width = math.gcd(count, HEADS_PER_STEP)
+
+    def several(index, carry):
+        for offset in range(width):
+            step(first + index * width + offset)
         return carry
 
-    lax.fori_loop(0, count // HEADS_PER_STEP, pair, None)
+    lax.fori_loop(0, count // width, several, None)
 
 
 def columns(head):

time: 83.5 us -> 82.9 us (level)
  Pallas kernels: 21.5 us -> 20.1 us
  waiting for transfers between devices: 28.3 us -> 29.5 us
    pallas_call x20, Pallas kernels: 20.1 us -> 18.7 us  [call(): pl.pallas_call(kernel, grid=grid or (), in_specs=[smem] * len(scalars) +...]
    ppermute x10, waiting for transfers between devices: 20.1 us -> 21 us  [shift(): lax.ppermute(value, 'seq', [(src, src + steps) for src in range(low, high)])]
  transfers between devices with their start and end apart: 18 -> 18, of which waited for: 6 -> 6; matrix products, arithmetic and copies ran while one was open for 0% -> 0% of each run, Pallas kernels for 25% -> 23%
where the time goes in v9:
time: 82.9 us; the launch traced here: 82.5 us
  starting transfers between devices  32 us (39%)
  waiting for transfers between devices  29.5 us (36%)
  Pallas kernels  20.1 us (24%)
  between operations  0.91 us (1%)
    ppermute x10, starting transfers between devices, shift(): lax.ppermute(value, 'seq', [(src, src + steps) for src in range(low, high)])  23 us
    ppermute x10, waiting for transfers between devices, shift(): lax.ppermute(value, 'seq', [(src, src + steps) for src in range(low, high)])  21 us
    pallas_call x20, Pallas kernels, call(): pl.pallas_call(kernel, grid=grid or (), in_specs=[smem] * len(scalars) +...  18.7 us
    ppermute x8, starting transfers between devices, swap(): return lax.ppermute(value, axis, pairs)  9.04 us
    ppermute x8, waiting for transfers between devices, swap(): return lax.ppermute(value, axis, pairs)  8.53 us
  transfers between devices with their start and end apart: 18, of which 6 were waited for; matrix products, arithmetic and copies ran while one was open for 0% of the time, Pallas kernels for 23%

profile of v9, /device:TPU:0, one launch (start us, length us, event | category | flops | bytes accessed | tf_op | source)
XLA Modules:
  0.0 82.5 jit_solution(11652249031273085035)
XLA Ops:
  0.7 3.1 %collective-permute-start.1 = (bf16[256,512]{1,0:T(8,128)(2,1)}, bf16[256,512]{1,0:T(8,128)(2,1)S(1)}, u32[]{:S(2)}, u32[]{:S(2)}) collective-permute-start(bf16[256,512]{1,0:T(8,128)(2,1)} %refs_3_.1), channel_id=1, source_target_pairs={{0,2},{1,3},{2,0},{3,1},{4,6},{5,7},{6,4},{7,5},{8,10},{9,11},{10,... | collective-permute-start | bytes 786440 | tf_op jit(solution)/shard_map/ppermute | solution.py:31
  3.7 1.3 %collective-permute-start.3 = (bf16[256,1024]{1,0:T(8,128)(2,1)}, bf16[256,1024]{1,0:T(8,128)(2,1)S(1)}, u32[]{:S(2)}, u32[]{:S(2)}) collective-permute-start(bf16[256,1024]{1,0:T(8,128)(2,1)} %refs_0_.1), channel_id=1, source_target_pairs={{8,0},{12,4},{16,8},{20,12},{24,16},{28,20},{9,1},{13,5},{17,9},{2... | collective-permute-start | bytes 1572872 | tf_op jit(solution)/shard_map/ppermute | solution.py:26
  5.0 0.1 collective-permute-start
  5.1 5.1 %collective-permute-done.1.refs_1_ = bf16[256,512]{1,0:T(8,128)(2,1)S(1)} collective-permute-done((bf16[256,512]{1,0:T(8,128)(2,1)}, bf16[256,512]{1,0:T(8,128)(2,1)S(1)}, u32[]{:S(2)}, u32[]{:S(2)}) %collective-permute-start.1) | collective-permute-done | bytes 262176 | tf_op jit(solution)/shard_map/ppermute | solution.py:31
  10.2 0.0 collective-permute-start.2
  10.2 3.7 %collective-permute-start.4 = (bf16[256,1024]{1,0:T(8,128)(2,1)}, bf16[256,1024]{1,0:T(8,128)(2,1)S(1)}, u32[]{:S(2)}, u32[]{:S(2)}) collective-permute-start(bf16[256,1024]{1,0:T(8,128)(2,1)} %refs_1_.2), channel_id=1, source_target_pairs={{0,8},{4,12},{8,16},{12,20},{16,24},{20,28},{1,9},{5,13},{9,17},{1... | collective-permute-start | bytes 1572872 | tf_op jit(solution)/shard_map/ppermute | solution.py:26
  14.0 1.6 %collective-permute-start.5 = (bf16[256,1024]{1,0:T(8,128)(2,1)}, bf16[256,1024]{1,0:T(8,128)(2,1)S(1)}, u32[]{:S(2)}, u32[]{:S(2)}) collective-permute-start(bf16[256,1024]{1,0:T(8,128)(2,1)} %refs_1_.2), channel_id=1, source_target_pairs={{0,4},{4,0},{8,12},{12,8},{16,20},{20,16},{24,28},{28,24},{1,5},{5... | collective-permute-start | bytes 1572872 | tf_op jit(solution)/shard_map/ppermute | solution.py:31
  15.5 3.5 %collective-permute-start.6 = (bf16[256,1024]{1,0:T(8,128)(2,1)}, bf16[256,1024]{1,0:T(8,128)(2,1)S(1)}, u32[]{:S(2)}, u32[]{:S(2)}) collective-permute-start(bf16[256,1024]{1,0:T(8,128)(2,1)} %refs_2_.1), channel_id=1, source_target_pairs={{0,8},{4,12},{8,16},{12,20},{16,24},{20,28},{1,9},{5,13},{9,17},{1... | collective-permute-start | bytes 1572872 | tf_op jit(solution)/shard_map/ppermute | solution.py:26
  19.0 0.6 collective-permute-start.7
  19.6 4.2 %shard_map.94.refs_1_.g.refs_0_ = bf16[256,1024]{1,0:T(8,128)(2,1)S(1)} custom-call(bf16[256,512]{1,0:T(8,128)(2,1)S(1)} %collective-permute-done.refs_0_, bf16[256,512]{1,0:T(8,128)(2,1)S(1)} %collective-permute-done.1.refs_1_, bf16[256,512]{1,0:T(8,128)(2,1)S(1)} %collective-permute-done.2.refs_2_, bf16[256,512]{1,0:T(8,128)(2,1)} %refs_3_.1, ...), custom_call_target="tpu_custom_call" | custom-call | flops 1073741824 | tf_op jit(solution)/shard_map/pallas_call | solution.py:51
  23.8 0.0 collective-permute-done.3.refs_4_.refs_0_
  23.8 1.3 %collective-permute-start.8 = (bf16[256,1024]{1,0:T(8,128)(2,1)S(1)}, bf16[256,1024]{1,0:T(8,128)(2,1)S(1)}, u32[]{:S(2)}, u32[]{:S(2)}) collective-permute-start(bf16[256,1024]{1,0:T(8,128)(2,1)S(1)} %shard_map.94.refs_1_.g.refs_0_), channel_id=1, source_target_pairs={{8,0},{12,4},{16,8},{20,12},{24,16},{28,20},{9,1},{13,5},{17,9},{2... | collective-permute-start | bytes 1572872 | tf_op jit(solution)/shard_map/ppermute | solution.py:26
  25.2 0.6 shard_map.95.refs_0_
  25.8 1.4 %stage.1 = (bf16[256,1024]{1,0:T(8,128)(2,1)S(1)}, bf16[256,1024]{1,0:T(8,128)(2,1)S(1)}, bf16[256,1024]{1,0:T(8,128)(2,1)S(1)}) custom-call(bf16[256,1024]{1,0:T(8,128)(2,1)} %refs_0_.1, bf16[256,1024]{1,0:T(8,128)(2,1)} %refs_1_.2, bf16[256,1024]{1,0:T(8,128)(2,1)} %refs_2_.1), custom_call_target="tpu_custom_call" | custom-call | flops 1000000 | tf_op jit(solution)/shard_map/stage/pallas_call | solution.py:158
  27.2 0.0 collective-permute-done.4.refs_5_.refs_2_
  27.2 1.8 %collective-permute-done.5.refs_6_.refs_3_ = bf16[256,1024]{1,0:T(8,128)(2,1)S(1)} collective-permute-done((bf16[256,1024]{1,0:T(8,128)(2,1)}, bf16[256,1024]{1,0:T(8,128)(2,1)S(1)}, u32[]{:S(2)}, u32[]{:S(2)}) %collective-permute-start.5) | collective-permute-done | bytes 524320 | tf_op jit(solution)/shard_map/ppermute | solution.py:31
  29.0 3.1 %shard_map.96 = (f32[3,8,256]{2,1,0:T(8,128)S(1)}, f32[3,8,256]{2,1,0:T(8,128)S(1)}, f32[3,8,256]{2,1,0:T(8,128)S(1)}, f32[3,8,256]{2,1,0:T(8,128)S(1)}, f32[8,2...) custom-call(bf16[256,1024]{1,0:T(8,128)(2,1)S(1)} %get-tuple-element, ...), custom_call_target="tpu_custom_call" | custom-call | flops 671088640 | tf_op jit(solution)/shard_map/pallas_call | solution.py:51
  32.1 5.2 %collective-permute-done.6.v_up.refs_1_ = bf16[256,1024]{1,0:T(8,128)(2,1)S(1)} collective-permute-done((bf16[256,1024]{1,0:T(8,128)(2,1)}, bf16[256,1024]{1,0:T(8,128)(2,1)S(1)}, u32[]{:S(2)}, u32[]{:S(2)}) %collective-permute-start.6) | collective-permute-done | bytes 524320 | tf_op jit(solution)/shard_map/ppermute | solution.py:26
  37.3 0.7 shard_map.97
  38.0 1.5 %collective-permute-done.7.refs_1_.refs_2_ = bf16[256,1024]{1,0:T(8,128)(2,1)S(1)} collective-permute-done((bf16[256,1024]{1,0:T(8,128)(2,1)}, bf16[256,1024]{1,0:T(8,128)(2,1)S(1)}, u32[]{:S(2)}, u32[]{:S(2)}) %collective-permute-start.7) | collective-permute-done | bytes 524320 | tf_op jit(solution)/shard_map/ppermute | solution.py:31
  39.5 1.3 %collective-permute-start.10 = (f32[5,8,256]{2,1,0:T(8,128)S(1)}, f32[5,8,256]{2,1,0:T(8,128)S(1)}, u32[]{:S(2)}, u32[]{:S(2)}) collective-permute-start(f32[5,8,256]{2,1,0:T(8,128)S(1)} %shard_map.101), channel_id=1, source_target_pairs={{8,0},{12,4},{16,8},{20,12},{24,16},{28,20},{9,1},{13,5},{17,9},{2... | collective-permute-start | bytes 122888 | tf_op jit(solution)/shard_map/ppermute | solution.py:26
  40.8 0.0 collective-permute-done.8.refs_0_.refs_1_
  40.9 1.0 %shard_map.99 = (f32[6,8,256]{2,1,0:T(8,128)S(1)}, f32[8,256,256]{2,1,0:T(8,128)S(1)}, f32[8,256,256]{2,1,0:T(8,128)S(1)}) custom-call(bf16[256,1024]{1,0:T(8,128)(2,1)S(1)} %collective-permute-done.8.refs_0_.refs_1_, bf16[256,1024]{1,0:T(8,128)(2,1)S(1)} %collective-permute-done.6.v_up.refs_1_, ...), custom_call_target="tpu_custom_call", output_to_operand_aliasing={{2}: (7, {})} | custom-call | flops 268435456 | tf_op jit(solution)/shard_map/pallas_call | solution.py:51
  41.9 4.5 %collective-permute-start.9 = (f32[6,8,256]{2,1,0:T(8,128)S(1)}, f32[6,8,256]{2,1,0:T(8,128)S(1)}, u32[]{:S(2)}, u32[]{:S(2)}) collective-permute-start(f32[6,8,256]{2,1,0:T(8,128)S(1)} %get-tuple-element.73.refs_1_), channel_id=1, source_target_pairs={{0,8},{4,12},{8,16},{12,20},{16,24},{20,28},{1,9},{5,13},{9,17},{1... | collective-permute-start | bytes 147464 | tf_op jit(solution)/shard_map/ppermute | solution.py:26
  46.4 0.0 collective-permute-done.10.refs_0_
  46.5 0.6 shard_map.103
  47.1 1.0 %shard_map.104 = (bf16[256,1024]{1,0:T(8,128)(2,1)S(1)}, f32[256,512]{1,0:T(8,128)S(1)}, f32[256,512]{1,0:T(8,128)S(1)}, f32[256,512]{1,0:T(8,128)S(1)}, f32[256,512]{1,0:T(8,128)S(1)}) custom-call(bf16[256,1024]{1,0:T(8,128)(2,1)S(1)} %collective-permute-done.3.refs_4_.refs_0_, ...), custom_call_target="tpu_custom_call", output_to_operand_aliasing={{0}: (10, {})} | custom-call | flops 402653184 | tf_op jit(solution)/shard_map/pallas_call | solution.py:51
  48.2 0.6 shard_map.105
  48.8 3.5 %collective-permute-start.11 = (bf16[256,1024]{1,0:T(8,128)(2,1)S(1)}, bf16[256,1024]{1,0:T(8,128)(2,1)S(1)}, u32[]{:S(2)}, u32[]{:S(2)}) collective-permute-start(bf16[256,1024]{1,0:T(8,128)(2,1)S(1)} %get-tuple-element.102), channel_id=1, source_target_pairs={{0,8},{4,12},{8,16},{12,20},{16,24},{20,28},{1,9},{5,13},{9,17},{1... | collective-permute-start | bytes 1572872 | tf_op jit(solution)/shard_map/ppermute | solution.py:26
  52.4 0.4 shard_map.106
  52.8 0.9 %shard_map.107 = (f32[256,1024]{1,0:T(8,128)S(1)}, bf16[512,512]{1,0:T(8,128)(2,1)S(1)}, bf16[512,512]{1,0:T(8,128)(2,1)S(1)}) custom-call(bf16[256,1024]{1,0:T(8,128)(2,1)S(1)} %get-tuple-element.60.refs_0_.q, bf16[256,1024]{1,0:T(8,128)(2,1)S(1)} %shard_map.94.refs_1_.g.refs_0_, ...), custom_call_target="tpu_custom_call", output_to_operand_aliasing={{0}: (14, {})} | custom-call | flops 402653184 | tf_op jit(solution)/shard_map/pallas_call | solution.py:51
  53.6 1.3 %collective-permute-start.14 = (bf16[512,512]{1,0:T(8,128)(2,1)S(1)}, bf16[512,512]{1,0:T(8,128)(2,1)S(1)}, u32[]{:S(2)}, u32[]{:S(2)}) collective-permute-start(bf16[512,512]{1,0:T(8,128)(2,1)S(1)} %get-tuple-element.107), channel_id=1, source_target_pairs={{8,0},{12,4},{16,8},{20,12},{24,16},{28,20},{9,1},{13,5},{17,9},{2... | collective-permute-start | bytes 1572872 | tf_op jit(solution)/shard_map/ppermute | solution.py:26
  54.9 1.6 %collective-permute-start.15 = (bf16[512,512]{1,0:T(8,128)(2,1)S(1)}, bf16[512,512]{1,0:T(8,128)(2,1)S(1)}, u32[]{:S(2)}, u32[]{:S(2)}) collective-permute-start(bf16[512,512]{1,0:T(8,128)(2,1)S(1)} %get-tuple-element.108), channel_id=1, source_target_pairs={{0,4},{4,0},{8,12},{12,8},{16,20},{20,16},{24,28},{28,24},{1,5},{5... | collective-permute-start | bytes 1572872 | tf_op jit(solution)/shard_map/ppermute | solution.py:31
  56.5 1.3 %collective-permute-start.16 = (bf16[512,256]{1,0:T(8,128)(2,1)S(1)}, bf16[512,256]{1,0:T(8,128)(2,1)S(1)}, u32[]{:S(2)}, u32[]{:S(2)}) collective-permute-start(bf16[512,256]{1,0:T(8,128)(2,1)S(1)} %get-tuple-element.109), channel_id=1, source_target_pairs={{8,0},{12,4},{16,8},{20,12},{24,16},{28,20},{9,1},{13,5},{17,9},{2... | collective-permute-start | bytes 786440 | tf_op jit(solution)/shard_map/ppermute | solution.py:26
  57.8 0.6 collective-permute-start.17
  58.4 0.4 shard_map.108
  58.8 14.7 %collective-permute-done.16.refs_2_ = bf16[512,256]{1,0:T(8,128)(2,1)S(1)} collective-permute-done((bf16[512,256]{1,0:T(8,128)(2,1)S(1)}, bf16[512,256]{1,0:T(8,128)(2,1)S(1)}, u32[]{:S(2)}, u32[]{:S(2)}) %collective-permute-start.16) | collective-permute-done | bytes 262176 | tf_op jit(solution)/shard_map/ppermute | solution.py:26
  73.5 1.3 %collective-permute-start.12 = (bf16[512,256]{1,0:T(8,128)(2,1)S(1)}, bf16[512,256]{1,0:T(8,128)(2,1)S(1)}, u32[]{:S(2)}, u32[]{:S(2)}) collective-permute-start(bf16[512,256]{1,0:T(8,128)(2,1)S(1)} %get-tuple-element.105), channel_id=1, source_target_pairs={{8,0},{12,4},{16,8},{20,12},{24,16},{28,20},{9,1},{13,5},{17,9},{2... | collective-permute-start | bytes 786440 | tf_op jit(solution)/shard_map/ppermute | solution.py:26
  74.8 1.6 %collective-permute-start.13 = (bf16[512,256]{1,0:T(8,128)(2,1)S(1)}, bf16[512,256]{1,0:T(8,128)(2,1)S(1)}, u32[]{:S(2)}, u32[]{:S(2)}) collective-permute-start(bf16[512,256]{1,0:T(8,128)(2,1)S(1)} %get-tuple-element.106), channel_id=1, source_target_pairs={{0,4},{4,0},{8,12},{12,8},{16,20},{20,16},{24,28},{28,24},{1,5},{5... | collective-permute-start | bytes 786440 | tf_op jit(solution)/shard_map/ppermute | solution.py:31
  76.4 1.3 %shard_map.109 = (f32[256,1024]{1,0:T(8,128)S(1)}, f32[256,1024]{1,0:T(8,128)S(1)}, f32[256,1024]{1,0:T(8,128)S(1)}) custom-call(bf16[256,1024]{1,0:T(8,128)(2,1)S(1)} %get-tuple-element.60.refs_0_.q, bf16[256,1024]{1,0:T(8,128)(2,1)S(1)} %shard_map.94.refs_1_.g.refs_0_, bf16[256,1024]{1,0:T(8,128)(2,1)S(1)} %get-tuple-element.61.refs_2_.k, ...), custom_call_target="tpu_custom_call" | custom-call | flops 402653184 | tf_op jit(solution)/shard_map/pallas_call | solution.py:51
  77.7 0.8 shard_map.111
  78.4 0.0 collective-permute-done.11.guest
  78.4 1.4 %shard_map.110 = bf16[256,1024]{1,0:T(8,128)(2,1)} custom-call(f32[256,1024]{1,0:T(8,128)S(1)} %get-tuple-element.101.dq, bf16[256,1024]{1,0:T(8,128)(2,1)S(1)} %collective-permute-done.11.guest), custom_call_target="tpu_custom_call" | custom-call | flops 524288 | tf_op jit(solution)/shard_map/pallas_call | solution.py:51
  79.9 0.0 collective-permute-done.14.refs_2_
  79.9 0.0 collective-permute-done.15.refs_3_
  79.9 0.9 %shard_map.112 = (bf16[256,1024]{1,0:T(8,128)(2,1)}, bf16[256,1024]{1,0:T(8,128)(2,1)}) custom-call(f32[256,1024]{1,0:T(8,128)S(1)} %get-tuple-element.103.refs_0_, f32[256,1024]{1,0:T(8,128)S(1)} %get-tuple-element.104.refs_1_, bf16[512,512]{1,0:T(8,128)(2,1)S(1)} %collective-permute-done.14.refs_2_, ...), custom_call_target="tpu_custom_call", output_to_operand_aliasing={{0}: (4, {}), {1}: (5, {})} | custom-call | flops 33554432 | tf_op jit(solution)/shard_map/pallas_call | solution.py:51
  80.8 1.0 %collective-permute-done.12.refs_2_ = bf16[512,256]{1,0:T(8,128)(2,1)S(1)} collective-permute-done((bf16[512,256]{1,0:T(8,128)(2,1)S(1)}, bf16[512,256]{1,0:T(8,128)(2,1)S(1)}, u32[]{:S(2)}, u32[]{:S(2)}) %collective-permute-start.12) | collective-permute-done | bytes 262176 | tf_op jit(solution)/shard_map/ppermute | solution.py:26
  81.8 0.7 shard_map.113
  (13 shorter events, 0.1 us)
Async XLA Ops:
  0.6 24.5 %copy-start = (s32[8,3]{0,1:T(4,128)S(1)}, s32[8,3]{0,1:T(4,128)}, u32[]{:S(2)}) copy-start(s32[8,3]{0,1:T(4,128)} %param.12) | copy-start | bytes 292
  0.6 24.5 %copy-start.1 = (s32[1,3]{1,0:T(1,128)S(1)}, s32[1,3]{1,0:T(1,128)}, u32[]{:S(2)}) copy-start(s32[1,3]{1,0:T(1,128)} %refs_1_.3) | copy-start | bytes 40
  0.7 9.6 %collective-permute-start.1 = (bf16[256,512]{1,0:T(8,128)(2,1)}, bf16[256,512]{1,0:T(8,128)(2,1)S(1)}, u32[]{:S(2)}, u32[]{:S(2)}) collective-permute-start(bf16[256,512]{1,0:T(8,128)(2,1)} %refs_3_.1), channel_id=1, source_target_pairs={{0,2},{1,3},{2,0},{3,1},{4,6},{5,7},{6,4},{7,5},{8,10},{9,11},{10,... | collective-permute-start | bytes 786440 | tf_op jit(solution)/shard_map/ppermute | solution.py:31
  3.7 20.1 %collective-permute-start.3 = (bf16[256,1024]{1,0:T(8,128)(2,1)}, bf16[256,1024]{1,0:T(8,128)(2,1)S(1)}, u32[]{:S(2)}, u32[]{:S(2)}) collective-permute-start(bf16[256,1024]{1,0:T(8,128)(2,1)} %refs_0_.1), channel_id=1, source_target_pairs={{8,0},{12,4},{16,8},{20,12},{24,16},{28,20},{9,1},{13,5},{17,9},{2... | collective-permute-start | bytes 1572872 | tf_op jit(solution)/shard_map/ppermute | solution.py:26
  5.0 10.5 %collective-permute-start = (bf16[256,512]{1,0:T(8,128)(2,1)}, bf16[256,512]{1,0:T(8,128)(2,1)S(1)}, u32[]{:S(2)}, u32[]{:S(2)}) collective-permute-start(bf16[256,512]{1,0:T(8,128)(2,1)} %refs_3_.1), channel_id=1, source_target_pairs={{0,1},{1,0},{2,3},{3,2},{4,5},{5,4},{6,7},{7,6},{8,9},{9,8},{10,11... | collective-permute-start | bytes 786440 | tf_op jit(solution)/shard_map/ppermute | solution.py:31
  10.2 8.8 %collective-permute-start.2 = (bf16[256,512]{1,0:T(8,128)(2,1)S(1)}, bf16[256,512]{1,0:T(8,128)(2,1)S(1)}, u32[]{:S(2)}, u32[]{:S(2)}) collective-permute-start(bf16[256,512]{1,0:T(8,128)(2,1)S(1)} %collective-permute-done.1.refs_1_), channel_id=1, source_target_pairs={{0,1},{1,0},{2,3},{3,2},{4,5},{5,4},{6,7},{7,6},{8,9},{9,8},{10,11... | collective-permute-start | bytes 786440 | tf_op jit(solution)/shard_map/ppermute | solution.py:31
  10.2 17.0 %collective-permute-start.4 = (bf16[256,1024]{1,0:T(8,128)(2,1)}, bf16[256,1024]{1,0:T(8,128)(2,1)S(1)}, u32[]{:S(2)}, u32[]{:S(2)}) collective-permute-start(bf16[256,1024]{1,0:T(8,128)(2,1)} %refs_1_.2), channel_id=1, source_target_pairs={{0,8},{4,12},{8,16},{12,20},{16,24},{20,28},{1,9},{5,13},{9,17},{1... | collective-permute-start | bytes 1572872 | tf_op jit(solution)/shard_map/ppermute | solution.py:26
  14.0 15.1 %collective-permute-start.5 = (bf16[256,1024]{1,0:T(8,128)(2,1)}, bf16[256,1024]{1,0:T(8,128)(2,1)S(1)}, u32[]{:S(2)}, u32[]{:S(2)}) collective-permute-start(bf16[256,1024]{1,0:T(8,128)(2,1)} %refs_1_.2), channel_id=1, source_target_pairs={{0,4},{4,0},{8,12},{12,8},{16,20},{20,16},{24,28},{28,24},{1,5},{5... | collective-permute-start | bytes 1572872 | tf_op jit(solution)/shard_map/ppermute | solution.py:31
  15.5 21.8 %collective-permute-start.6 = (bf16[256,1024]{1,0:T(8,128)(2,1)}, bf16[256,1024]{1,0:T(8,128)(2,1)S(1)}, u32[]{:S(2)}, u32[]{:S(2)}) collective-permute-start(bf16[256,1024]{1,0:T(8,128)(2,1)} %refs_2_.1), channel_id=1, source_target_pairs={{0,8},{4,12},{8,16},{12,20},{16,24},{20,28},{1,9},{5,13},{9,17},{1... | collective-permute-start | bytes 1572872 | tf_op jit(solution)/shard_map/ppermute | solution.py:26
  19.0 20.5 %collective-permute-start.7 = (bf16[256,1024]{1,0:T(8,128)(2,1)}, bf16[256,1024]{1,0:T(8,128)(2,1)S(1)}, u32[]{:S(2)}, u32[]{:S(2)}) collective-permute-start(bf16[256,1024]{1,0:T(8,128)(2,1)} %refs_2_.1), channel_id=1, source_target_pairs={{0,4},{4,0},{8,12},{12,8},{16,20},{20,16},{24,28},{28,24},{1,5},{5... | collective-permute-start | bytes 1572872 | tf_op jit(solution)/shard_map/ppermute | solution.py:31
  23.8 17.0 %collective-permute-start.8 = (bf16[256,1024]{1,0:T(8,128)(2,1)S(1)}, bf16[256,1024]{1,0:T(8,128)(2,1)S(1)}, u32[]{:S(2)}, u32[]{:S(2)}) collective-permute-start(bf16[256,1024]{1,0:T(8,128)(2,1)S(1)} %shard_map.94.refs_1_.g.refs_0_), channel_id=1, source_target_pairs={{8,0},{12,4},{16,8},{20,12},{24,16},{28,20},{9,1},{13,5},{17,9},{2... | collective-permute-start | bytes 1572872 | tf_op jit(solution)/shard_map/ppermute | solution.py:26
  39.5 6.9 %collective-permute-start.10 = (f32[5,8,256]{2,1,0:T(8,128)S(1)}, f32[5,8,256]{2,1,0:T(8,128)S(1)}, u32[]{:S(2)}, u32[]{:S(2)}) collective-permute-start(f32[5,8,256]{2,1,0:T(8,128)S(1)} %shard_map.101), channel_id=1, source_target_pairs={{8,0},{12,4},{16,8},{20,12},{24,16},{28,20},{9,1},{13,5},{17,9},{2... | collective-permute-start | bytes 122888 | tf_op jit(solution)/shard_map/ppermute | solution.py:26
  41.9 10.4 %collective-permute-start.9 = (f32[6,8,256]{2,1,0:T(8,128)S(1)}, f32[6,8,256]{2,1,0:T(8,128)S(1)}, u32[]{:S(2)}, u32[]{:S(2)}) collective-permute-start(f32[6,8,256]{2,1,0:T(8,128)S(1)} %get-tuple-element.73.refs_1_), channel_id=1, source_target_pairs={{0,8},{4,12},{8,16},{12,20},{16,24},{20,28},{1,9},{5,13},{9,17},{1... | collective-permute-start | bytes 147464 | tf_op jit(solution)/shard_map/ppermute | solution.py:26
  48.8 29.6 %collective-permute-start.11 = (bf16[256,1024]{1,0:T(8,128)(2,1)S(1)}, bf16[256,1024]{1,0:T(8,128)(2,1)S(1)}, u32[]{:S(2)}, u32[]{:S(2)}) collective-permute-start(bf16[256,1024]{1,0:T(8,128)(2,1)S(1)} %get-tuple-element.102), channel_id=1, source_target_pairs={{0,8},{4,12},{8,16},{12,20},{16,24},{20,28},{1,9},{5,13},{9,17},{1... | collective-permute-start | bytes 1572872 | tf_op jit(solution)/shard_map/ppermute | solution.py:26
  53.6 26.2 %collective-permute-start.14 = (bf16[512,512]{1,0:T(8,128)(2,1)S(1)}, bf16[512,512]{1,0:T(8,128)(2,1)S(1)}, u32[]{:S(2)}, u32[]{:S(2)}) collective-permute-start(bf16[512,512]{1,0:T(8,128)(2,1)S(1)} %get-tuple-element.107), channel_id=1, source_target_pairs={{8,0},{12,4},{16,8},{20,12},{24,16},{28,20},{9,1},{13,5},{17,9},{2... | collective-permute-start | bytes 1572872 | tf_op jit(solution)/shard_map/ppermute | solution.py:26
  54.9 24.9 %collective-permute-start.15 = (bf16[512,512]{1,0:T(8,128)(2,1)S(1)}, bf16[512,512]{1,0:T(8,128)(2,1)S(1)}, u32[]{:S(2)}, u32[]{:S(2)}) collective-permute-start(bf16[512,512]{1,0:T(8,128)(2,1)S(1)} %get-tuple-element.108), channel_id=1, source_target_pairs={{0,4},{4,0},{8,12},{12,8},{16,20},{20,16},{24,28},{28,24},{1,5},{5... | collective-permute-start | bytes 1572872 | tf_op jit(solution)/shard_map/ppermute | solution.py:31
  56.5 17.0 %collective-permute-start.16 = (bf16[512,256]{1,0:T(8,128)(2,1)S(1)}, bf16[512,256]{1,0:T(8,128)(2,1)S(1)}, u32[]{:S(2)}, u32[]{:S(2)}) collective-permute-start(bf16[512,256]{1,0:T(8,128)(2,1)S(1)} %get-tuple-element.109), channel_id=1, source_target_pairs={{8,0},{12,4},{16,8},{20,12},{24,16},{28,20},{9,1},{13,5},{17,9},{2... | collective-permute-start | bytes 786440 | tf_op jit(solution)/shard_map/ppermute | solution.py:26
  57.8 17.0 %collective-permute-start.17 = (bf16[512,256]{1,0:T(8,128)(2,1)S(1)}, bf16[512,256]{1,0:T(8,128)(2,1)S(1)}, u32[]{:S(2)}, u32[]{:S(2)}) collective-permute-start(bf16[512,256]{1,0:T(8,128)(2,1)S(1)} %get-tuple-element.110), channel_id=1, source_target_pairs={{0,4},{4,0},{8,12},{12,8},{16,20},{20,16},{24,28},{28,24},{1,5},{5... | collective-permute-start | bytes 786440 | tf_op jit(solution)/shard_map/ppermute | solution.py:31
  73.5 8.3 %collective-permute-start.12 = (bf16[512,256]{1,0:T(8,128)(2,1)S(1)}, bf16[512,256]{1,0:T(8,128)(2,1)S(1)}, u32[]{:S(2)}, u32[]{:S(2)}) collective-permute-start(bf16[512,256]{1,0:T(8,128)(2,1)S(1)} %get-tuple-element.105), channel_id=1, source_target_pairs={{8,0},{12,4},{16,8},{20,12},{24,16},{28,20},{9,1},{13,5},{17,9},{2... | collective-permute-start | bytes 786440 | tf_op jit(solution)/shard_map/ppermute | solution.py:26
  74.8 7.0 %collective-permute-start.13 = (bf16[512,256]{1,0:T(8,128)(2,1)S(1)}, bf16[512,256]{1,0:T(8,128)(2,1)S(1)}, u32[]{:S(2)}, u32[]{:S(2)}) collective-permute-start(bf16[512,256]{1,0:T(8,128)(2,1)S(1)} %get-tuple-element.106), channel_id=1, source_target_pairs={{0,4},{4,0},{8,12},{12,8},{16,20},{20,16},{24,28},{28,24},{1,5},{5... | collective-permute-start | bytes 786440 | tf_op jit(solution)/shard_map/ppermute | solution.py:31

commit v10 on v9

--- a/solution.py
+++ b/solution.py
@@ -224,7 +224,7 @@
             key_up, query, guest = k_up[:, at], q[:, at], qf[:, at]
             soft_set(head, k[:, at], query, pr_own, own, diagonal=True)
             delta_set(head, v[:, at], g[:, at], pr_own, pg_own, own)
-            soft_set(head, key_up, query, pr_mid, mid)
+            soft_set(head, k[:, at], guest, pr_mid, mid)
             soft_set(head, key_up, guest, pr_far, far)
             soft_set(head, k_x[:, at], query if odd else guest, pr_near, near)
 
@@ -233,12 +233,12 @@
     by_parity(near_span, run)
 
 
-def delta_mid_kernel(g, v_up, probs, soft, stats, pgrads):
+def delta_kernel(g, values, probs, soft, stats, pgrads):
     stats[0:2] = soft[0:2]
 
     def step(head):
         at = columns(head)
-        delta_set(head, v_up[:, at], g[:, at], probs, pgrads, stats)
+        delta_set(head, values[:, at], g[:, at], probs, pgrads, stats)
 
     each_head(0, probs.shape[0], step)
 
@@ -246,24 +246,20 @@
 def delta_near_kernel(near_span, g, v_x, probs, soft, stats, pgrads):
     def run(odd):
         if odd:
-            delta_mid_kernel(g, v_x, probs, soft, stats, pgrads)
+            delta_kernel(g, v_x, probs, soft, stats, pgrads)
 
     by_parity(near_span, run)
 
 
-def delta_guest_kernel(near_span, gf, v_up, v_x, pr_far, far, pr_near, near, _, up, pg_far, pg_near):
-    up[0:2] = far[0:2]
-    up[3:5] = near[0:2]
-
-    def run(odd):
-        def step(head):
-            at = columns(head)
-            grad = gf[:, at]
-            delta_set(head, v_up[:, at], grad, pr_far, pg_far, up)
-            if not odd:
-                delta_set(head, v_x[:, at], grad, pr_near, pg_near, up, 3)
-
-        each_head(0, pr_far.shape[0], step)
+def delta_guest_kernel(
+    near_span, gf, v, v_x, pr_mid, mid_soft, pr_near, near_soft, _stats, _pgrads,
+    mid, pg_mid, near, pg_near,
+):
+    delta_kernel(gf, v, pr_mid, mid_soft, mid, pg_mid)
+
+    def run(odd):
+        if not odd:
+            delta_kernel(gf, v_x, pr_near, near_soft, near, pg_near)
 
     by_parity(near_span, run)
 
@@ -298,41 +294,45 @@
         out[section] = flags.bias(section, out.shape[1:])
 
 
-def combine_local_kernel(near_span, bias, own, mid, near, out):
-    def run(odd):
-        near_bias = bias[NEAR]
-        parts = [part_of(own), part_of(mid, bias[MID])]
+def combine_local_kernel(near_span, bias, own, near, out):
+    out[3:6] = bias[0:3]
+
+    def run(odd):
+        parts = [part_of(own)]
         if odd:
-            parts.append(part_of(near, near_bias))
-            near_bias = jnp.full(near_bias.shape, -BIG, jnp.float32)
+            parts.append(part_of(near, bias[NEAR]))
         merged, _ = merge(parts)
-        for index, row in enumerate((*merged, bias[FAR], near_bias)):
+        for index, row in enumerate(merged):
             out[index] = row
 
     by_parity(near_span, run)
 
 
-def combine_own_kernel(near_span, bias, own, mid, near, up, *outs):
-    def run(odd):
-        parts = [part_of(own), part_of(mid, bias[MID])]
-        parts.append(part_of(near, bias[NEAR]) if odd else part_of(up, bias[NEAR], 3))
-        parts.append(part_of(up, bias[FAR]))
+def combine_guest_kernel(near_span, guest, far, mid, near, up, *outs):
+    def run(odd):
+        parts = [part_of(far, guest[3 + FAR]), part_of(mid, guest[3 + MID])]
+        if not odd:
+            parts.append(part_of(near, guest[3 + NEAR]))
+        merged, _ = merge(parts)
+        for index, row in enumerate(merged):
+            up[index] = row
+        merged, factors = merge([*parts, part_of(guest)])
+        put_norm(outs, factors[:-1], merged)
+
+    by_parity(near_span, run)
+
+
+def combine_own_kernel(spans, bias, own, near, up, *outs):
+    held = lax.axis_index("seq") >= spans[MID]
+
+    def run(odd):
+        parts = [part_of(own), part_of(up, jnp.where(held, 0.0, -BIG))]
+        if odd:
+            parts.insert(1, part_of(near, bias[NEAR]))
         merged, factors = merge(parts)
-        put_norm(outs if odd else outs[:2], factors, merged)
-
-    by_parity(near_span, run)
-
-
-def combine_guest_kernel(near_span, guest, up, far_out, near_out):
-    def run(odd):
-        parts = [part_of(up, guest[3])]
-        if not odd:
-            parts.append(part_of(up, guest[4], 3))
-        parts.append(part_of(guest))
-        merged, factors = merge(parts)
-        put_norm((far_out, near_out), factors[:-1], merged)
-
-    by_parity(near_span, run)
+        put_norm(outs, factors[:-1], merged)
+
+    by_parity(spans[NEAR], run)
 
 
 def pair_terms(head, query, grad, keys, probs, pgrads, norm):
@@ -355,17 +355,25 @@
 
 
 def guest_terms_kernel(
-    near_span, first, q, g, k_up, k_x, norm_far, norm_near, pr_far, pg_far, pr_near, pg_near, *refs
+    near_span, first, q, g, k, k_up, k_x, norm_far, norm_mid, norm_near,
+    pr_far, pg_far, pr_mid, pg_mid, pr_near, pg_near, *refs,
 ):
-    dq, dk_far, dv_far, dk_near, dv_near = refs[-5:]
+    dq, back, dk_mid, dv_mid, dk_near, dv_near = refs[-6:]
+    rows = q.shape[0]
 
     def run(odd):
         def step(head):
             at, out = columns(head), columns(head - first)
             query, grad = q[:, at], g[:, at]
-            query_term, dk_far[:, out], dv_far[:, out] = pair_terms(
+            query_term, key_term, value_term = pair_terms(
                 head, query, grad, k_up[:, at], pr_far, pg_far, norm_far
             )
+            back[:rows, out] = (key_term * SCALE).astype(back.dtype)
+            back[rows:, out] = value_term.astype(back.dtype)
+            more, dk_mid[:, out], dv_mid[:, out] = pair_terms(
+                head, query, grad, k[:, at], pr_mid, pg_mid, norm_mid
+            )
+            query_term = query_term + more
             if not odd:
                 more, dk_near[:, out], dv_near[:, out] = pair_terms(
                     head, query, grad, k_x[:, at], pr_near, pg_near, norm_near
@@ -373,37 +381,30 @@
                 query_term = query_term + more
             dq[:, at] = (query_term * SCALE).T.astype(dq.dtype)
 
-        each_head(first, dk_far.shape[1] // HDIM, step)
+        each_head(first, back.shape[1] // HDIM, step)
 
     by_parity(near_span, run)
 
 
 def own_terms_kernel(
-    near_span, first, q, g, k_up, k_x, norm_mid, norm_near, pr_mid, pg_mid, pr_near, pg_near,
-    dk_far, dv_far, dk_near, dv_near, *refs,
+    near_span, first, q, g, k_x, norm_near, pr_near, pg_near, dk_near, dv_near, *refs
 ):
-    dq, back, cross = refs[-3:]
+    dq, cross = refs[-2:]
     rows = q.shape[0]
 
     def run(odd):
         def step(head):
             at, out = columns(head), columns(head - first)
-            query, grad = q[:, at], g[:, at]
-            query_term, key_term, value_term = pair_terms(
-                head, query, grad, k_up[:, at], pr_mid, pg_mid, norm_mid
-            )
-            back[:rows, out] = ((key_term + dk_far[:, out]) * SCALE).astype(back.dtype)
-            back[rows:, out] = (value_term + dv_far[:, out]).astype(back.dtype)
             if odd:
-                more, key_term, value_term = pair_terms(
-                    head, query, grad, k_x[:, at], pr_near, pg_near, norm_near
+                query_term, key_term, value_term = pair_terms(
+                    head, q[:, at], g[:, at], k_x[:, at], pr_near, pg_near, norm_near
                 )
-                query_term = query_term + more
+                dq[:, at] = query_term.T
             else:
                 key_term, value_term = dk_near[:, out], dv_near[:, out]
+                dq[:, at] = jnp.zeros_like(key_term)
             cross[:rows, out] = (key_term * SCALE).astype(cross.dtype)
             cross[rows:, out] = value_term.astype(cross.dtype)
-            dq[:, at] = query_term.T
 
         each_head(first, cross.shape[1] // HDIM, step)
 
@@ -414,13 +415,13 @@
     return pl.ds(pl.multiple_of(pl.program_id(0) * block + first, block), block)
 
 
-def finish_kernel(first, dk, dv, back, cross, *refs):
+def finish_kernel(first, dk, dv, dk_mid, dv_mid, back, cross, *refs):
     key_out, value_out = refs[-2:]
     rows, block = key_out.shape
     here, at = step_columns(block), step_columns(block, first)
     for rows_at, total, out in (
-        (slice(0, rows), dk[:, at] * SCALE, key_out),
-        (slice(rows, 2 * rows), dv[:, at], value_out),
+        (slice(0, rows), (dk[:, at] + dk_mid[:, here]) * SCALE, key_out),
+        (slice(rows, 2 * rows), dv[:, at] + dv_mid[:, here], value_out),
     ):
         for ref in (back, cross):
             total = total + ref[rows_at, here].astype(jnp.float32)
@@ -480,69 +481,80 @@
     )
     self_prob, mid_prob, far_prob, near_prob = probs
 
-    def deltas(kernel, *ins):
-        return call(kernel, [], ins, [stat, square], heads * pair_work)
-
-    mid_stats, mid_pgrad = deltas(delta_mid_kernel, grads, value_up, mid_prob, mid_soft)
-    near_stats, near_pgrad = deltas(
-        bound(delta_near_kernel, near_span), grads, value_x, near_prob, near_soft
+    near_stats, near_pgrad = call(
+        bound(delta_near_kernel, near_span),
+        [],
+        [grads, value_x, near_prob, near_soft],
+        [stat, square],
+        heads * pair_work,
     )
     (merged,) = call(
         bound(combine_local_kernel, near_span),
         [],
-        [bias, self_stats, mid_stats, near_stats],
-        [table(5)],
+        [bias, self_stats, near_stats],
+        [table(6)],
         row_work,
     )
     guest_stats = shift(merged, -mid_span)
-    ins = [guest_grad, value_up, value_x, far_prob, far_soft, near_prob, near_soft, near_pgrad]
-    up_part, far_pgrad, near_pgrad = call(
+    ins = [guest_grad, value, value_x, mid_prob, mid_soft, near_prob, near_soft]
+    mid_stats, mid_pgrad, near_stats, near_pgrad = call(
         bound(delta_guest_kernel, near_span),
         [],
-        ins,
-        [table(6), square, square],
+        [*ins, near_stats, near_pgrad],
+        [stat, square] * 2,
         heads * 2 * pair_work,
-        {len(ins) - 1: 2},
+        {len(ins): 2, len(ins) + 1: 3},
+    )
+    far_stats, far_pgrad = call(
+        delta_kernel,
+        [],
+        [guest_grad, value_up, far_prob, far_soft],
+        [stat, square],
+        heads * pair_work,
+    )
+    up_part, *guest_norms = call(
+        bound(combine_guest_kernel, near_span),
+        [],
+        [guest_stats, far_stats, mid_stats, near_stats],
+        [stat] + [norm] * 3,
+        row_work,
     )
     up_stats = shift(up_part, mid_span)
-    far_norm, near_norm_guest = call(
-        bound(combine_guest_kernel, near_span), [], [guest_stats, up_part], [norm] * 2, row_work
+    self_norm, near_norm = call(
+        bound(combine_own_kernel, spans),
+        [],
+        [bias, self_stats, near_stats, up_stats],
+        [norm] * 2,
+        row_work,
     )
     near_squares = [near_prob, near_pgrad]
-    self_norm, mid_norm, near_norm = call(
-        bound(combine_own_kernel, near_span),
-        [],
-        [bias, self_stats, mid_stats, near_stats, up_stats],
-        [norm] * 3,
-        row_work,
-    )
     guest_part, query_part, returned = [], [], []
     first = 0
     for group in GROUPS:
-        narrow = (rows, group * HDIM)
-        ins = [guest_query, guest_grad, key_up, key_x, far_norm, near_norm_guest]
-        ins += [far_prob, far_pgrad, *near_squares]
-        *guest_part, far_key, far_value, near_key, near_value = call(
+        narrow = ((rows, group * HDIM), jnp.float32)
+        half = ((2 * rows, group * HDIM), jnp.bfloat16)
+        ins = [guest_query, guest_grad, key, key_up, key_x, *guest_norms]
+        ins += [far_prob, far_pgrad, mid_prob, mid_pgrad, *near_squares]
+        *guest_part, back, mid_key, mid_value, near_key, near_value = call(
             bound(guest_terms_kernel, near_span, first),
             [],
             ins + guest_part,
-            [wide_bf16] + [(narrow, jnp.float32)] * 4,
-            group * 6 * pair_work,
+            [wide_bf16, half] + [narrow] * 4,
+            group * 9 * pair_work,
             {len(ins): 0} if guest_part else {},
         )
-        ins = [query, grads, key_up, key_x, mid_norm, near_norm, mid_prob, mid_pgrad]
-        ins += [*near_squares, far_key, far_value, near_key, near_value]
-        half = ((2 * rows, group * HDIM), jnp.bfloat16)
-        *query_part, back, cross = call(
+        ins = [query, grads, key_x, near_norm, *near_squares, near_key, near_value]
+        *query_part, cross = call(
             bound(own_terms_kernel, near_span, first),
             [],
             ins + query_part,
-            [wide_f32, half, half],
-            group * 6 * pair_work,
+            [wide_f32, half],
+            group * 3 * pair_work,
             {len(ins): 0} if query_part else {},
         )
         back = shift(back, -mid_span)
-        returned.append((back, swap(cross, "seq", near_span)))
+        cross = swap(cross, "seq", near_span)
+        returned.append((mid_key, mid_value, back, cross))
         first += group
     (guest_part,) = guest_part
     guest_part = shift(guest_part, mid_span)

time: 82.9 us -> 84 us (1.013)
  waiting for transfers between devices: 29.5 us -> 31.2 us
    ppermute x8, waiting for transfers between devices: 8.53 us -> 14.4 us  [swap(): return lax.ppermute(value, axis, pairs)]
    ppermute x10, waiting for transfers between devices: 21 us -> 16.8 us  [shift(): lax.ppermute(value, 'seq', [(src, src + steps) for src in range(low, high)])]
    ppermute x10, starting transfers between devices: 23 us -> 22.1 us  [shift(): lax.ppermute(value, 'seq', [(src, src + steps) for src in range(low, high)])]
where the time goes in v10:
time: 84 us; the launch traced here: 83.6 us
  starting transfers between devices  31.4 us (37%)
  waiting for transfers between devices  31.2 us (37%)
  Pallas kernels  20 us (24%)
  between operations  0.92 us (1%)
    ppermute x10, starting transfers between devices, shift(): lax.ppermute(value, 'seq', [(src, src + steps) for src in range(low, high)])  22.1 us
    pallas_call x20, Pallas kernels, call(): pl.pallas_call(kernel, grid=grid or (), in_specs=[smem] * len(scalars) +...  18.6 us
    ppermute x10, waiting for transfers between devices, shift(): lax.ppermute(value, 'seq', [(src, src + steps) for src in range(low, high)])  16.8 us
    ppermute x8, waiting for transfers between devices, swap(): return lax.ppermute(value, axis, pairs)  14.4 us
    ppermute x8, starting transfers between devices, swap(): return lax.ppermute(value, axis, pairs)  9.38 us
  transfers between devices with their start and end apart: 18, of which 6 were waited for; matrix products, arithmetic and copies ran while one was open for 0% of the time, Pallas kernels for 23%

profile of v10, /device:TPU:0, one launch (start us, length us, event | category | flops | bytes accessed | tf_op | source)
XLA Modules:
  0.0 83.6 jit_solution(17864412177245515850)
XLA Ops:
  0.7 3.1 %collective-permute-start.1 = (bf16[256,512]{1,0:T(8,128)(2,1)}, bf16[256,512]{1,0:T(8,128)(2,1)S(1)}, u32[]{:S(2)}, u32[]{:S(2)}) collective-permute-start(bf16[256,512]{1,0:T(8,128)(2,1)} %refs_3_.1), channel_id=1, source_target_pairs={{0,2},{1,3},{2,0},{3,1},{4,6},{5,7},{6,4},{7,5},{8,10},{9,11},{10,... | collective-permute-start | bytes 786440 | tf_op jit(solution)/shard_map/ppermute | solution.py:31
  3.7 1.3 %collective-permute-start.3 = (bf16[256,1024]{1,0:T(8,128)(2,1)}, bf16[256,1024]{1,0:T(8,128)(2,1)S(1)}, u32[]{:S(2)}, u32[]{:S(2)}) collective-permute-start(bf16[256,1024]{1,0:T(8,128)(2,1)} %refs_0_.1), channel_id=1, source_target_pairs={{8,0},{12,4},{16,8},{20,12},{24,16},{28,20},{9,1},{13,5},{17,9},{2... | collective-permute-start | bytes 1572872 | tf_op jit(solution)/shard_map/ppermute | solution.py:26
  5.0 0.1 collective-permute-start
  5.1 5.1 %collective-permute-done.1.refs_1_ = bf16[256,512]{1,0:T(8,128)(2,1)S(1)} collective-permute-done((bf16[256,512]{1,0:T(8,128)(2,1)}, bf16[256,512]{1,0:T(8,128)(2,1)S(1)}, u32[]{:S(2)}, u32[]{:S(2)}) %collective-permute-start.1) | collective-permute-done | bytes 262176 | tf_op jit(solution)/shard_map/ppermute | solution.py:31
  10.2 0.0 collective-permute-start.2
  10.2 3.7 %collective-permute-start.4 = (bf16[256,1024]{1,0:T(8,128)(2,1)}, bf16[256,1024]{1,0:T(8,128)(2,1)S(1)}, u32[]{:S(2)}, u32[]{:S(2)}) collective-permute-start(bf16[256,1024]{1,0:T(8,128)(2,1)} %refs_1_.2), channel_id=1, source_target_pairs={{0,8},{4,12},{8,16},{12,20},{16,24},{20,28},{1,9},{5,13},{9,17},{1... | collective-permute-start | bytes 1572872 | tf_op jit(solution)/shard_map/ppermute | solution.py:26
  14.0 1.6 %collective-permute-start.5 = (bf16[256,1024]{1,0:T(8,128)(2,1)}, bf16[256,1024]{1,0:T(8,128)(2,1)S(1)}, u32[]{:S(2)}, u32[]{:S(2)}) collective-permute-start(bf16[256,1024]{1,0:T(8,128)(2,1)} %refs_1_.2), channel_id=1, source_target_pairs={{0,4},{4,0},{8,12},{12,8},{16,20},{20,16},{24,28},{28,24},{1,5},{5... | collective-permute-start | bytes 1572872 | tf_op jit(solution)/shard_map/ppermute | solution.py:31
  15.5 0.5 collective-permute-start.7
  16.1 0.0 collective-permute-done.2.refs_2_
  16.1 3.5 %collective-permute-start.9 = (bf16[256,1024]{1,0:T(8,128)(2,1)}, bf16[256,1024]{1,0:T(8,128)(2,1)S(1)}, u32[]{:S(2)}, u32[]{:S(2)}) collective-permute-start(bf16[256,1024]{1,0:T(8,128)(2,1)} %refs_2_.1), channel_id=1, source_target_pairs={{0,8},{4,12},{8,16},{12,20},{16,24},{20,28},{1,9},{5,13},{9,17},{1... | collective-permute-start | bytes 1572872 | tf_op jit(solution)/shard_map/ppermute | solution.py:26
  19.5 4.2 %shard_map.94.refs_1_.refs_0_.g = bf16[256,1024]{1,0:T(8,128)(2,1)S(1)} custom-call(bf16[256,512]{1,0:T(8,128)(2,1)S(1)} %collective-permute-done.refs_0_, bf16[256,512]{1,0:T(8,128)(2,1)S(1)} %collective-permute-done.1.refs_1_, bf16[256,512]{1,0:T(8,128)(2,1)S(1)} %collective-permute-done.2.refs_2_, bf16[256,512]{1,0:T(8,128)(2,1)} %refs_3_.1, ...), custom_call_target="tpu_custom_call" | custom-call | flops 1073741824 | tf_op jit(solution)/shard_map/pallas_call | solution.py:51
  23.8 1.3 %collective-permute-start.6 = (bf16[256,1024]{1,0:T(8,128)(2,1)S(1)}, bf16[256,1024]{1,0:T(8,128)(2,1)S(1)}, u32[]{:S(2)}, u32[]{:S(2)}) collective-permute-start(bf16[256,1024]{1,0:T(8,128)(2,1)S(1)} %shard_map.94.refs_1_.refs_0_.g), channel_id=1, source_target_pairs={{8,0},{12,4},{16,8},{20,12},{24,16},{28,20},{9,1},{13,5},{17,9},{2... | collective-permute-start | bytes 1572872 | tf_op jit(solution)/shard_map/ppermute | solution.py:26
  25.1 0.6 shard_map.95.refs_0_
  25.7 1.4 %stage.1 = (bf16[256,1024]{1,0:T(8,128)(2,1)S(1)}, bf16[256,1024]{1,0:T(8,128)(2,1)S(1)}, bf16[256,1024]{1,0:T(8,128)(2,1)S(1)}) custom-call(bf16[256,1024]{1,0:T(8,128)(2,1)} %refs_0_.1, bf16[256,1024]{1,0:T(8,128)(2,1)} %refs_1_.2, bf16[256,1024]{1,0:T(8,128)(2,1)} %refs_2_.1), custom_call_target="tpu_custom_call" | custom-call | flops 1000000 | tf_op jit(solution)/shard_map/stage/pallas_call | solution.py:158
  27.1 1.9 %collective-permute-done.5.refs_6_.refs_4_.refs_2_ = bf16[256,1024]{1,0:T(8,128)(2,1)S(1)} collective-permute-done((bf16[256,1024]{1,0:T(8,128)(2,1)}, bf16[256,1024]{1,0:T(8,128)(2,1)S(1)}, u32[]{:S(2)}, u32[]{:S(2)}) %collective-permute-start.5) | collective-permute-done | bytes 524320 | tf_op jit(solution)/shard_map/ppermute | solution.py:31
  29.0 3.2 %shard_map.96 = (f32[3,8,256]{2,1,0:T(8,128)S(1)}, f32[3,8,256]{2,1,0:T(8,128)S(1)}, f32[3,8,256]{2,1,0:T(8,128)S(1)}, f32[3,8,256]{2,1,0:T(8,128)S(1)}, f32[8,2...) custom-call(bf16[256,1024]{1,0:T(8,128)(2,1)S(1)} %get-tuple-element, ...), custom_call_target="tpu_custom_call" | custom-call | flops 671088640 | tf_op jit(solution)/shard_map/pallas_call | solution.py:51
  32.3 7.3 %collective-permute-done.7.refs_1_.refs_2_ = bf16[256,1024]{1,0:T(8,128)(2,1)S(1)} collective-permute-done((bf16[256,1024]{1,0:T(8,128)(2,1)}, bf16[256,1024]{1,0:T(8,128)(2,1)S(1)}, u32[]{:S(2)}, u32[]{:S(2)}) %collective-permute-start.7) | collective-permute-done | bytes 524320 | tf_op jit(solution)/shard_map/ppermute | solution.py:31
  39.5 1.3 %collective-permute-start.8 = (f32[6,8,256]{2,1,0:T(8,128)S(1)}, f32[6,8,256]{2,1,0:T(8,128)S(1)}, u32[]{:S(2)}, u32[]{:S(2)}) collective-permute-start(f32[6,8,256]{2,1,0:T(8,128)S(1)} %shard_map.99), channel_id=1, source_target_pairs={{8,0},{12,4},{16,8},{20,12},{24,16},{28,20},{9,1},{13,5},{17,9},{2... | collective-permute-start | bytes 147464 | tf_op jit(solution)/shard_map/ppermute | solution.py:26
  40.9 0.0 collective-permute-done.6.refs_0_.g.refs_1_
  40.9 0.7 shard_map.100
  41.6 1.4 %shard_map.98 = (f32[3,8,256]{2,1,0:T(8,128)S(1)}, f32[8,256,256]{2,1,0:T(8,128)S(1)}, f32[3,8,256]{2,1,0:T(8,128)S(1)}, f32[8,256,256]{2,1,0:T(8,128)S(1)}) custom-call(bf16[256,1024]{1,0:T(8,128)(2,1)S(1)} %collective-permute-done.6.refs_0_.g.refs_1_, ...), custom_call_target="tpu_custom_call", output_to_operand_aliasing={{2}: (7, {}), {3}: (8, {})} | custom-call | flops 268435456 | tf_op jit(solution)/shard_map/pallas_call | solution.py:51
  42.9 2.6 %collective-permute-done.8.refs_0_ = f32[6,8,256]{2,1,0:T(8,128)S(1)} collective-permute-done((f32[6,8,256]{2,1,0:T(8,128)S(1)}, f32[6,8,256]{2,1,0:T(8,128)S(1)}, u32[]{:S(2)}, u32[]{:S(2)}) %collective-permute-start.8) | collective-permute-done | bytes 49184 | tf_op jit(solution)/shard_map/ppermute | solution.py:26
  45.6 3.5 %collective-permute-start.10 = (f32[3,8,256]{2,1,0:T(8,128)S(1)}, f32[3,8,256]{2,1,0:T(8,128)S(1)}, u32[]{:S(2)}, u32[]{:S(2)}) collective-permute-start(f32[3,8,256]{2,1,0:T(8,128)S(1)} %get-tuple-element.77), channel_id=1, source_target_pairs={{0,8},{4,12},{8,16},{12,20},{16,24},{20,28},{1,9},{5,13},{9,17},{1... | collective-permute-start | bytes 73736 | tf_op jit(solution)/shard_map/ppermute | solution.py:26
  49.0 0.8 shard_map.103
  49.8 1.4 %shard_map.104 = (bf16[256,1024]{1,0:T(8,128)(2,1)S(1)}, bf16[512,512]{1,0:T(8,128)(2,1)S(1)}, f32[256,512]{1,0:T(8,128)S(1)}, f32[256,512]{1,0:T(8,128)S(1)}, f...) custom-call(bf16[256,1024]{1,0:T(8,128)(2,1)S(1)} %collective-permute-done.3.refs_4_.refs_0_, ...), custom_call_target="tpu_custom_call", output_to_operand_aliasing={{0}: (14, {})} | custom-call | flops 603979776 | tf_op jit(solution)/shard_map/pallas_call | solution.py:51
  51.2 0.8 shard_map.105
  52.0 3.5 %collective-permute-start.11 = (bf16[256,1024]{1,0:T(8,128)(2,1)S(1)}, bf16[256,1024]{1,0:T(8,128)(2,1)S(1)}, u32[]{:S(2)}, u32[]{:S(2)}) collective-permute-start(bf16[256,1024]{1,0:T(8,128)(2,1)S(1)} %get-tuple-element.100), channel_id=1, source_target_pairs={{0,8},{4,12},{8,16},{12,20},{16,24},{20,28},{1,9},{5,13},{9,17},{1... | collective-permute-start | bytes 1572872 | tf_op jit(solution)/shard_map/ppermute | solution.py:26
  55.5 1.5 %collective-permute-start.14 = (bf16[512,512]{1,0:T(8,128)(2,1)S(1)}, bf16[512,512]{1,0:T(8,128)(2,1)S(1)}, u32[]{:S(2)}, u32[]{:S(2)}) collective-permute-start(bf16[512,512]{1,0:T(8,128)(2,1)S(1)} %get-tuple-element.109), channel_id=1, source_target_pairs={{8,0},{12,4},{16,8},{20,12},{24,16},{28,20},{9,1},{13,5},{17,9},{2... | collective-permute-start | bytes 1572872 | tf_op jit(solution)/shard_map/ppermute | solution.py:26
  57.0 0.0 collective-permute-done.10.refs_3_
  57.1 0.1 shard_map.106
  57.2 0.2 shard_map.107
  57.3 2.4 %collective-permute-start.15 = (bf16[512,512]{1,0:T(8,128)(2,1)S(1)}, bf16[512,512]{1,0:T(8,128)(2,1)S(1)}, u32[]{:S(2)}, u32[]{:S(2)}) collective-permute-start(bf16[512,512]{1,0:T(8,128)(2,1)S(1)} %get-tuple-element.110), channel_id=1, source_target_pairs={{0,4},{4,0},{8,12},{12,8},{16,20},{20,16},{24,28},{28,24},{1,5},{5... | collective-permute-start | bytes 1572872 | tf_op jit(solution)/shard_map/ppermute | solution.py:31
  59.7 1.3 %collective-permute-start.16 = (bf16[512,256]{1,0:T(8,128)(2,1)S(1)}, bf16[512,256]{1,0:T(8,128)(2,1)S(1)}, u32[]{:S(2)}, u32[]{:S(2)}) collective-permute-start(bf16[512,256]{1,0:T(8,128)(2,1)S(1)} %get-tuple-element.113), channel_id=1, source_target_pairs={{8,0},{12,4},{16,8},{20,12},{24,16},{28,20},{9,1},{13,5},{17,9},{2... | collective-permute-start | bytes 786440 | tf_op jit(solution)/shard_map/ppermute | solution.py:26
  61.0 0.1 collective-permute-start.17
  61.1 0.1 shard_map.108
  61.2 13.3 %collective-permute-done.16.refs_4_ = bf16[512,256]{1,0:T(8,128)(2,1)S(1)} collective-permute-done((bf16[512,256]{1,0:T(8,128)(2,1)S(1)}, bf16[512,256]{1,0:T(8,128)(2,1)S(1)}, u32[]{:S(2)}, u32[]{:S(2)}) %collective-permute-start.16) | collective-permute-done | bytes 262176 | tf_op jit(solution)/shard_map/ppermute | solution.py:26
  74.5 1.3 %collective-permute-start.12 = (bf16[512,256]{1,0:T(8,128)(2,1)S(1)}, bf16[512,256]{1,0:T(8,128)(2,1)S(1)}, u32[]{:S(2)}, u32[]{:S(2)}) collective-permute-start(bf16[512,256]{1,0:T(8,128)(2,1)S(1)} %get-tuple-element.105), channel_id=1, source_target_pairs={{8,0},{12,4},{16,8},{20,12},{24,16},{28,20},{9,1},{13,5},{17,9},{2... | collective-permute-start | bytes 786440 | tf_op jit(solution)/shard_map/ppermute | solution.py:26
  75.8 0.0 collective-permute-done.17.refs_5_
  75.8 1.7 %collective-permute-start.13 = (bf16[512,256]{1,0:T(8,128)(2,1)S(1)}, bf16[512,256]{1,0:T(8,128)(2,1)S(1)}, u32[]{:S(2)}, u32[]{:S(2)}) collective-permute-start(bf16[512,256]{1,0:T(8,128)(2,1)S(1)} %get-tuple-element.106), channel_id=1, source_target_pairs={{0,4},{4,0},{8,12},{12,8},{16,20},{20,16},{24,28},{28,24},{1,5},{5... | collective-permute-start | bytes 786440 | tf_op jit(solution)/shard_map/ppermute | solution.py:31
  77.5 1.3 %shard_map.109 = (f32[256,1024]{1,0:T(8,128)S(1)}, f32[256,1024]{1,0:T(8,128)S(1)}, f32[256,1024]{1,0:T(8,128)S(1)}) custom-call(bf16[256,1024]{1,0:T(8,128)(2,1)S(1)} %get-tuple-element.62.refs_0_.q, bf16[256,1024]{1,0:T(8,128)(2,1)S(1)} %shard_map.94.refs_1_.refs_0_.g, bf16[256,1024]{1,0:T(8,128)(2,1)S(1)} %get-tuple-element.63.refs_2_.k, ...), custom_call_target="tpu_custom_call" | custom-call | flops 402653184 | tf_op jit(solution)/shard_map/pallas_call | solution.py:51
  78.8 0.8 shard_map.111
  79.5 0.0 collective-permute-done.11.guest
  79.6 1.4 %shard_map.110 = bf16[256,1024]{1,0:T(8,128)(2,1)} custom-call(f32[256,1024]{1,0:T(8,128)S(1)} %get-tuple-element.99.dq, bf16[256,1024]{1,0:T(8,128)(2,1)S(1)} %collective-permute-done.11.guest), custom_call_target="tpu_custom_call" | custom-call | flops 524288 | tf_op jit(solution)/shard_map/pallas_call | solution.py:51
  81.0 0.0 collective-permute-done.14.refs_4_
  81.0 0.0 collective-permute-done.15.refs_5_
  81.0 0.9 %shard_map.112 = (bf16[256,1024]{1,0:T(8,128)(2,1)}, bf16[256,1024]{1,0:T(8,128)(2,1)}) custom-call(f32[256,1024]{1,0:T(8,128)S(1)} %get-tuple-element.101.refs_0_, f32[256,1024]{1,0:T(8,128)S(1)} %get-tuple-element.102.refs_1_, f32[256,512]{1,0:T(8,128)S(1)} %get-tuple-element.107.refs_2_, ...), custom_call_target="tpu_custom_call", output_to_operand_aliasing={{0}: (6, {}), {1}: (7, {})} | custom-call | flops 33554432 | tf_op jit(solution)/shard_map/pallas_call | solution.py:51
  81.9 0.9 %collective-permute-done.12.refs_4_ = bf16[512,256]{1,0:T(8,128)(2,1)S(1)} collective-permute-done((bf16[512,256]{1,0:T(8,128)(2,1)S(1)}, bf16[512,256]{1,0:T(8,128)(2,1)S(1)}, u32[]{:S(2)}, u32[]{:S(2)}) %collective-permute-start.12) | collective-permute-done | bytes 262176 | tf_op jit(solution)/shard_map/ppermute | solution.py:26
  82.8 0.8 shard_map.113
  (13 shorter events, 0.1 us)
Async XLA Ops:
  0.6 24.4 %copy-start = (s32[8,3]{0,1:T(4,128)S(1)}, s32[8,3]{0,1:T(4,128)}, u32[]{:S(2)}) copy-start(s32[8,3]{0,1:T(4,128)} %param.12) | copy-start | bytes 292
  0.6 24.4 %copy-start.1 = (s32[1,3]{1,0:T(1,128)S(1)}, s32[1,3]{1,0:T(1,128)}, u32[]{:S(2)}) copy-start(s32[1,3]{1,0:T(1,128)} %refs_1_.3) | copy-start | bytes 40
  0.7 9.6 %collective-permute-start.1 = (bf16[256,512]{1,0:T(8,128)(2,1)}, bf16[256,512]{1,0:T(8,128)(2,1)S(1)}, u32[]{:S(2)}, u32[]{:S(2)}) collective-permute-start(bf16[256,512]{1,0:T(8,128)(2,1)} %refs_3_.1), channel_id=1, source_target_pairs={{0,2},{1,3},{2,0},{3,1},{4,6},{5,7},{6,4},{7,5},{8,10},{9,11},{10,... | collective-permute-start | bytes 786440 | tf_op jit(solution)/shard_map/ppermute | solution.py:31
  3.7 20.1 %collective-permute-start.3 = (bf16[256,1024]{1,0:T(8,128)(2,1)}, bf16[256,1024]{1,0:T(8,128)(2,1)S(1)}, u32[]{:S(2)}, u32[]{:S(2)}) collective-permute-start(bf16[256,1024]{1,0:T(8,128)(2,1)} %refs_0_.1), channel_id=1, source_target_pairs={{8,0},{12,4},{16,8},{20,12},{24,16},{28,20},{9,1},{13,5},{17,9},{2... | collective-permute-start | bytes 1572872 | tf_op jit(solution)/shard_map/ppermute | solution.py:26
  5.0 10.5 %collective-permute-start = (bf16[256,512]{1,0:T(8,128)(2,1)}, bf16[256,512]{1,0:T(8,128)(2,1)S(1)}, u32[]{:S(2)}, u32[]{:S(2)}) collective-permute-start(bf16[256,512]{1,0:T(8,128)(2,1)} %refs_3_.1), channel_id=1, source_target_pairs={{0,1},{1,0},{2,3},{3,2},{4,5},{5,4},{6,7},{7,6},{8,9},{9,8},{10,11... | collective-permute-start | bytes 786440 | tf_op jit(solution)/shard_map/ppermute | solution.py:31
  10.2 5.8 %collective-permute-start.2 = (bf16[256,512]{1,0:T(8,128)(2,1)S(1)}, bf16[256,512]{1,0:T(8,128)(2,1)S(1)}, u32[]{:S(2)}, u32[]{:S(2)}) collective-permute-start(bf16[256,512]{1,0:T(8,128)(2,1)S(1)} %collective-permute-done.1.refs_1_), channel_id=1, source_target_pairs={{0,1},{1,0},{2,3},{3,2},{4,5},{5,4},{6,7},{7,6},{8,9},{9,8},{10,11... | collective-permute-start | bytes 786440 | tf_op jit(solution)/shard_map/ppermute | solution.py:31
  10.2 16.9 %collective-permute-start.4 = (bf16[256,1024]{1,0:T(8,128)(2,1)}, bf16[256,1024]{1,0:T(8,128)(2,1)S(1)}, u32[]{:S(2)}, u32[]{:S(2)}) collective-permute-start(bf16[256,1024]{1,0:T(8,128)(2,1)} %refs_1_.2), channel_id=1, source_target_pairs={{0,8},{4,12},{8,16},{12,20},{16,24},{20,28},{1,9},{5,13},{9,17},{1... | collective-permute-start | bytes 1572872 | tf_op jit(solution)/shard_map/ppermute | solution.py:26
  14.0 15.1 %collective-permute-start.5 = (bf16[256,1024]{1,0:T(8,128)(2,1)}, bf16[256,1024]{1,0:T(8,128)(2,1)S(1)}, u32[]{:S(2)}, u32[]{:S(2)}) collective-permute-start(bf16[256,1024]{1,0:T(8,128)(2,1)} %refs_1_.2), channel_id=1, source_target_pairs={{0,4},{4,0},{8,12},{12,8},{16,20},{20,16},{24,28},{28,24},{1,5},{5... | collective-permute-start | bytes 1572872 | tf_op jit(solution)/shard_map/ppermute | solution.py:31
  15.5 24.0 %collective-permute-start.7 = (bf16[256,1024]{1,0:T(8,128)(2,1)}, bf16[256,1024]{1,0:T(8,128)(2,1)S(1)}, u32[]{:S(2)}, u32[]{:S(2)}) collective-permute-start(bf16[256,1024]{1,0:T(8,128)(2,1)} %refs_2_.1), channel_id=1, source_target_pairs={{0,4},{4,0},{8,12},{12,8},{16,20},{20,16},{24,28},{28,24},{1,5},{5... | collective-permute-start | bytes 1572872 | tf_op jit(solution)/shard_map/ppermute | solution.py:31
  16.1 24.8 %collective-permute-start.9 = (bf16[256,1024]{1,0:T(8,128)(2,1)}, bf16[256,1024]{1,0:T(8,128)(2,1)S(1)}, u32[]{:S(2)}, u32[]{:S(2)}) collective-permute-start(bf16[256,1024]{1,0:T(8,128)(2,1)} %refs_2_.1), channel_id=1, source_target_pairs={{0,8},{4,12},{8,16},{12,20},{16,24},{20,28},{1,9},{5,13},{9,17},{1... | collective-permute-start | bytes 1572872 | tf_op jit(solution)/shard_map/ppermute | solution.py:26
  23.8 17.1 %collective-permute-start.6 = (bf16[256,1024]{1,0:T(8,128)(2,1)S(1)}, bf16[256,1024]{1,0:T(8,128)(2,1)S(1)}, u32[]{:S(2)}, u32[]{:S(2)}) collective-permute-start(bf16[256,1024]{1,0:T(8,128)(2,1)S(1)} %shard_map.94.refs_1_.refs_0_.g), channel_id=1, source_target_pairs={{8,0},{12,4},{16,8},{20,12},{24,16},{28,20},{9,1},{13,5},{17,9},{2... | collective-permute-start | bytes 1572872 | tf_op jit(solution)/shard_map/ppermute | solution.py:26
  39.5 6.0 %collective-permute-start.8 = (f32[6,8,256]{2,1,0:T(8,128)S(1)}, f32[6,8,256]{2,1,0:T(8,128)S(1)}, u32[]{:S(2)}, u32[]{:S(2)}) collective-permute-start(f32[6,8,256]{2,1,0:T(8,128)S(1)} %shard_map.99), channel_id=1, source_target_pairs={{8,0},{12,4},{16,8},{20,12},{24,16},{28,20},{9,1},{13,5},{17,9},{2... | collective-permute-start | bytes 147464 | tf_op jit(solution)/shard_map/ppermute | solution.py:26
  45.6 11.5 %collective-permute-start.10 = (f32[3,8,256]{2,1,0:T(8,128)S(1)}, f32[3,8,256]{2,1,0:T(8,128)S(1)}, u32[]{:S(2)}, u32[]{:S(2)}) collective-permute-start(f32[3,8,256]{2,1,0:T(8,128)S(1)} %get-tuple-element.77), channel_id=1, source_target_pairs={{0,8},{4,12},{8,16},{12,20},{16,24},{20,28},{1,9},{5,13},{9,17},{1... | collective-permute-start | bytes 73736 | tf_op jit(solution)/shard_map/ppermute | solution.py:26
  52.0 27.5 %collective-permute-start.11 = (bf16[256,1024]{1,0:T(8,128)(2,1)S(1)}, bf16[256,1024]{1,0:T(8,128)(2,1)S(1)}, u32[]{:S(2)}, u32[]{:S(2)}) collective-permute-start(bf16[256,1024]{1,0:T(8,128)(2,1)S(1)} %get-tuple-element.100), channel_id=1, source_target_pairs={{0,8},{4,12},{8,16},{12,20},{16,24},{20,28},{1,9},{5,13},{9,17},{1... | collective-permute-start | bytes 1572872 | tf_op jit(solution)/shard_map/ppermute | solution.py:26
  55.5 25.5 %collective-permute-start.14 = (bf16[512,512]{1,0:T(8,128)(2,1)S(1)}, bf16[512,512]{1,0:T(8,128)(2,1)S(1)}, u32[]{:S(2)}, u32[]{:S(2)}) collective-permute-start(bf16[512,512]{1,0:T(8,128)(2,1)S(1)} %get-tuple-element.109), channel_id=1, source_target_pairs={{8,0},{12,4},{16,8},{20,12},{24,16},{28,20},{9,1},{13,5},{17,9},{2... | collective-permute-start | bytes 1572872 | tf_op jit(solution)/shard_map/ppermute | solution.py:26
  57.3 23.7 %collective-permute-start.15 = (bf16[512,512]{1,0:T(8,128)(2,1)S(1)}, bf16[512,512]{1,0:T(8,128)(2,1)S(1)}, u32[]{:S(2)}, u32[]{:S(2)}) collective-permute-start(bf16[512,512]{1,0:T(8,128)(2,1)S(1)} %get-tuple-element.110), channel_id=1, source_target_pairs={{0,4},{4,0},{8,12},{12,8},{16,20},{20,16},{24,28},{28,24},{1,5},{5... | collective-permute-start | bytes 1572872 | tf_op jit(solution)/shard_map/ppermute | solution.py:31
  59.7 14.8 %collective-permute-start.16 = (bf16[512,256]{1,0:T(8,128)(2,1)S(1)}, bf16[512,256]{1,0:T(8,128)(2,1)S(1)}, u32[]{:S(2)}, u32[]{:S(2)}) collective-permute-start(bf16[512,256]{1,0:T(8,128)(2,1)S(1)} %get-tuple-element.113), channel_id=1, source_target_pairs={{8,0},{12,4},{16,8},{20,12},{24,16},{28,20},{9,1},{13,5},{17,9},{2... | collective-permute-start | bytes 786440 | tf_op jit(solution)/shard_map/ppermute | solution.py:26
  61.0 14.8 %collective-permute-start.17 = (bf16[512,256]{1,0:T(8,128)(2,1)S(1)}, bf16[512,256]{1,0:T(8,128)(2,1)S(1)}, u32[]{:S(2)}, u32[]{:S(2)}) collective-permute-start(bf16[512,256]{1,0:T(8,128)(2,1)S(1)} %get-tuple-element.114), channel_id=1, source_target_pairs={{0,4},{4,0},{8,12},{12,8},{16,20},{20,16},{24,28},{28,24},{1,5},{5... | collective-permute-start | bytes 786440 | tf_op jit(solution)/shard_map/ppermute | solution.py:31
  74.5 8.3 %collective-permute-start.12 = (bf16[512,256]{1,0:T(8,128)(2,1)S(1)}, bf16[512,256]{1,0:T(8,128)(2,1)S(1)}, u32[]{:S(2)}, u32[]{:S(2)}) collective-permute-start(bf16[512,256]{1,0:T(8,128)(2,1)S(1)} %get-tuple-element.105), channel_id=1, source_target_pairs={{8,0},{12,4},{16,8},{20,12},{24,16},{28,20},{9,1},{13,5},{17,9},{2... | collective-permute-start | bytes 786440 | tf_op jit(solution)/shard_map/ppermute | solution.py:26
  75.8 7.0 %collective-permute-start.13 = (bf16[512,256]{1,0:T(8,128)(2,1)S(1)}, bf16[512,256]{1,0:T(8,128)(2,1)S(1)}, u32[]{:S(2)}, u32[]{:S(2)}) collective-permute-start(bf16[512,256]{1,0:T(8,128)(2,1)S(1)} %get-tuple-element.106), channel_id=1, source_target_pairs={{0,4},{4,0},{8,12},{12,8},{16,20},{20,16},{24,28},{28,24},{1,5},{5... | collective-permute-start | bytes 786440 | tf_op jit(solution)/shard_map/ppermute | solution.py:31

commit v11 on v10

--- a/solution.py
+++ b/solution.py
@@ -295,8 +295,6 @@
 
 
 def combine_local_kernel(near_span, bias, own, near, out):
-    out[3:6] = bias[0:3]
-
     def run(odd):
         parts = [part_of(own)]
         if odd:
@@ -308,15 +306,23 @@
     by_parity(near_span, run)
 
 
-def combine_guest_kernel(near_span, guest, far, mid, near, up, *outs):
-    def run(odd):
-        parts = [part_of(far, guest[3 + FAR]), part_of(mid, guest[3 + MID])]
-        if not odd:
-            parts.append(part_of(near, guest[3 + NEAR]))
-        merged, _ = merge(parts)
+def guest_parts(odd, bias, far, mid, near):
+    parts = [part_of(far, bias[FAR]), part_of(mid, bias[MID])]
+    return parts if odd else [*parts, part_of(near, bias[NEAR])]
+
+
+def merge_up_kernel(near_span, bias, far, mid, near, up):
+    def run(odd):
+        merged, _ = merge(guest_parts(odd, bias, far, mid, near))
         for index, row in enumerate(merged):
             up[index] = row
-        merged, factors = merge([*parts, part_of(guest)])
+
+    by_parity(near_span, run)
+
+
+def combine_guest_kernel(near_span, bias, guest, far, mid, near, *outs):
+    def run(odd):
+        merged, factors = merge([*guest_parts(odd, bias, far, mid, near), part_of(guest)])
         put_norm(outs, factors[:-1], merged)
 
     by_parity(near_span, run)
@@ -354,59 +360,61 @@
     each_head(0, probs.shape[0], step)
 
 
-def guest_terms_kernel(
-    near_span, first, q, g, k, k_up, k_x, norm_far, norm_mid, norm_near,
-    pr_far, pg_far, pr_mid, pg_mid, pr_near, pg_near, *refs,
+def far_terms_kernel(first, q, g, k_up, norm, probs, pgrads, dq, back):
+    rows = q.shape[0]
+
+    def step(head):
+        at, out = columns(head), columns(head - first)
+        query_term, key_term, value_term = pair_terms(
+            head, q[:, at], g[:, at], k_up[:, at], probs, pgrads, norm
+        )
+        dq[:, out] = query_term.T
+        back[:rows, out] = (key_term * SCALE).astype(back.dtype)
+        back[rows:, out] = value_term.astype(back.dtype)
+
+    each_head(first, back.shape[1] // HDIM, step)
+
+
+def near_terms_kernel(
+    near_span, first, q, g, qf, gf, k_x, norm_own, norm_guest, probs, pgrads, dq, cross
 ):
-    dq, back, dk_mid, dv_mid, dk_near, dv_near = refs[-6:]
     rows = q.shape[0]
 
     def run(odd):
+        query, grad, norm = (q, g, norm_own) if odd else (qf, gf, norm_guest)
+
         def step(head):
             at, out = columns(head), columns(head - first)
-            query, grad = q[:, at], g[:, at]
             query_term, key_term, value_term = pair_terms(
-                head, query, grad, k_up[:, at], pr_far, pg_far, norm_far
+                head, query[:, at], grad[:, at], k_x[:, at], probs, pgrads, norm
             )
-            back[:rows, out] = (key_term * SCALE).astype(back.dtype)
-            back[rows:, out] = value_term.astype(back.dtype)
-            more, dk_mid[:, out], dv_mid[:, out] = pair_terms(
-                head, query, grad, k[:, at], pr_mid, pg_mid, norm_mid
-            )
-            query_term = query_term + more
-            if not odd:
-                more, dk_near[:, out], dv_near[:, out] = pair_terms(
-                    head, query, grad, k_x[:, at], pr_near, pg_near, norm_near
-                )
-                query_term = query_term + more
-            dq[:, at] = (query_term * SCALE).T.astype(dq.dtype)
-
-        each_head(first, back.shape[1] // HDIM, step)
-
-    by_parity(near_span, run)
-
-
-def own_terms_kernel(
-    near_span, first, q, g, k_x, norm_near, pr_near, pg_near, dk_near, dv_near, *refs
+            dq[:, out] = query_term.T
+            cross[:rows, out] = (key_term * SCALE).astype(cross.dtype)
+            cross[rows:, out] = value_term.astype(cross.dtype)
+
+        each_head(first, cross.shape[1] // HDIM, step)
+
+    by_parity(near_span, run)
+
+
+def mid_terms_kernel(
+    near_span, first, q, g, k, norm, probs, pgrads, dq_far, dq_near, *refs
 ):
-    dq, cross = refs[-2:]
-    rows = q.shape[0]
+    guest_dq, own_dq, dk, dv = refs[-4:]
 
     def run(odd):
         def step(head):
             at, out = columns(head), columns(head - first)
-            if odd:
-                query_term, key_term, value_term = pair_terms(
-                    head, q[:, at], g[:, at], k_x[:, at], pr_near, pg_near, norm_near
-                )
-                dq[:, at] = query_term.T
-            else:
-                key_term, value_term = dk_near[:, out], dv_near[:, out]
-                dq[:, at] = jnp.zeros_like(key_term)
-            cross[:rows, out] = (key_term * SCALE).astype(cross.dtype)
-            cross[rows:, out] = value_term.astype(cross.dtype)
-
-        each_head(first, cross.shape[1] // HDIM, step)
+            query_term, dk[:, out], dv[:, out] = pair_terms(
+                head, q[:, at], g[:, at], k[:, at], probs, pgrads, norm
+            )
+            total = query_term.T + dq_far[:, out]
+            if not odd:
+                total = total + dq_near[:, out]
+            guest_dq[:, at] = (total * SCALE).astype(guest_dq.dtype)
+            own_dq[:, at] = dq_near[:, out] if odd else jnp.zeros_like(total)
+
+        each_head(first, dk.shape[1] // HDIM, step)
 
     by_parity(near_span, run)
 
@@ -472,6 +480,7 @@
     query, key, value = staged(queries, key_rows, value_rows)
 
     (bias,) = call(bound(bias_kernel, spans), flags, [], [stat], row_work)
+    guest_bias = shift(bias, -mid_span)
     self_stats, mid_soft, far_soft, near_soft, *probs, self_pgrad = call(
         bound(soft_kernel, near_span),
         [],
@@ -489,11 +498,7 @@
         heads * pair_work,
     )
     (merged,) = call(
-        bound(combine_local_kernel, near_span),
-        [],
-        [bias, self_stats, near_stats],
-        [table(6)],
-        row_work,
+        bound(combine_local_kernel, near_span), [], [bias, self_stats, near_stats], [stat], row_work
     )
     guest_stats = shift(merged, -mid_span)
     ins = [guest_grad, value, value_x, mid_prob, mid_soft, near_prob, near_soft]
@@ -512,14 +517,16 @@
         [stat, square],
         heads * pair_work,
     )
-    up_part, *guest_norms = call(
+    parts = [far_stats, mid_stats, near_stats]
+    (up_part,) = call(bound(merge_up_kernel, near_span), [], [guest_bias, *parts], [stat], row_work)
+    up_stats = shift(up_part, mid_span)
+    guest_norms = call(
         bound(combine_guest_kernel, near_span),
         [],
-        [guest_stats, far_stats, mid_stats, near_stats],
-        [stat] + [norm] * 3,
+        [guest_bias, guest_stats, *parts],
+        [norm] * 3,
         row_work,
     )
-    up_stats = shift(up_part, mid_span)
     self_norm, near_norm = call(
         bound(combine_own_kernel, spans),
         [],
@@ -527,41 +534,45 @@
         [norm] * 2,
         row_work,
     )
-    near_squares = [near_prob, near_pgrad]
-    guest_part, query_part, returned = [], [], []
+    far_norm, mid_norm, near_norm_guest = guest_norms
+    near_ins = [query, grads, guest_query, guest_grad, key_x, near_norm, near_norm_guest]
+    near_ins += [near_prob, near_pgrad]
+    parts, returned = [], []
     first = 0
     for group in GROUPS:
         narrow = ((rows, group * HDIM), jnp.float32)
         half = ((2 * rows, group * HDIM), jnp.bfloat16)
-        ins = [guest_query, guest_grad, key, key_up, key_x, *guest_norms]
-        ins += [far_prob, far_pgrad, mid_prob, mid_pgrad, *near_squares]
-        *guest_part, back, mid_key, mid_value, near_key, near_value = call(
-            bound(guest_terms_kernel, near_span, first),
+        work = group * 3 * pair_work
+        far_query, back = call(
+            bound(far_terms_kernel, first),
             [],
-            ins + guest_part,
-            [wide_bf16, half] + [narrow] * 4,
-            group * 9 * pair_work,
-            {len(ins): 0} if guest_part else {},
+            [guest_query, guest_grad, key_up, far_norm, far_prob, far_pgrad],
+            [narrow, half],
+            work,
         )
-        ins = [query, grads, key_x, near_norm, *near_squares, near_key, near_value]
-        *query_part, cross = call(
-            bound(own_terms_kernel, near_span, first),
+        near_query, cross = call(
+            bound(near_terms_kernel, near_span, first), [], near_ins, [narrow, half], work
+        )
+        ins = [guest_query, guest_grad, key, mid_norm, mid_prob, mid_pgrad]
+        ins += [far_query, near_query]
+        *parts, mid_key, mid_value = call(
+            bound(mid_terms_kernel, near_span, first),
             [],
-            ins + query_part,
-            [wide_f32, half],
-            group * 3 * pair_work,
-            {len(ins): 0} if query_part else {},
+            ins + parts,
+            [wide_bf16, wide_f32, narrow, narrow],
+            work,
+            {len(ins) + number: number for number in range(len(parts))},
         )
         back = shift(back, -mid_span)
         cross = swap(cross, "seq", near_span)
         returned.append((mid_key, mid_value, back, cross))
         first += group
-    (guest_part,) = guest_part
+    guest_part, query_part = parts
     guest_part = shift(guest_part, mid_span)
     query_sum, *self_terms = call(
         self_kernel,
         [],
-        [query, grads, key, self_norm, self_prob, self_pgrad, *query_part],
+        [query, grads, key, self_norm, self_prob, self_pgrad, query_part],
         [wide_f32] * 3,
         heads * 3 * pair_work,
     )

time: 84 us -> 82.4 us (0.981)
  waiting for transfers between devices: 31.2 us -> 27.7 us
  Pallas kernels: 20 us -> 21 us
  starting transfers between devices: 31.4 us -> 32.4 us
    ppermute x8, waiting for transfers between devices: 14.4 us -> 9.48 us  [swap(): return lax.ppermute(value, axis, pairs)]
    ppermute x10 -> x11, starting transfers between devices: 22.1 us -> 23.9 us  [shift(): lax.ppermute(value, 'seq', [(src, src + steps) for src in range(low, high)])]
    ppermute x10 -> x11, waiting for transfers between devices: 16.8 us -> 18.2 us  [shift(): lax.ppermute(value, 'seq', [(src, src + steps) for src in range(low, high)])]
    pallas_call x20 -> x24, Pallas kernels: 18.6 us -> 19.6 us  [call(): pl.pallas_call(kernel, grid=grid or (), in_specs=[smem] * len(scalars) +...]
    ppermute x8, starting transfers between devices: 9.38 us -> 8.52 us  [swap(): return lax.ppermute(value, axis, pairs)]
  transfers between devices with their start and end apart: 18 -> 19, of which waited for: 6 -> 7; matrix products, arithmetic and copies ran while one was open for 0% -> 0% of each run, Pallas kernels for 23% -> 21%
where the time goes in v11:
time: 82.4 us; the launch traced here: 82 us
  starting transfers between devices  32.4 us (39%)
  waiting for transfers between devices  27.7 us (34%)
  Pallas kernels  21 us (25%)
  between operations  0.95 us (1%)
    ppermute x11, starting transfers between devices, shift(): lax.ppermute(value, 'seq', [(src, src + steps) for src in range(low, high)])  23.9 us
    pallas_call x24, Pallas kernels, call(): pl.pallas_call(kernel, grid=grid or (), in_specs=[smem] * len(scalars) +...  19.6 us
    ppermute x11, waiting for transfers between devices, shift(): lax.ppermute(value, 'seq', [(src, src + steps) for src in range(low, high)])  18.2 us
    ppermute x8, waiting for transfers between devices, swap(): return lax.ppermute(value, axis, pairs)  9.48 us
    ppermute x8, starting transfers between devices, swap(): return lax.ppermute(value, axis, pairs)  8.52 us
  transfers between devices with their start and end apart: 19, of which 7 were waited for; matrix products, arithmetic and copies ran while one was open for 0% of the time, Pallas kernels for 21%

profile of v11, /device:TPU:0, one launch (start us, length us, event | category | flops | bytes accessed | tf_op | source)
XLA Modules:
  0.0 82.0 jit_solution(8663518401326742572)
XLA Ops:
  0.7 3.1 %collective-permute-start.1 = (bf16[256,512]{1,0:T(8,128)(2,1)}, bf16[256,512]{1,0:T(8,128)(2,1)S(1)}, u32[]{:S(2)}, u32[]{:S(2)}) collective-permute-start(bf16[256,512]{1,0:T(8,128)(2,1)} %refs_3_.1), channel_id=1, source_target_pairs={{0,2},{1,3},{2,0},{3,1},{4,6},{5,7},{6,4},{7,5},{8,10},{9,11},{10,... | collective-permute-start | bytes 786440 | tf_op jit(solution)/shard_map/ppermute | solution.py:31
  3.7 1.3 %collective-permute-start.3 = (bf16[256,1024]{1,0:T(8,128)(2,1)}, bf16[256,1024]{1,0:T(8,128)(2,1)S(1)}, u32[]{:S(2)}, u32[]{:S(2)}) collective-permute-start(bf16[256,1024]{1,0:T(8,128)(2,1)} %refs_0_.1), channel_id=1, source_target_pairs={{8,0},{12,4},{16,8},{20,12},{24,16},{28,20},{9,1},{13,5},{17,9},{2... | collective-permute-start | bytes 1572872 | tf_op jit(solution)/shard_map/ppermute | solution.py:26
  5.0 0.1 collective-permute-start
  5.1 5.1 %collective-permute-done.1.refs_1_ = bf16[256,512]{1,0:T(8,128)(2,1)S(1)} collective-permute-done((bf16[256,512]{1,0:T(8,128)(2,1)}, bf16[256,512]{1,0:T(8,128)(2,1)S(1)}, u32[]{:S(2)}, u32[]{:S(2)}) %collective-permute-start.1) | collective-permute-done | bytes 262176 | tf_op jit(solution)/shard_map/ppermute | solution.py:31
  10.2 1.7 %collective-permute-start.5 = (bf16[256,1024]{1,0:T(8,128)(2,1)}, bf16[256,1024]{1,0:T(8,128)(2,1)S(1)}, u32[]{:S(2)}, u32[]{:S(2)}) collective-permute-start(bf16[256,1024]{1,0:T(8,128)(2,1)} %refs_1_.2), channel_id=1, source_target_pairs={{0,4},{4,0},{8,12},{12,8},{16,20},{20,16},{24,28},{28,24},{1,5},{5... | collective-permute-start | bytes 1572872 | tf_op jit(solution)/shard_map/ppermute | solution.py:31
  11.9 3.5 %collective-permute-start.4 = (bf16[256,1024]{1,0:T(8,128)(2,1)}, bf16[256,1024]{1,0:T(8,128)(2,1)S(1)}, u32[]{:S(2)}, u32[]{:S(2)}) collective-permute-start(bf16[256,1024]{1,0:T(8,128)(2,1)} %refs_1_.2), channel_id=1, source_target_pairs={{0,8},{4,12},{8,16},{12,20},{16,24},{20,28},{1,9},{5,13},{9,17},{1... | collective-permute-start | bytes 1572872 | tf_op jit(solution)/shard_map/ppermute | solution.py:26
  15.5 0.0 collective-permute-done.refs_0_
  15.5 3.5 %collective-permute-start.9 = (bf16[256,1024]{1,0:T(8,128)(2,1)}, bf16[256,1024]{1,0:T(8,128)(2,1)S(1)}, u32[]{:S(2)}, u32[]{:S(2)}) collective-permute-start(bf16[256,1024]{1,0:T(8,128)(2,1)} %refs_2_.1), channel_id=1, source_target_pairs={{0,8},{4,12},{8,16},{12,20},{16,24},{20,28},{1,9},{5,13},{9,17},{1... | collective-permute-start | bytes 1572872 | tf_op jit(solution)/shard_map/ppermute | solution.py:26
  19.0 0.0 collective-permute-done.2.refs_2_
  19.0 0.6 collective-permute-start.7
  19.6 4.2 %shard_map.94.refs_1_.refs_0_.g = bf16[256,1024]{1,0:T(8,128)(2,1)S(1)} custom-call(bf16[256,512]{1,0:T(8,128)(2,1)S(1)} %collective-permute-done.refs_0_, bf16[256,512]{1,0:T(8,128)(2,1)S(1)} %collective-permute-done.1.refs_1_, bf16[256,512]{1,0:T(8,128)(2,1)S(1)} %collective-permute-done.2.refs_2_, bf16[256,512]{1,0:T(8,128)(2,1)} %refs_3_.1, ...), custom_call_target="tpu_custom_call" | custom-call | flops 1073741824 | tf_op jit(solution)/shard_map/pallas_call | solution.py:51
  23.8 1.3 %collective-permute-start.6 = (bf16[256,1024]{1,0:T(8,128)(2,1)S(1)}, bf16[256,1024]{1,0:T(8,128)(2,1)S(1)}, u32[]{:S(2)}, u32[]{:S(2)}) collective-permute-start(bf16[256,1024]{1,0:T(8,128)(2,1)S(1)} %shard_map.94.refs_1_.refs_0_.g), channel_id=1, source_target_pairs={{8,0},{12,4},{16,8},{20,12},{24,16},{28,20},{9,1},{13,5},{17,9},{2... | collective-permute-start | bytes 1572872 | tf_op jit(solution)/shard_map/ppermute | solution.py:26
  25.1 0.6 shard_map.95.refs_0_
  25.7 1.4 %stage.1 = (bf16[256,1024]{1,0:T(8,128)(2,1)S(1)}, bf16[256,1024]{1,0:T(8,128)(2,1)S(1)}, bf16[256,1024]{1,0:T(8,128)(2,1)S(1)}) custom-call(bf16[256,1024]{1,0:T(8,128)(2,1)} %refs_0_.1, bf16[256,1024]{1,0:T(8,128)(2,1)} %refs_1_.2, bf16[256,1024]{1,0:T(8,128)(2,1)} %refs_2_.1), custom_call_target="tpu_custom_call" | custom-call | flops 1000000 | tf_op jit(solution)/shard_map/stage/pallas_call | solution.py:158
  27.1 1.3 %collective-permute-start.8 = (f32[3,8,256]{2,1,0:T(8,128)S(1)}, f32[3,8,256]{2,1,0:T(8,128)S(1)}, u32[]{:S(2)}, u32[]{:S(2)}) collective-permute-start(f32[3,8,256]{2,1,0:T(8,128)S(1)} %shard_map.95.refs_0_), channel_id=1, source_target_pairs={{8,0},{12,4},{16,8},{20,12},{24,16},{28,20},{9,1},{13,5},{17,9},{2... | collective-permute-start | bytes 73736 | tf_op jit(solution)/shard_map/ppermute | solution.py:26
  28.4 0.0 collective-permute-done.4.refs_5_.refs_2_
  28.5 3.2 %shard_map.96 = (f32[3,8,256]{2,1,0:T(8,128)S(1)}, f32[3,8,256]{2,1,0:T(8,128)S(1)}, f32[3,8,256]{2,1,0:T(8,128)S(1)}, f32[3,8,256]{2,1,0:T(8,128)S(1)}, f32[8,2...) custom-call(bf16[256,1024]{1,0:T(8,128)(2,1)S(1)} %get-tuple-element, ...), custom_call_target="tpu_custom_call" | custom-call | flops 671088640 | tf_op jit(solution)/shard_map/pallas_call | solution.py:51
  31.7 4.3 %collective-permute-done.7.refs_1_.refs_2_ = bf16[256,1024]{1,0:T(8,128)(2,1)S(1)} collective-permute-done((bf16[256,1024]{1,0:T(8,128)(2,1)}, bf16[256,1024]{1,0:T(8,128)(2,1)S(1)}, u32[]{:S(2)}, u32[]{:S(2)}) %collective-permute-start.7) | collective-permute-done | bytes 524320 | tf_op jit(solution)/shard_map/ppermute | solution.py:31
  36.0 1.3 %collective-permute-start.11 = (f32[3,8,256]{2,1,0:T(8,128)S(1)}, f32[3,8,256]{2,1,0:T(8,128)S(1)}, u32[]{:S(2)}, u32[]{:S(2)}) collective-permute-start(f32[3,8,256]{2,1,0:T(8,128)S(1)} %shard_map.102), channel_id=1, source_target_pairs={{8,0},{12,4},{16,8},{20,12},{24,16},{28,20},{9,1},{13,5},{17,9},{2... | collective-permute-start | bytes 73736 | tf_op jit(solution)/shard_map/ppermute | solution.py:26
  37.3 1.2 %collective-permute-done.9.values = bf16[256,1024]{1,0:T(8,128)(2,1)S(1)} collective-permute-done((bf16[256,1024]{1,0:T(8,128)(2,1)}, bf16[256,1024]{1,0:T(8,128)(2,1)S(1)}, u32[]{:S(2)}, u32[]{:S(2)}) %collective-permute-start.9) | collective-permute-done | bytes 524320 | tf_op jit(solution)/shard_map/ppermute | solution.py:26
  38.5 0.6 collective-permute-done.6.refs_0_.g.refs_1_.refs_3_
  39.2 0.7 shard_map.99
  39.9 1.4 %shard_map.98 = (f32[3,8,256]{2,1,0:T(8,128)S(1)}, f32[8,256,256]{2,1,0:T(8,128)S(1)}, f32[3,8,256]{2,1,0:T(8,128)S(1)}, f32[8,256,256]{2,1,0:T(8,128)S(1)}) custom-call(bf16[256,1024]{1,0:T(8,128)(2,1)S(1)} %collective-permute-done.6.refs_0_.g.refs_1_.refs_3_, ...), custom_call_target="tpu_custom_call", output_to_operand_aliasing={{2}: (7, {}), {3}: (8, {})} | custom-call | flops 268435456 | tf_op jit(solution)/shard_map/pallas_call | solution.py:51
  41.3 3.6 %collective-permute-start.10 = (f32[3,8,256]{2,1,0:T(8,128)S(1)}, f32[3,8,256]{2,1,0:T(8,128)S(1)}, u32[]{:S(2)}, u32[]{:S(2)}) collective-permute-start(f32[3,8,256]{2,1,0:T(8,128)S(1)} %shard_map.100), channel_id=1, source_target_pairs={{0,8},{4,12},{8,16},{12,20},{16,24},{20,28},{1,9},{5,13},{9,17},{1... | collective-permute-start | bytes 73736 | tf_op jit(solution)/shard_map/ppermute | solution.py:26
  45.0 0.4 shard_map.108
  45.4 0.4 shard_map.104
  45.7 0.5 shard_map.106
  46.3 0.2 collective-permute-done.10.refs_3_
  46.5 0.4 shard_map.109
  46.9 0.4 shard_map.105
  47.2 0.6 shard_map.107
  47.8 0.4 shard_map.110
  48.2 0.8 shard_map.111
  49.0 0.4 shard_map.112
  49.4 4.2 %collective-permute-start.12 = (bf16[256,1024]{1,0:T(8,128)(2,1)S(1)}, bf16[256,1024]{1,0:T(8,128)(2,1)S(1)}, u32[]{:S(2)}, u32[]{:S(2)}) collective-permute-start(bf16[256,1024]{1,0:T(8,128)(2,1)S(1)} %get-tuple-element.98), channel_id=1, source_target_pairs={{0,8},{4,12},{8,16},{12,20},{16,24},{20,28},{1,9},{5,13},{9,17},{1... | collective-permute-start | bytes 1572872 | tf_op jit(solution)/shard_map/ppermute | solution.py:26
  53.7 1.3 %collective-permute-start.15 = (bf16[512,512]{1,0:T(8,128)(2,1)S(1)}, bf16[512,512]{1,0:T(8,128)(2,1)S(1)}, u32[]{:S(2)}, u32[]{:S(2)}) collective-permute-start(bf16[512,512]{1,0:T(8,128)(2,1)S(1)} %get-tuple-element.107), channel_id=1, source_target_pairs={{8,0},{12,4},{16,8},{20,12},{24,16},{28,20},{9,1},{13,5},{17,9},{2... | collective-permute-start | bytes 1572872 | tf_op jit(solution)/shard_map/ppermute | solution.py:26
  55.0 0.9 %collective-permute-start.16 = (bf16[512,512]{1,0:T(8,128)(2,1)S(1)}, bf16[512,512]{1,0:T(8,128)(2,1)S(1)}, u32[]{:S(2)}, u32[]{:S(2)}) collective-permute-start(bf16[512,512]{1,0:T(8,128)(2,1)S(1)} %get-tuple-element.108), channel_id=1, source_target_pairs={{0,4},{4,0},{8,12},{12,8},{16,20},{20,16},{24,28},{28,24},{1,5},{5... | collective-permute-start | bytes 1572872 | tf_op jit(solution)/shard_map/ppermute | solution.py:31
  55.9 1.3 %collective-permute-start.17 = (bf16[512,256]{1,0:T(8,128)(2,1)S(1)}, bf16[512,256]{1,0:T(8,128)(2,1)S(1)}, u32[]{:S(2)}, u32[]{:S(2)}) collective-permute-start(bf16[512,256]{1,0:T(8,128)(2,1)S(1)} %get-tuple-element.111), channel_id=1, source_target_pairs={{8,0},{12,4},{16,8},{20,12},{24,16},{28,20},{9,1},{13,5},{17,9},{2... | collective-permute-start | bytes 786440 | tf_op jit(solution)/shard_map/ppermute | solution.py:26
  57.2 1.2 %collective-permute-start.18 = (bf16[512,256]{1,0:T(8,128)(2,1)S(1)}, bf16[512,256]{1,0:T(8,128)(2,1)S(1)}, u32[]{:S(2)}, u32[]{:S(2)}) collective-permute-start(bf16[512,256]{1,0:T(8,128)(2,1)S(1)} %get-tuple-element.112), channel_id=1, source_target_pairs={{0,4},{4,0},{8,12},{12,8},{16,20},{20,16},{24,28},{28,24},{1,5},{5... | collective-permute-start | bytes 786440 | tf_op jit(solution)/shard_map/ppermute | solution.py:31
  58.4 14.6 %collective-permute-done.17.refs_4_ = bf16[512,256]{1,0:T(8,128)(2,1)S(1)} collective-permute-done((bf16[512,256]{1,0:T(8,128)(2,1)S(1)}, bf16[512,256]{1,0:T(8,128)(2,1)S(1)}, u32[]{:S(2)}, u32[]{:S(2)}) %collective-permute-start.17) | collective-permute-done | bytes 262176 | tf_op jit(solution)/shard_map/ppermute | solution.py:26
  73.0 1.3 %collective-permute-start.13 = (bf16[512,256]{1,0:T(8,128)(2,1)S(1)}, bf16[512,256]{1,0:T(8,128)(2,1)S(1)}, u32[]{:S(2)}, u32[]{:S(2)}) collective-permute-start(bf16[512,256]{1,0:T(8,128)(2,1)S(1)} %get-tuple-element.103), channel_id=1, source_target_pairs={{8,0},{12,4},{16,8},{20,12},{24,16},{28,20},{9,1},{13,5},{17,9},{2... | collective-permute-start | bytes 786440 | tf_op jit(solution)/shard_map/ppermute | solution.py:26
  74.3 0.9 %collective-permute-start.14 = (bf16[512,256]{1,0:T(8,128)(2,1)S(1)}, bf16[512,256]{1,0:T(8,128)(2,1)S(1)}, u32[]{:S(2)}, u32[]{:S(2)}) collective-permute-start(bf16[512,256]{1,0:T(8,128)(2,1)S(1)} %get-tuple-element.104), channel_id=1, source_target_pairs={{0,4},{4,0},{8,12},{12,8},{16,20},{20,16},{24,28},{28,24},{1,5},{5... | collective-permute-start | bytes 786440 | tf_op jit(solution)/shard_map/ppermute | solution.py:31
  75.2 1.3 %shard_map.113 = (f32[256,1024]{1,0:T(8,128)S(1)}, f32[256,1024]{1,0:T(8,128)S(1)}, f32[256,1024]{1,0:T(8,128)S(1)}) custom-call(bf16[256,1024]{1,0:T(8,128)(2,1)S(1)} %get-tuple-element.61.refs_0_.q, bf16[256,1024]{1,0:T(8,128)(2,1)S(1)} %shard_map.94.refs_1_.refs_0_.g, bf16[256,1024]{1,0:T(8,128)(2,1)S(1)} %get-tuple-element.62.refs_2_.k, ...), custom_call_target="tpu_custom_call" | custom-call | flops 402653184 | tf_op jit(solution)/shard_map/pallas_call | solution.py:51
  76.5 0.8 shard_map.115
  77.2 1.4 %shard_map.114 = bf16[256,1024]{1,0:T(8,128)(2,1)} custom-call(f32[256,1024]{1,0:T(8,128)S(1)} %get-tuple-element.97.dq, bf16[256,1024]{1,0:T(8,128)(2,1)S(1)} %collective-permute-done.12.guest), custom_call_target="tpu_custom_call" | custom-call | flops 524288 | tf_op jit(solution)/shard_map/pallas_call | solution.py:51
  78.7 0.9 %shard_map.116 = (bf16[256,1024]{1,0:T(8,128)(2,1)}, bf16[256,1024]{1,0:T(8,128)(2,1)}) custom-call(f32[256,1024]{1,0:T(8,128)S(1)} %get-tuple-element.99.refs_0_, f32[256,1024]{1,0:T(8,128)S(1)} %get-tuple-element.100.refs_1_, f32[256,512]{1,0:T(8,128)S(1)} %get-tuple-element.105.refs_2_, ...), custom_call_target="tpu_custom_call", output_to_operand_aliasing={{0}: (6, {}), {1}: (7, {})} | custom-call | flops 33554432 | tf_op jit(solution)/shard_map/pallas_call | solution.py:51
  79.6 1.6 %collective-permute-done.13.refs_4_ = bf16[512,256]{1,0:T(8,128)(2,1)S(1)} collective-permute-done((bf16[512,256]{1,0:T(8,128)(2,1)S(1)}, bf16[512,256]{1,0:T(8,128)(2,1)S(1)}, u32[]{:S(2)}, u32[]{:S(2)}) %collective-permute-start.13) | collective-permute-done | bytes 262176 | tf_op jit(solution)/shard_map/ppermute | solution.py:26
  81.2 0.8 shard_map.117
  (19 shorter events, 0.1 us)
Async XLA Ops:
  0.6 24.5 %copy-start.1 = (s32[1,3]{1,0:T(1,128)S(1)}, s32[1,3]{1,0:T(1,128)}, u32[]{:S(2)}) copy-start(s32[1,3]{1,0:T(1,128)} %refs_1_.3) | copy-start | bytes 40
  0.6 24.5 %copy-start = (s32[8,3]{0,1:T(4,128)S(1)}, s32[8,3]{0,1:T(4,128)}, u32[]{:S(2)}) copy-start(s32[8,3]{0,1:T(4,128)} %param.12) | copy-start | bytes 292
  0.7 9.6 %collective-permute-start.1 = (bf16[256,512]{1,0:T(8,128)(2,1)}, bf16[256,512]{1,0:T(8,128)(2,1)S(1)}, u32[]{:S(2)}, u32[]{:S(2)}) collective-permute-start(bf16[256,512]{1,0:T(8,128)(2,1)} %refs_3_.1), channel_id=1, source_target_pairs={{0,2},{1,3},{2,0},{3,1},{4,6},{5,7},{6,4},{7,5},{8,10},{9,11},{10,... | collective-permute-start | bytes 786440 | tf_op jit(solution)/shard_map/ppermute | solution.py:31
  3.7 20.1 %collective-permute-start.3 = (bf16[256,1024]{1,0:T(8,128)(2,1)}, bf16[256,1024]{1,0:T(8,128)(2,1)S(1)}, u32[]{:S(2)}, u32[]{:S(2)}) collective-permute-start(bf16[256,1024]{1,0:T(8,128)(2,1)} %refs_0_.1), channel_id=1, source_target_pairs={{8,0},{12,4},{16,8},{20,12},{24,16},{28,20},{9,1},{13,5},{17,9},{2... | collective-permute-start | bytes 1572872 | tf_op jit(solution)/shard_map/ppermute | solution.py:26
  5.0 10.5 %collective-permute-start = (bf16[256,512]{1,0:T(8,128)(2,1)}, bf16[256,512]{1,0:T(8,128)(2,1)S(1)}, u32[]{:S(2)}, u32[]{:S(2)}) collective-permute-start(bf16[256,512]{1,0:T(8,128)(2,1)} %refs_3_.1), channel_id=1, source_target_pairs={{0,1},{1,0},{2,3},{3,2},{4,5},{5,4},{6,7},{7,6},{8,9},{9,8},{10,11... | collective-permute-start | bytes 786440 | tf_op jit(solution)/shard_map/ppermute | solution.py:31
  10.2 8.7 %collective-permute-start.2 = (bf16[256,512]{1,0:T(8,128)(2,1)S(1)}, bf16[256,512]{1,0:T(8,128)(2,1)S(1)}, u32[]{:S(2)}, u32[]{:S(2)}) collective-permute-start(bf16[256,512]{1,0:T(8,128)(2,1)S(1)} %collective-permute-done.1.refs_1_), channel_id=1, source_target_pairs={{0,1},{1,0},{2,3},{3,2},{4,5},{5,4},{6,7},{7,6},{8,9},{9,8},{10,11... | collective-permute-start | bytes 786440 | tf_op jit(solution)/shard_map/ppermute | solution.py:31
  10.2 16.9 %collective-permute-start.5 = (bf16[256,1024]{1,0:T(8,128)(2,1)}, bf16[256,1024]{1,0:T(8,128)(2,1)S(1)}, u32[]{:S(2)}, u32[]{:S(2)}) collective-permute-start(bf16[256,1024]{1,0:T(8,128)(2,1)} %refs_1_.2), channel_id=1, source_target_pairs={{0,4},{4,0},{8,12},{12,8},{16,20},{20,16},{24,28},{28,24},{1,5},{5... | collective-permute-start | bytes 1572872 | tf_op jit(solution)/shard_map/ppermute | solution.py:31
  11.9 16.5 %collective-permute-start.4 = (bf16[256,1024]{1,0:T(8,128)(2,1)}, bf16[256,1024]{1,0:T(8,128)(2,1)S(1)}, u32[]{:S(2)}, u32[]{:S(2)}) collective-permute-start(bf16[256,1024]{1,0:T(8,128)(2,1)} %refs_1_.2), channel_id=1, source_target_pairs={{0,8},{4,12},{8,16},{12,20},{16,24},{20,28},{1,9},{5,13},{9,17},{1... | collective-permute-start | bytes 1572872 | tf_op jit(solution)/shard_map/ppermute | solution.py:26
  15.5 23.1 %collective-permute-start.9 = (bf16[256,1024]{1,0:T(8,128)(2,1)}, bf16[256,1024]{1,0:T(8,128)(2,1)S(1)}, u32[]{:S(2)}, u32[]{:S(2)}) collective-permute-start(bf16[256,1024]{1,0:T(8,128)(2,1)} %refs_2_.1), channel_id=1, source_target_pairs={{0,8},{4,12},{8,16},{12,20},{16,24},{20,28},{1,9},{5,13},{9,17},{1... | collective-permute-start | bytes 1572872 | tf_op jit(solution)/shard_map/ppermute | solution.py:26
  19.0 17.0 %collective-permute-start.7 = (bf16[256,1024]{1,0:T(8,128)(2,1)}, bf16[256,1024]{1,0:T(8,128)(2,1)S(1)}, u32[]{:S(2)}, u32[]{:S(2)}) collective-permute-start(bf16[256,1024]{1,0:T(8,128)(2,1)} %refs_2_.1), channel_id=1, source_target_pairs={{0,4},{4,0},{8,12},{12,8},{16,20},{20,16},{24,28},{28,24},{1,5},{5... | collective-permute-start | bytes 1572872 | tf_op jit(solution)/shard_map/ppermute | solution.py:31
  23.8 15.4 %collective-permute-start.6 = (bf16[256,1024]{1,0:T(8,128)(2,1)S(1)}, bf16[256,1024]{1,0:T(8,128)(2,1)S(1)}, u32[]{:S(2)}, u32[]{:S(2)}) collective-permute-start(bf16[256,1024]{1,0:T(8,128)(2,1)S(1)} %shard_map.94.refs_1_.refs_0_.g), channel_id=1, source_target_pairs={{8,0},{12,4},{16,8},{20,12},{24,16},{28,20},{9,1},{13,5},{17,9},{2... | collective-permute-start | bytes 1572872 | tf_op jit(solution)/shard_map/ppermute | solution.py:26
  27.1 14.1 %collective-permute-start.8 = (f32[3,8,256]{2,1,0:T(8,128)S(1)}, f32[3,8,256]{2,1,0:T(8,128)S(1)}, u32[]{:S(2)}, u32[]{:S(2)}) collective-permute-start(f32[3,8,256]{2,1,0:T(8,128)S(1)} %shard_map.95.refs_0_), channel_id=1, source_target_pairs={{8,0},{12,4},{16,8},{20,12},{24,16},{28,20},{9,1},{13,5},{17,9},{2... | collective-permute-start | bytes 73736 | tf_op jit(solution)/shard_map/ppermute | solution.py:26
  36.0 8.9 %collective-permute-start.11 = (f32[3,8,256]{2,1,0:T(8,128)S(1)}, f32[3,8,256]{2,1,0:T(8,128)S(1)}, u32[]{:S(2)}, u32[]{:S(2)}) collective-permute-start(f32[3,8,256]{2,1,0:T(8,128)S(1)} %shard_map.102), channel_id=1, source_target_pairs={{8,0},{12,4},{16,8},{20,12},{24,16},{28,20},{9,1},{13,5},{17,9},{2... | collective-permute-start | bytes 73736 | tf_op jit(solution)/shard_map/ppermute | solution.py:26
  41.3 5.2 %collective-permute-start.10 = (f32[3,8,256]{2,1,0:T(8,128)S(1)}, f32[3,8,256]{2,1,0:T(8,128)S(1)}, u32[]{:S(2)}, u32[]{:S(2)}) collective-permute-start(f32[3,8,256]{2,1,0:T(8,128)S(1)} %shard_map.100), channel_id=1, source_target_pairs={{0,8},{4,12},{8,16},{12,20},{16,24},{20,28},{1,9},{5,13},{9,17},{1... | collective-permute-start | bytes 73736 | tf_op jit(solution)/shard_map/ppermute | solution.py:26
  49.4 27.8 %collective-permute-start.12 = (bf16[256,1024]{1,0:T(8,128)(2,1)S(1)}, bf16[256,1024]{1,0:T(8,128)(2,1)S(1)}, u32[]{:S(2)}, u32[]{:S(2)}) collective-permute-start(bf16[256,1024]{1,0:T(8,128)(2,1)S(1)} %get-tuple-element.98), channel_id=1, source_target_pairs={{0,8},{4,12},{8,16},{12,20},{16,24},{20,28},{1,9},{5,13},{9,17},{1... | collective-permute-start | bytes 1572872 | tf_op jit(solution)/shard_map/ppermute | solution.py:26
  53.7 25.0 %collective-permute-start.15 = (bf16[512,512]{1,0:T(8,128)(2,1)S(1)}, bf16[512,512]{1,0:T(8,128)(2,1)S(1)}, u32[]{:S(2)}, u32[]{:S(2)}) collective-permute-start(bf16[512,512]{1,0:T(8,128)(2,1)S(1)} %get-tuple-element.107), channel_id=1, source_target_pairs={{8,0},{12,4},{16,8},{20,12},{24,16},{28,20},{9,1},{13,5},{17,9},{2... | collective-permute-start | bytes 1572872 | tf_op jit(solution)/shard_map/ppermute | solution.py:26
  55.0 23.7 %collective-permute-start.16 = (bf16[512,512]{1,0:T(8,128)(2,1)S(1)}, bf16[512,512]{1,0:T(8,128)(2,1)S(1)}, u32[]{:S(2)}, u32[]{:S(2)}) collective-permute-start(bf16[512,512]{1,0:T(8,128)(2,1)S(1)} %get-tuple-element.108), channel_id=1, source_target_pairs={{0,4},{4,0},{8,12},{12,8},{16,20},{20,16},{24,28},{28,24},{1,5},{5... | collective-permute-start | bytes 1572872 | tf_op jit(solution)/shard_map/ppermute | solution.py:31
  55.9 17.1 %collective-permute-start.17 = (bf16[512,256]{1,0:T(8,128)(2,1)S(1)}, bf16[512,256]{1,0:T(8,128)(2,1)S(1)}, u32[]{:S(2)}, u32[]{:S(2)}) collective-permute-start(bf16[512,256]{1,0:T(8,128)(2,1)S(1)} %get-tuple-element.111), channel_id=1, source_target_pairs={{8,0},{12,4},{16,8},{20,12},{24,16},{28,20},{9,1},{13,5},{17,9},{2... | collective-permute-start | bytes 786440 | tf_op jit(solution)/shard_map/ppermute | solution.py:26
  57.2 17.1 %collective-permute-start.18 = (bf16[512,256]{1,0:T(8,128)(2,1)S(1)}, bf16[512,256]{1,0:T(8,128)(2,1)S(1)}, u32[]{:S(2)}, u32[]{:S(2)}) collective-permute-start(bf16[512,256]{1,0:T(8,128)(2,1)S(1)} %get-tuple-element.112), channel_id=1, source_target_pairs={{0,4},{4,0},{8,12},{12,8},{16,20},{20,16},{24,28},{28,24},{1,5},{5... | collective-permute-start | bytes 786440 | tf_op jit(solution)/shard_map/ppermute | solution.py:31
  73.0 8.3 %collective-permute-start.13 = (bf16[512,256]{1,0:T(8,128)(2,1)S(1)}, bf16[512,256]{1,0:T(8,128)(2,1)S(1)}, u32[]{:S(2)}, u32[]{:S(2)}) collective-permute-start(bf16[512,256]{1,0:T(8,128)(2,1)S(1)} %get-tuple-element.103), channel_id=1, source_target_pairs={{8,0},{12,4},{16,8},{20,12},{24,16},{28,20},{9,1},{13,5},{17,9},{2... | collective-permute-start | bytes 786440 | tf_op jit(solution)/shard_map/ppermute | solution.py:26
  74.3 7.0 %collective-permute-start.14 = (bf16[512,256]{1,0:T(8,128)(2,1)S(1)}, bf16[512,256]{1,0:T(8,128)(2,1)S(1)}, u32[]{:S(2)}, u32[]{:S(2)}) collective-permute-start(bf16[512,256]{1,0:T(8,128)(2,1)S(1)} %get-tuple-element.104), channel_id=1, source_target_pairs={{0,4},{4,0},{8,12},{12,8},{16,20},{20,16},{24,28},{28,24},{1,5},{5... | collective-permute-start | bytes 786440 | tf_op jit(solution)/shard_map/ppermute | solution.py:31

commit v12 on v11

--- a/solution.py
+++ b/solution.py
@@ -12,7 +12,7 @@
 FAR, MID, NEAR = range(3)
 SECTIONS = 3
 GROUPS = (2, 4, 2)
-HEADS_PER_STEP = 4
+HEADS_PER_STEP = 8
 KERNEL_VMEM = 8 * 2**20
 BIG = 1e30
 SCALE = 1.0 / math.sqrt(HDIM)
@@ -295,6 +295,9 @@
 
 
 def combine_local_kernel(near_span, bias, own, near, out):
+    lane = lax.broadcasted_iota(jnp.int32, bias.shape[1:], 1)
+    out[3] = jnp.where(lane == FAR, bias[FAR], jnp.where(lane == MID, bias[MID], bias[NEAR]))
+
     def run(odd):
         parts = [part_of(own)]
         if odd:
@@ -306,23 +309,18 @@
     by_parity(near_span, run)
 
 
-def guest_parts(odd, bias, far, mid, near):
-    parts = [part_of(far, bias[FAR]), part_of(mid, bias[MID])]
-    return parts if odd else [*parts, part_of(near, bias[NEAR])]
-
-
-def merge_up_kernel(near_span, bias, far, mid, near, up):
-    def run(odd):
-        merged, _ = merge(guest_parts(odd, bias, far, mid, near))
+def combine_guest_kernel(near_span, guest, far, mid, near, up, *outs):
+    def run(odd):
+        def bias(section):
+            return guest[3][:, section : section + 1]
+
+        parts = [part_of(far, bias(FAR)), part_of(mid, bias(MID))]
+        if not odd:
+            parts.append(part_of(near, bias(NEAR)))
+        merged, _ = merge(parts)
         for index, row in enumerate(merged):
             up[index] = row
-
-    by_parity(near_span, run)
-
-
-def combine_guest_kernel(near_span, bias, guest, far, mid, near, *outs):
-    def run(odd):
-        merged, factors = merge([*guest_parts(odd, bias, far, mid, near), part_of(guest)])
+        merged, factors = merge([*parts, part_of(guest)])
         put_norm(outs, factors[:-1], merged)
 
     by_parity(near_span, run)
@@ -480,7 +478,6 @@
     query, key, value = staged(queries, key_rows, value_rows)
 
     (bias,) = call(bound(bias_kernel, spans), flags, [], [stat], row_work)
-    guest_bias = shift(bias, -mid_span)
     self_stats, mid_soft, far_soft, near_soft, *probs, self_pgrad = call(
         bound(soft_kernel, near_span),
         [],
@@ -498,7 +495,11 @@
         heads * pair_work,
     )
     (merged,) = call(
-        bound(combine_local_kernel, near_span), [], [bias, self_stats, near_stats], [stat], row_work
+        bound(combine_local_kernel, near_span),
+        [],
+        [bias, self_stats, near_stats],
+        [table(4)],
+        row_work,
     )
     guest_stats = shift(merged, -mid_span)
     ins = [guest_grad, value, value_x, mid_prob, mid_soft, near_prob, near_soft]
@@ -517,16 +518,14 @@
         [stat, square],
         heads * pair_work,
     )
-    parts = [far_stats, mid_stats, near_stats]
-    (up_part,) = call(bound(merge_up_kernel, near_span), [], [guest_bias, *parts], [stat], row_work)
+    up_part, *guest_norms = call(
+        bound(combine_guest_kernel, near_span),
+        [],
+        [guest_stats, far_stats, mid_stats, near_stats],
+        [stat] + [norm] * 3,
+        row_work,
+    )
     up_stats = shift(up_part, mid_span)
-    guest_norms = call(
-        bound(combine_guest_kernel, near_span),
-        [],
-        [guest_bias, guest_stats, *parts],
-        [norm] * 3,
-        row_work,
-    )
     self_norm, near_norm = call(
         bound(combine_own_kernel, spans),
         [],

time: 82.4 us -> 82.2 us (level)
  Pallas kernels: 21 us -> 19.7 us
  waiting for transfers between devices: 27.7 us -> 28.9 us
    pallas_call x24 -> x23, Pallas kernels: 19.6 us -> 18.3 us  [call(): pl.pallas_call(kernel, grid=grid or (), in_specs=[smem] * len(scalars) +...]
    ppermute x11 -> x10, starting transfers between devices: 23.9 us -> 22.7 us  [shift(): lax.ppermute(value, 'seq', [(src, src + steps) for src in range(low, high)])]
    ppermute x8, starting transfers between devices: 8.52 us -> 9.68 us  [swap(): return lax.ppermute(value, axis, pairs)]
    ppermute x11 -> x10, waiting for transfers between devices: 18.2 us -> 18.7 us  [shift(): lax.ppermute(value, 'seq', [(src, src + steps) for src in range(low, high)])]
  transfers between devices with their start and end apart: 19 -> 18, of which waited for: 7 -> 9; matrix products, arithmetic and copies ran while one was open for 0% -> 0% of each run, Pallas kernels for 21% -> 19%
where the time goes in v12:
time: 82.2 us; the launch traced here: 81.8 us
  starting transfers between devices  32.3 us (39%)
  waiting for transfers between devices  28.9 us (35%)
  Pallas kernels  19.7 us (24%)
  between operations  0.91 us (1%)
    ppermute x10, starting transfers between devices, shift(): lax.ppermute(value, 'seq', [(src, src + steps) for src in range(low, high)])  22.7 us
    ppermute x10, waiting for transfers between devices, shift(): lax.ppermute(value, 'seq', [(src, src + steps) for src in range(low, high)])  18.7 us
    pallas_call x23, Pallas kernels, call(): pl.pallas_call(kernel, grid=grid or (), in_specs=[smem] * len(scalars) +...  18.3 us
    ppermute x8, waiting for transfers between devices, swap(): return lax.ppermute(value, axis, pairs)  10.2 us
    ppermute x8, starting transfers between devices, swap(): return lax.ppermute(value, axis, pairs)  9.68 us
  transfers between devices with their start and end apart: 18, of which 9 were waited for; matrix products, arithmetic and copies ran while one was open for 0% of the time, Pallas kernels for 19%

profile of v12, /device:TPU:0, one launch (start us, length us, event | category | flops | bytes accessed | tf_op | source)
XLA Modules:
  0.0 81.8 jit_solution(12359697986937245040)
XLA Ops:
  0.7 3.1 %collective-permute-start.1 = (bf16[256,512]{1,0:T(8,128)(2,1)}, bf16[256,512]{1,0:T(8,128)(2,1)S(1)}, u32[]{:S(2)}, u32[]{:S(2)}) collective-permute-start(bf16[256,512]{1,0:T(8,128)(2,1)} %refs_3_.1), channel_id=1, source_target_pairs={{0,2},{1,3},{2,0},{3,1},{4,6},{5,7},{6,4},{7,5},{8,10},{9,11},{10,... | collective-permute-start | bytes 786440 | tf_op jit(solution)/shard_map/ppermute | solution.py:31
  3.7 1.3 %collective-permute-start.3 = (bf16[256,1024]{1,0:T(8,128)(2,1)}, bf16[256,1024]{1,0:T(8,128)(2,1)S(1)}, u32[]{:S(2)}, u32[]{:S(2)}) collective-permute-start(bf16[256,1024]{1,0:T(8,128)(2,1)} %refs_0_.1), channel_id=1, source_target_pairs={{8,0},{12,4},{16,8},{20,12},{24,16},{28,20},{9,1},{13,5},{17,9},{2... | collective-permute-start | bytes 1572872 | tf_op jit(solution)/shard_map/ppermute | solution.py:26
  5.0 0.1 collective-permute-start
  5.1 5.1 %collective-permute-done.1.refs_1_ = bf16[256,512]{1,0:T(8,128)(2,1)S(1)} collective-permute-done((bf16[256,512]{1,0:T(8,128)(2,1)}, bf16[256,512]{1,0:T(8,128)(2,1)S(1)}, u32[]{:S(2)}, u32[]{:S(2)}) %collective-permute-start.1) | collective-permute-done | bytes 262176 | tf_op jit(solution)/shard_map/ppermute | solution.py:31
  10.2 1.7 %collective-permute-start.5 = (bf16[256,1024]{1,0:T(8,128)(2,1)}, bf16[256,1024]{1,0:T(8,128)(2,1)S(1)}, u32[]{:S(2)}, u32[]{:S(2)}) collective-permute-start(bf16[256,1024]{1,0:T(8,128)(2,1)} %refs_1_.2), channel_id=1, source_target_pairs={{0,4},{4,0},{8,12},{12,8},{16,20},{20,16},{24,28},{28,24},{1,5},{5... | collective-permute-start | bytes 1572872 | tf_op jit(solution)/shard_map/ppermute | solution.py:31
  11.9 3.5 %collective-permute-start.4 = (bf16[256,1024]{1,0:T(8,128)(2,1)}, bf16[256,1024]{1,0:T(8,128)(2,1)S(1)}, u32[]{:S(2)}, u32[]{:S(2)}) collective-permute-start(bf16[256,1024]{1,0:T(8,128)(2,1)} %refs_1_.2), channel_id=1, source_target_pairs={{0,8},{4,12},{8,16},{12,20},{16,24},{20,28},{1,9},{5,13},{9,17},{1... | collective-permute-start | bytes 1572872 | tf_op jit(solution)/shard_map/ppermute | solution.py:26
  15.5 0.0 collective-permute-done.refs_0_
  15.5 3.5 %collective-permute-start.9 = (bf16[256,1024]{1,0:T(8,128)(2,1)}, bf16[256,1024]{1,0:T(8,128)(2,1)S(1)}, u32[]{:S(2)}, u32[]{:S(2)}) collective-permute-start(bf16[256,1024]{1,0:T(8,128)(2,1)} %refs_2_.1), channel_id=1, source_target_pairs={{0,8},{4,12},{8,16},{12,20},{16,24},{20,28},{1,9},{5,13},{9,17},{1... | collective-permute-start | bytes 1572872 | tf_op jit(solution)/shard_map/ppermute | solution.py:26
  19.0 0.6 collective-permute-start.7
  19.6 4.2 %shard_map.94.refs_1_.refs_0_.g = bf16[256,1024]{1,0:T(8,128)(2,1)S(1)} custom-call(bf16[256,512]{1,0:T(8,128)(2,1)S(1)} %collective-permute-done.refs_0_, bf16[256,512]{1,0:T(8,128)(2,1)S(1)} %collective-permute-done.1.refs_1_, bf16[256,512]{1,0:T(8,128)(2,1)S(1)} %collective-permute-done.2.refs_2_, bf16[256,512]{1,0:T(8,128)(2,1)} %refs_3_.1, ...), custom_call_target="tpu_custom_call" | custom-call | flops 1073741824 | tf_op jit(solution)/shard_map/pallas_call | solution.py:51
  23.8 1.3 %collective-permute-start.6 = (bf16[256,1024]{1,0:T(8,128)(2,1)S(1)}, bf16[256,1024]{1,0:T(8,128)(2,1)S(1)}, u32[]{:S(2)}, u32[]{:S(2)}) collective-permute-start(bf16[256,1024]{1,0:T(8,128)(2,1)S(1)} %shard_map.94.refs_1_.refs_0_.g), channel_id=1, source_target_pairs={{8,0},{12,4},{16,8},{20,12},{24,16},{28,20},{9,1},{13,5},{17,9},{2... | collective-permute-start | bytes 1572872 | tf_op jit(solution)/shard_map/ppermute | solution.py:26
  25.1 0.6 shard_map.95.refs_0_
  25.7 1.4 %stage.1 = (bf16[256,1024]{1,0:T(8,128)(2,1)S(1)}, bf16[256,1024]{1,0:T(8,128)(2,1)S(1)}, bf16[256,1024]{1,0:T(8,128)(2,1)S(1)}) custom-call(bf16[256,1024]{1,0:T(8,128)(2,1)} %refs_0_.1, bf16[256,1024]{1,0:T(8,128)(2,1)} %refs_1_.2, bf16[256,1024]{1,0:T(8,128)(2,1)} %refs_2_.1), custom_call_target="tpu_custom_call" | custom-call | flops 1000000 | tf_op jit(solution)/shard_map/stage/pallas_call | solution.py:158
  27.1 0.9 %collective-permute-done.4.refs_5_.refs_2_ = bf16[256,1024]{1,0:T(8,128)(2,1)S(1)} collective-permute-done((bf16[256,1024]{1,0:T(8,128)(2,1)}, bf16[256,1024]{1,0:T(8,128)(2,1)S(1)}, u32[]{:S(2)}, u32[]{:S(2)}) %collective-permute-start.4) | collective-permute-done | bytes 524320 | tf_op jit(solution)/shard_map/ppermute | solution.py:26
  28.0 2.9 %shard_map.96 = (f32[3,8,256]{2,1,0:T(8,128)S(1)}, f32[3,8,256]{2,1,0:T(8,128)S(1)}, f32[3,8,256]{2,1,0:T(8,128)S(1)}, f32[3,8,256]{2,1,0:T(8,128)S(1)}, f32[8,2...) custom-call(bf16[256,1024]{1,0:T(8,128)(2,1)S(1)} %get-tuple-element, ...), custom_call_target="tpu_custom_call" | custom-call | flops 671088640 | tf_op jit(solution)/shard_map/pallas_call | solution.py:51
  31.0 5.0 %collective-permute-done.7.refs_1_.refs_2_ = bf16[256,1024]{1,0:T(8,128)(2,1)S(1)} collective-permute-done((bf16[256,1024]{1,0:T(8,128)(2,1)}, bf16[256,1024]{1,0:T(8,128)(2,1)S(1)}, u32[]{:S(2)}, u32[]{:S(2)}) %collective-permute-start.7) | collective-permute-done | bytes 524320 | tf_op jit(solution)/shard_map/ppermute | solution.py:31
  36.0 1.3 %collective-permute-start.8 = (f32[4,8,256]{2,1,0:T(8,128)S(1)}, f32[4,8,256]{2,1,0:T(8,128)S(1)}, u32[]{:S(2)}, u32[]{:S(2)}) collective-permute-start(f32[4,8,256]{2,1,0:T(8,128)S(1)} %shard_map.99), channel_id=1, source_target_pairs={{8,0},{12,4},{16,8},{20,12},{24,16},{28,20},{9,1},{13,5},{17,9},{2... | collective-permute-start | bytes 98312 | tf_op jit(solution)/shard_map/ppermute | solution.py:26
  37.3 1.2 %collective-permute-done.9.values = bf16[256,1024]{1,0:T(8,128)(2,1)S(1)} collective-permute-done((bf16[256,1024]{1,0:T(8,128)(2,1)}, bf16[256,1024]{1,0:T(8,128)(2,1)S(1)}, u32[]{:S(2)}, u32[]{:S(2)}) %collective-permute-start.9) | collective-permute-done | bytes 524320 | tf_op jit(solution)/shard_map/ppermute | solution.py:26
  38.5 0.4 collective-permute-done.6.refs_0_.g.refs_1_.refs_3_
  38.9 0.4 shard_map.100
  39.4 0.9 %shard_map.98 = (f32[3,8,256]{2,1,0:T(8,128)S(1)}, f32[8,256,256]{2,1,0:T(8,128)S(1)}, f32[3,8,256]{2,1,0:T(8,128)S(1)}, f32[8,256,256]{2,1,0:T(8,128)S(1)}) custom-call(bf16[256,1024]{1,0:T(8,128)(2,1)S(1)} %collective-permute-done.6.refs_0_.g.refs_1_.refs_3_, ...), custom_call_target="tpu_custom_call", output_to_operand_aliasing={{2}: (7, {}), {3}: (8, {})} | custom-call | flops 268435456 | tf_op jit(solution)/shard_map/pallas_call | solution.py:51
  40.3 1.6 %collective-permute-done.8.refs_0_ = f32[4,8,256]{2,1,0:T(8,128)S(1)} collective-permute-done((f32[4,8,256]{2,1,0:T(8,128)S(1)}, f32[4,8,256]{2,1,0:T(8,128)S(1)}, u32[]{:S(2)}, u32[]{:S(2)}) %collective-permute-start.8) | collective-permute-done | bytes 32800 | tf_op jit(solution)/shard_map/ppermute | solution.py:26
  41.8 0.1 shard_map.101
  41.9 3.7 %collective-permute-start.10 = (f32[3,8,256]{2,1,0:T(8,128)S(1)}, f32[3,8,256]{2,1,0:T(8,128)S(1)}, u32[]{:S(2)}, u32[]{:S(2)}) collective-permute-start(f32[3,8,256]{2,1,0:T(8,128)S(1)} %get-tuple-element.77), channel_id=1, source_target_pairs={{0,8},{4,12},{8,16},{12,20},{16,24},{20,28},{1,9},{5,13},{9,17},{1... | collective-permute-start | bytes 73736 | tf_op jit(solution)/shard_map/ppermute | solution.py:26
  45.7 0.4 shard_map.107
  46.0 0.4 shard_map.103
  46.4 0.5 shard_map.105
  46.9 0.2 collective-permute-done.10.refs_3_
  47.2 0.4 shard_map.108
  47.6 0.6 shard_map.104
  48.1 0.6 shard_map.106
  48.7 0.4 shard_map.109
  49.1 0.6 shard_map.110
  49.7 0.4 shard_map.111
  50.1 4.2 %collective-permute-start.11 = (bf16[256,1024]{1,0:T(8,128)(2,1)S(1)}, bf16[256,1024]{1,0:T(8,128)(2,1)S(1)}, u32[]{:S(2)}, u32[]{:S(2)}) collective-permute-start(bf16[256,1024]{1,0:T(8,128)(2,1)S(1)} %get-tuple-element.100), channel_id=1, source_target_pairs={{0,8},{4,12},{8,16},{12,20},{16,24},{20,28},{1,9},{5,13},{9,17},{1... | collective-permute-start | bytes 1572872 | tf_op jit(solution)/shard_map/ppermute | solution.py:26
  54.4 1.3 %collective-permute-start.14 = (bf16[512,512]{1,0:T(8,128)(2,1)S(1)}, bf16[512,512]{1,0:T(8,128)(2,1)S(1)}, u32[]{:S(2)}, u32[]{:S(2)}) collective-permute-start(bf16[512,512]{1,0:T(8,128)(2,1)S(1)} %get-tuple-element.109), channel_id=1, source_target_pairs={{8,0},{12,4},{16,8},{20,12},{24,16},{28,20},{9,1},{13,5},{17,9},{2... | collective-permute-start | bytes 1572872 | tf_op jit(solution)/shard_map/ppermute | solution.py:26
  55.7 2.1 %collective-permute-start.15 = (bf16[512,512]{1,0:T(8,128)(2,1)S(1)}, bf16[512,512]{1,0:T(8,128)(2,1)S(1)}, u32[]{:S(2)}, u32[]{:S(2)}) collective-permute-start(bf16[512,512]{1,0:T(8,128)(2,1)S(1)} %get-tuple-element.110), channel_id=1, source_target_pairs={{0,4},{4,0},{8,12},{12,8},{16,20},{20,16},{24,28},{28,24},{1,5},{5... | collective-permute-start | bytes 1572872 | tf_op jit(solution)/shard_map/ppermute | solution.py:31
  57.8 1.3 %collective-permute-start.16 = (bf16[512,256]{1,0:T(8,128)(2,1)S(1)}, bf16[512,256]{1,0:T(8,128)(2,1)S(1)}, u32[]{:S(2)}, u32[]{:S(2)}) collective-permute-start(bf16[512,256]{1,0:T(8,128)(2,1)S(1)} %get-tuple-element.113), channel_id=1, source_target_pairs={{8,0},{12,4},{16,8},{20,12},{24,16},{28,20},{9,1},{13,5},{17,9},{2... | collective-permute-start | bytes 786440 | tf_op jit(solution)/shard_map/ppermute | solution.py:26
  59.0 0.1 collective-permute-start.17
  59.1 13.7 %collective-permute-done.16.refs_4_ = bf16[512,256]{1,0:T(8,128)(2,1)S(1)} collective-permute-done((bf16[512,256]{1,0:T(8,128)(2,1)S(1)}, bf16[512,256]{1,0:T(8,128)(2,1)S(1)}, u32[]{:S(2)}, u32[]{:S(2)}) %collective-permute-start.16) | collective-permute-done | bytes 262176 | tf_op jit(solution)/shard_map/ppermute | solution.py:26
  72.8 1.3 %collective-permute-start.12 = (bf16[512,256]{1,0:T(8,128)(2,1)S(1)}, bf16[512,256]{1,0:T(8,128)(2,1)S(1)}, u32[]{:S(2)}, u32[]{:S(2)}) collective-permute-start(bf16[512,256]{1,0:T(8,128)(2,1)S(1)} %get-tuple-element.105), channel_id=1, source_target_pairs={{8,0},{12,4},{16,8},{20,12},{24,16},{28,20},{9,1},{13,5},{17,9},{2... | collective-permute-start | bytes 786440 | tf_op jit(solution)/shard_map/ppermute | solution.py:26
  74.1 2.1 %collective-permute-start.13 = (bf16[512,256]{1,0:T(8,128)(2,1)S(1)}, bf16[512,256]{1,0:T(8,128)(2,1)S(1)}, u32[]{:S(2)}, u32[]{:S(2)}) collective-permute-start(bf16[512,256]{1,0:T(8,128)(2,1)S(1)} %get-tuple-element.106), channel_id=1, source_target_pairs={{0,4},{4,0},{8,12},{12,8},{16,20},{20,16},{24,28},{28,24},{1,5},{5... | collective-permute-start | bytes 786440 | tf_op jit(solution)/shard_map/ppermute | solution.py:31
  76.2 1.0 %shard_map.112 = (f32[256,1024]{1,0:T(8,128)S(1)}, f32[256,1024]{1,0:T(8,128)S(1)}, f32[256,1024]{1,0:T(8,128)S(1)}) custom-call(bf16[256,1024]{1,0:T(8,128)(2,1)S(1)} %get-tuple-element.62.refs_0_.q, bf16[256,1024]{1,0:T(8,128)(2,1)S(1)} %shard_map.94.refs_1_.refs_0_.g, bf16[256,1024]{1,0:T(8,128)(2,1)S(1)} %get-tuple-element.63.refs_2_.k, ...), custom_call_target="tpu_custom_call" | custom-call | flops 402653184 | tf_op jit(solution)/shard_map/pallas_call | solution.py:51
  77.1 0.8 shard_map.114
  77.9 1.4 %shard_map.113 = bf16[256,1024]{1,0:T(8,128)(2,1)} custom-call(f32[256,1024]{1,0:T(8,128)S(1)} %get-tuple-element.99.dq, bf16[256,1024]{1,0:T(8,128)(2,1)S(1)} %collective-permute-done.11.guest), custom_call_target="tpu_custom_call" | custom-call | flops 524288 | tf_op jit(solution)/shard_map/pallas_call | solution.py:51
  79.4 0.9 %shard_map.115 = (bf16[256,1024]{1,0:T(8,128)(2,1)}, bf16[256,1024]{1,0:T(8,128)(2,1)}) custom-call(f32[256,1024]{1,0:T(8,128)S(1)} %get-tuple-element.101.refs_0_, f32[256,1024]{1,0:T(8,128)S(1)} %get-tuple-element.102.refs_1_, f32[256,512]{1,0:T(8,128)S(1)} %get-tuple-element.107.refs_2_, ...), custom_call_target="tpu_custom_call", output_to_operand_aliasing={{0}: (6, {}), {1}: (7, {})} | custom-call | flops 33554432 | tf_op jit(solution)/shard_map/pallas_call | solution.py:51
  80.3 0.8 collective-permute-done.12.refs_4_
  81.0 0.8 shard_map.116
  (16 shorter events, 0.1 us)
Async XLA Ops:
  0.6 24.5 %copy-start.1 = (s32[1,3]{1,0:T(1,128)S(1)}, s32[1,3]{1,0:T(1,128)}, u32[]{:S(2)}) copy-start(s32[1,3]{1,0:T(1,128)} %refs_1_.3) | copy-start | bytes 40
  0.6 24.5 %copy-start = (s32[8,3]{0,1:T(4,128)S(1)}, s32[8,3]{0,1:T(4,128)}, u32[]{:S(2)}) copy-start(s32[8,3]{0,1:T(4,128)} %param.12) | copy-start | bytes 292
  0.7 9.6 %collective-permute-start.1 = (bf16[256,512]{1,0:T(8,128)(2,1)}, bf16[256,512]{1,0:T(8,128)(2,1)S(1)}, u32[]{:S(2)}, u32[]{:S(2)}) collective-permute-start(bf16[256,512]{1,0:T(8,128)(2,1)} %refs_3_.1), channel_id=1, source_target_pairs={{0,2},{1,3},{2,0},{3,1},{4,6},{5,7},{6,4},{7,5},{8,10},{9,11},{10,... | collective-permute-start | bytes 786440 | tf_op jit(solution)/shard_map/ppermute | solution.py:31
  3.7 20.1 %collective-permute-start.3 = (bf16[256,1024]{1,0:T(8,128)(2,1)}, bf16[256,1024]{1,0:T(8,128)(2,1)S(1)}, u32[]{:S(2)}, u32[]{:S(2)}) collective-permute-start(bf16[256,1024]{1,0:T(8,128)(2,1)} %refs_0_.1), channel_id=1, source_target_pairs={{8,0},{12,4},{16,8},{20,12},{24,16},{28,20},{9,1},{13,5},{17,9},{2... | collective-permute-start | bytes 1572872 | tf_op jit(solution)/shard_map/ppermute | solution.py:26
  5.0 10.5 %collective-permute-start = (bf16[256,512]{1,0:T(8,128)(2,1)}, bf16[256,512]{1,0:T(8,128)(2,1)S(1)}, u32[]{:S(2)}, u32[]{:S(2)}) collective-permute-start(bf16[256,512]{1,0:T(8,128)(2,1)} %refs_3_.1), channel_id=1, source_target_pairs={{0,1},{1,0},{2,3},{3,2},{4,5},{5,4},{6,7},{7,6},{8,9},{9,8},{10,11... | collective-permute-start | bytes 786440 | tf_op jit(solution)/shard_map/ppermute | solution.py:31
  10.2 8.7 %collective-permute-start.2 = (bf16[256,512]{1,0:T(8,128)(2,1)S(1)}, bf16[256,512]{1,0:T(8,128)(2,1)S(1)}, u32[]{:S(2)}, u32[]{:S(2)}) collective-permute-start(bf16[256,512]{1,0:T(8,128)(2,1)S(1)} %collective-permute-done.1.refs_1_), channel_id=1, source_target_pairs={{0,1},{1,0},{2,3},{3,2},{4,5},{5,4},{6,7},{7,6},{8,9},{9,8},{10,11... | collective-permute-start | bytes 786440 | tf_op jit(solution)/shard_map/ppermute | solution.py:31
  10.2 16.9 %collective-permute-start.5 = (bf16[256,1024]{1,0:T(8,128)(2,1)}, bf16[256,1024]{1,0:T(8,128)(2,1)S(1)}, u32[]{:S(2)}, u32[]{:S(2)}) collective-permute-start(bf16[256,1024]{1,0:T(8,128)(2,1)} %refs_1_.2), channel_id=1, source_target_pairs={{0,4},{4,0},{8,12},{12,8},{16,20},{20,16},{24,28},{28,24},{1,5},{5... | collective-permute-start | bytes 1572872 | tf_op jit(solution)/shard_map/ppermute | solution.py:31
  11.9 16.1 %collective-permute-start.4 = (bf16[256,1024]{1,0:T(8,128)(2,1)}, bf16[256,1024]{1,0:T(8,128)(2,1)S(1)}, u32[]{:S(2)}, u32[]{:S(2)}) collective-permute-start(bf16[256,1024]{1,0:T(8,128)(2,1)} %refs_1_.2), channel_id=1, source_target_pairs={{0,8},{4,12},{8,16},{12,20},{16,24},{20,28},{1,9},{5,13},{9,17},{1... | collective-permute-start | bytes 1572872 | tf_op jit(solution)/shard_map/ppermute | solution.py:26
  15.5 23.1 %collective-permute-start.9 = (bf16[256,1024]{1,0:T(8,128)(2,1)}, bf16[256,1024]{1,0:T(8,128)(2,1)S(1)}, u32[]{:S(2)}, u32[]{:S(2)}) collective-permute-start(bf16[256,1024]{1,0:T(8,128)(2,1)} %refs_2_.1), channel_id=1, source_target_pairs={{0,8},{4,12},{8,16},{12,20},{16,24},{20,28},{1,9},{5,13},{9,17},{1... | collective-permute-start | bytes 1572872 | tf_op jit(solution)/shard_map/ppermute | solution.py:26
  19.0 17.0 %collective-permute-start.7 = (bf16[256,1024]{1,0:T(8,128)(2,1)}, bf16[256,1024]{1,0:T(8,128)(2,1)S(1)}, u32[]{:S(2)}, u32[]{:S(2)}) collective-permute-start(bf16[256,1024]{1,0:T(8,128)(2,1)} %refs_2_.1), channel_id=1, source_target_pairs={{0,4},{4,0},{8,12},{12,8},{16,20},{20,16},{24,28},{28,24},{1,5},{5... | collective-permute-start | bytes 1572872 | tf_op jit(solution)/shard_map/ppermute | solution.py:31
  23.8 15.1 %collective-permute-start.6 = (bf16[256,1024]{1,0:T(8,128)(2,1)S(1)}, bf16[256,1024]{1,0:T(8,128)(2,1)S(1)}, u32[]{:S(2)}, u32[]{:S(2)}) collective-permute-start(bf16[256,1024]{1,0:T(8,128)(2,1)S(1)} %shard_map.94.refs_1_.refs_0_.g), channel_id=1, source_target_pairs={{8,0},{12,4},{16,8},{20,12},{24,16},{28,20},{9,1},{13,5},{17,9},{2... | collective-permute-start | bytes 1572872 | tf_op jit(solution)/shard_map/ppermute | solution.py:26
  36.0 5.8 %collective-permute-start.8 = (f32[4,8,256]{2,1,0:T(8,128)S(1)}, f32[4,8,256]{2,1,0:T(8,128)S(1)}, u32[]{:S(2)}, u32[]{:S(2)}) collective-permute-start(f32[4,8,256]{2,1,0:T(8,128)S(1)} %shard_map.99), channel_id=1, source_target_pairs={{8,0},{12,4},{16,8},{20,12},{24,16},{28,20},{9,1},{13,5},{17,9},{2... | collective-permute-start | bytes 98312 | tf_op jit(solution)/shard_map/ppermute | solution.py:26
  41.9 5.2 %collective-permute-start.10 = (f32[3,8,256]{2,1,0:T(8,128)S(1)}, f32[3,8,256]{2,1,0:T(8,128)S(1)}, u32[]{:S(2)}, u32[]{:S(2)}) collective-permute-start(f32[3,8,256]{2,1,0:T(8,128)S(1)} %get-tuple-element.77), channel_id=1, source_target_pairs={{0,8},{4,12},{8,16},{12,20},{16,24},{20,28},{1,9},{5,13},{9,17},{1... | collective-permute-start | bytes 73736 | tf_op jit(solution)/shard_map/ppermute | solution.py:26
  50.1 27.8 %collective-permute-start.11 = (bf16[256,1024]{1,0:T(8,128)(2,1)S(1)}, bf16[256,1024]{1,0:T(8,128)(2,1)S(1)}, u32[]{:S(2)}, u32[]{:S(2)}) collective-permute-start(bf16[256,1024]{1,0:T(8,128)(2,1)S(1)} %get-tuple-element.100), channel_id=1, source_target_pairs={{0,8},{4,12},{8,16},{12,20},{16,24},{20,28},{1,9},{5,13},{9,17},{1... | collective-permute-start | bytes 1572872 | tf_op jit(solution)/shard_map/ppermute | solution.py:26
  54.4 25.0 %collective-permute-start.14 = (bf16[512,512]{1,0:T(8,128)(2,1)S(1)}, bf16[512,512]{1,0:T(8,128)(2,1)S(1)}, u32[]{:S(2)}, u32[]{:S(2)}) collective-permute-start(bf16[512,512]{1,0:T(8,128)(2,1)S(1)} %get-tuple-element.109), channel_id=1, source_target_pairs={{8,0},{12,4},{16,8},{20,12},{24,16},{28,20},{9,1},{13,5},{17,9},{2... | collective-permute-start | bytes 1572872 | tf_op jit(solution)/shard_map/ppermute | solution.py:26
  55.7 23.7 %collective-permute-start.15 = (bf16[512,512]{1,0:T(8,128)(2,1)S(1)}, bf16[512,512]{1,0:T(8,128)(2,1)S(1)}, u32[]{:S(2)}, u32[]{:S(2)}) collective-permute-start(bf16[512,512]{1,0:T(8,128)(2,1)S(1)} %get-tuple-element.110), channel_id=1, source_target_pairs={{0,4},{4,0},{8,12},{12,8},{16,20},{20,16},{24,28},{28,24},{1,5},{5... | collective-permute-start | bytes 1572872 | tf_op jit(solution)/shard_map/ppermute | solution.py:31
  57.8 15.0 %collective-permute-start.16 = (bf16[512,256]{1,0:T(8,128)(2,1)S(1)}, bf16[512,256]{1,0:T(8,128)(2,1)S(1)}, u32[]{:S(2)}, u32[]{:S(2)}) collective-permute-start(bf16[512,256]{1,0:T(8,128)(2,1)S(1)} %get-tuple-element.113), channel_id=1, source_target_pairs={{8,0},{12,4},{16,8},{20,12},{24,16},{28,20},{9,1},{13,5},{17,9},{2... | collective-permute-start | bytes 786440 | tf_op jit(solution)/shard_map/ppermute | solution.py:26
  59.0 15.0 %collective-permute-start.17 = (bf16[512,256]{1,0:T(8,128)(2,1)S(1)}, bf16[512,256]{1,0:T(8,128)(2,1)S(1)}, u32[]{:S(2)}, u32[]{:S(2)}) collective-permute-start(bf16[512,256]{1,0:T(8,128)(2,1)S(1)} %get-tuple-element.114), channel_id=1, source_target_pairs={{0,4},{4,0},{8,12},{12,8},{16,20},{20,16},{24,28},{28,24},{1,5},{5... | collective-permute-start | bytes 786440 | tf_op jit(solution)/shard_map/ppermute | solution.py:31
  72.8 8.3 %collective-permute-start.12 = (bf16[512,256]{1,0:T(8,128)(2,1)S(1)}, bf16[512,256]{1,0:T(8,128)(2,1)S(1)}, u32[]{:S(2)}, u32[]{:S(2)}) collective-permute-start(bf16[512,256]{1,0:T(8,128)(2,1)S(1)} %get-tuple-element.105), channel_id=1, source_target_pairs={{8,0},{12,4},{16,8},{20,12},{24,16},{28,20},{9,1},{13,5},{17,9},{2... | collective-permute-start | bytes 786440 | tf_op jit(solution)/shard_map/ppermute | solution.py:26
  74.1 7.0 %collective-permute-start.13 = (bf16[512,256]{1,0:T(8,128)(2,1)S(1)}, bf16[512,256]{1,0:T(8,128)(2,1)S(1)}, u32[]{:S(2)}, u32[]{:S(2)}) collective-permute-start(bf16[512,256]{1,0:T(8,128)(2,1)S(1)} %get-tuple-element.106), channel_id=1, source_target_pairs={{0,4},{4,0},{8,12},{12,8},{16,20},{20,16},{24,28},{28,24},{1,5},{5... | collective-permute-start | bytes 786440 | tf_op jit(solution)/shard_map/ppermute | solution.py:31
